TPU v7x, 32 devices: a whole 2x2x4 slice. The times are simulated.
32 devices in a mesh: context: 4 (over x, core), fsdp: 8 (over z, y).
Axes of the slice: x: 2, y: 2, z: 4, core: 2. Of those that a mesh axis runs over, the one named last changes fastest.
Arguments:
- tokens: bfloat16 [8, 2048, 2048], P('fsdp', 'context'), may hold values from -6 to 6
- segment_ids: int32 [8, 2048], P('fsdp', 'context'), may hold values from 0 to 3, as said below
- norm1_gain: bfloat16 [2048], P('fsdp'), may hold values from 0.5 to 1.5
- w_query: bfloat16 [2048, 256], P('fsdp'), may hold values from -0.125 to 0.125
- w_key: bfloat16 [2048, 256], P('fsdp'), may hold values from -0.125 to 0.125
- w_value: bfloat16 [2048, 2048], P('fsdp'), may hold values from -0.125 to 0.125
- w_out: bfloat16 [2048, 2048], P('fsdp'), may hold values from -1 to 1
- norm2_gain: bfloat16 [2048], P('fsdp'), may hold values from 0.5 to 1.5
- w_gate: bfloat16 [2048, 5632], P('fsdp'), may hold values from -0.125 to 0.125
- w_up: bfloat16 [2048, 5632], P('fsdp'), may hold values from -0.125 to 0.125
- w_down: bfloat16 [5632, 2048], P('fsdp'), may hold values from -0.078125 to 0.078125
- cotangent: bfloat16 [8, 2048, 2048], P('fsdp', 'context'), may hold values from -6 to 6
Outputs:
- block_out: bfloat16 [8, 2048, 2048], P('fsdp', 'context')
- input_grad: float32 [8, 2048, 2048], P('fsdp', 'context')
- grad_norm1_gain: float32 [2048], P('fsdp')
- grad_w_query: float32 [2048, 256], P('fsdp')
- grad_w_key: float32 [2048, 256], P('fsdp')
- grad_w_value: float32 [2048, 2048], P('fsdp')
- grad_w_out: float32 [2048, 2048], P('fsdp')
- grad_norm2_gain: float32 [2048], P('fsdp')
- grad_w_gate: float32 [2048, 5632], P('fsdp')
- grad_w_up: float32 [2048, 5632], P('fsdp')
- grad_w_down: float32 [5632, 2048], P('fsdp')
Inputs may be any that keep to these rules, and one draw needn't show every extreme that they name: `segment_ids`: within each sequence the ids start at 0, never fall and step by one; there are 4 documents of 200 to 1024 tokens, one of exactly 1024.
All inputs are finite; a program needn't handle non-finite values.
Results may differ from a plain program's by a relative error of at most 0.019.
Values may be sent and summed in bfloat16 or wider, within the bound.
No kernel may reach another device: no remote copies, remote signals or barrier semaphores. Data moves between devices by JAX's collectives and lax.ppermute only.
A program may use at most 448 MiB of HBM per device.

v0:
```python
import jax
import jax.numpy as jnp
from jax import lax
from jax.sharding import PartitionSpec as P

HEADS = 16
QK = 16
VH = 128
BLOCK = 512


EPS = 1e-05
HIGHEST = lax.Precision.HIGHEST


def entering(value, axis, combine, identity):
    peers, here = (lax.axis_size(axis), lax.axis_index(axis))
    everything = jax.tree.map(
        lambda part, kind: lax.all_gather(part.astype(kind), axis),
        value,
        (
            jnp.bfloat16,
            jnp.bfloat16,
            jnp.bfloat16,
            jnp.bfloat16,
            jnp.bfloat16,
            jnp.bfloat16,
            jnp.bfloat16,
        ),
    )
    start = jax.tree.map(
        lambda part, zero: jnp.broadcast_to(jnp.asarray(zero, part.dtype), part.shape),
        value,
        identity,
    )

    def turn(k, before):
        reached = k < here
        new = combine(
            before, jax.tree.map(lambda part, own: part[k].astype(own.dtype), everything, value)
        )
        return jax.tree.map(lambda a, b: jnp.where(reached, a, b), new, before)

    return lax.fori_loop(0, peers, turn, start)


def entering_2(value, axis, combine, identity):
    peers, here = (lax.axis_size(axis), lax.axis_index(axis))
    everything = jax.tree.map(
        lambda part, kind: lax.all_gather(part.astype(kind), axis),
        value,
        jax.tree.map(lambda a: jnp.bfloat16 if a.dtype == jnp.float32 else a.dtype, value),
    )
    start = jax.tree.map(
        lambda part, zero: jnp.broadcast_to(jnp.asarray(zero, part.dtype), part.shape),
        value,
        identity,
    )

    def turn(k, before):
        at = peers - 1 - k
        reached = at > here
        new = combine(
            before, jax.tree.map(lambda part, own: part[at].astype(own.dtype), everything, value)
        )
        return jax.tree.map(lambda a, b: jnp.where(reached, a, b), new, before)

    return lax.fori_loop(0, peers, turn, start)


def rms_scale(values):
    return lax.rsqrt(jnp.mean(values * values, axis=-1, keepdims=True) + EPS)


def feature_maps(vectors):
    feature_width = vectors.shape[-1]
    linear = vectors * feature_width ** (-0.25)
    square = (vectors[:, :, :, None] * vectors[:, :, None, :]).reshape(
        vectors.shape[0], vectors.shape[1], feature_width * feature_width
    )
    return (linear, square * (2.0 * feature_width) ** (-0.5))


def feature_back(vectors, grad_linear, grad_square):
    feature_width = vectors.shape[-1]
    outer_grad = grad_square.reshape(
        vectors.shape[0], vectors.shape[1], feature_width, feature_width
    )
    paired = outer_grad + jnp.swapaxes(outer_grad, 2, 3)
    folded = jnp.sum(paired * vectors[:, :, None, :], axis=-1)
    return grad_linear * feature_width ** (-0.25) + folded * (2.0 * feature_width) ** (-0.5)


def combine_states(earlier, later):
    joined = jnp.logical_or(later[-1] < 0.0, earlier[-1] == later[-1]).astype(jnp.float32)[0]
    summed = tuple(
        (
            later_part + joined * earlier_part
            for earlier_part, later_part in zip(earlier[:-1], later[:-1])
        )
    )
    return summed + (jnp.where(later[-1] < 0.0, earlier[-1], later[-1]),)


def empty_like(members):
    return tuple((jnp.zeros_like(member) for member in members[:-1])) + (
        jnp.full((1,), -1.0, jnp.float32),
    )


def block_scores(block_index, queries, key_heads, segments):
    first_row = block_index * BLOCK
    position_rows = first_row + jnp.arange(BLOCK, dtype=jnp.int32)
    positions = jnp.arange(key_heads.shape[0], dtype=jnp.int32)
    allowed = jnp.logical_and(
        positions[None, :] <= position_rows[:, None], segments[None, :] == segments[:, None]
    )
    scores = jnp.einsum("thd,uhd->htu", queries, key_heads, precision=HIGHEST) * QK ** (-0.5)
    return (queries, scores, allowed[None])


def local(
    tokens,
    segment_ids,
    norm1_gain,
    w_query,
    w_key,
    w_value,
    w_out,
    norm2_gain,
    w_gate,
    w_up,
    w_down,
    cotangent,
):
    inputs = tokens[0].astype(jnp.float32)
    segments = segment_ids[0]
    rows_here = inputs.shape[0]
    gain_one, query_full, key_full, value_full, out_full = (
        lax.all_gather(norm1_gain, "fsdp", axis=0, tiled=True),
        lax.all_gather(w_query, "fsdp", axis=0, tiled=True),
        lax.all_gather(w_key, "fsdp", axis=0, tiled=True),
        lax.all_gather(w_value, "fsdp", axis=0, tiled=True),
        lax.all_gather(w_out, "fsdp", axis=0, tiled=True),
    )
    gain_two, gate_full, up_full, down_full = (
        lax.all_gather(norm2_gain, "fsdp", axis=0, tiled=True),
        lax.all_gather(w_gate, "fsdp", axis=0, tiled=True),
        lax.all_gather(w_up, "fsdp", axis=0, tiled=True),
        lax.all_gather(w_down, "fsdp", axis=0, tiled=True),
    )
    gain_one = gain_one.astype(jnp.float32)
    gain_two = gain_two.astype(jnp.float32)
    scale_one = rms_scale(inputs)
    unit_one = inputs * scale_one
    normed_one = (unit_one * gain_one).astype(jnp.bfloat16)
    query_low = jnp.dot(normed_one, query_full, preferred_element_type=jnp.float32).astype(
        jnp.bfloat16
    )
    key_low = jnp.dot(normed_one, key_full, preferred_element_type=jnp.float32).astype(jnp.bfloat16)
    value_low = jnp.dot(normed_one, value_full, preferred_element_type=jnp.float32).astype(
        jnp.bfloat16
    )
    query_heads = query_low.astype(jnp.float32).reshape(rows_here, HEADS, QK)
    key_heads = key_low.astype(jnp.float32).reshape(rows_here, HEADS, QK)
    value_heads = value_low.astype(jnp.float32).reshape(rows_here, HEADS, VH)
    block_ids = jnp.arange(rows_here // BLOCK, dtype=jnp.int32)

    def forward_block(block_index):
        query_rows, scores, allowed = block_scores(block_index, query_heads, key_heads, segments)
        weight = jnp.where(allowed, 1.0 + scores + 0.5 * scores * scores, 0.0)
        numerator = jnp.einsum("htu,uhv->thv", weight, value_heads, precision=HIGHEST)
        return (numerator, jnp.transpose(jnp.sum(weight, axis=-1)))

    numerator_blocks, denominator_blocks = lax.map(forward_block, block_ids)
    numerator_local = numerator_blocks.reshape(rows_here, HEADS, VH)
    denominator_local = denominator_blocks.reshape(rows_here, HEADS)
    tail_id = segments[-1]
    own_mask = (segments == tail_id).astype(jnp.float32)
    key_linear, key_square = feature_maps(key_heads)
    query_linear, query_square = feature_maps(query_heads)
    masked_linear = key_linear * own_mask[:, None, None]
    masked_square = key_square * own_mask[:, None, None]
    state_base = jnp.einsum("t,thv->hv", own_mask, value_heads, precision=HIGHEST)
    state_linear = jnp.einsum("thi,thv->hiv", masked_linear, value_heads, precision=HIGHEST)
    state_square = jnp.einsum("thi,thv->hiv", masked_square, value_heads, precision=HIGHEST)
    count_base = jnp.sum(own_mask) * jnp.ones((HEADS,), jnp.float32)
    count_linear = jnp.sum(masked_linear, axis=0)
    count_square = jnp.sum(masked_square, axis=0)
    tail_key = tail_id.astype(jnp.float32).reshape(1)
    forward_identity = empty_like(
        (state_base, state_linear, state_square, count_base, count_linear, count_square, tail_key)
    )
    carry_base, carry_linear, carry_square, total_base, total_linear, total_square, carry_key = (
        entering(
            (
                state_base,
                state_linear,
                state_square,
                count_base,
                count_linear,
                count_square,
                tail_key,
            ),
            "context",
            combine_states,
            forward_identity,
        )
    )
    carry_mask = (segments.astype(jnp.float32) == carry_key[0]).astype(jnp.float32)
    carry_numerator = (
        carry_base[None]
        + jnp.einsum("thi,hiv->thv", query_linear, carry_linear, precision=HIGHEST)
        + jnp.einsum("thi,hiv->thv", query_square, carry_square, precision=HIGHEST)
    )
    carry_denominator = (
        total_base[None]
        + jnp.einsum("thi,hi->th", query_linear, total_linear, precision=HIGHEST)
        + jnp.einsum("thi,hi->th", query_square, total_square, precision=HIGHEST)
    )
    numerator = numerator_local + carry_mask[:, None, None] * carry_numerator
    denominator = denominator_local + carry_mask[:, None] * carry_denominator
    mixed = numerator / denominator[:, :, None]
    mixed_low = mixed.reshape(rows_here, HEADS * VH).astype(jnp.bfloat16)
    residual = inputs + jnp.dot(mixed_low, out_full, preferred_element_type=jnp.float32)
    scale_two = rms_scale(residual)
    unit_two = residual * scale_two
    normed_two = (unit_two * gain_two).astype(jnp.bfloat16)
    gate_pre = jnp.dot(normed_two, gate_full, preferred_element_type=jnp.float32)
    up_pre = jnp.dot(normed_two, up_full, preferred_element_type=jnp.float32)
    sigmoid_gate = jax.nn.sigmoid(gate_pre)
    silu_gate = jax.nn.silu(gate_pre)
    hidden_low = (silu_gate * up_pre).astype(jnp.bfloat16)
    outputs = residual + jnp.dot(hidden_low, down_full, preferred_element_type=jnp.float32)
    block_out = outputs.astype(jnp.bfloat16)[None]
    grad_top = cotangent[0]
    grad_w_down = jnp.einsum("tf,td->fd", hidden_low, grad_top, preferred_element_type=jnp.float32)
    grad_hidden = jnp.einsum("td,fd->tf", grad_top, down_full, preferred_element_type=jnp.float32)
    grad_gate = (
        grad_hidden * up_pre * sigmoid_gate * (1.0 + gate_pre * (1.0 - sigmoid_gate))
    ).astype(jnp.bfloat16)
    grad_up = (grad_hidden * silu_gate).astype(jnp.bfloat16)
    grad_w_gate = jnp.einsum("td,tf->df", normed_two, grad_gate, preferred_element_type=jnp.float32)
    grad_w_up = jnp.einsum("td,tf->df", normed_two, grad_up, preferred_element_type=jnp.float32)
    grad_normed_two = jnp.einsum(
        "tf,df->td", grad_gate, gate_full, preferred_element_type=jnp.float32
    ) + jnp.einsum("tf,df->td", grad_up, up_full, preferred_element_type=jnp.float32)
    grad_gain_two = jnp.sum(grad_normed_two * unit_two, axis=0)
    gained_two = grad_normed_two * gain_two
    grad_residual = grad_top.astype(jnp.float32) + scale_two * (
        gained_two - unit_two * jnp.mean(gained_two * unit_two, axis=-1, keepdims=True)
    )
    grad_branch = grad_residual.astype(jnp.bfloat16)
    grad_w_out = jnp.einsum("tv,td->vd", mixed_low, grad_branch, preferred_element_type=jnp.float32)
    grad_mixed = jnp.einsum(
        "td,vd->tv", grad_branch, out_full, preferred_element_type=jnp.float32
    ).reshape(rows_here, HEADS, VH)
    grad_numerator = grad_mixed / denominator[:, :, None]
    grad_denominator = -jnp.sum(grad_mixed * mixed, axis=-1) / denominator

    def backward_block(sums, block_index):
        query_rows, scores, allowed = block_scores(block_index, query_heads, key_heads, segments)
        weight = jnp.where(allowed, 1.0 + scores + 0.5 * scores * scores, 0.0)
        grad_weight = (
            jnp.einsum("thv,uhv->htu", grad_numerator, value_heads, precision=HIGHEST)
            + jnp.transpose(grad_denominator)[:, :, None]
        )
        grad_scores = jnp.where(allowed, grad_weight * (1.0 + scores), 0.0) * QK ** (-0.5)
        grad_query_rows = jnp.einsum("htu,uhd->thd", grad_scores, key_heads, precision=HIGHEST)
        key_sum = sums[0] + jnp.einsum("htu,thd->uhd", grad_scores, query_rows, precision=HIGHEST)
        value_sum = sums[1] + jnp.einsum("htu,thv->uhv", weight, grad_numerator, precision=HIGHEST)
        return ((key_sum, value_sum), grad_query_rows)

    local_sums, grad_query_blocks = lax.scan(
        backward_block, (jnp.zeros_like(key_heads), jnp.zeros_like(value_heads)), block_ids
    )
    grad_key_local, grad_value_local = local_sums
    grad_query_local = grad_query_blocks.reshape(rows_here, HEADS, QK)
    grad_query_linear = carry_mask[:, None, None] * (
        jnp.einsum("hiv,thv->thi", carry_linear, grad_numerator, precision=HIGHEST)
        + total_linear[None] * grad_denominator[:, :, None]
    )
    grad_query_square = carry_mask[:, None, None] * (
        jnp.einsum("hiv,thv->thi", carry_square, grad_numerator, precision=HIGHEST)
        + total_square[None] * grad_denominator[:, :, None]
    )
    grad_query = grad_query_local + feature_back(query_heads, grad_query_linear, grad_query_square)
    weighted_linear = query_linear * carry_mask[:, None, None]
    weighted_square = query_square * carry_mask[:, None, None]
    back_base = jnp.einsum("t,thv->hv", carry_mask, grad_numerator, precision=HIGHEST)
    back_linear = jnp.einsum("thi,thv->hiv", weighted_linear, grad_numerator, precision=HIGHEST)
    back_square = jnp.einsum("thi,thv->hiv", weighted_square, grad_numerator, precision=HIGHEST)
    back_count_linear = jnp.einsum(
        "thi,th->hi", weighted_linear, grad_denominator, precision=HIGHEST
    )
    back_count_square = jnp.einsum(
        "thi,th->hi", weighted_square, grad_denominator, precision=HIGHEST
    )
    backward_identity = empty_like(
        (back_base, back_linear, back_square, back_count_linear, back_count_square, carry_key)
    )
    far_base, far_linear, far_square, far_count_linear, far_count_square, far_key = entering_2(
        (back_base, back_linear, back_square, back_count_linear, back_count_square, carry_key),
        "context",
        combine_states,
        backward_identity,
    )
    use_factor = (far_key[0] == tail_key[0]).astype(jnp.float32)
    token_weight = (own_mask * use_factor)[:, None, None]
    grad_value_far = token_weight * (
        far_base[None]
        + jnp.einsum("thi,hiv->thv", key_linear, far_linear, precision=HIGHEST)
        + jnp.einsum("thi,hiv->thv", key_square, far_square, precision=HIGHEST)
    )
    grad_key_linear = token_weight * (
        jnp.einsum("hiv,thv->thi", far_linear, value_heads, precision=HIGHEST)
        + far_count_linear[None]
    )
    grad_key_square = token_weight * (
        jnp.einsum("hiv,thv->thi", far_square, value_heads, precision=HIGHEST)
        + far_count_square[None]
    )
    grad_key = grad_key_local + feature_back(key_heads, grad_key_linear, grad_key_square)
    grad_value = grad_value_local + grad_value_far
    grad_query_low = grad_query.reshape(rows_here, HEADS * QK).astype(jnp.bfloat16)
    grad_key_low = grad_key.reshape(rows_here, HEADS * QK).astype(jnp.bfloat16)
    grad_value_low = grad_value.reshape(rows_here, HEADS * VH).astype(jnp.bfloat16)
    grad_w_query = jnp.einsum(
        "td,tq->dq", normed_one, grad_query_low, preferred_element_type=jnp.float32
    )
    grad_w_key = jnp.einsum(
        "td,tq->dq", normed_one, grad_key_low, preferred_element_type=jnp.float32
    )
    grad_w_value = jnp.einsum(
        "td,tv->dv", normed_one, grad_value_low, preferred_element_type=jnp.float32
    )
    grad_normed_one = jnp.einsum(
        "tq,dq->td", grad_query_low, query_full, preferred_element_type=jnp.float32
    )
    grad_normed_one = grad_normed_one + jnp.einsum(
        "tq,dq->td", grad_key_low, key_full, preferred_element_type=jnp.float32
    )
    grad_normed_one = grad_normed_one + jnp.einsum(
        "tv,dv->td", grad_value_low, value_full, preferred_element_type=jnp.float32
    )
    grad_gain_one = jnp.sum(grad_normed_one * unit_one, axis=0)
    gained_one = grad_normed_one * gain_one
    input_grad = grad_residual + scale_one * (
        gained_one - unit_one * jnp.mean(gained_one * unit_one, axis=-1, keepdims=True)
    )
    shards = (
        lax.psum_scatter(
            grad_gain_one.astype(jnp.bfloat16), "fsdp", scatter_dimension=0, tiled=True
        ).astype(jnp.float32),
        lax.psum_scatter(
            grad_w_query.astype(jnp.bfloat16), "fsdp", scatter_dimension=0, tiled=True
        ).astype(jnp.float32),
        lax.psum_scatter(
            grad_w_key.astype(jnp.bfloat16), "fsdp", scatter_dimension=0, tiled=True
        ).astype(jnp.float32),
        lax.psum_scatter(
            grad_w_value.astype(jnp.bfloat16), "fsdp", scatter_dimension=0, tiled=True
        ).astype(jnp.float32),
        lax.psum_scatter(
            grad_w_out.astype(jnp.bfloat16), "fsdp", scatter_dimension=0, tiled=True
        ).astype(jnp.float32),
        lax.psum_scatter(
            grad_gain_two.astype(jnp.bfloat16), "fsdp", scatter_dimension=0, tiled=True
        ).astype(jnp.float32),
        lax.psum_scatter(
            grad_w_gate.astype(jnp.bfloat16), "fsdp", scatter_dimension=0, tiled=True
        ).astype(jnp.float32),
        lax.psum_scatter(
            grad_w_up.astype(jnp.bfloat16), "fsdp", scatter_dimension=0, tiled=True
        ).astype(jnp.float32),
        lax.psum_scatter(
            grad_w_down.astype(jnp.bfloat16), "fsdp", scatter_dimension=0, tiled=True
        ).astype(jnp.float32),
    )
    totals = (
        lax.psum(shards[0].astype(jnp.bfloat16), "context").astype(jnp.float32),
        lax.psum(shards[1].astype(jnp.bfloat16), "context").astype(jnp.float32),
        lax.psum(shards[2].astype(jnp.bfloat16), "context").astype(jnp.float32),
        lax.psum(shards[3].astype(jnp.bfloat16), "context").astype(jnp.float32),
        lax.psum(shards[4].astype(jnp.bfloat16), "context").astype(jnp.float32),
        lax.psum(shards[5].astype(jnp.bfloat16), "context").astype(jnp.float32),
        lax.psum(shards[6].astype(jnp.bfloat16), "context").astype(jnp.float32),
        lax.psum(shards[7].astype(jnp.bfloat16), "context").astype(jnp.float32),
        lax.psum(shards[8].astype(jnp.bfloat16), "context").astype(jnp.float32),
    )
    return (
        block_out,
        input_grad[None],
        totals[0],
        totals[1],
        totals[2],
        totals[3],
        totals[4],
        totals[5],
        totals[6],
        totals[7],
        totals[8],
    )


def solution(mesh):
    return jax.shard_map(
        local,
        mesh=mesh,
        in_specs=(
            P("fsdp", "context", None),
            P("fsdp", "context"),
            P("fsdp"),
            P("fsdp", None),
            P("fsdp", None),
            P("fsdp", None),
            P("fsdp", None),
            P("fsdp"),
            P("fsdp", None),
            P("fsdp", None),
            P("fsdp", None),
            P("fsdp", "context", None),
        ),
        out_specs=(
            P("fsdp", "context", None),
            P("fsdp", "context", None),
            P("fsdp"),
            P("fsdp", None),
            P("fsdp", None),
            P("fsdp", None),
            P("fsdp", None),
            P("fsdp"),
            P("fsdp", None),
            P("fsdp", None),
            P("fsdp", None),
        ),
        check_vma=False,
    )
```

profile of v0, /device:TPU:17, one launch (start us, length us, event | category | flops | bytes accessed | tf_op | source)
XLA Modules:
  0.0 3685.8 jit_solution(2346260351133019788)
XLA Ops:
  10.1 11.8 all-gather.9
  27.2 21.9 all-gather.25.cloned.1.call-done
  56.2 12.1 bitcast_multiply_fusion.2
  68.3 106.9 %all-gather.21.cloned.1.call-done = bf16[2048,2048]{1,0:T(8,128)(2,1)} async-done(((bf16[256,2048]{1,0:T(8,128)(2,1)}), bf16[2048,2048]{1,0:T(8,128)(2,1)}) %all-gather.21.cloned.1.call-update) | async-done | bytes 8388624 | tf_op jit(solution)/shard_map/all_gather | solution.py:143
  175.2 8.4 fusion.58
  196.0 6.4 all-reduce.7
  202.6 11.3 all-gather.10
  214.3 8.7 all_gather.115
  223.0 5.4 all_gather.116
  235.6 8.3 fusion.27
  245.0 5.4 all-gather
  251.6 5.9 all-gather.1
  257.5 21.3 while.18
  280.0 16.0 fusion.28
  296.0 6.0 all-reduce.2
  302.4 12.0 bitcast_multiply_fusion
  314.5 7.5 fusion.124
  324.5 5.5 copy.88
  334.2 12.5 fusion.150
  346.7 31.0 all-gather.27.cloned.1.call-done
  377.7 10.0 multiply_reduce_fusion.4
  390.3 429.9 %all-gather.29.cloned.1.call-done = bf16[2048,5632]{1,0:T(8,128)(2,1)} async-done(((bf16[256,5632]{1,0:T(8,128)(2,1)}), bf16[2048,5632]{1,0:T(8,128)(2,1)}) %all-gather.29.cloned.1.call-update) | async-done | bytes 23068688 | tf_op jit(solution)/shard_map/all_gather | solution.py:148
  820.1 19.1 fusion.153
  839.3 423.4 %all-gather.31.cloned.1.call-done = bf16[2048,5632]{1,0:T(8,128)(2,1)} async-done(((bf16[256,5632]{1,0:T(8,128)(2,1)}), bf16[2048,5632]{1,0:T(8,128)(2,1)}) %all-gather.31.cloned.1.call-update) | async-done | bytes 23068688 | tf_op jit(solution)/shard_map/all_gather | solution.py:149
  1262.7 19.1 fusion.154
  1281.8 423.5 %all-gather.33.cloned.1.call-done = bf16[5632,2048]{1,0:T(8,128)(2,1)} async-done(((bf16[704,2048]{1,0:T(8,128)(2,1)}), bf16[5632,2048]{1,0:T(8,128)(2,1)}) %all-gather.33.cloned.1.call-update) | async-done | bytes 23068688 | tf_op jit(solution)/shard_map/all_gather | solution.py:150
  1705.3 28.4 multiply_convert_fusion
  1733.7 19.6 fusion.155
  1753.3 19.4 multiply_reduce_fusion.1
  1775.9 9.7 fusion.89
  1785.6 5.4 copy.79
  1791.0 5.5 fusion.39
  1796.4 10.7 convolution_convert_fusion.8
  1812.6 10.2 fusion.121
  1822.8 5.8 all-gather.7
  1828.6 5.4 all-gather.3
  1834.0 5.5 all-gather.8
  1842.9 5.9 all-gather.5
  1848.8 10.1 fusion.18
  1858.9 15.4 fusion.17
  1877.0 17.1 select_multiply_fusion
  1894.2 9.3 fusion.83
  1905.8 21.1 while.64
  1926.9 7.9 add_multiply_fusion
  1934.8 15.4 fusion.15
  1952.0 11.8 fusion.84
  1966.7 10.7 convolution_convert_fusion.3
  1978.3 24.5 fusion.26
  2006.3 9.7 add_convert_fusion
  2017.4 7.7 convolution_convert_fusion.4
  2026.7 18.0 convolution_convert_fusion.2
  2044.7 18.3 convolution_convert_fusion.1
  2064.7 18.2 convolution_convert_fusion
  2087.5 98.1 %reduce-scatter.14.cloned.1.call-done = bf16[256,2048]{1,0:T(8,128)(2,1)} async-done(((bf16[2048,2048]{1,0:T(8,128)(2,1)}), bf16[256,2048]{1,0:T(8,128)(2,1)}) %reduce-scatter.14.cloned.1.call-update) | async-done | bytes 1048592 | tf_op jit(solution)/shard_map/reduce_scatter | solution.py:364
  2185.7 150.2 %reduce-scatter.12.cloned.1.call-done = bf16[256,2048]{1,0:T(8,128)(2,1)} async-done(((bf16[2048,2048]{1,0:T(8,128)(2,1)}), bf16[256,2048]{1,0:T(8,128)(2,1)}) %reduce-scatter.12.cloned.1.call-update) | async-done | bytes 1048592 | tf_op jit(solution)/shard_map/reduce_scatter | solution.py:361
  2335.9 375.8 %reduce-scatter.16.cloned.1.call-done = bf16[256,5632]{1,0:T(8,128)(2,1)} async-done(((bf16[2048,5632]{1,0:T(8,128)(2,1)}), bf16[256,5632]{1,0:T(8,128)(2,1)}) %reduce-scatter.16.cloned.1.call-update) | async-done | bytes 2883600 | tf_op jit(solution)/shard_map/reduce_scatter | solution.py:370
  2711.7 375.8 %reduce-scatter.18.cloned.1.call-done = bf16[256,5632]{1,0:T(8,128)(2,1)} async-done(((bf16[2048,5632]{1,0:T(8,128)(2,1)}), bf16[256,5632]{1,0:T(8,128)(2,1)}) %reduce-scatter.18.cloned.1.call-update) | async-done | bytes 2883600 | tf_op jit(solution)/shard_map/reduce_scatter | solution.py:373
  3087.5 375.8 %reduce-scatter.20.cloned.1.call-done = bf16[704,2048]{1,0:T(8,128)(2,1)} async-done(((bf16[5632,2048]{1,0:T(8,128)(2,1)}), bf16[704,2048]{1,0:T(8,128)(2,1)}) %reduce-scatter.20.cloned.1.call-update) | async-done | bytes 2883600 | tf_op jit(solution)/shard_map/reduce_scatter | solution.py:376
  3463.4 19.9 fusion.42
  3483.3 7.1 fusion.157
  3494.4 12.5 all-reduce.5
  3507.1 9.0 all-reduce.6
  3517.3 7.0 fusion.34
  3524.3 137.3 %all-reduce.11.cloned.1.call-done = (bf16[256,256]{1,0:T(8,128)(2,1)}, bf16[256,256]{1,0:T(8,128)(2,1)}, bf16[256,2048]{1,0:T(8,128)(2,1)}, bf16[256,2048]{1,0:T...) async-done(((bf16[256,256]{1,0:T(8,128)(2,1)}, bf16[256,256]{1,0:T(8,128)(2,1)}, bf16[256,2048]{1,0:T(8,128)(2,1)}, ...) | async-done | bytes 11010064 | tf_op jit(solution)/shard_map/psum | solution.py:382
  (317 shorter events, 131.0 us)
Async XLA Ops:
  7.2 41.9 %all-gather.25.cloned.1.call-start = ((), (), s32[]{:S(2)}) async-start(), calls=%async_computation.9 | async-start | bytes 1179648 | tf_op jit(solution)/shard_map/all_gather | solution.py:142
  7.9 167.3 %all-gather.21.cloned.1.call-start = ((), (), s32[]{:S(2)}) async-start(), calls=%async_computation.7 | async-start | bytes 9437184 | tf_op jit(solution)/shard_map/all_gather | solution.py:143
  8.7 219.7 %all-gather.23.cloned.1.call-start = ((), (), s32[]{:S(2)}) async-start(), calls=%async_computation.8 | async-start | bytes 1179648 | tf_op jit(solution)/shard_map/all_gather | solution.py:141
  9.4 248.0 %all-gather.35.cloned.1.call-start = ((), (), s32[]{:S(2)}) async-start(), calls=%async_computation.21 | async-start | bytes 5242880 | tf_op jit(solution)/shard_map/all_gather | solution.py:19
  21.9 206.5 %copy-start.57 = (f32[8,1,256]{2,1,0:T(1,128)}, f32[8,1,256]{2,1,0:T(1,128)S(1)}, u32[]{:S(2)}) copy-start(f32[8,1,256]{2,1,0:T(1,128)S(1)} %convert_element_type.502) | copy-start | bytes 24580
  24.0 204.4 %copy-start.63 = (f32[512]{0:T(512)}, f32[512]{0:T(512)S(1)}, u32[]{:S(2)}) copy-start(f32[512]{0:T(512)S(1)} %add_rsqrt_fusion.1) | copy-start | bytes 6148
  26.6 29.6 copy-start.65
  51.9 198.5 %copy-start.30 = (bf16[512,256]{0,1:T(8,128)(2,1)}, bf16[512,256]{0,1:T(8,128)(2,1)S(1)}, u32[]{:S(2)}) copy-start(bf16[512,256]{0,1:T(8,128)(2,1)S(1)} %get-tuple-element.864) | copy-start | bytes 786436
  56.2 119.0 %copy-start.5 = (bf16[1,512,2048]{2,1,0:T(8,128)(2,1)S(1)}, bf16[1,512,2048]{2,1,0:T(8,128)(2,1)}, u32[]{:S(2)}) copy-start(bf16[1,512,2048]{2,1,0:T(8,128)(2,1)} %param.16) | copy-start | bytes 6291460
  175.2 9.8 copy-start.3
  189.9 187.9 %all-gather.27.cloned.1.call-start = ((), (), s32[]{:S(2)}) async-start(), calls=%async_computation.10 | async-start | bytes 9437184 | tf_op jit(solution)/shard_map/all_gather | solution.py:144
  190.5 12.1 copy-start.69
  190.5 23.4 copy-start.59
  190.5 629.7 %all-gather.29.cloned.1.call-start = ((), (), s32[]{:S(2)}) async-start(), calls=%async_computation.11 | async-start | bytes 25952256 | tf_op jit(solution)/shard_map/all_gather | solution.py:148
  191.1 1071.7 %all-gather.31.cloned.1.call-start = ((), (), s32[]{:S(2)}) async-start(), calls=%async_computation.12 | async-start | bytes 25952256 | tf_op jit(solution)/shard_map/all_gather | solution.py:149
  191.8 1513.5 %all-gather.33.cloned.1.call-start = ((), (), s32[]{:S(2)}) async-start(), calls=%async_computation.13 | async-start | bytes 25952256 | tf_op jit(solution)/shard_map/all_gather | solution.py:150
  192.6 1713.1 %all-gather.37.cloned.1.call-start = ((), (), s32[]{:S(2)}) async-start(), calls=%async_computation.22 | async-start | bytes 5242880 | tf_op jit(solution)/shard_map/all_gather | solution.py:50
  214.1 65.9 %copy-start.53 = (pred[512,512]{0,1:T(8,128)(4,1)}, pred[512,512]{0,1:T(8,128)(4,1)S(1)}, u32[]{:S(2)}) copy-start(pred[512,512]{0,1:T(8,128)(4,1)S(1)} %fusion.91) | copy-start | bytes 786436
  231.2 99.4 %copy-start.32 = (bf16[512,256]{0,1:T(8,128)(2,1)}, bf16[512,256]{0,1:T(8,128)(2,1)S(1)}, u32[]{:S(2)}) copy-start(bf16[512,256]{0,1:T(8,128)(2,1)S(1)} %get-tuple-element.866) | copy-start | bytes 786436
  235.6 8.3 copy-start.11
  278.8 23.3 copy-start.51
  278.8 35.7 copy-start.48
  278.8 51.9 %copy-start.24 = (f32[16,16,128]{2,1,0:T(8,128)}, f32[16,16,128]{2,1,0:T(8,128)S(1)}, u32[]{:S(2)}) copy-start(f32[16,16,128]{2,1,0:T(8,128)S(1)} %get-tuple-element.664) | copy-start | bytes 393220
  278.8 55.4 %copy-start.1 = (f32[16,256,128]{2,1,0:T(8,128)}, f32[16,256,128]{2,1,0:T(8,128)S(1)}, u32[]{:S(2)}) copy-start(f32[16,256,128]{2,1,0:T(8,128)S(1)} %get-tuple-element.665) | copy-start | bytes 6291460
  302.0 32.2 copy-start.61
  322.0 12.2 copy-start.45
  390.2 872.5 %copy-start.34 = (bf16[512,2048]{1,0:T(8,128)(2,1)}, bf16[512,2048]{1,0:T(8,128)(2,1)S(1)}, u32[]{:S(2)}) copy-start(bf16[512,2048]{1,0:T(8,128)(2,1)S(1)} %multiply_convert_fusion.3) | copy-start | bytes 6291460
  1753.3 19.5 copy-start.17
  1753.3 19.5 copy-start.38
  1785.6 5.4 copy-start.60
  1791.0 5.5 copy-start.14
  1791.0 5.5 copy-start.46
  1807.2 280.4 %reduce-scatter.8.cloned.1.call-start = ((), (), s32[]{:S(2)}) async-start(), calls=%async_computation.14 | async-start | bytes 1179648 | tf_op jit(solution)/shard_map/reduce_scatter | solution.py:355
  1807.2 4.6 copy-start.33
  1812.5 26.9 copy-start.15
  1839.4 9.4 copy-start.2
  1839.4 9.4 copy-start.49
  1839.4 9.4 copy-start.62
  1848.8 10.1 copy-start.22
  1858.9 15.4 copy-start.25
  1858.9 15.4 copy-start.52
  1877.0 17.1 copy-start.31
  1894.1 9.4 copy-start.6
  1894.2 9.4 copy-start.58
  1894.2 9.4 copy-start.64
  1905.6 181.9 %reduce-scatter.10.cloned.1.call-start = ((), (), s32[]{:S(2)}) async-start(), calls=%async_computation.15 | async-start | bytes 1179648 | tf_op jit(solution)/shard_map/reduce_scatter | solution.py:358
  1905.8 21.1 copy-start.66
  1926.9 7.9 copy-start.20
  1934.8 15.4 copy-start.13
  1952.0 12.6 copy-start.7
  1966.6 219.0 %reduce-scatter.14.cloned.1.call-start = ((), (), s32[]{:S(2)}) async-start(), calls=%async_computation.17 | async-start | bytes 9437184 | tf_op jit(solution)/shard_map/reduce_scatter | solution.py:364
  1977.4 358.5 %reduce-scatter.12.cloned.1.call-start = ((), (), s32[]{:S(2)}) async-start(), calls=%async_computation.16 | async-start | bytes 9437184 | tf_op jit(solution)/shard_map/reduce_scatter | solution.py:361
  2006.3 11.1 copy-start.8
  2025.1 686.6 %reduce-scatter.16.cloned.1.call-start = ((), (), s32[]{:S(2)}) async-start(), calls=%async_computation.18 | async-start | bytes 25952256 | tf_op jit(solution)/shard_map/reduce_scatter | solution.py:370
  2044.7 1042.8 %reduce-scatter.18.cloned.1.call-start = ((), (), s32[]{:S(2)}) async-start(), calls=%async_computation.19 | async-start | bytes 25952256 | tf_op jit(solution)/shard_map/reduce_scatter | solution.py:373
  2063.1 1400.3 %reduce-scatter.20.cloned.1.call-start = ((), (), s32[]{:S(2)}) async-start(), calls=%async_computation.20 | async-start | bytes 25952256 | tf_op jit(solution)/shard_map/reduce_scatter | solution.py:376
  2082.9 1578.7 %all-reduce.11.cloned.1.call-start = ((), (), s32[]{:S(2)}) async-start(), calls=%async_computation.23 | async-start | bytes 22020096 | tf_op jit(solution)/shard_map/psum | solution.py:382
  3463.4 19.9 copy-start.37
  3483.3 7.2 copy-start.4
  3483.3 7.2 copy-start.9
  3483.3 7.2 copy-start.41
  3483.3 7.2 copy-start.42
  3661.6 6.2 copy-start.43
  3661.6 7.8 copy-start.29
  (26 other events, 63.6 us)
Sparse Core Ops, SparseCore 0:
  10.1 38.8 all-gather.24
  51.2 123.9 all-gather.20
  177.3 37.7 all-gather.22
  217.1 36.0 all-gather.34
  255.2 122.5 all-gather.26
  379.1 440.9 all-gather.28
  821.7 441.0 all-gather.30
  1264.3 440.9 all-gather.32
  1807.3 35.0 all-gather.36
  1905.8 60.5 reduce-scatter.7
  1970.4 63.2 reduce-scatter.9
  2037.1 148.5 reduce-scatter.13
  2189.3 146.5 reduce-scatter.11
  2339.6 372.0 reduce-scatter.15
  2715.4 372.0 reduce-scatter.17
  3091.2 372.0 reduce-scatter.19
  3466.4 195.1 all-reduce.10
where the time goes:
time: 3700 us; the launch traced here: 3690 us
  waiting for transfers between devices  2950 us (80%)
  matrix products  434 us (12%)
  other arithmetic  122 us (3%)
  blocking collectives  105 us (3%)
  local copies, waits for them, and re-layouts  37 us (1%)
    all_gather x1, waiting for transfers between devices, local(): lax.all_gather(w_gate, 'fsdp', axis=0, tiled=True)  430 us
    all_gather x1, waiting for transfers between devices, local(): lax.all_gather(w_down, 'fsdp', axis=0, tiled=True)  423 us
    all_gather x1, waiting for transfers between devices, local(): lax.all_gather(w_up, 'fsdp', axis=0, tiled=True)  423 us
    reduce_scatter x1, waiting for transfers between devices, local(): lax.psum_scatter(grad_w_down.astype(jnp.bfloat16), 'fsdp', scatter_dimens...  376 us
    reduce_scatter x1, waiting for transfers between devices, local(): lax.psum_scatter(grad_w_gate.astype(jnp.bfloat16), 'fsdp', scatter_dimens...  376 us
    reduce_scatter x1, waiting for transfers between devices, local(): lax.psum_scatter(grad_w_up.astype(jnp.bfloat16), 'fsdp', scatter_dimensio...  376 us
    reduce_scatter x1, waiting for transfers between devices, local(): lax.psum_scatter(grad_w_value.astype(jnp.bfloat16), 'fsdp', scatter_dimen...  150 us
    psum x1, waiting for transfers between devices, local(): lax.psum(shards[1].astype(jnp.bfloat16), 'context').astype(jnp.float32)  137 us
  transfers between devices with their start and end apart: 17, of which 12 were waited for; matrix products, arithmetic and copies ran while one was open for 13% of the time, Pallas kernels for 0%

commit v1 on v0

v1 whole, which is shorter than its diff:
```python
import functools

import jax
import jax.numpy as jnp
from jax import lax
from jax.experimental import pallas as pl
from jax.experimental.pallas import tpu as pltpu
from jax.sharding import PartitionSpec as P

HEADS = 16
QK = 16
VH = 128
EPS = 1e-05

C = "context"
F = "fsdp"
BF = jnp.bfloat16
F32 = jnp.float32


def ring_order(n):
    if n % 2:
        return list(range(n))
    return list(range(0, n, 2)) + list(range(n - 1, 0, -2))


class Ring:
    def __init__(self):
        self.n = n = lax.axis_size(F)
        order = ring_order(n)
        where = [order.index(i) for i in range(n)]
        self.order = jnp.array(order + order, jnp.int32)
        self.pos = jnp.array(where, jnp.int32)[lax.axis_index(F)]
        self.up = [(order[i], order[(i + 1) % n]) for i in range(n)]
        self.down = [(b, a) for a, b in self.up]

    def member(self, distance):
        return self.order[lax.rem(self.pos + distance + self.n, self.n)]

    def paths(self, flip):
        long, short = self.n // 2, (self.n - 1) // 2
        if flip:
            long, short = short, long
        return ((self.up, 1, long), (self.down, -1, short))

    def gather(self, block, flip=False):
        out = jnp.zeros((self.n,) + block.shape, block.dtype)
        out = lax.dynamic_update_index_in_dim(out, block, lax.axis_index(F), 0)
        for perm, sign, steps in self.paths(flip):
            moving = block
            for d in range(1, steps + 1):
                moving = lax.ppermute(moving, F, perm)
                out = lax.dynamic_update_index_in_dim(out, moving, self.member(-sign * d), 0)
        return out

    def scatter_sum(self, stacked, flip=False):
        def part(index):
            return lax.dynamic_index_in_dim(stacked, index, 0, keepdims=False)

        total = part(lax.axis_index(F)).astype(F32)
        for perm, sign, steps in self.paths(flip):
            if not steps:
                continue
            moving = part(self.member(sign * steps))
            for d in range(steps - 1, -1, -1):
                arrived = lax.ppermute(moving, F, perm)
                if d:
                    moving = (
                        arrived.astype(F32) + part(self.member(sign * d)).astype(F32)
                    ).astype(stacked.dtype)
                else:
                    total = total + arrived.astype(F32)
        return total


def chips():
    return lax.axis_size(C) // 2


def core_swap(value):
    n = lax.axis_size(C)
    return lax.ppermute(value, C, [(i, i ^ 1) for i in range(n)])


def chip_shift(value, k):
    n = lax.axis_size(C)
    return lax.ppermute(value, C, [(i, (i + 2 * k) % n) for i in range(n)])


def spread(block):
    out = []
    for k in range(chips()):
        near = chip_shift(block, k) if k else block
        out += [near, core_swap(near)]
    return out


def spread_index():
    n, me = lax.axis_size(C), lax.axis_index(C)
    out = []
    for k in range(chips()):
        near = lax.rem(me - 2 * k + n, n)
        out += [near, near ^ 1]
    return out


def gather_back(parts):
    total = None
    for k in range(chips()):
        mine = parts[2 * k].astype(F32) + core_swap(parts[2 * k + 1].astype(BF)).astype(F32)
        if k:
            mine = chip_shift(mine.astype(BF), -k).astype(F32)
        total = mine if total is None else total + mine
    return total


def in_order(parts):
    out = jnp.zeros((len(parts),) + parts[0].shape, parts[0].dtype)
    for index, part in zip(spread_index(), parts):
        out = lax.dynamic_update_index_in_dim(out, part, index, 0)
    return out


def group_pairs(back):
    nc, nf = lax.axis_size(C), lax.axis_size(F)
    m = nf // nc
    out = []
    for q in range(nc):
        pairs = [
            (c * nf + m * c + s, c * nf + s * nc + q) for c in range(nc) for s in range(m)
        ]
        out.append([(b, a) for a, b in pairs] if back else pairs)
    return out


def group_pieces(shard):
    nc = lax.axis_size(C)
    rows = shard.shape[0] // nc
    out = None
    for q, pairs in enumerate(group_pairs(False)):
        got = lax.ppermute(shard[q * rows : (q + 1) * rows], (C, F), pairs)
        out = got if out is None else out + got
    return out


def ungroup_pieces(piece):
    nc, nf = lax.axis_size(C), lax.axis_size(F)
    m = nf // nc
    shard = jnp.concatenate(
        [lax.ppermute(piece, (C, F), pairs) for pairs in group_pairs(True)], axis=0
    )
    out = shard
    for k in range(1, nc // 2):
        out = out + lax.ppermute(
            shard, (C, F), [((j // m) * nf + j, ((j // m + 2 * k) % nc) * nf + j) for j in range(nf)]
        )
    holders = [((j // m) % 2, j) for j in range(nf)]
    swap = [
        ((2 * x + h) * nf + j, (2 * x + 1 - h) * nf + j) for h, j in holders for x in range(nc // 2)
    ]
    return out + lax.ppermute(out, (C, F), swap)


def dot_nt(a, b):
    return lax.dot_general(a, b, (((1,), (1,)), ((), ())), preferred_element_type=F32)


def dot_nn(a, b):
    return lax.dot_general(a, b, (((1,), (0,)), ((), ())), preferred_element_type=F32)


def with_one(values, width):
    rows = values.shape[0]
    padded = jnp.concatenate([values, jnp.zeros((rows, 128 - width), values.dtype)], axis=1)
    lane = lax.broadcasted_iota(jnp.int32, (rows, 128), 1)
    return jnp.where(lane == width, jnp.ones_like(padded), padded)


def one_head(values, head, width):
    lane = lax.broadcasted_iota(jnp.int32, values.shape, 1)
    keep = jnp.logical_or(lane // QK == head, lane == width)
    return jnp.where(keep, values, jnp.zeros_like(values))


def needed(meta, a, b, nb):
    before = meta[b] < meta[a]
    return jnp.logical_and(before, meta[nb + a] <= meta[2 * nb + b])


def forward_kernel(meta, qkv, seg_col, seg_row, mixed, den, num_sum, den_sum, *, heads, rows, nb):
    width = heads * QK
    a = pl.program_id(0)
    here = pl.ds(pl.multiple_of(a * rows, rows), rows)
    queries = with_one(qkv[here, :width] * 0.25, width)
    seg_q = seg_col[here, :]
    num_sum[...] = jnp.zeros_like(num_sum)
    den_sum[...] = jnp.zeros_like(den_sum)

    def pair(b, diagonal):
        there = pl.ds(pl.multiple_of(b * rows, rows), rows)
        keys = with_one(qkv[there, width : 2 * width], width)
        allowed = seg_q == seg_row[b]
        if diagonal:
            t = lax.broadcasted_iota(jnp.int32, (rows, rows), 0)
            u = lax.broadcasted_iota(jnp.int32, (rows, rows), 1)
            allowed = jnp.logical_and(allowed, u <= t)
        for h in range(heads):
            shifted = dot_nt(one_head(queries, h, width), keys)
            weight = jnp.where(allowed, shifted * shifted + 1.0, 0.0)
            lanes = slice(h * VH, (h + 1) * VH)
            values = qkv[there, 2 * width + h * VH : 2 * width + (h + 1) * VH]
            num_sum[:, lanes] += dot_nn(weight.astype(BF), values)
            den_sum[:, lanes] += jnp.broadcast_to(
                jnp.sum(weight, axis=1, keepdims=True), (rows, VH)
            )

    pair(a, True)

    @pl.loop(0, nb)
    def _(b):
        @pl.when(needed(meta, a, b, nb))
        def _():
            pair(b, False)

    mixed[...] = (num_sum[...] / den_sum[...]).astype(BF)
    for h in range(heads):
        den[:, h : h + 1] = den_sum[:, h * VH : h * VH + 1]


def backward_kernel(
    meta, qkv, seg_col, seg_row, gm, mixed, den, scale, out, key_sum, value_sum, query_sum, *, heads, rows, nb
):
    width = heads * QK
    a = pl.program_id(0)
    here = pl.ds(pl.multiple_of(a * rows, rows), rows)
    queries = with_one(qkv[here, :width] * 0.25, width)
    seg_q = seg_row[a]

    @pl.when(a == 0)
    def _():
        key_sum[...] = jnp.zeros_like(key_sum)
        value_sum[...] = jnp.zeros_like(value_sum)
        query_sum[...] = jnp.zeros_like(query_sum)

    grads, offsets, head_queries = [], [], []
    for h in range(heads):
        g = gm[:, h * VH : (h + 1) * VH].astype(F32)
        d = den[:, h : h + 1]
        grads.append((g / d).astype(BF))
        inner = -jnp.sum(g * mixed[:, h * VH : (h + 1) * VH].astype(F32), axis=1, keepdims=True) / d
        offsets.append(jnp.transpose(jnp.broadcast_to(inner, (rows, 128)))[0:1, :])
        head_queries.append(one_head(queries, h, width))

    def pair(b, diagonal):
        there = pl.ds(pl.multiple_of(b * rows, rows), rows)
        raw = qkv[there, width : 2 * width]
        keys = with_one(raw, width)
        turned = jnp.transpose(keys)
        allowed = seg_col[there, :] == seg_q
        if diagonal:
            u = lax.broadcasted_iota(jnp.int32, (rows, rows), 0)
            t = lax.broadcasted_iota(jnp.int32, (rows, rows), 1)
            allowed = jnp.logical_and(allowed, u <= t)
        for h in range(heads):
            lanes = slice(h * VH, (h + 1) * VH)
            shifted = dot_nt(keys, head_queries[h])
            weight = jnp.where(allowed, shifted * shifted + 1.0, 0.0).astype(BF)
            value_sum[there, lanes] += dot_nn(weight, grads[h])
            values = qkv[there, 2 * width + h * VH : 2 * width + (h + 1) * VH]
            grad = dot_nt(values, grads[h]) + offsets[h]
            score = jnp.where(allowed, grad * shifted, 0.0).astype(BF)
            key_sum[there, :] += dot_nn(score, head_queries[h])
            query_sum[a, h * QK : (h + 1) * QK, :] += dot_nn(turned[h * QK : (h + 1) * QK, :], score)

    pair(a, True)

    @pl.loop(0, nb)
    def _(b):
        @pl.when(needed(meta, a, b, nb))
        def _():
            pair(b, False)

    @pl.when(a == nb - 1)
    def _():
        for b in range(nb):
            span = slice(b * rows, (b + 1) * rows)
            s = scale[span, :]
            grad_q = jnp.transpose(query_sum[b]) * (0.5 * s)
            out[span, :width] = grad_q.astype(BF)
            out[span, width : 2 * width] = (key_sum[span, :width] * (2.0 * s)).astype(BF)
            out[span, 2 * width :] = (value_sum[span, :] * s).astype(BF)


def block_spec(shape, index):
    return pl.BlockSpec(shape, index)


def whole(shape):
    return pl.BlockSpec(shape, lambda a, *_: (0,) * len(shape))


def attention_forward(meta, qkv, seg_col, seg_row, heads, rows):
    tokens = qkv.shape[0]
    nb = tokens // rows
    values = heads * VH
    return pl.pallas_call(
        functools.partial(forward_kernel, heads=heads, rows=rows, nb=nb),
        out_shape=(
            jax.ShapeDtypeStruct((tokens, values), BF),
            jax.ShapeDtypeStruct((tokens, heads), F32),
        ),
        grid_spec=pltpu.PrefetchScalarGridSpec(
            num_scalar_prefetch=1,
            grid=(nb,),
            in_specs=[whole(qkv.shape), whole(seg_col.shape), whole(seg_row.shape)],
            out_specs=[
                pl.BlockSpec((rows, values), lambda a, *_: (a, 0)),
                pl.BlockSpec((rows, heads), lambda a, *_: (a, 0)),
            ],
            scratch_shapes=[pltpu.VMEM((rows, values), F32), pltpu.VMEM((rows, values), F32)],
        ),
        cost_estimate=pl.CostEstimate(
            flops=4 * tokens * tokens * values, transcendentals=0, bytes_accessed=8 * tokens * values
        ),
        name="attention_forward",
    )(meta, qkv, seg_col, seg_row)


def attention_backward(meta, qkv, seg_col, seg_row, gm, mixed, den, scale, heads, rows):
    tokens = qkv.shape[0]
    nb = tokens // rows
    values = heads * VH
    width = heads * QK
    return pl.pallas_call(
        functools.partial(backward_kernel, heads=heads, rows=rows, nb=nb),
        out_shape=jax.ShapeDtypeStruct((tokens, 2 * width + values), BF),
        grid_spec=pltpu.PrefetchScalarGridSpec(
            num_scalar_prefetch=1,
            grid=(nb,),
            in_specs=[
                whole(qkv.shape),
                whole(seg_col.shape),
                whole(seg_row.shape),
                pl.BlockSpec((rows, values), lambda a, *_: (a, 0)),
                pl.BlockSpec((rows, values), lambda a, *_: (a, 0)),
                pl.BlockSpec((rows, heads), lambda a, *_: (a, 0)),
                whole(scale.shape),
            ],
            out_specs=whole((tokens, 2 * width + values)),
            scratch_shapes=[
                pltpu.VMEM((tokens, 128), F32),
                pltpu.VMEM((tokens, values), F32),
                pltpu.VMEM((nb, width, rows), F32),
            ],
        ),
        cost_estimate=pl.CostEstimate(
            flops=10 * tokens * tokens * values, transcendentals=0, bytes_accessed=16 * tokens * values
        ),
        name="attention_backward",
    )(meta, qkv, seg_col, seg_row, gm, mixed, den, scale)


def mm(a, b):
    return jnp.dot(a, b, preferred_element_type=F32)


def mm_tn(a, b):
    return lax.dot_general(a, b, (((0,), (0,)), ((), ())), preferred_element_type=F32)


def mm_nt(a, b):
    return lax.dot_general(a, b, (((1,), (1,)), ((), ())), preferred_element_type=F32)


def inverse_rms(values):
    return lax.rsqrt(jnp.mean(values * values, axis=-1, keepdims=True) + EPS)


def local(
    tokens,
    segment_ids,
    norm1_gain,
    w_query,
    w_key,
    w_value,
    w_out,
    norm2_gain,
    w_gate,
    w_up,
    w_down,
    cotangent,
):
    nc, nf = lax.axis_size(C), lax.axis_size(F)
    c = lax.axis_index(C)
    ring = Ring()
    rows, width = tokens.shape[1], tokens.shape[2]
    heads = HEADS // nc
    qk = heads * QK
    hidden_all = w_gate.shape[1]
    seg_len = hidden_all // (nc * nf)
    hidden = seg_len * nf
    shard = w_gate.shape[0]

    own = tokens[0]
    grad_top = cotangent[0]
    gain_one = norm1_gain.astype(F32)[:, None]
    gain_two = norm2_gain.astype(F32)[:, None]

    def columns(weight, size):
        return lax.dynamic_slice_in_dim(weight, c * size, size, axis=1)

    part_qkv = (
        jnp.concatenate(
            [columns(w_query, qk), columns(w_key, qk), columns(w_value, heads * VH)], axis=1
        ).astype(F32)
        * gain_one
    ).astype(BF)

    def hidden_columns(weight):
        picked = lax.dynamic_index_in_dim(
            weight.reshape(shard, nf, nc, seg_len), c, axis=2, keepdims=False
        )
        return (picked.reshape(shard, hidden).astype(F32) * gain_two).astype(BF)

    part_out = group_pieces(w_out)
    part_gate = hidden_columns(w_gate)
    part_up = hidden_columns(w_up)
    part_down = lax.dynamic_slice_in_dim(w_down, c * seg_len, seg_len, axis=0)

    x_all = jnp.concatenate(spread(own), axis=0)
    seg_all = jnp.concatenate(spread(segment_ids[0]), axis=0)
    g_all = jnp.concatenate(spread(grad_top), axis=0)
    nb = nc
    seg_row = seg_all.reshape(nb, 1, rows)
    seg_col = seg_all.reshape(nb * rows, 1)
    meta = jnp.concatenate(
        [jnp.stack(spread_index()), seg_row[:, 0, 0], seg_row[:, 0, rows - 1]]
    ).astype(jnp.int32)

    full_qkv = ring.gather(part_qkv).reshape(width, -1)
    full_out = ring.gather(part_out, True).reshape(heads * VH, width)
    x_all32 = x_all.astype(F32)
    scale_one = inverse_rms(x_all32)
    qkv = (mm(x_all, full_qkv) * scale_one).astype(BF)
    mixed, den = attention_forward(meta, qkv, seg_col, seg_row, heads, rows)

    def blocks(value):
        return [value[i * rows : (i + 1) * rows] for i in range(nb)]

    residual = own.astype(F32) + gather_back(blocks(mm(mixed, full_out).astype(BF)))

    scale_two = inverse_rms(residual)
    unit_two = residual * scale_two
    n_all = jnp.concatenate(spread(unit_two.astype(BF)), axis=0)
    full_gate = ring.gather(part_gate).reshape(width, hidden)
    full_up = ring.gather(part_up, True).reshape(width, hidden)
    full_down = ring.gather(part_down).reshape(hidden, width)
    gate = mm(n_all, full_gate)
    up = mm(n_all, full_up)
    sigmoid = jax.nn.sigmoid(gate)
    silu = gate * sigmoid
    act = (silu * up).astype(BF)
    block_out = residual + gather_back(blocks(mm(act, full_down).astype(BF)))

    grad_hidden = mm_nt(g_all, full_down)
    grad_gate = (grad_hidden * up * sigmoid * (1.0 + gate * (1.0 - sigmoid))).astype(BF)
    grad_up = (grad_hidden * silu).astype(BF)
    grad_unit_two = gather_back(
        blocks((mm_nt(grad_gate, full_gate) + mm_nt(grad_up, full_up)).astype(BF))
    )
    sum_down = ring.scatter_sum(mm_tn(act, g_all).astype(BF).reshape(nf, seg_len, width))
    sum_gate = ring.scatter_sum(mm_tn(n_all, grad_gate).astype(BF).reshape(nf, shard, hidden))
    sum_up = ring.scatter_sum(mm_tn(n_all, grad_up).astype(BF).reshape(nf, shard, hidden), True)

    grad_residual = grad_top.astype(F32) + scale_two * (
        grad_unit_two - unit_two * jnp.mean(grad_unit_two * unit_two, axis=-1, keepdims=True)
    )
    b_all = jnp.concatenate(spread(grad_residual.astype(BF)), axis=0)

    grad_mixed = mm_nt(b_all, full_out)
    sum_out = ring.scatter_sum(
        mm_tn(mixed, b_all).astype(BF).reshape(nf, (heads * VH) // nf, width), True
    )
    grad_qkv = attention_backward(
        meta, qkv, seg_col, seg_row, grad_mixed, mixed, den, scale_one, heads, rows
    )
    grad_unit_one = gather_back(blocks(mm_nt(grad_qkv, full_qkv).astype(BF)))
    sum_qkv = ring.scatter_sum(mm_tn(x_all, grad_qkv).astype(BF).reshape(nf, shard, -1))

    unit_one = own.astype(F32) * inverse_rms(own.astype(F32))
    input_grad = grad_residual + grad_unit_one - unit_one * jnp.mean(
        grad_unit_one * unit_one, axis=-1, keepdims=True
    )

    def over_context(value):
        return in_order(spread(value.astype(BF)))

    def from_hidden(stacked):
        return (
            stacked.reshape(nc, shard, nf, seg_len)
            .transpose(1, 2, 0, 3)
            .reshape(shard, hidden_all)
            .astype(F32)
        )

    def side_by_side(stacked):
        return stacked.transpose(1, 0, 2).reshape(stacked.shape[1], -1).astype(F32)

    all_down = over_context(sum_down).reshape(nc * seg_len, width).astype(F32)
    all_gate = from_hidden(over_context(sum_gate))
    all_up = from_hidden(over_context(sum_up))
    all_qkv = over_context(sum_qkv)
    all_query = side_by_side(all_qkv[:, :, :qk])
    all_key = side_by_side(all_qkv[:, :, qk : 2 * qk])
    all_value = side_by_side(all_qkv[:, :, 2 * qk :])
    all_out = ungroup_pieces(sum_out.astype(BF)).astype(F32)

    def along(weight, grad):
        return jnp.sum(weight.astype(F32) * grad, axis=1)

    grad_gain_one = along(w_query, all_query) + along(w_key, all_key) + along(w_value, all_value)
    grad_gain_two = along(w_gate, all_gate) + along(w_up, all_up)
    return (
        block_out.astype(BF)[None],
        input_grad[None],
        grad_gain_one,
        all_query * gain_one,
        all_key * gain_one,
        all_value * gain_one,
        all_out,
        grad_gain_two,
        all_gate * gain_two,
        all_up * gain_two,
        all_down,
    )


def solution(mesh):
    rows = P(F, None)
    acts = P(F, C, None)
    return jax.shard_map(
        local,
        mesh=mesh,
        in_specs=(acts, P(F, C), P(F), rows, rows, rows, rows, P(F), rows, rows, rows, acts),
        out_specs=(acts, acts, P(F), rows, rows, rows, rows, P(F), rows, rows, rows),
        check_vma=False,
    )
```

time: 3700 us -> 1200 us (0.32)
  waiting for transfers between devices: 2950 us -> 386 us
  matrix products: 434 us -> 244 us
  local copies, waits for them, and re-layouts: 37 us -> 227 us
  starting transfers between devices: 0.85 us -> 149 us
  blocking collectives: 105 us -> 0 us
  Pallas kernels: 0 us -> 39.8 us
    all_gather x9 -> x0, waiting for transfers between devices: 1440 us -> none  [the longest x1 430 us: local(): lax.all_gather(w_gate, 'fsdp', axis=0, tiled=True)]
    reduce_scatter x7 -> x0, waiting for transfers between devices: 1380 us -> none  [the longest x1 376 us: local(): lax.psum_scatter(grad_w_down.astype(jnp.bfloat16), 'fsdp', scatter_dimens...]
    ppermute x0 -> x119, waiting for transfers between devices: none -> 386 us  [the longest x13 183 us: chip_shift(): return lax.ppermute(value, C, [(i, (i + 2 * k) % n) for i in range(n)])]
    dot_general x45 -> x15, matrix products: 434 us -> 244 us  [the longest x5 93.1 us: mm_nt(): lax.dot_general(a, b, (((1,), (1,)), ((), ())), preferred_element_type=F32)]
    ppermute x0 -> x119, starting transfers between devices: none -> 149 us  [the longest x26 52.3 us: core_swap(): return lax.ppermute(value, C, [(i, i ^ 1) for i in range(n)])]
    psum x1 -> x0, waiting for transfers between devices: 137 us -> none  [local(): lax.psum(shards[1].astype(jnp.bfloat16), 'context').astype(jnp.float32)]
    all_gather x10 -> x0, blocking collectives: 70.9 us -> none  [the longest x4 25.4 us: entering(): lax.all_gather(part.astype(kind), axis)]
    dynamic_update_slice x0 -> x50, local copies, waits for them, and re-layouts: none -> 63 us  [the longest x35 47.9 us: gather(): lax.dynamic_update_index_in_dim(out, moving, self.member(-sign * d), 0)]
  transfers between devices with their start and end apart: 17 -> 119, of which waited for: 12 -> 41; matrix products, arithmetic and copies ran while one was open for 13% -> 39% of each run, Pallas kernels for 0% -> 2%
where the time goes in v1:
time: 1200 us; the launch traced here: 1180 us
  waiting for transfers between devices  386 us (32%)
  matrix products  244 us (20%)
  local copies, waits for them, and re-layouts  227 us (19%)
  starting transfers between devices  149 us (12%)
  other arithmetic  109 us (9%)
  Pallas kernels  39.8 us (3%)
  between operations  22.5 us (2%)
    ppermute x13, waiting for transfers between devices, chip_shift(): return lax.ppermute(value, C, [(i, (i + 2 * k) % n) for i in range(n)])  183 us
    ppermute x35, waiting for transfers between devices, scatter_sum(): arrived = lax.ppermute(moving, F, perm)  110 us
    dot_general x5, matrix products, mm_nt(): lax.dot_general(a, b, (((1,), (1,)), ((), ())), preferred_element_type=F32)  93.1 us
    ppermute x35, waiting for transfers between devices, gather(): moving = lax.ppermute(moving, F, perm)  92.7 us
    dot_general x5, matrix products, mm(): return jnp.dot(a, b, preferred_element_type=F32)  84.2 us
    dot_general x5, matrix products, mm_tn(): lax.dot_general(a, b, (((0,), (0,)), ((), ())), preferred_element_type=F32)  66.8 us
    unnamed x161, local copies, waits for them, and re-layouts  64.6 us
    ppermute x26, starting transfers between devices, core_swap(): return lax.ppermute(value, C, [(i, i ^ 1) for i in range(n)])  52.3 us
  transfers between devices with their start and end apart: 119, of which 41 were waited for; matrix products, arithmetic and copies ran while one was open for 39% of the time, Pallas kernels for 2%

profile of v1, /device:TPU:17, one launch (start us, length us, event | category | flops | bytes accessed | tf_op | source)
XLA Modules:
  0.0 1177.8 jit_solution(8041075699113970703)
XLA Ops:
  21.9 4.6 copy.82
  41.6 4.9 collective-permute-start
  88.8 3.7 collective-permute-done.18
  109.1 4.1 collective-permute-done.4
  121.2 6.3 multiply_reduce_fusion
  127.5 15.1 %multiply_convert_fusion.3.qkv = bf16[2048,640]{1,0:T(8,128)(2,1)} fusion(bf16[2048,640]{1,0:T(8,128)(2,1)} %bitcast.34, f32[2048]{0:T(1024)S(1)} %add_rsqrt_fusion, bf16[512,2048]{1,0:T(8,128)(2,1)S(1)} %collective-permute-done.5, bf16[512,2048]{1,0:T(8,128)(2,1)} %collective-permute-done.4, bf16[512,2048]{1,0:T(8,128)(2,1)S(1)} %collective-permute-done.3, ...), kind=kOutput, calls=%fused_computation.28 | convolution fusion | flops 5404884992 | bytes 13639680 | tf_op jit(solution)/shard_map/dot_general | solution.py:364
  142.6 14.9 %attention_forward.1 = (bf16[2048,512]{1,0:T(8,128)(2,1)}, f32[2048,4]{1,0:T(8,128)}) custom-call(s32[12]{0:T(128)} %concatenate.55.meta, bf16[2048,640]{1,0:T(8,128)(2,1)} %multiply_convert_fusion.3.qkv, s32[2048,1]{1,0:T(8,128)} %copy.72.seg_col, s32[4,1,512]{2,1,0:T(1,128)} %copy-done.47), custom_call_target="tpu_custom_call" | custom-call | flops 8589934592 | bytes 8388608 | tf_op jit(solution)/shard_map/attention_forward/pallas_call | solution.py:306
  157.5 6.7 convolution_convert_fusion.2
  170.3 6.1 collective-permute-start.37
  200.4 22.2 %collective-permute-done.44 = bf16[176,2048]{1,0:T(8,128)(2,1)} collective-permute-done((bf16[176,2048]{1,0:T(8,128)(2,1)}, bf16[176,2048]{1,0:T(8,128)(2,1)}, u32[]{:S(2)}, u32[]{:S(2)}) %collective-permute-start.44) | collective-permute-done | bytes 720928 | tf_op jit(solution)/shard_map/ppermute | solution.py:52
  231.0 4.4 add_convert_fusion.5
  263.4 5.5 collective-permute-done.45
  270.9 13.4 %collective-permute-done.39 = bf16[256,1408]{0,1:T(8,128)(2,1)} collective-permute-done((bf16[256,1408]{0,1:T(8,128)(2,1)}, bf16[256,1408]{0,1:T(8,128)(2,1)}, u32[]{:S(2)}, u32[]{:S(2)}) %collective-permute-start.39) | collective-permute-done | bytes 720928 | tf_op jit(solution)/shard_map/ppermute | solution.py:52
  298.6 4.4 multiply_reduce_fusion.2
  323.6 5.1 collective-permute-done.49
  328.7 5.2 collective-permute-start.54
  333.9 10.3 collective-permute-done.43
  344.2 5.0 collective-permute-start.56
  357.0 11.0 collective-permute-done.47
  371.8 3.6 collective-permute-done.28
  387.6 22.2 %fusion.56 = f32[2048,1408]{1,0:T(8,128)} fusion(bf16[2048,1408]{1,0:T(8,128)(2,1)} %bitcast.68, bf16[512,2048]{1,0:T(8,128)(2,1)} %collective-permute-done.29, bf16[512,2048]{1,0:T(8,128)(2,1)} %collective-permute-done.28, bf16[512,2048]{1,0:T(8,128)(2,1)S(1)} %collective-permute-done.27, bf16[512,2048]{1,0:T(8,128)(2,1)} %multiply_convert_fusion.4), kind=kOutput, calls=%fused_computation.244 | convolution fusion | flops 11844714496 | bytes 25690112 | tf_op jit(solution)/shard_map/dot_general | solution.py:364
  409.8 21.6 %fusion.57 = f32[2048,1408]{1,0:T(8,128)} fusion(bf16[2048,1408]{1,0:T(8,128)(2,1)} %bitcast.57, bf16[512,2048]{1,0:T(8,128)(2,1)} %collective-permute-done.29, bf16[512,2048]{1,0:T(8,128)(2,1)} %collective-permute-done.28, bf16[512,2048]{1,0:T(8,128)(2,1)S(1)} %collective-permute-done.27, bf16[512,2048]{1,0:T(8,128)(2,1)} %multiply_convert_fusion.4), kind=kOutput, calls=%fused_computation.245 | convolution fusion | flops 11844714496 | bytes 25690112 | tf_op jit(solution)/shard_map/dot_general | solution.py:364
  431.4 29.0 %multiply_convert_fusion = (bf16[2048,1408]{1,0:T(8,128)(2,1)}, bf16[2048,1408]{1,0:T(8,128)(2,1)}, bf16[2048,1408]{1,0:T(8,128)(2,1)}) fusion(f32[2048,1408]{1,0:T(8,128)} %fusion.57, f32[2048,1408]{1,0:T(8,128)} %fusion.56, bf16[1408,2048]{1,0:T(8,128)(2,1)} %bitcast.77, bf16[512,2048]{1,0:T(8,128)(2,1)} %collective-permute-done.56, ...), kind=kOutput, calls=%fused_computation.2 | convolution fusion | flops 11887968256 | bytes 54525952 | tf_op jit(solution)/shard_map/dot_general | solution.py:372
  460.3 18.6 %convolution_convert_fusion.1 = bf16[2048,2048]{1,0:T(8,128)(2,1)} fusion(bf16[2048,1408]{1,0:T(8,128)(2,1)} %get-tuple-element.59, bf16[1408,2048]{1,0:T(8,128)(2,1)} %bitcast.77), kind=kOutput, calls=%fused_computation.12 | convolution fusion | flops 11815354368 | bytes 19922944 | tf_op jit(solution)/shard_map/dot_general | solution.py:364
  478.9 14.6 %convolution_convert_fusion.3 = bf16[1408,2048]{1,0:T(8,128)(2,1)S(1)} fusion(bf16[2048,1408]{1,0:T(8,128)(2,1)S(1)} %copy-done.61, bf16[512,2048]{1,0:T(8,128)(2,1)} %collective-permute-done.56, bf16[512,2048]{1,0:T(8,128)(2,1)} %collective-permute-done.55, bf16[512,2048]{1,0:T(8,128)(2,1)} %collective-permute-done.54, bf16[512,2048]{1,0:T(8,128)(2,1)} %bitcast.79), kind=kOutput, calls=%fused_computation.14 | convolution fusion | flops 11847598080 | bytes 19922944 | tf_op jit(solution)/shard_map/dot_general | solution.py:368
  497.1 19.7 %fusion.69 = f32[2048,2048]{1,0:T(8,128)} fusion(bf16[2048,1408]{1,0:T(8,128)(2,1)} %get-tuple-element.58, bf16[2048,1408]{1,0:T(8,128)(2,1)} %bitcast.57), kind=kOutput, calls=%fused_computation.253 | convolution fusion | flops 11811160064 | bytes 28311552 | tf_op jit(solution)/shard_map/dot_general | solution.py:372
  516.8 17.5 %convolution_convert_fusion.5 = bf16[2048,1408]{1,0:T(8,128)(2,1)S(1)} fusion(bf16[2048,1408]{1,0:T(8,128)(2,1)} %get-tuple-element.58, bf16[512,2048]{1,0:T(8,128)(2,1)} %collective-permute-done.29, bf16[512,2048]{1,0:T(8,128)(2,1)} %collective-permute-done.28, bf16[512,2048]{1,0:T(8,128)(2,1)} %copy-done.57, bf16[512,2048]{1,0:T(8,128)(2,1)} %multiply_convert_fusion.4), kind=kOutput, calls=%fused_computation.16 | convolution fusion | flops 11847598080 | bytes 19922944 | tf_op jit(solution)/shard_map/dot_general | solution.py:368
  534.4 19.3 %convolution_convert_fusion.4 = bf16[2048,1408]{1,0:T(8,128)(2,1)} fusion(bf16[2048,1408]{1,0:T(8,128)(2,1)} %get-tuple-element.57, bf16[512,2048]{1,0:T(8,128)(2,1)} %collective-permute-done.29, bf16[512,2048]{1,0:T(8,128)(2,1)} %collective-permute-done.28, bf16[512,2048]{1,0:T(8,128)(2,1)} %copy-done.57, bf16[512,2048]{1,0:T(8,128)(2,1)} %multiply_convert_fusion.4), kind=kOutput, calls=%fused_computation.15 | convolution fusion | flops 11847598080 | bytes 19922944 | tf_op jit(solution)/shard_map/dot_general | solution.py:368
  553.6 6.5 constant_dynamic-slice_fusion.7
  576.8 21.9 %add_convert_fusion = bf16[2048,2048]{1,0:T(8,128)(2,1)} fusion(f32[2048,2048]{1,0:T(8,128)} %fusion.69, bf16[2048,1408]{1,0:T(8,128)(2,1)} %get-tuple-element.57, bf16[2048,1408]{1,0:T(8,128)(2,1)} %bitcast.68), kind=kOutput, calls=%fused_computation | convolution fusion | flops 11819548672 | bytes 36700160 | tf_op jit(solution)/shard_map/dot_general | solution.py:372
  598.7 5.1 fusion.65
  631.3 6.9 collective-permute-done.102
  638.6 7.3 collective-permute-done.90
  647.7 13.7 %collective-permute-done.110 = bf16[176,2048]{1,0:T(8,128)(2,1)S(1)} collective-permute-done((bf16[176,2048]{1,0:T(8,128)(2,1)S(1)}, bf16[176,2048]{1,0:T(8,128)(2,1)S(1)}, u32[]{:S(2)}, u32[]{:S(2)}) %collective-permute-start.110) | collective-permute-done | bytes 720928 | tf_op jit(solution)/shard_map/ppermute | solution.py:66
  664.8 12.1 %collective-permute-done.100 = bf16[256,1408]{0,1:T(8,128)(2,1)S(1)} collective-permute-done((bf16[256,1408]{0,1:T(8,128)(2,1)S(1)}, bf16[256,1408]{0,1:T(8,128)(2,1)S(1)}, u32[]{:S(2)}, u32[]{:S(2)}) %collective-permute-start.100) | collective-permute-done | bytes 720928 | tf_op jit(solution)/shard_map/ppermute | solution.py:66
  680.1 27.7 %collective-permute-done.91 = bf16[256,1408]{0,1:T(8,128)(2,1)S(1)} collective-permute-done((bf16[256,1408]{0,1:T(8,128)(2,1)S(1)}, bf16[256,1408]{0,1:T(8,128)(2,1)S(1)}, u32[]{:S(2)}, u32[]{:S(2)}) %collective-permute-start.91) | collective-permute-done | bytes 720928 | tf_op jit(solution)/shard_map/ppermute | solution.py:66
  711.7 12.7 %collective-permute-done.95 = bf16[256,1408]{0,1:T(8,128)(2,1)S(1)} collective-permute-done((bf16[256,1408]{0,1:T(8,128)(2,1)S(1)}, bf16[256,1408]{0,1:T(8,128)(2,1)S(1)}, u32[]{:S(2)}, u32[]{:S(2)}) %collective-permute-start.95) | collective-permute-done | bytes 720928 | tf_op jit(solution)/shard_map/ppermute | solution.py:66
  730.4 8.7 collective-permute-done.101
  741.7 5.7 collective-permute-start.96
  747.4 7.2 collective-permute-done.112
  757.9 3.7 add_convert_fusion.4
  768.6 72.1 %collective-permute-done.97 = bf16[256,1408]{0,1:T(8,128)(2,1)} collective-permute-done((bf16[256,1408]{0,1:T(8,128)(2,1)}, bf16[256,1408]{0,1:T(8,128)(2,1)}, u32[]{:S(2)}, u32[]{:S(2)}) %collective-permute-start.97) | collective-permute-done | bytes 720928 | tf_op jit(solution)/shard_map/ppermute | solution.py:87
  840.7 7.0 collective-permute-start.116
  852.3 14.4 %collective-permute-done.117 = bf16[176,2048]{1,0:T(8,128)(2,1)} collective-permute-done((bf16[176,2048]{1,0:T(8,128)(2,1)S(1)}, bf16[176,2048]{1,0:T(8,128)(2,1)}, u32[]{:S(2)}, u32[]{:S(2)}) %collective-permute-start.117) | collective-permute-done | bytes 720928 | tf_op jit(solution)/shard_map/ppermute | solution.py:87
  868.1 14.1 %collective-permute-done.107 = bf16[256,1408]{0,1:T(8,128)(2,1)} collective-permute-done((bf16[256,1408]{0,1:T(8,128)(2,1)}, bf16[256,1408]{0,1:T(8,128)(2,1)}, u32[]{:S(2)}, u32[]{:S(2)}) %collective-permute-start.107) | collective-permute-done | bytes 720928 | tf_op jit(solution)/shard_map/ppermute | solution.py:87
  883.1 8.1 fusion.62
  897.4 40.9 %collective-permute-done.61 = bf16[512,2048]{1,0:T(8,128)(2,1)S(1)} collective-permute-done((bf16[512,2048]{1,0:T(8,128)(2,1)S(1)}, bf16[512,2048]{1,0:T(8,128)(2,1)S(1)}, u32[]{:S(2)}, u32[]{:S(2)}) %collective-permute-start.61) | collective-permute-done | bytes 2097184 | tf_op jit(solution)/shard_map/ppermute | solution.py:87
  944.1 5.8 bitcast_multiply_fusion
  949.9 7.0 convolution_convert_fusion.7
  960.8 10.8 fusion.34.gm
  971.6 24.9 %attention_backward.1 = bf16[2048,640]{1,0:T(8,128)(2,1)} custom-call(s32[12]{0:T(128)} %concatenate.55.meta, bf16[2048,640]{1,0:T(8,128)(2,1)} %multiply_convert_fusion.3.qkv, s32[2048,1]{1,0:T(8,128)} %copy.72.seg_col, s32[4,1,512]{2,1,0:T(1,128)} %copy-done.47, f32[2048,512]{1,0:T(8,128)} %fusion.34.gm, bf16[2048,512]{1,0:T(8,128)(2,1)} %get-tuple-element.13.mixed, ...), custom_call_target="tpu_custom_call" | custom-call | flops 21474836480 | bytes 16777216 | tf_op jit(solution)/shard_map/attention_backward/pallas_call | solution.py:334
  996.5 11.8 %convolution_convert_fusion = bf16[2048,2048]{1,0:T(8,128)(2,1)} fusion(bf16[2048,640]{1,0:T(8,128)(2,1)} %attention_backward.1, bf16[2048,640]{1,0:T(8,128)(2,1)} %bitcast.34), kind=kOutput, calls=%fused_computation.11 | convolution fusion | flops 5372903424 | bytes 13631488 | tf_op jit(solution)/shard_map/dot_general | solution.py:372
  1008.3 8.4 convolution_convert_fusion.6
  1019.8 7.3 collective-permute-start.66
  1028.9 4.8 fusion.63
  1072.4 4.3 collective-permute-start.83
  1080.3 6.4 copy.128
  1086.6 6.2 copy.129
  1100.1 6.8 collective-permute-start.74
  1107.7 7.2 collective-permute-done.74
  1115.6 4.4 add_convert_fusion.1
  1141.2 26.8 %collective-permute-done.65 = bf16[512,2048]{1,0:T(8,128)(2,1)} collective-permute-done((bf16[512,2048]{1,0:T(8,128)(2,1)}, bf16[512,2048]{1,0:T(8,128)(2,1)}, u32[]{:S(2)}, u32[]{:S(2)}) %collective-permute-start.65) | collective-permute-done | bytes 2097184 | tf_op jit(solution)/shard_map/ppermute | solution.py:87
  1168.0 4.2 fusion.5
  1172.2 5.5 fusion.7
  (524 shorter events, 388.2 us)
Async XLA Ops:
  3.0 62.7 %collective-permute-start.13 = (bf16[64,2048]{1,0:T(8,128)(2,1)}, bf16[64,2048]{1,0:T(8,128)(2,1)}, u32[]{:S(2)}, u32[]{:S(2)}) collective-permute-start(bf16[64,2048]{1,0:T(8,128)(2,1)} %get-tuple-element.117), channel_id=1, source_target_pairs={{0,0},{1,4},{10,8},{11,12},{20,16},{21,20},{30,24},{31,28}} | collective-permute-start | bytes 786440 | tf_op jit(solution)/shard_map/ppermute | solution.py:141
  4.3 62.6 %collective-permute-start.14 = (bf16[64,2048]{1,0:T(8,128)(2,1)}, bf16[64,2048]{1,0:T(8,128)(2,1)}, u32[]{:S(2)}, u32[]{:S(2)}) collective-permute-start(bf16[64,2048]{1,0:T(8,128)(2,1)} %get-tuple-element.116), channel_id=1, source_target_pairs={{0,1},{1,5},{10,9},{11,13},{20,17},{21,21},{30,25},{31,29}} | collective-permute-start | bytes 786440 | tf_op jit(solution)/shard_map/ppermute | solution.py:141
  5.7 62.1 %collective-permute-start.15 = (bf16[64,2048]{1,0:T(8,128)(2,1)}, bf16[64,2048]{1,0:T(8,128)(2,1)}, u32[]{:S(2)}, u32[]{:S(2)}) collective-permute-start(bf16[64,2048]{1,0:T(8,128)(2,1)} %get-tuple-element.119), channel_id=1, source_target_pairs={{0,2},{1,6},{10,10},{11,14},{20,18},{21,22},{30,26},{31,30}} | collective-permute-start | bytes 786440 | tf_op jit(solution)/shard_map/ppermute | solution.py:141
  7.0 60.8 %collective-permute-start.16 = (bf16[64,2048]{1,0:T(8,128)(2,1)}, bf16[64,2048]{1,0:T(8,128)(2,1)}, u32[]{:S(2)}, u32[]{:S(2)}) collective-permute-start(bf16[64,2048]{1,0:T(8,128)(2,1)} %get-tuple-element.118), channel_id=1, source_target_pairs={{0,3},{1,7},{10,11},{11,15},{20,19},{21,23},{30,27},{31,31}} | collective-permute-start | bytes 786440 | tf_op jit(solution)/shard_map/ppermute | solution.py:141
  8.4 33.2 %collective-permute-start.1 = (s32[512]{0:T(512)}, s32[512]{0:T(512)S(1)}, u32[]{:S(2)}, u32[]{:S(2)}) collective-permute-start(s32[512]{0:T(512)} %bitcast.364), channel_id=1, source_target_pairs={{0,16},{8,24},{16,0},{24,8},{1,17},{9,25},{17,1},{25,9},{2,18},{10... | collective-permute-start | bytes 6152 | tf_op jit(solution)/shard_map/ppermute | solution.py:87
  66.8 46.3 %collective-permute-start.4 = (bf16[512,2048]{1,0:T(8,128)(2,1)S(1)}, bf16[512,2048]{1,0:T(8,128)(2,1)}, u32[]{:S(2)}, u32[]{:S(2)}) collective-permute-start(bf16[512,2048]{1,0:T(8,128)(2,1)S(1)} %bitcast.326), channel_id=1, source_target_pairs={{0,16},{8,24},{16,0},{24,8},{1,17},{9,25},{17,1},{25,9},{2,18},{10... | collective-permute-start | bytes 6291464 | tf_op jit(solution)/shard_map/ppermute | solution.py:87
  96.5 24.7 %collective-permute-start.3 = (bf16[512,2048]{1,0:T(8,128)(2,1)S(1)}, bf16[512,2048]{1,0:T(8,128)(2,1)S(1)}, u32[]{:S(2)}, u32[]{:S(2)}) collective-permute-start(bf16[512,2048]{1,0:T(8,128)(2,1)S(1)} %bitcast.327), channel_id=1, source_target_pairs={{0,8},{8,0},{16,24},{24,16},{1,9},{9,1},{17,25},{25,17},{2,10},{10... | collective-permute-start | bytes 6291464 | tf_op jit(solution)/shard_map/ppermute | solution.py:82
  168.9 59.4 %collective-permute-start.25 = (bf16[512,2048]{1,0:T(8,128)(2,1)}, bf16[512,2048]{1,0:T(8,128)(2,1)}, u32[]{:S(2)}, u32[]{:S(2)}) collective-permute-start(bf16[512,2048]{1,0:T(8,128)(2,1)} %get-tuple-element.67), channel_id=1, source_target_pairs={{0,8},{8,0},{16,24},{24,16},{1,9},{9,1},{17,25},{25,17},{2,10},{10... | collective-permute-start | bytes 6291464 | tf_op jit(solution)/shard_map/ppermute | solution.py:82
  170.3 24.7 %collective-permute-start.37 = (bf16[256,1408]{0,1:T(8,128)(2,1)}, bf16[256,1408]{0,1:T(8,128)(2,1)}, u32[]{:S(2)}, u32[]{:S(2)}) collective-permute-start(bf16[256,1408]{0,1:T(8,128)(2,1)} %get-tuple-element.123), channel_id=1, source_target_pairs={{0,2},{2,4},{4,6},{6,7},{7,5},{5,3},{3,1},{1,0},{8,10},{10,12},{12... | collective-permute-start | bytes 2162696 | tf_op jit(solution)/shard_map/ppermute | solution.py:52
  176.4 24.0 %collective-permute-start.40 = (bf16[256,1408]{0,1:T(8,128)(2,1)}, bf16[256,1408]{0,1:T(8,128)(2,1)}, u32[]{:S(2)}, u32[]{:S(2)}) collective-permute-start(bf16[256,1408]{0,1:T(8,128)(2,1)} %get-tuple-element.123), channel_id=1, source_target_pairs={{2,0},{4,2},{6,4},{7,6},{5,7},{3,5},{1,3},{0,1},{10,8},{12,10},{14... | collective-permute-start | bytes 2162696 | tf_op jit(solution)/shard_map/ppermute | solution.py:52
  176.4 49.7 %collective-permute-start.30 = (bf16[256,1408]{0,1:T(8,128)(2,1)}, bf16[256,1408]{0,1:T(8,128)(2,1)}, u32[]{:S(2)}, u32[]{:S(2)}) collective-permute-start(bf16[256,1408]{0,1:T(8,128)(2,1)} %get-tuple-element.122), channel_id=1, source_target_pairs={{0,2},{2,4},{4,6},{6,7},{7,5},{5,3},{3,1},{1,0},{8,10},{10,12},{12... | collective-permute-start | bytes 2162696 | tf_op jit(solution)/shard_map/ppermute | solution.py:52
  183.5 39.1 %collective-permute-start.44 = (bf16[176,2048]{1,0:T(8,128)(2,1)}, bf16[176,2048]{1,0:T(8,128)(2,1)}, u32[]{:S(2)}, u32[]{:S(2)}) collective-permute-start(bf16[176,2048]{1,0:T(8,128)(2,1)} %get-tuple-element.52), channel_id=1, source_target_pairs={{0,2},{2,4},{4,6},{6,7},{7,5},{5,3},{3,1},{1,0},{8,10},{10,12},{12... | collective-permute-start | bytes 2162696 | tf_op jit(solution)/shard_map/ppermute | solution.py:52
  195.0 33.3 %collective-permute-start.34 = (bf16[256,1408]{0,1:T(8,128)(2,1)}, bf16[256,1408]{0,1:T(8,128)(2,1)}, u32[]{:S(2)}, u32[]{:S(2)}) collective-permute-start(bf16[256,1408]{0,1:T(8,128)(2,1)} %get-tuple-element.122), channel_id=1, source_target_pairs={{2,0},{4,2},{6,4},{7,6},{5,7},{3,5},{1,3},{0,1},{10,8},{12,10},{14... | collective-permute-start | bytes 2162696 | tf_op jit(solution)/shard_map/ppermute | solution.py:52
  200.4 37.7 %collective-permute-start.38 = (bf16[256,1408]{0,1:T(8,128)(2,1)}, bf16[256,1408]{0,1:T(8,128)(2,1)S(1)}, u32[]{:S(2)}, u32[]{:S(2)}) collective-permute-start(bf16[256,1408]{0,1:T(8,128)(2,1)} %collective-permute-done.37), channel_id=1, source_target_pairs={{0,2},{2,4},{4,6},{6,7},{7,5},{5,3},{3,1},{1,0},{8,10},{10,12},{12... | collective-permute-start | bytes 2162696 | tf_op jit(solution)/shard_map/ppermute | solution.py:52
  226.1 27.4 %collective-permute-start.31 = (bf16[256,1408]{0,1:T(8,128)(2,1)}, bf16[256,1408]{0,1:T(8,128)(2,1)}, u32[]{:S(2)}, u32[]{:S(2)}) collective-permute-start(bf16[256,1408]{0,1:T(8,128)(2,1)} %collective-permute-done.30), channel_id=1, source_target_pairs={{0,2},{2,4},{4,6},{6,7},{7,5},{5,3},{3,1},{1,0},{8,10},{10,12},{12... | collective-permute-start | bytes 2162696 | tf_op jit(solution)/shard_map/ppermute | solution.py:52
  228.3 27.4 %collective-permute-start.35 = (bf16[256,1408]{0,1:T(8,128)(2,1)}, bf16[256,1408]{0,1:T(8,128)(2,1)}, u32[]{:S(2)}, u32[]{:S(2)}) collective-permute-start(bf16[256,1408]{0,1:T(8,128)(2,1)} %collective-permute-done.34), channel_id=1, source_target_pairs={{2,0},{4,2},{6,4},{7,6},{5,7},{3,5},{1,3},{0,1},{10,8},{12,10},{14... | collective-permute-start | bytes 2162696 | tf_op jit(solution)/shard_map/ppermute | solution.py:52
  228.3 68.8 %collective-permute-start.24 = (bf16[512,2048]{1,0:T(8,128)(2,1)}, bf16[512,2048]{1,0:T(8,128)(2,1)}, u32[]{:S(2)}, u32[]{:S(2)}) collective-permute-start(bf16[512,2048]{1,0:T(8,128)(2,1)} %get-tuple-element.66), channel_id=1, source_target_pairs={{0,8},{8,0},{16,24},{24,16},{1,9},{9,1},{17,25},{25,17},{2,10},{10... | collective-permute-start | bytes 6291464 | tf_op jit(solution)/shard_map/ppermute | solution.py:82
  238.0 59.2 %collective-permute-start.26 = (bf16[512,2048]{1,0:T(8,128)(2,1)}, bf16[512,2048]{1,0:T(8,128)(2,1)}, u32[]{:S(2)}, u32[]{:S(2)}) collective-permute-start(bf16[512,2048]{1,0:T(8,128)(2,1)} %add_convert_fusion.5), channel_id=1, source_target_pairs={{0,16},{8,24},{16,0},{24,8},{1,17},{9,25},{17,1},{25,9},{2,18},{10... | collective-permute-start | bytes 6291464 | tf_op jit(solution)/shard_map/ppermute | solution.py:87
  244.1 24.8 %collective-permute-start.45 = (bf16[176,2048]{1,0:T(8,128)(2,1)}, bf16[176,2048]{1,0:T(8,128)(2,1)}, u32[]{:S(2)}, u32[]{:S(2)}) collective-permute-start(bf16[176,2048]{1,0:T(8,128)(2,1)} %collective-permute-done.44), channel_id=1, source_target_pairs={{0,2},{2,4},{4,6},{6,7},{7,5},{5,3},{3,1},{1,0},{8,10},{10,12},{12... | collective-permute-start | bytes 2162696 | tf_op jit(solution)/shard_map/ppermute | solution.py:52
  257.1 27.2 %collective-permute-start.39 = (bf16[256,1408]{0,1:T(8,128)(2,1)}, bf16[256,1408]{0,1:T(8,128)(2,1)}, u32[]{:S(2)}, u32[]{:S(2)}) collective-permute-start(bf16[256,1408]{0,1:T(8,128)(2,1)} %copy-done.37), channel_id=1, source_target_pairs={{0,2},{2,4},{4,6},{6,7},{7,5},{5,3},{3,1},{1,0},{8,10},{10,12},{12... | collective-permute-start | bytes 2162696 | tf_op jit(solution)/shard_map/ppermute | solution.py:52
  259.4 27.2 %collective-permute-start.42 = (bf16[256,1408]{0,1:T(8,128)(2,1)}, bf16[256,1408]{0,1:T(8,128)(2,1)}, u32[]{:S(2)}, u32[]{:S(2)}) collective-permute-start(bf16[256,1408]{0,1:T(8,128)(2,1)} %collective-permute-done.41), channel_id=1, source_target_pairs={{2,0},{4,2},{6,4},{7,6},{5,7},{3,5},{1,3},{0,1},{10,8},{12,10},{14... | collective-permute-start | bytes 2162696 | tf_op jit(solution)/shard_map/ppermute | solution.py:52
  268.9 37.8 %collective-permute-start.48 = (bf16[176,2048]{1,0:T(8,128)(2,1)}, bf16[176,2048]{1,0:T(8,128)(2,1)}, u32[]{:S(2)}, u32[]{:S(2)}) collective-permute-start(bf16[176,2048]{1,0:T(8,128)(2,1)} %get-tuple-element.52), channel_id=1, source_target_pairs={{2,0},{4,2},{6,4},{7,6},{5,7},{3,5},{1,3},{0,1},{10,8},{12,10},{14... | collective-permute-start | bytes 2162696 | tf_op jit(solution)/shard_map/ppermute | solution.py:52
  284.4 49.5 %collective-permute-start.55 = (bf16[512,2048]{1,0:T(8,128)(2,1)}, bf16[512,2048]{1,0:T(8,128)(2,1)}, u32[]{:S(2)}, u32[]{:S(2)}) collective-permute-start(bf16[512,2048]{1,0:T(8,128)(2,1)} %bitcast.79), channel_id=1, source_target_pairs={{0,16},{8,24},{16,0},{24,8},{1,17},{9,25},{17,1},{25,9},{2,18},{10... | collective-permute-start | bytes 6291464 | tf_op jit(solution)/shard_map/ppermute | solution.py:87
  306.7 68.7 %collective-permute-start.28 = (bf16[512,2048]{1,0:T(8,128)(2,1)}, bf16[512,2048]{1,0:T(8,128)(2,1)}, u32[]{:S(2)}, u32[]{:S(2)}) collective-permute-start(bf16[512,2048]{1,0:T(8,128)(2,1)} %multiply_convert_fusion.4), channel_id=1, source_target_pairs={{0,16},{8,24},{16,0},{24,8},{1,17},{9,25},{17,1},{25,9},{2,18},{10... | collective-permute-start | bytes 6291464 | tf_op jit(solution)/shard_map/ppermute | solution.py:87
  314.7 29.4 %collective-permute-start.43 = (bf16[256,1408]{0,1:T(8,128)(2,1)}, bf16[256,1408]{0,1:T(8,128)(2,1)S(1)}, u32[]{:S(2)}, u32[]{:S(2)}) collective-permute-start(bf16[256,1408]{0,1:T(8,128)(2,1)} %collective-permute-done.42), channel_id=1, source_target_pairs={{2,0},{4,2},{6,4},{7,6},{5,7},{3,5},{1,3},{0,1},{10,8},{12,10},{14... | collective-permute-start | bytes 2162696 | tf_op jit(solution)/shard_map/ppermute | solution.py:52
  318.5 32.2 %collective-permute-start.33 = (bf16[256,1408]{0,1:T(8,128)(2,1)}, bf16[256,1408]{0,1:T(8,128)(2,1)}, u32[]{:S(2)}, u32[]{:S(2)}) collective-permute-start(bf16[256,1408]{0,1:T(8,128)(2,1)} %collective-permute-done.32), channel_id=1, source_target_pairs={{0,2},{2,4},{4,6},{6,7},{7,5},{5,3},{3,1},{1,0},{8,10},{10,12},{12... | collective-permute-start | bytes 2162696 | tf_op jit(solution)/shard_map/ppermute | solution.py:52
  328.7 102.7 %collective-permute-start.54 = (bf16[512,2048]{1,0:T(8,128)(2,1)}, bf16[512,2048]{1,0:T(8,128)(2,1)}, u32[]{:S(2)}, u32[]{:S(2)}) collective-permute-start(bf16[512,2048]{1,0:T(8,128)(2,1)} %bitcast.79), channel_id=1, source_target_pairs={{0,8},{8,0},{16,24},{24,16},{1,9},{9,1},{17,25},{25,17},{2,10},{10... | collective-permute-start | bytes 6291464 | tf_op jit(solution)/shard_map/ppermute | solution.py:82
  333.9 49.7 %collective-permute-start.50 = (bf16[176,2048]{1,0:T(8,128)(2,1)}, bf16[176,2048]{1,0:T(8,128)(2,1)}, u32[]{:S(2)}, u32[]{:S(2)}) collective-permute-start(bf16[176,2048]{1,0:T(8,128)(2,1)} %collective-permute-done.49), channel_id=1, source_target_pairs={{2,0},{4,2},{6,4},{7,6},{5,7},{3,5},{1,3},{0,1},{10,8},{12,10},{14... | collective-permute-start | bytes 2162696 | tf_op jit(solution)/shard_map/ppermute | solution.py:52
  344.2 87.2 %collective-permute-start.56 = (bf16[512,2048]{1,0:T(8,128)(2,1)}, bf16[512,2048]{1,0:T(8,128)(2,1)}, u32[]{:S(2)}, u32[]{:S(2)}) collective-permute-start(bf16[512,2048]{1,0:T(8,128)(2,1)} %collective-permute-done.55), channel_id=1, source_target_pairs={{0,8},{8,0},{16,24},{24,16},{1,9},{9,1},{17,25},{25,17},{2,10},{10... | collective-permute-start | bytes 6291464 | tf_op jit(solution)/shard_map/ppermute | solution.py:82
  495.0 133.4 %collective-permute-start.109 = (bf16[176,2048]{1,0:T(8,128)(2,1)}, bf16[176,2048]{1,0:T(8,128)(2,1)}, u32[]{:S(2)}, u32[]{:S(2)}) collective-permute-start(bf16[176,2048]{1,0:T(8,128)(2,1)} %get-tuple-element.72), channel_id=1, source_target_pairs={{0,2},{2,4},{4,6},{6,7},{7,5},{5,3},{3,1},{1,0},{8,10},{10,12},{12... | collective-permute-start | bytes 2162696 | tf_op jit(solution)/shard_map/ppermute | solution.py:66
  497.1 149.0 %collective-permute-start.113 = (bf16[176,2048]{1,0:T(8,128)(2,1)}, bf16[176,2048]{1,0:T(8,128)(2,1)}, u32[]{:S(2)}, u32[]{:S(2)}) collective-permute-start(bf16[176,2048]{1,0:T(8,128)(2,1)} %get-tuple-element.73), channel_id=1, source_target_pairs={{2,0},{4,2},{6,4},{7,6},{5,7},{3,5},{1,3},{0,1},{10,8},{12,10},{14... | collective-permute-start | bytes 2162696 | tf_op jit(solution)/shard_map/ppermute | solution.py:66
  562.5 59.2 %collective-permute-start.89 = (bf16[256,1408]{0,1:T(8,128)(2,1)}, bf16[256,1408]{0,1:T(8,128)(2,1)}, u32[]{:S(2)}, u32[]{:S(2)}) collective-permute-start(bf16[256,1408]{0,1:T(8,128)(2,1)} %bitcast.357), channel_id=1, source_target_pairs={{0,2},{2,4},{4,6},{6,7},{7,5},{5,3},{3,1},{1,0},{8,10},{10,12},{12... | collective-permute-start | bytes 2162696 | tf_op jit(solution)/shard_map/ppermute | solution.py:66
  568.5 54.8 %collective-permute-start.93 = (bf16[256,1408]{0,1:T(8,128)(2,1)}, bf16[256,1408]{0,1:T(8,128)(2,1)}, u32[]{:S(2)}, u32[]{:S(2)}) collective-permute-start(bf16[256,1408]{0,1:T(8,128)(2,1)} %bitcast.356), channel_id=1, source_target_pairs={{2,0},{4,2},{6,4},{7,6},{5,7},{3,5},{1,3},{0,1},{10,8},{12,10},{14... | collective-permute-start | bytes 2162696 | tf_op jit(solution)/shard_map/ppermute | solution.py:66
  575.4 51.0 %collective-permute-start.99 = (bf16[256,1408]{0,1:T(8,128)(2,1)}, bf16[256,1408]{0,1:T(8,128)(2,1)}, u32[]{:S(2)}, u32[]{:S(2)}) collective-permute-start(bf16[256,1408]{0,1:T(8,128)(2,1)} %bitcast.131), channel_id=1, source_target_pairs={{0,2},{2,4},{4,6},{6,7},{7,5},{5,3},{3,1},{1,0},{8,10},{10,12},{12... | collective-permute-start | bytes 2162696 | tf_op jit(solution)/shard_map/ppermute | solution.py:66
  623.3 118.4 %collective-permute-start.52 = (bf16[512,2048]{1,0:T(8,128)(2,1)}, bf16[512,2048]{1,0:T(8,128)(2,1)S(1)}, u32[]{:S(2)}, u32[]{:S(2)}) collective-permute-start(bf16[512,2048]{1,0:T(8,128)(2,1)} %get-tuple-element.65), channel_id=1, source_target_pairs={{0,8},{8,0},{16,24},{24,16},{1,9},{9,1},{17,25},{25,17},{2,10},{10... | collective-permute-start | bytes 6291464 | tf_op jit(solution)/shard_map/ppermute | solution.py:82
  626.4 52.4 %collective-permute-start.58 = (bf16[512,2048]{1,0:T(8,128)(2,1)S(1)}, bf16[512,2048]{1,0:T(8,128)(2,1)S(1)}, u32[]{:S(2)}, u32[]{:S(2)}) collective-permute-start(bf16[512,2048]{1,0:T(8,128)(2,1)S(1)} %copy-done.35), channel_id=1, source_target_pairs={{0,8},{8,0},{16,24},{24,16},{1,9},{9,1},{17,25},{25,17},{2,10},{10... | collective-permute-start | bytes 6291464 | tf_op jit(solution)/shard_map/ppermute | solution.py:82
  638.1 23.3 %collective-permute-start.110 = (bf16[176,2048]{1,0:T(8,128)(2,1)S(1)}, bf16[176,2048]{1,0:T(8,128)(2,1)S(1)}, u32[]{:S(2)}, u32[]{:S(2)}) collective-permute-start(bf16[176,2048]{1,0:T(8,128)(2,1)S(1)} %fusion.14), channel_id=1, source_target_pairs={{0,2},{2,4},{4,6},{6,7},{7,5},{5,3},{3,1},{1,0},{8,10},{10,12},{12... | collective-permute-start | bytes 2162696 | tf_op jit(solution)/shard_map/ppermute | solution.py:66
  646.2 30.7 %collective-permute-start.100 = (bf16[256,1408]{0,1:T(8,128)(2,1)S(1)}, bf16[256,1408]{0,1:T(8,128)(2,1)S(1)}, u32[]{:S(2)}, u32[]{:S(2)}) collective-permute-start(bf16[256,1408]{0,1:T(8,128)(2,1)S(1)} %fusion.21), channel_id=1, source_target_pairs={{0,2},{2,4},{4,6},{6,7},{7,5},{5,3},{3,1},{1,0},{8,10},{10,12},{12... | collective-permute-start | bytes 2162696 | tf_op jit(solution)/shard_map/ppermute | solution.py:66
  663.1 46.6 %collective-permute-start.111 = (bf16[176,2048]{1,0:T(8,128)(2,1)S(1)}, bf16[176,2048]{1,0:T(8,128)(2,1)S(1)}, u32[]{:S(2)}, u32[]{:S(2)}) collective-permute-start(bf16[176,2048]{1,0:T(8,128)(2,1)S(1)} %get-tuple-element.70), channel_id=1, source_target_pairs={{0,2},{2,4},{4,6},{6,7},{7,5},{5,3},{3,1},{1,0},{8,10},{10,12},{12... | collective-permute-start | bytes 2162696 | tf_op jit(solution)/shard_map/ppermute | solution.py:66
  676.9 34.0 %collective-permute-start.114 = (bf16[176,2048]{1,0:T(8,128)(2,1)S(1)}, bf16[176,2048]{1,0:T(8,128)(2,1)S(1)}, u32[]{:S(2)}, u32[]{:S(2)}) collective-permute-start(bf16[176,2048]{1,0:T(8,128)(2,1)S(1)} %get-tuple-element.71), channel_id=1, source_target_pairs={{2,0},{4,2},{6,4},{7,6},{5,7},{3,5},{1,3},{0,1},{10,8},{12,10},{14... | collective-permute-start | bytes 2162696 | tf_op jit(solution)/shard_map/ppermute | solution.py:66
  677.5 30.2 %collective-permute-start.91 = (bf16[256,1408]{0,1:T(8,128)(2,1)S(1)}, bf16[256,1408]{0,1:T(8,128)(2,1)S(1)}, u32[]{:S(2)}, u32[]{:S(2)}) collective-permute-start(bf16[256,1408]{0,1:T(8,128)(2,1)S(1)} %fusion.27), channel_id=1, source_target_pairs={{0,2},{2,4},{4,6},{6,7},{7,5},{5,3},{3,1},{1,0},{8,10},{10,12},{12... | collective-permute-start | bytes 2162696 | tf_op jit(solution)/shard_map/ppermute | solution.py:66
  678.8 29.6 %collective-permute-start.104 = (bf16[256,1408]{0,1:T(8,128)(2,1)S(1)}, bf16[256,1408]{0,1:T(8,128)(2,1)S(1)}, u32[]{:S(2)}, u32[]{:S(2)}) collective-permute-start(bf16[256,1408]{0,1:T(8,128)(2,1)S(1)} %fusion.18), channel_id=1, source_target_pairs={{2,0},{4,2},{6,4},{7,6},{5,7},{3,5},{1,3},{0,1},{10,8},{12,10},{14... | collective-permute-start | bytes 2162696 | tf_op jit(solution)/shard_map/ppermute | solution.py:66
  709.7 29.4 %collective-permute-start.101 = (bf16[256,1408]{0,1:T(8,128)(2,1)S(1)}, bf16[256,1408]{0,1:T(8,128)(2,1)S(1)}, u32[]{:S(2)}, u32[]{:S(2)}) collective-permute-start(bf16[256,1408]{0,1:T(8,128)(2,1)S(1)} %fusion.20), channel_id=1, source_target_pairs={{0,2},{2,4},{4,6},{6,7},{7,5},{5,3},{3,1},{1,0},{8,10},{10,12},{12... | collective-permute-start | bytes 2162696 | tf_op jit(solution)/shard_map/ppermute | solution.py:66
  710.9 29.1 %collective-permute-start.105 = (bf16[256,1408]{0,1:T(8,128)(2,1)S(1)}, bf16[256,1408]{0,1:T(8,128)(2,1)S(1)}, u32[]{:S(2)}, u32[]{:S(2)}) collective-permute-start(bf16[256,1408]{0,1:T(8,128)(2,1)S(1)} %fusion.17), channel_id=1, source_target_pairs={{2,0},{4,2},{6,4},{7,6},{5,7},{3,5},{1,3},{0,1},{10,8},{12,10},{14... | collective-permute-start | bytes 2162696 | tf_op jit(solution)/shard_map/ppermute | solution.py:66
  724.5 124.4 %collective-permute-start.57 = (bf16[512,2048]{1,0:T(8,128)(2,1)S(1)}, bf16[512,2048]{1,0:T(8,128)(2,1)S(1)}, u32[]{:S(2)}, u32[]{:S(2)}) collective-permute-start(bf16[512,2048]{1,0:T(8,128)(2,1)S(1)} %copy-done.33), channel_id=1, source_target_pairs={{0,8},{8,0},{16,24},{24,16},{1,9},{9,1},{17,25},{25,17},{2,10},{10... | collective-permute-start | bytes 6291464 | tf_op jit(solution)/shard_map/ppermute | solution.py:82
  727.8 26.9 %collective-permute-start.112 = (bf16[176,2048]{1,0:T(8,128)(2,1)S(1)}, bf16[176,2048]{1,0:T(8,128)(2,1)S(1)}, u32[]{:S(2)}, u32[]{:S(2)}) collective-permute-start(bf16[176,2048]{1,0:T(8,128)(2,1)S(1)} %get-tuple-element.68), channel_id=1, source_target_pairs={{0,2},{2,4},{4,6},{6,7},{7,5},{5,3},{3,1},{1,0},{8,10},{10,12},{12... | collective-permute-start | bytes 2162696 | tf_op jit(solution)/shard_map/ppermute | solution.py:66
  739.2 109.8 %collective-permute-start.59 = (bf16[512,2048]{1,0:T(8,128)(2,1)S(1)}, bf16[512,2048]{1,0:T(8,128)(2,1)S(1)}, u32[]{:S(2)}, u32[]{:S(2)}) collective-permute-start(bf16[512,2048]{1,0:T(8,128)(2,1)S(1)} %add_convert_fusion.2), channel_id=1, source_target_pairs={{0,16},{8,24},{16,0},{24,8},{1,17},{9,25},{17,1},{25,9},{2,18},{10... | collective-permute-start | bytes 6291464 | tf_op jit(solution)/shard_map/ppermute | solution.py:87
  761.6 90.1 %collective-permute-start.51 = (bf16[512,2048]{1,0:T(8,128)(2,1)}, bf16[512,2048]{1,0:T(8,128)(2,1)S(1)}, u32[]{:S(2)}, u32[]{:S(2)}) collective-permute-start(bf16[512,2048]{1,0:T(8,128)(2,1)} %get-tuple-element.64), channel_id=1, source_target_pairs={{0,8},{8,0},{16,24},{24,16},{1,9},{9,1},{17,25},{25,17},{2,10},{10... | collective-permute-start | bytes 6291464 | tf_op jit(solution)/shard_map/ppermute | solution.py:82
  764.7 118.3 %collective-permute-start.53 = (bf16[512,2048]{1,0:T(8,128)(2,1)}, bf16[512,2048]{1,0:T(8,128)(2,1)}, u32[]{:S(2)}, u32[]{:S(2)}) collective-permute-start(bf16[512,2048]{1,0:T(8,128)(2,1)} %add_convert_fusion.4), channel_id=1, source_target_pairs={{0,16},{8,24},{16,0},{24,8},{1,17},{9,25},{17,1},{25,9},{2,18},{10... | collective-permute-start | bytes 6291464 | tf_op jit(solution)/shard_map/ppermute | solution.py:87
  764.8 75.9 %collective-permute-start.97 = (bf16[256,1408]{0,1:T(8,128)(2,1)}, bf16[256,1408]{0,1:T(8,128)(2,1)}, u32[]{:S(2)}, u32[]{:S(2)}) collective-permute-start(bf16[256,1408]{0,1:T(8,128)(2,1)} %get-tuple-element.46), channel_id=1, source_target_pairs={{0,16},{8,24},{16,0},{24,8},{1,17},{9,25},{17,1},{25,9},{2,18},{10... | collective-permute-start | bytes 2162696 | tf_op jit(solution)/shard_map/ppermute | solution.py:87
  840.7 51.6 %collective-permute-start.116 = (bf16[176,2048]{1,0:T(8,128)(2,1)S(1)}, bf16[176,2048]{1,0:T(8,128)(2,1)}, u32[]{:S(2)}, u32[]{:S(2)}) collective-permute-start(bf16[176,2048]{1,0:T(8,128)(2,1)S(1)} %get-tuple-element.42), channel_id=1, source_target_pairs={{0,8},{8,0},{16,24},{24,16},{1,9},{9,1},{17,25},{25,17},{2,10},{10... | collective-permute-start | bytes 2162696 | tf_op jit(solution)/shard_map/ppermute | solution.py:82
  849.0 33.2 %collective-permute-start.107 = (bf16[256,1408]{0,1:T(8,128)(2,1)}, bf16[256,1408]{0,1:T(8,128)(2,1)}, u32[]{:S(2)}, u32[]{:S(2)}) collective-permute-start(bf16[256,1408]{0,1:T(8,128)(2,1)} %get-tuple-element.44), channel_id=1, source_target_pairs={{0,16},{8,24},{16,0},{24,8},{1,17},{9,25},{17,1},{25,9},{2,18},{10... | collective-permute-start | bytes 2162696 | tf_op jit(solution)/shard_map/ppermute | solution.py:87
  851.7 43.4 %collective-permute-start.98 = (bf16[256,1408]{0,1:T(8,128)(2,1)}, bf16[256,1408]{0,1:T(8,128)(2,1)}, u32[]{:S(2)}, u32[]{:S(2)}) collective-permute-start(bf16[256,1408]{0,1:T(8,128)(2,1)} %collective-permute-done.97), channel_id=1, source_target_pairs={{0,8},{8,0},{16,24},{24,16},{1,9},{9,1},{17,25},{25,17},{2,10},{10... | collective-permute-start | bytes 2162696 | tf_op jit(solution)/shard_map/ppermute | solution.py:82
  866.7 75.0 %collective-permute-start.118 = (bf16[176,2048]{1,0:T(8,128)(2,1)}, bf16[176,2048]{1,0:T(8,128)(2,1)}, u32[]{:S(2)}, u32[]{:S(2)}) collective-permute-start(bf16[176,2048]{1,0:T(8,128)(2,1)} %collective-permute-done.117), channel_id=1, source_target_pairs={{0,8},{8,0},{16,24},{24,16},{1,9},{9,1},{17,25},{25,17},{2,10},{10... | collective-permute-start | bytes 2162696 | tf_op jit(solution)/shard_map/ppermute | solution.py:82
  891.1 47.2 %collective-permute-start.61 = (bf16[512,2048]{1,0:T(8,128)(2,1)S(1)}, bf16[512,2048]{1,0:T(8,128)(2,1)S(1)}, u32[]{:S(2)}, u32[]{:S(2)}) collective-permute-start(bf16[512,2048]{1,0:T(8,128)(2,1)S(1)} %get-tuple-element.49), channel_id=1, source_target_pairs={{0,16},{8,24},{16,0},{24,8},{1,17},{9,25},{17,1},{25,9},{2,18},{10... | collective-permute-start | bytes 6291464 | tf_op jit(solution)/shard_map/ppermute | solution.py:87
  894.7 55.2 %collective-permute-start.60 = (bf16[512,2048]{1,0:T(8,128)(2,1)S(1)}, bf16[512,2048]{1,0:T(8,128)(2,1)}, u32[]{:S(2)}, u32[]{:S(2)}) collective-permute-start(bf16[512,2048]{1,0:T(8,128)(2,1)S(1)} %get-tuple-element.49), channel_id=1, source_target_pairs={{0,8},{8,0},{16,24},{24,16},{1,9},{9,1},{17,25},{25,17},{2,10},{10... | collective-permute-start | bytes 6291464 | tf_op jit(solution)/shard_map/ppermute | solution.py:82
  959.1 67.9 %collective-permute-start.79 = (bf16[64,2048]{1,0:T(8,128)(2,1)}, bf16[64,2048]{1,0:T(8,128)(2,1)}, u32[]{:S(2)}, u32[]{:S(2)}) collective-permute-start(bf16[64,2048]{1,0:T(8,128)(2,1)} %get-tuple-element.108), channel_id=1, source_target_pairs={{2,0},{4,2},{6,4},{7,6},{5,7},{3,5},{1,3},{0,1},{10,8},{12,10},{14... | collective-permute-start | bytes 786440 | tf_op jit(solution)/shard_map/ppermute | solution.py:66
  959.7 85.2 %collective-permute-start.76 = (bf16[64,2048]{1,0:T(8,128)(2,1)}, bf16[64,2048]{1,0:T(8,128)(2,1)}, u32[]{:S(2)}, u32[]{:S(2)}) collective-permute-start(bf16[64,2048]{1,0:T(8,128)(2,1)} %get-tuple-element.107), channel_id=1, source_target_pairs={{0,2},{2,4},{4,6},{6,7},{7,5},{5,3},{3,1},{1,0},{8,10},{10,12},{12... | collective-permute-start | bytes 786440 | tf_op jit(solution)/shard_map/ppermute | solution.py:66
  1041.3 74.3 %collective-permute-start.64 = (bf16[512,2048]{1,0:T(8,128)(2,1)}, bf16[512,2048]{1,0:T(8,128)(2,1)}, u32[]{:S(2)}, u32[]{:S(2)}) collective-permute-start(bf16[512,2048]{1,0:T(8,128)(2,1)} %get-tuple-element.61), channel_id=1, source_target_pairs={{0,8},{8,0},{16,24},{24,16},{1,9},{9,1},{17,25},{25,17},{2,10},{10... | collective-permute-start | bytes 6291464 | tf_op jit(solution)/shard_map/ppermute | solution.py:82
  1063.1 31.2 %collective-permute-start.72 = (bf16[256,640]{0,1:T(8,128)(2,1)}, bf16[256,640]{0,1:T(8,128)(2,1)S(1)}, u32[]{:S(2)}, u32[]{:S(2)}) collective-permute-start(bf16[256,640]{0,1:T(8,128)(2,1)} %fusion.35), channel_id=1, source_target_pairs={{2,0},{4,2},{6,4},{7,6},{5,7},{3,5},{1,3},{0,1},{10,8},{12,10},{14... | collective-permute-start | bytes 983048 | tf_op jit(solution)/shard_map/ppermute | solution.py:66
  1065.9 29.2 %collective-permute-start.69 = (bf16[256,640]{0,1:T(8,128)(2,1)}, bf16[256,640]{0,1:T(8,128)(2,1)S(1)}, u32[]{:S(2)}, u32[]{:S(2)}) collective-permute-start(bf16[256,640]{0,1:T(8,128)(2,1)} %fusion.37), channel_id=1, source_target_pairs={{0,2},{2,4},{4,6},{6,7},{7,5},{5,3},{3,1},{1,0},{8,10},{10,12},{12... | collective-permute-start | bytes 983048 | tf_op jit(solution)/shard_map/ppermute | solution.py:66
  1072.4 25.4 %collective-permute-start.83 = (bf16[64,2048]{1,0:T(8,128)(2,1)}, bf16[64,2048]{1,0:T(8,128)(2,1)}, u32[]{:S(2)}, u32[]{:S(2)}) collective-permute-start(bf16[64,2048]{1,0:T(8,128)(2,1)} %fusion.48), channel_id=1, source_target_pairs={{0,0},{4,1},{8,10},{12,11},{16,20},{20,21},{24,30},{28,31}} | collective-permute-start | bytes 786440 | tf_op jit(solution)/shard_map/ppermute | solution.py:150
  1094.3 46.9 %collective-permute-start.63 = (bf16[512,2048]{1,0:T(8,128)(2,1)}, bf16[512,2048]{1,0:T(8,128)(2,1)}, u32[]{:S(2)}, u32[]{:S(2)}) collective-permute-start(bf16[512,2048]{1,0:T(8,128)(2,1)} %get-tuple-element.60), channel_id=1, source_target_pairs={{0,8},{8,0},{16,24},{24,16},{1,9},{9,1},{17,25},{25,17},{2,10},{10... | collective-permute-start | bytes 6291464 | tf_op jit(solution)/shard_map/ppermute | solution.py:82
  1120.1 48.0 %collective-permute-start.65 = (bf16[512,2048]{1,0:T(8,128)(2,1)}, bf16[512,2048]{1,0:T(8,128)(2,1)}, u32[]{:S(2)}, u32[]{:S(2)}) collective-permute-start(bf16[512,2048]{1,0:T(8,128)(2,1)} %add_convert_fusion.1), channel_id=1, source_target_pairs={{0,16},{8,24},{16,0},{24,8},{1,17},{9,25},{17,1},{25,9},{2,18},{10... | collective-permute-start | bytes 6291464 | tf_op jit(solution)/shard_map/ppermute | solution.py:87
  (121 other events, 1949.9 us)

commit v2 on v1

--- a/solution.py
+++ b/solution.py
@@ -18,59 +18,72 @@
 F32 = jnp.float32
 
 
-def ring_order(n):
-    if n % 2:
-        return list(range(n))
-    return list(range(0, n, 2)) + list(range(n - 1, 0, -2))
-
-
-class Ring:
-    def __init__(self):
-        self.n = n = lax.axis_size(F)
-        order = ring_order(n)
-        where = [order.index(i) for i in range(n)]
-        self.order = jnp.array(order + order, jnp.int32)
-        self.pos = jnp.array(where, jnp.int32)[lax.axis_index(F)]
-        self.up = [(order[i], order[(i + 1) % n]) for i in range(n)]
-        self.down = [(b, a) for a, b in self.up]
-
-    def member(self, distance):
-        return self.order[lax.rem(self.pos + distance + self.n, self.n)]
-
-    def paths(self, flip):
-        long, short = self.n // 2, (self.n - 1) // 2
-        if flip:
-            long, short = short, long
-        return ((self.up, 1, long), (self.down, -1, short))
-
-    def gather(self, block, flip=False):
-        out = jnp.zeros((self.n,) + block.shape, block.dtype)
-        out = lax.dynamic_update_index_in_dim(out, block, lax.axis_index(F), 0)
-        for perm, sign, steps in self.paths(flip):
-            moving = block
-            for d in range(1, steps + 1):
-                moving = lax.ppermute(moving, F, perm)
-                out = lax.dynamic_update_index_in_dim(out, moving, self.member(-sign * d), 0)
-        return out
-
-    def scatter_sum(self, stacked, flip=False):
-        def part(index):
-            return lax.dynamic_index_in_dim(stacked, index, 0, keepdims=False)
-
-        total = part(lax.axis_index(F)).astype(F32)
-        for perm, sign, steps in self.paths(flip):
-            if not steps:
-                continue
-            moving = part(self.member(sign * steps))
-            for d in range(steps - 1, -1, -1):
-                arrived = lax.ppermute(moving, F, perm)
-                if d:
-                    moving = (
-                        arrived.astype(F32) + part(self.member(sign * d)).astype(F32)
-                    ).astype(stacked.dtype)
-                else:
-                    total = total + arrived.astype(F32)
-        return total
+def after(value, *earlier):
+    return lax.optimization_barrier((value,) + earlier)[0]
+
+
+def lines():
+    return lax.axis_size(F) // 2
+
+
+def line_shift(value, k):
+    n, m = lax.axis_size(F), lines()
+    return lax.ppermute(value, F, [(j, (j // 2 + k) % m * 2 + j % 2) for j in range(n)])
+
+
+def side_swap(value):
+    return lax.ppermute(value, F, [(j, j ^ 1) for j in range(lax.axis_size(F))])
+
+
+def line_and_side():
+    me = lax.axis_index(F)
+    return me // 2, lax.rem(me, 2)
+
+
+def interleave(own, other):
+    n, m = lax.axis_size(F), lines()
+    line, side = line_and_side()
+    both = jnp.concatenate([own, other], axis=0)
+    size = both.shape[0] // n
+    places = [
+        lax.rem(j // 2 - line + m, m) + m * jnp.where(side == j % 2, 0, 1) for j in range(n)
+    ]
+    return jnp.concatenate(
+        [lax.dynamic_slice_in_dim(both, p * size, size, axis=0) for p in places], axis=0
+    )
+
+
+def scatter_sides(total):
+    m = lines()
+    _, side = line_and_side()
+    parts = total.reshape(m, 2, total.shape[0] // (2 * m), total.shape[1])
+    mine = lax.dynamic_index_in_dim(parts, side, 1, keepdims=False)
+    return mine, side_swap(lax.dynamic_index_in_dim(parts, 1 - side, 1, keepdims=False))
+
+
+def scatter_lines(total):
+    m = lines()
+    line, _ = line_and_side()
+
+    def part(k):
+        return lax.dynamic_index_in_dim(total, lax.rem(line + k, m), 0, keepdims=False)
+
+    return [part(0)] + [line_shift(part(k), k) for k in range(1, m)]
+
+
+def gather_all(block):
+    return lax.all_gather(block, F, axis=0, tiled=True)
+
+
+def scatter_all(total):
+    return lax.psum_scatter(total, F, scatter_dimension=0, tiled=True)
+
+
+def add_all(parts):
+    total = parts[0].astype(F32)
+    for part in parts[1:]:
+        total = total + part.astype(F32)
+    return total
 
 
 def chips():
@@ -104,14 +117,23 @@
     return out
 
 
+def add_cores(parts):
+    sums = []
+    for k in range(chips()):
+        both = parts[2 * k].astype(F32) + core_swap(parts[2 * k + 1]).astype(F32)
+        sums.append(both.astype(BF) if k else both)
+    return sums
+
+
+def add_chips(sums):
+    total = sums[0]
+    for k in range(1, chips()):
+        total = total + chip_shift(sums[k], -k).astype(F32)
+    return total
+
+
 def gather_back(parts):
-    total = None
-    for k in range(chips()):
-        mine = parts[2 * k].astype(F32) + core_swap(parts[2 * k + 1].astype(BF)).astype(F32)
-        if k:
-            mine = chip_shift(mine.astype(BF), -k).astype(F32)
-        total = mine if total is None else total + mine
-    return total
+    return add_chips(add_cores(parts))
 
 
 def in_order(parts):
@@ -320,7 +342,7 @@
             scratch_shapes=[pltpu.VMEM((rows, values), F32), pltpu.VMEM((rows, values), F32)],
         ),
         cost_estimate=pl.CostEstimate(
-            flops=4 * tokens * tokens * values, transcendentals=0, bytes_accessed=8 * tokens * values
+            flops=4 * tokens * values, transcendentals=0, bytes_accessed=8 * tokens
         ),
         name="attention_forward",
     )(meta, qkv, seg_col, seg_row)
@@ -354,7 +376,7 @@
             ],
         ),
         cost_estimate=pl.CostEstimate(
-            flops=10 * tokens * tokens * values, transcendentals=0, bytes_accessed=16 * tokens * values
+            flops=10 * tokens * values, transcendentals=0, bytes_accessed=16 * tokens
         ),
         name="attention_backward",
     )(meta, qkv, seg_col, seg_row, gm, mixed, den, scale)
@@ -392,7 +414,6 @@
 ):
     nc, nf = lax.axis_size(C), lax.axis_size(F)
     c = lax.axis_index(C)
-    ring = Ring()
     rows, width = tokens.shape[1], tokens.shape[2]
     heads = HEADS // nc
     qk = heads * QK
@@ -427,9 +448,7 @@
     part_up = hidden_columns(w_up)
     part_down = lax.dynamic_slice_in_dim(w_down, c * seg_len, seg_len, axis=0)
 
-    x_all = jnp.concatenate(spread(own), axis=0)
     seg_all = jnp.concatenate(spread(segment_ids[0]), axis=0)
-    g_all = jnp.concatenate(spread(grad_top), axis=0)
     nb = nc
     seg_row = seg_all.reshape(nb, 1, rows)
     seg_col = seg_all.reshape(nb * rows, 1)
@@ -437,55 +456,85 @@
         [jnp.stack(spread_index()), seg_row[:, 0, 0], seg_row[:, 0, rows - 1]]
     ).astype(jnp.int32)
 
-    full_qkv = ring.gather(part_qkv).reshape(width, -1)
-    full_out = ring.gather(part_out, True).reshape(heads * VH, width)
-    x_all32 = x_all.astype(F32)
-    scale_one = inverse_rms(x_all32)
-    qkv = (mm(x_all, full_qkv) * scale_one).astype(BF)
+    full_qkv = gather_all(part_qkv)
+    full_out = gather_all(part_out)
+    full_gate = gather_all(part_gate)
+    full_up = gather_all(part_up)
+    down_lines = [line_shift(part_down, -k) for k in range(1, lax.axis_size(F) // 2)]
+
+    x_all = jnp.concatenate(spread(own), axis=0)
+    scale_one = inverse_rms(x_all.astype(F32))
+    qkv = (mm(after(x_all, *down_lines[:2]), full_qkv) * scale_one).astype(BF)
+    g_parts = spread(grad_top)
+    qkv = after(qkv, *down_lines)
+    down_side = jnp.concatenate([part_down] + down_lines, axis=0)
+    down_other = side_swap(down_side)
     mixed, den = attention_forward(meta, qkv, seg_col, seg_row, heads, rows)
 
     def blocks(value):
         return [value[i * rows : (i + 1) * rows] for i in range(nb)]
 
-    residual = own.astype(F32) + gather_back(blocks(mm(mixed, full_out).astype(BF)))
+    projected = mm(after(mixed, *g_parts), full_out).astype(BF)
+    residual = own.astype(F32) + gather_back(blocks(projected))
 
     scale_two = inverse_rms(residual)
     unit_two = residual * scale_two
     n_all = jnp.concatenate(spread(unit_two.astype(BF)), axis=0)
-    full_gate = ring.gather(part_gate).reshape(width, hidden)
-    full_up = ring.gather(part_up, True).reshape(width, hidden)
-    full_down = ring.gather(part_down).reshape(hidden, width)
-    gate = mm(n_all, full_gate)
+    full_down = interleave(down_side, down_other)
+    g_all = jnp.concatenate(g_parts, axis=0)
+    grad_hidden = mm_nt(g_all, full_down)
+    gate = mm(after(n_all, grad_hidden), full_gate)
     up = mm(n_all, full_up)
     sigmoid = jax.nn.sigmoid(gate)
     silu = gate * sigmoid
     act = (silu * up).astype(BF)
-    block_out = residual + gather_back(blocks(mm(act, full_down).astype(BF)))
-
-    grad_hidden = mm_nt(g_all, full_down)
     grad_gate = (grad_hidden * up * sigmoid * (1.0 + gate * (1.0 - sigmoid))).astype(BF)
     grad_up = (grad_hidden * silu).astype(BF)
-    grad_unit_two = gather_back(
-        blocks((mm_nt(grad_gate, full_gate) + mm_nt(grad_up, full_up)).astype(BF))
-    )
-    sum_down = ring.scatter_sum(mm_tn(act, g_all).astype(BF).reshape(nf, seg_len, width))
-    sum_gate = ring.scatter_sum(mm_tn(n_all, grad_gate).astype(BF).reshape(nf, shard, hidden))
-    sum_up = ring.scatter_sum(mm_tn(n_all, grad_up).astype(BF).reshape(nf, shard, hidden), True)
+    projected_two = mm(act, full_down).astype(BF)
+    out_sums = add_cores(blocks(projected_two))
+    grad_gate = after(grad_gate, projected_two)
+    back_two = (mm_nt(grad_gate, full_gate) + mm_nt(grad_up, full_up)).astype(BF)
+    block_out = residual + add_chips(out_sums)
+    back_sums = add_cores(blocks(after(back_two, block_out)))
+
+    total_down = mm_tn(after(act, back_two), g_all).astype(BF)
+    sum_down = scatter_all(total_down)
+    total_gate = mm_tn(n_all, after(grad_gate, total_down, *back_sums)).astype(BF)
+    mine_gate, sent_gate = scatter_sides(total_gate)
+    total_up = mm_tn(n_all, after(grad_up, total_gate)).astype(BF)
+    mine_up, sent_up = scatter_sides(total_up)
+    grad_unit_two = add_chips([after(back_sums[0], total_up)] + back_sums[1:])
 
     grad_residual = grad_top.astype(F32) + scale_two * (
         grad_unit_two - unit_two * jnp.mean(grad_unit_two * unit_two, axis=-1, keepdims=True)
     )
-    b_all = jnp.concatenate(spread(grad_residual.astype(BF)), axis=0)
-
-    grad_mixed = mm_nt(b_all, full_out)
-    sum_out = ring.scatter_sum(
-        mm_tn(mixed, b_all).astype(BF).reshape(nf, (heads * VH) // nf, width), True
-    )
+    branch = grad_residual.astype(BF)
+    b_all = jnp.concatenate(spread(branch), axis=0)
+
+    def both(mine, sent):
+        return (mine.astype(F32) + sent.astype(F32)).astype(BF)
+
+    both_gate = both(mine_gate, after(sent_gate, branch))
+    lines_gate = scatter_lines(both_gate)
+
+    b_all = after(b_all, both_gate)
+    total_out = mm_tn(mixed, b_all).astype(BF)
+    grad_mixed = mm_nt(after(b_all, total_out), full_out)
     grad_qkv = attention_backward(
         meta, qkv, seg_col, seg_row, grad_mixed, mixed, den, scale_one, heads, rows
     )
-    grad_unit_one = gather_back(blocks(mm_nt(grad_qkv, full_qkv).astype(BF)))
-    sum_qkv = ring.scatter_sum(mm_tn(x_all, grad_qkv).astype(BF).reshape(nf, shard, -1))
+    both_up = both(mine_up, after(sent_up, grad_qkv))
+    lines_up = scatter_lines(both_up)
+    grad_qkv = after(grad_qkv, sum_down, both_up, *lines_gate)
+    sum_out = scatter_all(after(total_out, grad_qkv))
+    back_one = mm_nt(grad_qkv, full_qkv).astype(BF)
+    one_sums = add_cores(blocks(back_one))
+    total_qkv = mm_tn(x_all, after(grad_qkv, *one_sums)).astype(BF)
+    grad_unit_one = add_chips(one_sums)
+    sum_qkv = scatter_all(total_qkv)
+    sum_down = after(sum_down, total_qkv)
+    sum_gate = add_all([after(lines_gate[0], grad_unit_one)] + lines_gate[1:])
+    sum_up = add_all([after(lines_up[0], grad_unit_one)] + lines_up[1:])
 
     unit_one = own.astype(F32) * inverse_rms(own.astype(F32))
     input_grad = grad_residual + grad_unit_one - unit_one * jnp.mean(

time: 1200 us -> 1060 us (0.88)
  local copies, waits for them, and re-layouts: 227 us -> 109 us
  starting transfers between devices: 149 us -> 206 us
  waiting for transfers between devices: 386 us -> 331 us
    ppermute x26, starting transfers between devices: 52.3 us -> 126 us  [core_swap(): return lax.ppermute(value, C, [(i, i ^ 1) for i in range(n)])]
    ppermute x13, waiting for transfers between devices: 183 us -> 128 us  [chip_shift(): return lax.ppermute(value, C, [(i, (i + 2 * k) % n) for i in range(n)])]
    dynamic_update_slice x38 -> x0, local copies, waits for them, and re-layouts: 52.1 us -> none  [the longest x35 47.9 us: gather(): lax.dynamic_update_index_in_dim(out, moving, self.member(-sign * d), 0)]
    broadcast_in_dim x17 -> x4, local copies, waits for them, and re-layouts: 32.5 us -> 2.64 us  [in_order(): out = lax.dynamic_update_index_in_dim(out, part, index, 0)]
    ppermute x70 -> x12, waiting for transfers between devices: 202 us -> 182 us  [the longest x9 91.4 us: line_shift(): lax.ppermute(value, F, [(j, (j // 2 + k) % m * 2 + j % 2) for j in range(...]
    unnamed x161 -> x114, local copies, waits for them, and re-layouts: 64.6 us -> 45.3 us
    ppermute x70 -> x12, starting transfers between devices: 67.9 us -> 49.2 us  [the longest x9 25.5 us: line_shift(): lax.ppermute(value, F, [(j, (j // 2 + k) % m * 2 + j % 2) for j in range(...]
    convert_element_type x26 -> x7, other arithmetic: 40.2 us -> 24.4 us  [the longest x4 14.3 us: add_cores(): sums.append(both.astype(BF) if k else both)]
  transfers between devices with their start and end apart: 119 -> 68, of which waited for: 41 -> 18; matrix products, arithmetic and copies ran while one was open for 39% -> 34% of each run, Pallas kernels for 2% -> 4%
where the time goes in v2:
time: 1060 us; the launch traced here: 1040 us
  waiting for transfers between devices  331 us (31%)
  matrix products  233 us (22%)
  starting transfers between devices  206 us (19%)
  local copies, waits for them, and re-layouts  109 us (10%)
  other arithmetic  104 us (10%)
  Pallas kernels  39.8 us (4%)
  between operations  15.4 us (1%)
    ppermute x13, waiting for transfers between devices, chip_shift(): return lax.ppermute(value, C, [(i, (i + 2 * k) % n) for i in range(n)])  128 us
    ppermute x26, starting transfers between devices, core_swap(): return lax.ppermute(value, C, [(i, i ^ 1) for i in range(n)])  126 us
    ppermute x9, waiting for transfers between devices, line_shift(): lax.ppermute(value, F, [(j, (j // 2 + k) % m * 2 + j % 2) for j in range(...  91.4 us
    ppermute x3, waiting for transfers between devices, side_swap(): return lax.ppermute(value, F, [(j, j ^ 1) for j in range(lax.axis_size(F))])  90.5 us
    dot_general x5, matrix products, mm(): return jnp.dot(a, b, preferred_element_type=F32)  82.3 us
    dot_general x5, matrix products, mm_nt(): lax.dot_general(a, b, (((1,), (1,)), ((), ())), preferred_element_type=F32)  78.1 us
    dot_general x5, matrix products, mm_tn(): lax.dot_general(a, b, (((0,), (0,)), ((), ())), preferred_element_type=F32)  72.5 us
    unnamed x114, local copies, waits for them, and re-layouts  45.3 us
  transfers between devices with their start and end apart: 68, of which 18 were waited for; matrix products, arithmetic and copies ran while one was open for 34% of the time, Pallas kernels for 4%

profile of v2, /device:TPU:17, one launch (start us, length us, event | category | flops | bytes accessed | tf_op | source)
XLA Modules:
  0.0 1037.8 jit_solution(3215383629389096029)
XLA Ops:
  15.6 14.2 %collective-permute-done.12 = bf16[64,2048]{1,0:T(8,128)(2,1)S(1)} collective-permute-done((bf16[64,2048]{1,0:T(8,128)(2,1)S(1)}, bf16[64,2048]{1,0:T(8,128)(2,1)S(1)}, u32[]{:S(2)}, u32[]{:S(2)}) %collective-permute-start.12) | collective-permute-done | bytes 262176 | tf_op jit(solution)/shard_map/ppermute | solution.py:163
  30.7 20.7 %collective-permute-start.3 = (bf16[512,2048]{1,0:T(8,128)(2,1)S(1)}, bf16[512,2048]{1,0:T(8,128)(2,1)}, u32[]{:S(2)}, u32[]{:S(2)}) collective-permute-start(bf16[512,2048]{1,0:T(8,128)(2,1)S(1)} %bitcast.145), channel_id=1, source_target_pairs={{0,8},{8,0},{16,24},{24,16},{1,9},{9,1},{17,25},{25,17},{2,10},{10... | collective-permute-start | bytes 6291464 | tf_op jit(solution)/shard_map/ppermute | solution.py:95
  51.4 4.5 copy.27
  56.0 4.6 copy.28
  60.6 37.4 %collective-permute-start.5 = (bf16[512,2048]{1,0:T(8,128)(2,1)}, bf16[512,2048]{1,0:T(8,128)(2,1)}, u32[]{:S(2)}, u32[]{:S(2)}) collective-permute-start(bf16[512,2048]{1,0:T(8,128)(2,1)} %collective-permute-done.4), channel_id=1, source_target_pairs={{0,8},{8,0},{16,24},{24,16},{1,9},{9,1},{17,25},{25,17},{2,10},{10... | collective-permute-start | bytes 6291464 | tf_op jit(solution)/shard_map/ppermute | solution.py:95
  104.3 19.5 %collective-permute-start.2 = (s32[512]{0:T(512)S(1)}, s32[512]{0:T(512)S(1)}, u32[]{:S(2)}, u32[]{:S(2)}) collective-permute-start(s32[512]{0:T(512)S(1)} %collective-permute-done.1), channel_id=1, source_target_pairs={{0,8},{8,0},{16,24},{24,16},{1,9},{9,1},{17,25},{25,17},{2,10},{10... | collective-permute-start | bytes 6152 | tf_op jit(solution)/shard_map/ppermute | solution.py:95
  127.1 11.9 %collective-permute-start.7 = (bf16[176,2048]{1,0:T(8,128)(2,1)S(1)}, bf16[176,2048]{1,0:T(8,128)(2,1)}, u32[]{:S(2)}, u32[]{:S(2)}) collective-permute-start(bf16[176,2048]{1,0:T(8,128)(2,1)S(1)} %get-tuple-element.79), channel_id=1, source_target_pairs={{0,4},{1,5},{2,6},{3,7},{4,0},{5,1},{6,2},{7,3},{8,12},{9,13},{10,... | collective-permute-start | bytes 2162696 | tf_op jit(solution)/shard_map/ppermute | solution.py:31
  144.0 7.3 multiply_reduce_fusion
  151.2 12.9 %collective-permute-done.6 = bf16[176,2048]{1,0:T(8,128)(2,1)S(1)} collective-permute-done((bf16[176,2048]{1,0:T(8,128)(2,1)S(1)}, bf16[176,2048]{1,0:T(8,128)(2,1)S(1)}, u32[]{:S(2)}, u32[]{:S(2)}) %collective-permute-start.6) | collective-permute-done | bytes 720928 | tf_op jit(solution)/shard_map/ppermute | solution.py:31
  164.2 47.7 %collective-permute-done.7 = bf16[176,2048]{1,0:T(8,128)(2,1)} collective-permute-done((bf16[176,2048]{1,0:T(8,128)(2,1)S(1)}, bf16[176,2048]{1,0:T(8,128)(2,1)}, u32[]{:S(2)}, u32[]{:S(2)}) %collective-permute-start.7) | collective-permute-done | bytes 720928 | tf_op jit(solution)/shard_map/ppermute | solution.py:31
  211.9 10.9 %multiply_convert_fusion.3.qkv = bf16[2048,640]{1,0:T(8,128)(2,1)} fusion(bf16[2048,2048]{1,0:T(8,128)(2,1)} %get-tuple-element.33, bf16[2048,640]{1,0:T(8,128)(2,1)} %all-gather.5.cloned.1.call-done, f32[2048]{0:T(1024)S(1)} %add_rsqrt_fusion), kind=kOutput, calls=%fused_computation.32 | convolution fusion | flops 5371330560 | bytes 13639680 | tf_op jit(solution)/shard_map/dot_general | solution.py:386
  222.8 18.4 %collective-permute-done.8 = bf16[176,2048]{1,0:T(8,128)(2,1)} collective-permute-done((bf16[176,2048]{1,0:T(8,128)(2,1)S(1)}, bf16[176,2048]{1,0:T(8,128)(2,1)}, u32[]{:S(2)}, u32[]{:S(2)}) %collective-permute-start.8) | collective-permute-done | bytes 720928 | tf_op jit(solution)/shard_map/ppermute | solution.py:31
  241.3 14.5 %attention_forward.1 = (bf16[2048,512]{1,0:T(8,128)(2,1)}, f32[2048,4]{1,0:T(8,128)}) custom-call(s32[12]{0:T(128)} %concatenate.50.meta, bf16[2048,640]{1,0:T(8,128)(2,1)} %multiply_convert_fusion.3.qkv, s32[2048,1]{1,0:T(8,128)} %copy.26.seg_col, s32[4,1,512]{2,1,0:T(1,128)} %copy-done.27), custom_call_target="tpu_custom_call" | custom-call | flops 4194304 | bytes 16384 | tf_op jit(solution)/shard_map/attention_forward/pallas_call | solution.py:328
  255.8 6.8 convolution_convert_fusion.2
  265.0 3.6 collective-permute-done.17
  271.9 5.0 pad_maximum_fusion.4
  277.0 19.1 %collective-permute-start.22 = (bf16[704,2048]{1,0:T(8,128)(2,1)}, bf16[704,2048]{1,0:T(8,128)(2,1)}, u32[]{:S(2)}, u32[]{:S(2)}) collective-permute-start(bf16[704,2048]{1,0:T(8,128)(2,1)} %pad_maximum_fusion.4), channel_id=1, source_target_pairs={{0,1},{1,0},{2,3},{3,2},{4,5},{5,4},{6,7},{7,6},{8,9},{9,8},{10,11... | collective-permute-start | bytes 8650760 | tf_op jit(solution)/shard_map/ppermute | solution.py:35
  301.2 16.7 %collective-permute-done.18 = bf16[512,2048]{1,0:T(8,128)(2,1)} collective-permute-done((bf16[512,2048]{1,0:T(8,128)(2,1)}, bf16[512,2048]{1,0:T(8,128)(2,1)}, u32[]{:S(2)}, u32[]{:S(2)}) %collective-permute-start.18) | collective-permute-done | bytes 2097184 | tf_op jit(solution)/shard_map/ppermute | solution.py:100
  317.9 5.0 multiply_reduce_fusion.2
  324.5 61.3 %collective-permute-done.22 = bf16[704,2048]{1,0:T(8,128)(2,1)} collective-permute-done((bf16[704,2048]{1,0:T(8,128)(2,1)}, bf16[704,2048]{1,0:T(8,128)(2,1)}, u32[]{:S(2)}, u32[]{:S(2)}) %collective-permute-start.22) | collective-permute-done | bytes 2883616 | tf_op jit(solution)/shard_map/ppermute | solution.py:35
  393.6 21.7 %fusion.13 = f32[2048,1408]{1,0:T(8,128)} fusion(bf16[1408,2048]{1,0:T(8,128)(2,1)} %copy-done.28, bf16[512,2048]{1,0:T(8,128)(2,1)} %collective-permute-done.11, bf16[512,2048]{1,0:T(8,128)(2,1)} %collective-permute-done.10, bf16[512,2048]{1,0:T(8,128)(2,1)} %collective-permute-done.9, bf16[512,2048]{1,0:T(8,128)(2,1)} %bitcast.158), kind=kOutput, calls=%fused_computation.66 | convolution fusion | flops 11844714496 | bytes 25690112 | tf_op jit(solution)/shard_map/dot_general | solution.py:394
  415.3 6.6 pad_maximum_fusion.1
  421.8 21.1 %fusion.18 = f32[2048,1408]{1,0:T(8,128)} fusion(bf16[2048,1408]{0,1:T(8,128)(2,1)} %all-gather.11.cloned.1.call-done, bf16[512,2048]{1,0:T(8,128)(2,1)} %collective-permute-done.21, bf16[512,2048]{1,0:T(8,128)(2,1)} %collective-permute-done.20, bf16[512,2048]{1,0:T(8,128)(2,1)} %collective-permute-done.19, bf16[512,2048]{1,0:T(8,128)(2,1)S(1)} %multiply_convert_fusion.4), kind=kOutput, calls=%fused_computation.137 | convolution fusion | flops 11844714496 | bytes 25690112 | tf_op jit(solution)/shard_map/dot_general | solution.py:386
  442.9 26.5 %multiply_convert_fusion = (bf16[2048,1408]{1,0:T(8,128)(2,1)}, bf16[2048,1408]{1,0:T(8,128)(2,1)}, bf16[2048,1408]{1,0:T(8,128)(2,1)}) fusion(f32[2048,1408]{1,0:T(8,128)} %fusion.13, f32[2048,1408]{1,0:T(8,128)} %fusion.18, bf16[2048,2048]{1,0:T(8,128)(2,1)} %pad_maximum_fusion.1, bf16[2048,1408]{0,1:T(8,128)(2,1)} %all-gather.9.cloned.1.call-done), kind=kOutput, calls=%fused_computation.2 | convolution fusion | flops 11854413824 | bytes 54525952 | tf_op jit(solution)/shard_map/dot_general | solution.py:386
  469.5 17.0 %convolution_convert_fusion.1 = bf16[2048,2048]{1,0:T(8,128)(2,1)S(1)} fusion(bf16[2048,1408]{1,0:T(8,128)(2,1)} %get-tuple-element.40, bf16[1408,2048]{1,0:T(8,128)(2,1)} %copy-done.28), kind=kOutput, calls=%fused_computation.12 | convolution fusion | flops 11815354368 | bytes 19922944 | tf_op jit(solution)/shard_map/dot_general | solution.py:386
  488.8 4.1 copy-done.41
  492.8 16.3 %fusion.25 = f32[2048,2048]{1,0:T(8,128)} fusion(bf16[2048,1408]{1,0:T(8,128)(2,1)S(1)} %copy-done.45, bf16[2048,1408]{0,1:T(8,128)(2,1)S(1)} %copy-done.41), kind=kOutput, calls=%fused_computation.144 | convolution fusion | flops 11811160064 | bytes 28311552 | tf_op jit(solution)/shard_map/dot_general | solution.py:394
  512.1 21.6 %add_convert_fusion = bf16[2048,2048]{1,0:T(8,128)(2,1)} fusion(f32[2048,2048]{1,0:T(8,128)} %fusion.25, bf16[2048,1408]{1,0:T(8,128)(2,1)} %get-tuple-element.42, bf16[2048,1408]{0,1:T(8,128)(2,1)} %all-gather.11.cloned.1.call-done), kind=kOutput, calls=%fused_computation | convolution fusion | flops 11819548672 | bytes 36700160 | tf_op jit(solution)/shard_map/dot_general | solution.py:394
  533.7 24.5 %collective-permute-done.25 = bf16[512,2048]{1,0:T(8,128)(2,1)} collective-permute-done((bf16[512,2048]{1,0:T(8,128)(2,1)S(1)}, bf16[512,2048]{1,0:T(8,128)(2,1)}, u32[]{:S(2)}, u32[]{:S(2)}) %collective-permute-start.25) | collective-permute-done | bytes 2097184 | tf_op jit(solution)/shard_map/ppermute | solution.py:100
  558.2 5.1 add_add_fusion
  566.5 18.1 %convolution_convert_fusion.5 = bf16[1408,2048]{1,0:T(8,128)(2,1)} fusion(bf16[2048,1408]{1,0:T(8,128)(2,1)} %get-tuple-element.40, bf16[512,2048]{1,0:T(8,128)(2,1)} %collective-permute-done.11, bf16[512,2048]{1,0:T(8,128)(2,1)} %collective-permute-done.10, bf16[512,2048]{1,0:T(8,128)(2,1)} %collective-permute-done.9, bf16[512,2048]{1,0:T(8,128)(2,1)S(1)} %bitcast.159), kind=kOutput, calls=%fused_computation.16 | convolution fusion | flops 11847598080 | bytes 19922944 | tf_op jit(solution)/shard_map/dot_general | solution.py:390
  584.7 6.9 add_convert_fusion.2
  593.1 19.0 %convolution_convert_fusion.4 = bf16[2048,1408]{1,0:T(8,128)(2,1)} fusion(bf16[2048,1408]{1,0:T(8,128)(2,1)} %get-tuple-element.41, bf16[512,2048]{1,0:T(8,128)(2,1)} %collective-permute-done.21, bf16[512,2048]{1,0:T(8,128)(2,1)} %collective-permute-done.20, bf16[512,2048]{1,0:T(8,128)(2,1)} %collective-permute-done.19, bf16[512,2048]{1,0:T(8,128)(2,1)S(1)} %copy-done.13), kind=kOutput, calls=%fused_computation.15 | convolution fusion | flops 11847598080 | bytes 19922944 | tf_op jit(solution)/shard_map/dot_general | solution.py:390
  612.1 19.3 %convolution_convert_fusion.3 = bf16[2048,1408]{1,0:T(8,128)(2,1)} fusion(bf16[2048,1408]{1,0:T(8,128)(2,1)} %get-tuple-element.42, bf16[512,2048]{1,0:T(8,128)(2,1)} %collective-permute-done.21, bf16[512,2048]{1,0:T(8,128)(2,1)} %collective-permute-done.20, bf16[512,2048]{1,0:T(8,128)(2,1)} %collective-permute-done.19, bf16[512,2048]{1,0:T(8,128)(2,1)S(1)} %copy-done.13), kind=kOutput, calls=%fused_computation.14 | convolution fusion | flops 11847598080 | bytes 19922944 | tf_op jit(solution)/shard_map/dot_general | solution.py:390
  631.5 7.1 collective-permute-done.28
  644.2 3.6 dynamic-slice_bitcast_fusion.1
  651.9 36.8 %collective-permute-done.30 = bf16[512,2048]{1,0:T(8,128)(2,1)} collective-permute-done((bf16[512,2048]{1,0:T(8,128)(2,1)S(1)}, bf16[512,2048]{1,0:T(8,128)(2,1)}, u32[]{:S(2)}, u32[]{:S(2)}) %collective-permute-start.30) | collective-permute-done | bytes 2097184 | tf_op jit(solution)/shard_map/ppermute | solution.py:100
  692.3 3.6 dynamic-slice_bitcast_fusion
  698.2 29.3 %collective-permute-done.32 = bf16[4,256,1408]{2,1,0:T(8,128)(2,1)} collective-permute-done((bf16[4,256,1408]{2,1,0:T(8,128)(2,1)}, bf16[4,256,1408]{2,1,0:T(8,128)(2,1)}, u32[]{:S(2)}, u32[]{:S(2)}) %collective-permute-start.32) | collective-permute-done | bytes 2883616 | tf_op jit(solution)/shard_map/ppermute | solution.py:35
  742.7 4.0 pad_maximum_fusion.3
  750.0 5.7 convolution_convert_fusion.7
  755.7 9.5 fusion.26.gm
  765.2 25.3 %attention_backward.1 = bf16[2048,640]{1,0:T(8,128)(2,1)} custom-call(s32[12]{0:T(128)} %concatenate.50.meta, bf16[2048,640]{1,0:T(8,128)(2,1)} %multiply_convert_fusion.3.qkv, s32[2048,1]{1,0:T(8,128)} %copy.26.seg_col, s32[4,1,512]{2,1,0:T(1,128)} %copy-done.27, f32[2048,512]{1,0:T(8,128)} %fusion.26.gm, bf16[2048,512]{1,0:T(8,128)(2,1)} %get-tuple-element.36.mixed, ...), custom_call_target="tpu_custom_call" | custom-call | flops 10485760 | bytes 32768 | tf_op jit(solution)/shard_map/attention_backward/pallas_call | solution.py:356
  790.5 3.4 fusion.1
  793.9 4.3 collective-permute-done.36
  798.2 9.1 convolution_convert_fusion
  816.4 4.4 add_convert_fusion.1
  820.9 10.3 convolution_convert_fusion.6
  841.6 3.9 collective-permute-start.53
  852.8 4.8 collective-permute-start.54
  857.7 3.5 bitcast_convert_fusion
  861.2 32.4 %collective-permute-done.39 = bf16[512,2048]{1,0:T(8,128)(2,1)S(1)} collective-permute-done((bf16[512,2048]{1,0:T(8,128)(2,1)}, bf16[512,2048]{1,0:T(8,128)(2,1)S(1)}, u32[]{:S(2)}, u32[]{:S(2)}) %collective-permute-start.39) | collective-permute-done | bytes 2097184 | tf_op jit(solution)/shard_map/ppermute | solution.py:100
  893.6 5.6 fusion.7
  906.0 8.1 collective-permute-done.54
  919.1 5.1 collective-permute-start.43
  925.0 6.3 fusion.9
  932.7 7.3 collective-permute-start.56
  940.8 15.3 %collective-permute-start.51 = (bf16[256,1408]{0,1:T(8,128)(2,1)}, bf16[256,1408]{0,1:T(8,128)(2,1)S(1)}, u32[]{:S(2)}, u32[]{:S(2)}) collective-permute-start(bf16[256,1408]{0,1:T(8,128)(2,1)} %collective-permute-done.50), channel_id=1, source_target_pairs={{0,8},{8,0},{16,24},{24,16},{1,9},{9,1},{17,25},{25,17},{2,10},{10... | collective-permute-start | bytes 2162696 | tf_op jit(solution)/shard_map/ppermute | solution.py:95
  960.1 4.0 collective-permute-start.57
  978.1 6.2 bitcast_multiply_fusion
  984.3 6.3 copy.54
  990.6 6.3 copy.55
  997.4 11.4 %collective-permute-start.40 = (bf16[256,640]{1,0:T(8,128)(2,1)}, bf16[256,640]{1,0:T(8,128)(2,1)}, u32[]{:S(2)}, u32[]{:S(2)}) collective-permute-start(bf16[256,640]{1,0:T(8,128)(2,1)} %reduce-scatter.6.cloned.1.call-done), channel_id=1, source_target_pairs={{0,8},{8,0},{16,24},{24,16},{1,9},{9,1},{17,25},{25,17},{2,10},{10... | collective-permute-start | bytes 983048 | tf_op jit(solution)/shard_map/ppermute | solution.py:95
  1010.4 7.9 collective-permute-done.41
  (304 shorter events, 161.8 us)
Async XLA Ops:
  7.2 204.7 %all-gather.5.cloned.1.call-start = ((), (), s32[]{:S(2)}) async-start(), calls=%async_computation.3 | async-start | bytes 2949120 | tf_op jit(solution)/shard_map/all_gather | solution.py:75
  10.9 244.9 %all-gather.7.cloned.1.call-start = ((), (), s32[]{:S(2)}) async-start(), calls=%async_computation.4 | async-start | bytes 2359296 | tf_op jit(solution)/shard_map/all_gather | solution.py:75
  12.3 17.5 %collective-permute-start.12 = (bf16[64,2048]{1,0:T(8,128)(2,1)S(1)}, bf16[64,2048]{1,0:T(8,128)(2,1)S(1)}, u32[]{:S(2)}, u32[]{:S(2)}) collective-permute-start(bf16[64,2048]{1,0:T(8,128)(2,1)S(1)} %get-tuple-element.117), channel_id=1, source_target_pairs={{0,0},{1,4},{10,8},{11,12},{20,16},{21,20},{30,24},{31,28}} | collective-permute-start | bytes 786440 | tf_op jit(solution)/shard_map/ppermute | solution.py:163
  13.6 16.2 %collective-permute-start.13 = (bf16[64,2048]{1,0:T(8,128)(2,1)S(1)}, bf16[64,2048]{1,0:T(8,128)(2,1)S(1)}, u32[]{:S(2)}, u32[]{:S(2)}) collective-permute-start(bf16[64,2048]{1,0:T(8,128)(2,1)S(1)} %get-tuple-element.116), channel_id=1, source_target_pairs={{0,1},{1,5},{10,9},{11,13},{20,17},{21,21},{30,25},{31,29}} | collective-permute-start | bytes 786440 | tf_op jit(solution)/shard_map/ppermute | solution.py:163
  14.2 15.6 %collective-permute-start.14 = (bf16[64,2048]{1,0:T(8,128)(2,1)S(1)}, bf16[64,2048]{1,0:T(8,128)(2,1)S(1)}, u32[]{:S(2)}, u32[]{:S(2)}) collective-permute-start(bf16[64,2048]{1,0:T(8,128)(2,1)S(1)} %get-tuple-element.119), channel_id=1, source_target_pairs={{0,2},{1,6},{10,10},{11,14},{20,18},{21,22},{30,26},{31,30}} | collective-permute-start | bytes 786440 | tf_op jit(solution)/shard_map/ppermute | solution.py:163
  14.9 14.9 %collective-permute-start.15 = (bf16[64,2048]{1,0:T(8,128)(2,1)S(1)}, bf16[64,2048]{1,0:T(8,128)(2,1)S(1)}, u32[]{:S(2)}, u32[]{:S(2)}) collective-permute-start(bf16[64,2048]{1,0:T(8,128)(2,1)S(1)} %get-tuple-element.118), channel_id=1, source_target_pairs={{0,3},{1,7},{10,11},{11,15},{20,19},{21,23},{30,27},{31,31}} | collective-permute-start | bytes 786440 | tf_op jit(solution)/shard_map/ppermute | solution.py:163
  30.6 391.2 %all-gather.11.cloned.1.call-start = ((), (), s32[]{:S(2)}) async-start(), calls=%async_computation.6 | async-start | bytes 6488064 | tf_op jit(solution)/shard_map/all_gather | solution.py:75
  30.7 29.9 %collective-permute-start.4 = (bf16[512,2048]{1,0:T(8,128)(2,1)S(1)}, bf16[512,2048]{1,0:T(8,128)(2,1)}, u32[]{:S(2)}, u32[]{:S(2)}) collective-permute-start(bf16[512,2048]{1,0:T(8,128)(2,1)S(1)} %bitcast.144), channel_id=1, source_target_pairs={{0,16},{8,24},{16,0},{24,8},{1,17},{9,25},{17,1},{25,9},{2,18},{10... | collective-permute-start | bytes 6291464 | tf_op jit(solution)/shard_map/ppermute | solution.py:100
  30.7 112.0 %collective-permute-start.3 = (bf16[512,2048]{1,0:T(8,128)(2,1)S(1)}, bf16[512,2048]{1,0:T(8,128)(2,1)}, u32[]{:S(2)}, u32[]{:S(2)}) collective-permute-start(bf16[512,2048]{1,0:T(8,128)(2,1)S(1)} %bitcast.145), channel_id=1, source_target_pairs={{0,8},{8,0},{16,24},{24,16},{1,9},{9,1},{17,25},{25,17},{2,10},{10... | collective-permute-start | bytes 6291464 | tf_op jit(solution)/shard_map/ppermute | solution.py:95
  51.4 91.3 %collective-permute-start.10 = (bf16[512,2048]{1,0:T(8,128)(2,1)}, bf16[512,2048]{1,0:T(8,128)(2,1)}, u32[]{:S(2)}, u32[]{:S(2)}) collective-permute-start(bf16[512,2048]{1,0:T(8,128)(2,1)} %bitcast.156), channel_id=1, source_target_pairs={{0,16},{8,24},{16,0},{24,8},{1,17},{9,25},{17,1},{25,9},{2,18},{10... | collective-permute-start | bytes 6291464 | tf_op jit(solution)/shard_map/ppermute | solution.py:100
  60.6 83.3 %collective-permute-start.5 = (bf16[512,2048]{1,0:T(8,128)(2,1)}, bf16[512,2048]{1,0:T(8,128)(2,1)}, u32[]{:S(2)}, u32[]{:S(2)}) collective-permute-start(bf16[512,2048]{1,0:T(8,128)(2,1)} %collective-permute-done.4), channel_id=1, source_target_pairs={{0,8},{8,0},{16,24},{24,16},{1,9},{9,1},{17,25},{25,17},{2,10},{10... | collective-permute-start | bytes 6291464 | tf_op jit(solution)/shard_map/ppermute | solution.py:95
  100.9 342.0 %all-gather.9.cloned.1.call-start = ((), (), s32[]{:S(2)}) async-start(), calls=%async_computation.5 | async-start | bytes 6488064 | tf_op jit(solution)/shard_map/all_gather | solution.py:75
  102.8 23.2 %collective-permute-start = (s32[512]{0:T(512)S(1)}, s32[512]{0:T(512)S(1)}, u32[]{:S(2)}, u32[]{:S(2)}) collective-permute-start(s32[512]{0:T(512)S(1)} %bitcast.169), channel_id=1, source_target_pairs={{0,8},{8,0},{16,24},{24,16},{1,9},{9,1},{17,25},{25,17},{2,10},{10... | collective-permute-start | bytes 6152 | tf_op jit(solution)/shard_map/ppermute | solution.py:95
  104.3 22.2 %collective-permute-start.2 = (s32[512]{0:T(512)S(1)}, s32[512]{0:T(512)S(1)}, u32[]{:S(2)}, u32[]{:S(2)}) collective-permute-start(s32[512]{0:T(512)S(1)} %collective-permute-done.1), channel_id=1, source_target_pairs={{0,8},{8,0},{16,24},{24,16},{1,9},{9,1},{17,25},{25,17},{2,10},{10... | collective-permute-start | bytes 6152 | tf_op jit(solution)/shard_map/ppermute | solution.py:95
  126.6 37.6 %collective-permute-start.6 = (bf16[176,2048]{1,0:T(8,128)(2,1)S(1)}, bf16[176,2048]{1,0:T(8,128)(2,1)S(1)}, u32[]{:S(2)}, u32[]{:S(2)}) collective-permute-start(bf16[176,2048]{1,0:T(8,128)(2,1)S(1)} %get-tuple-element.79), channel_id=1, source_target_pairs={{0,6},{1,7},{2,0},{3,1},{4,2},{5,3},{6,4},{7,5},{8,14},{9,15},{10,... | collective-permute-start | bytes 2162696 | tf_op jit(solution)/shard_map/ppermute | solution.py:31
  127.1 84.8 %collective-permute-start.7 = (bf16[176,2048]{1,0:T(8,128)(2,1)S(1)}, bf16[176,2048]{1,0:T(8,128)(2,1)}, u32[]{:S(2)}, u32[]{:S(2)}) collective-permute-start(bf16[176,2048]{1,0:T(8,128)(2,1)S(1)} %get-tuple-element.79), channel_id=1, source_target_pairs={{0,4},{1,5},{2,6},{3,7},{4,0},{5,1},{6,2},{7,3},{8,12},{9,13},{10,... | collective-permute-start | bytes 2162696 | tf_op jit(solution)/shard_map/ppermute | solution.py:31
  142.7 98.5 %collective-permute-start.8 = (bf16[176,2048]{1,0:T(8,128)(2,1)S(1)}, bf16[176,2048]{1,0:T(8,128)(2,1)}, u32[]{:S(2)}, u32[]{:S(2)}) collective-permute-start(bf16[176,2048]{1,0:T(8,128)(2,1)S(1)} %get-tuple-element.79), channel_id=1, source_target_pairs={{0,2},{1,3},{2,4},{3,5},{4,6},{5,7},{6,0},{7,1},{8,10},{9,11},{10,... | collective-permute-start | bytes 2162696 | tf_op jit(solution)/shard_map/ppermute | solution.py:31
  142.7 113.0 %collective-permute-start.9 = (bf16[512,2048]{1,0:T(8,128)(2,1)}, bf16[512,2048]{1,0:T(8,128)(2,1)}, u32[]{:S(2)}, u32[]{:S(2)}) collective-permute-start(bf16[512,2048]{1,0:T(8,128)(2,1)} %bitcast.157), channel_id=1, source_target_pairs={{0,8},{8,0},{16,24},{24,16},{1,9},{9,1},{17,25},{25,17},{2,10},{10... | collective-permute-start | bytes 6291464 | tf_op jit(solution)/shard_map/ppermute | solution.py:95
  143.9 111.9 %collective-permute-start.11 = (bf16[512,2048]{1,0:T(8,128)(2,1)}, bf16[512,2048]{1,0:T(8,128)(2,1)}, u32[]{:S(2)}, u32[]{:S(2)}) collective-permute-start(bf16[512,2048]{1,0:T(8,128)(2,1)} %collective-permute-done.10), channel_id=1, source_target_pairs={{0,8},{8,0},{16,24},{24,16},{1,9},{9,1},{17,25},{25,17},{2,10},{10... | collective-permute-start | bytes 6291464 | tf_op jit(solution)/shard_map/ppermute | solution.py:95
  264.5 4.2 collective-permute-start.17
  264.8 36.4 %collective-permute-start.16 = (bf16[512,2048]{1,0:T(8,128)(2,1)}, bf16[512,2048]{1,0:T(8,128)(2,1)}, u32[]{:S(2)}, u32[]{:S(2)}) collective-permute-start(bf16[512,2048]{1,0:T(8,128)(2,1)} %get-tuple-element.95), channel_id=1, source_target_pairs={{0,8},{8,0},{16,24},{24,16},{1,9},{9,1},{17,25},{25,17},{2,10},{10... | collective-permute-start | bytes 6291464 | tf_op jit(solution)/shard_map/ppermute | solution.py:95
  270.7 47.2 %collective-permute-start.18 = (bf16[512,2048]{1,0:T(8,128)(2,1)}, bf16[512,2048]{1,0:T(8,128)(2,1)}, u32[]{:S(2)}, u32[]{:S(2)}) collective-permute-start(bf16[512,2048]{1,0:T(8,128)(2,1)} %add_convert_fusion.4), channel_id=1, source_target_pairs={{0,16},{8,24},{16,0},{24,8},{1,17},{9,25},{17,1},{25,9},{2,18},{10... | collective-permute-start | bytes 6291464 | tf_op jit(solution)/shard_map/ppermute | solution.py:100
  277.0 108.8 %collective-permute-start.22 = (bf16[704,2048]{1,0:T(8,128)(2,1)}, bf16[704,2048]{1,0:T(8,128)(2,1)}, u32[]{:S(2)}, u32[]{:S(2)}) collective-permute-start(bf16[704,2048]{1,0:T(8,128)(2,1)} %pad_maximum_fusion.4), channel_id=1, source_target_pairs={{0,1},{1,0},{2,3},{3,2},{4,5},{5,4},{6,7},{7,6},{8,9},{9,8},{10,11... | collective-permute-start | bytes 8650760 | tf_op jit(solution)/shard_map/ppermute | solution.py:35
  296.1 502.1 %reduce-scatter.4.cloned.1.call-start = ((), (), s32[]{:S(2)}) async-start(), calls=%async_computation.7 | async-start | bytes 6488064 | tf_op jit(solution)/shard_map/reduce_scatter | solution.py:79
  323.2 67.9 %collective-permute-start.20 = (bf16[512,2048]{1,0:T(8,128)(2,1)S(1)}, bf16[512,2048]{1,0:T(8,128)(2,1)}, u32[]{:S(2)}, u32[]{:S(2)}) collective-permute-start(bf16[512,2048]{1,0:T(8,128)(2,1)S(1)} %multiply_convert_fusion.4), channel_id=1, source_target_pairs={{0,16},{8,24},{16,0},{24,8},{1,17},{9,25},{17,1},{25,9},{2,18},{10... | collective-permute-start | bytes 6291464 | tf_op jit(solution)/shard_map/ppermute | solution.py:100
  388.3 27.0 %collective-permute-start.19 = (bf16[512,2048]{1,0:T(8,128)(2,1)S(1)}, bf16[512,2048]{1,0:T(8,128)(2,1)}, u32[]{:S(2)}, u32[]{:S(2)}) collective-permute-start(bf16[512,2048]{1,0:T(8,128)(2,1)S(1)} %multiply_convert_fusion.4), channel_id=1, source_target_pairs={{0,8},{8,0},{16,24},{24,16},{1,9},{9,1},{17,25},{25,17},{2,10},{10... | collective-permute-start | bytes 6291464 | tf_op jit(solution)/shard_map/ppermute | solution.py:95
  391.2 24.1 %collective-permute-start.21 = (bf16[512,2048]{1,0:T(8,128)(2,1)}, bf16[512,2048]{1,0:T(8,128)(2,1)}, u32[]{:S(2)}, u32[]{:S(2)}) collective-permute-start(bf16[512,2048]{1,0:T(8,128)(2,1)} %collective-permute-done.20), channel_id=1, source_target_pairs={{0,8},{8,0},{16,24},{24,16},{1,9},{9,1},{17,25},{25,17},{2,10},{10... | collective-permute-start | bytes 6291464 | tf_op jit(solution)/shard_map/ppermute | solution.py:95
  488.2 20.9 %collective-permute-start.24 = (bf16[512,2048]{1,0:T(8,128)(2,1)S(1)}, bf16[512,2048]{1,0:T(8,128)(2,1)S(1)}, u32[]{:S(2)}, u32[]{:S(2)}) collective-permute-start(bf16[512,2048]{1,0:T(8,128)(2,1)S(1)} %get-tuple-element.94), channel_id=1, source_target_pairs={{0,8},{8,0},{16,24},{24,16},{1,9},{9,1},{17,25},{25,17},{2,10},{10... | collective-permute-start | bytes 6291464 | tf_op jit(solution)/shard_map/ppermute | solution.py:95
  488.3 45.4 %collective-permute-start.23 = (bf16[512,2048]{1,0:T(8,128)(2,1)}, bf16[512,2048]{1,0:T(8,128)(2,1)S(1)}, u32[]{:S(2)}, u32[]{:S(2)}) collective-permute-start(bf16[512,2048]{1,0:T(8,128)(2,1)} %get-tuple-element.93), channel_id=1, source_target_pairs={{0,8},{8,0},{16,24},{24,16},{1,9},{9,1},{17,25},{25,17},{2,10},{10... | collective-permute-start | bytes 6291464 | tf_op jit(solution)/shard_map/ppermute | solution.py:95
  510.0 48.2 %collective-permute-start.25 = (bf16[512,2048]{1,0:T(8,128)(2,1)S(1)}, bf16[512,2048]{1,0:T(8,128)(2,1)}, u32[]{:S(2)}, u32[]{:S(2)}) collective-permute-start(bf16[512,2048]{1,0:T(8,128)(2,1)S(1)} %add_convert_fusion.3), channel_id=1, source_target_pairs={{0,16},{8,24},{16,0},{24,8},{1,17},{9,25},{17,1},{25,9},{2,18},{10... | collective-permute-start | bytes 6291464 | tf_op jit(solution)/shard_map/ppermute | solution.py:100
  565.9 18.8 %collective-permute-start.26 = (bf16[512,2048]{1,0:T(8,128)(2,1)}, bf16[512,2048]{1,0:T(8,128)(2,1)}, u32[]{:S(2)}, u32[]{:S(2)}) collective-permute-start(bf16[512,2048]{1,0:T(8,128)(2,1)} %get-tuple-element.92), channel_id=1, source_target_pairs={{0,8},{8,0},{16,24},{24,16},{1,9},{9,1},{17,25},{25,17},{2,10},{10... | collective-permute-start | bytes 6291464 | tf_op jit(solution)/shard_map/ppermute | solution.py:95
  566.5 18.2 %collective-permute-start.27 = (bf16[512,2048]{1,0:T(8,128)(2,1)}, bf16[512,2048]{1,0:T(8,128)(2,1)}, u32[]{:S(2)}, u32[]{:S(2)}) collective-permute-start(bf16[512,2048]{1,0:T(8,128)(2,1)} %get-tuple-element.91), channel_id=1, source_target_pairs={{0,8},{8,0},{16,24},{24,16},{1,9},{9,1},{17,25},{25,17},{2,10},{10... | collective-permute-start | bytes 6291464 | tf_op jit(solution)/shard_map/ppermute | solution.py:95
  584.7 334.5 %reduce-scatter.8.cloned.1.call-start = ((), (), s32[]{:S(2)}) async-start(), calls=%async_computation.9 | async-start | bytes 2359296 | tf_op jit(solution)/shard_map/reduce_scatter | solution.py:79
  591.7 46.9 %collective-permute-start.28 = (bf16[512,2048]{1,0:T(8,128)(2,1)}, bf16[512,2048]{1,0:T(8,128)(2,1)S(1)}, u32[]{:S(2)}, u32[]{:S(2)}) collective-permute-start(bf16[512,2048]{1,0:T(8,128)(2,1)} %get-tuple-element.89), channel_id=1, source_target_pairs={{0,16},{8,24},{16,0},{24,8},{1,17},{9,25},{17,1},{25,9},{2,18},{10... | collective-permute-start | bytes 6291464 | tf_op jit(solution)/shard_map/ppermute | solution.py:100
  642.8 46.0 %collective-permute-start.30 = (bf16[512,2048]{1,0:T(8,128)(2,1)S(1)}, bf16[512,2048]{1,0:T(8,128)(2,1)}, u32[]{:S(2)}, u32[]{:S(2)}) collective-permute-start(bf16[512,2048]{1,0:T(8,128)(2,1)S(1)} %get-tuple-element.76), channel_id=1, source_target_pairs={{0,16},{8,24},{16,0},{24,8},{1,17},{9,25},{17,1},{25,9},{2,18},{10... | collective-permute-start | bytes 6291464 | tf_op jit(solution)/shard_map/ppermute | solution.py:100
  647.8 79.6 %collective-permute-start.32 = (bf16[4,256,1408]{2,1,0:T(8,128)(2,1)}, bf16[4,256,1408]{2,1,0:T(8,128)(2,1)}, u32[]{:S(2)}, u32[]{:S(2)}) collective-permute-start(bf16[4,256,1408]{2,1,0:T(8,128)(2,1)} %dynamic-slice_bitcast_fusion.1), channel_id=1, source_target_pairs={{0,1},{1,0},{2,3},{3,2},{4,5},{5,4},{6,7},{7,6},{8,9},{9,8},{10,11... | collective-permute-start | bytes 8650760 | tf_op jit(solution)/shard_map/ppermute | solution.py:35
  650.1 90.2 %collective-permute-start.29 = (bf16[512,2048]{1,0:T(8,128)(2,1)S(1)}, bf16[512,2048]{1,0:T(8,128)(2,1)}, u32[]{:S(2)}, u32[]{:S(2)}) collective-permute-start(bf16[512,2048]{1,0:T(8,128)(2,1)S(1)} %get-tuple-element.76), channel_id=1, source_target_pairs={{0,8},{8,0},{16,24},{24,16},{1,9},{9,1},{17,25},{25,17},{2,10},{10... | collective-permute-start | bytes 6291464 | tf_op jit(solution)/shard_map/ppermute | solution.py:95
  688.7 54.0 %collective-permute-start.31 = (bf16[512,2048]{1,0:T(8,128)(2,1)}, bf16[512,2048]{1,0:T(8,128)(2,1)}, u32[]{:S(2)}, u32[]{:S(2)}) collective-permute-start(bf16[512,2048]{1,0:T(8,128)(2,1)} %collective-permute-done.30), channel_id=1, source_target_pairs={{0,8},{8,0},{16,24},{24,16},{1,9},{9,1},{17,25},{25,17},{2,10},{10... | collective-permute-start | bytes 6291464 | tf_op jit(solution)/shard_map/ppermute | solution.py:95
  695.9 94.6 %collective-permute-start.33 = (bf16[4,256,1408]{2,1,0:T(8,128)(2,1)}, bf16[4,256,1408]{2,1,0:T(8,128)(2,1)}, u32[]{:S(2)}, u32[]{:S(2)}) collective-permute-start(bf16[4,256,1408]{2,1,0:T(8,128)(2,1)} %dynamic-slice_bitcast_fusion), channel_id=1, source_target_pairs={{0,1},{1,0},{2,3},{3,2},{4,5},{5,4},{6,7},{7,6},{8,9},{9,8},{10,11... | collective-permute-start | bytes 8650760 | tf_op jit(solution)/shard_map/ppermute | solution.py:35
  734.5 59.4 %collective-permute-start.34 = (bf16[256,1408]{0,1:T(8,128)(2,1)}, bf16[256,1408]{0,1:T(8,128)(2,1)}, u32[]{:S(2)}, u32[]{:S(2)}) collective-permute-start(bf16[256,1408]{0,1:T(8,128)(2,1)} %bitcast.161), channel_id=1, source_target_pairs={{0,2},{1,3},{2,4},{3,5},{4,6},{5,7},{6,0},{7,1},{8,10},{9,11},{10,... | collective-permute-start | bytes 2162696 | tf_op jit(solution)/shard_map/ppermute | solution.py:31
  736.7 57.2 %collective-permute-start.35 = (bf16[256,1408]{0,1:T(8,128)(2,1)}, bf16[256,1408]{0,1:T(8,128)(2,1)}, u32[]{:S(2)}, u32[]{:S(2)}) collective-permute-start(bf16[256,1408]{0,1:T(8,128)(2,1)} %bitcast.162), channel_id=1, source_target_pairs={{0,4},{1,5},{2,6},{3,7},{4,0},{5,1},{6,2},{7,3},{8,12},{9,13},{10,... | collective-permute-start | bytes 2162696 | tf_op jit(solution)/shard_map/ppermute | solution.py:31
  740.3 57.8 %collective-permute-start.36 = (bf16[256,1408]{0,1:T(8,128)(2,1)}, bf16[256,1408]{0,1:T(8,128)(2,1)}, u32[]{:S(2)}, u32[]{:S(2)}) collective-permute-start(bf16[256,1408]{0,1:T(8,128)(2,1)} %bitcast.163), channel_id=1, source_target_pairs={{0,6},{1,7},{2,0},{3,1},{4,2},{5,3},{6,4},{7,5},{8,14},{9,15},{10,... | collective-permute-start | bytes 2162696 | tf_op jit(solution)/shard_map/ppermute | solution.py:31
  811.8 4.6 collective-permute-start.38
  812.3 185.1 %reduce-scatter.6.cloned.1.call-start = ((), (), s32[]{:S(2)}) async-start(), calls=%async_computation.8 | async-start | bytes 2949120 | tf_op jit(solution)/shard_map/reduce_scatter | solution.py:79
  813.9 47.3 %collective-permute-start.37 = (bf16[512,2048]{1,0:T(8,128)(2,1)}, bf16[512,2048]{1,0:T(8,128)(2,1)}, u32[]{:S(2)}, u32[]{:S(2)}) collective-permute-start(bf16[512,2048]{1,0:T(8,128)(2,1)} %get-tuple-element.87), channel_id=1, source_target_pairs={{0,8},{8,0},{16,24},{24,16},{1,9},{9,1},{17,25},{25,17},{2,10},{10... | collective-permute-start | bytes 6291464 | tf_op jit(solution)/shard_map/ppermute | solution.py:95
  831.1 15.9 %collective-permute-start.58 = (bf16[176,2048]{1,0:T(8,128)(2,1)}, bf16[176,2048]{1,0:T(8,128)(2,1)}, u32[]{:S(2)}, u32[]{:S(2)}) collective-permute-start(bf16[176,2048]{1,0:T(8,128)(2,1)} %reduce-scatter.4.cloned.1.call-done), channel_id=1, source_target_pairs={{0,8},{8,0},{16,24},{24,16},{1,9},{9,1},{17,25},{25,17},{2,10},{10... | collective-permute-start | bytes 2162696 | tf_op jit(solution)/shard_map/ppermute | solution.py:95
  831.5 17.9 %collective-permute-start.59 = (bf16[176,2048]{1,0:T(8,128)(2,1)}, bf16[176,2048]{1,0:T(8,128)(2,1)}, u32[]{:S(2)}, u32[]{:S(2)}) collective-permute-start(bf16[176,2048]{1,0:T(8,128)(2,1)} %reduce-scatter.4.cloned.1.call-done), channel_id=1, source_target_pairs={{0,16},{8,24},{16,0},{24,8},{1,17},{9,25},{17,1},{25,9},{2,18},{10... | collective-permute-start | bytes 2162696 | tf_op jit(solution)/shard_map/ppermute | solution.py:100
  836.9 69.1 %collective-permute-start.52 = (bf16[256,1408]{0,1:T(8,128)(2,1)}, bf16[256,1408]{0,1:T(8,128)(2,1)}, u32[]{:S(2)}, u32[]{:S(2)}) collective-permute-start(bf16[256,1408]{0,1:T(8,128)(2,1)} %bitcast.50), channel_id=1, source_target_pairs={{0,2},{1,3},{2,4},{3,5},{4,6},{5,7},{6,0},{7,1},{8,10},{9,11},{10,... | collective-permute-start | bytes 2162696 | tf_op jit(solution)/shard_map/ppermute | solution.py:31
  841.6 64.4 %collective-permute-start.53 = (bf16[256,1408]{0,1:T(8,128)(2,1)}, bf16[256,1408]{0,1:T(8,128)(2,1)}, u32[]{:S(2)}, u32[]{:S(2)}) collective-permute-start(bf16[256,1408]{0,1:T(8,128)(2,1)} %bitcast.51), channel_id=1, source_target_pairs={{0,4},{1,5},{2,6},{3,7},{4,0},{5,1},{6,2},{7,3},{8,12},{9,13},{10,... | collective-permute-start | bytes 2162696 | tf_op jit(solution)/shard_map/ppermute | solution.py:31
  847.1 46.5 %collective-permute-start.39 = (bf16[512,2048]{1,0:T(8,128)(2,1)}, bf16[512,2048]{1,0:T(8,128)(2,1)S(1)}, u32[]{:S(2)}, u32[]{:S(2)}) collective-permute-start(bf16[512,2048]{1,0:T(8,128)(2,1)} %add_convert_fusion.1), channel_id=1, source_target_pairs={{0,16},{8,24},{16,0},{24,8},{1,17},{9,25},{17,1},{25,9},{2,18},{10... | collective-permute-start | bytes 6291464 | tf_op jit(solution)/shard_map/ppermute | solution.py:100
  852.8 61.3 %collective-permute-start.54 = (bf16[256,1408]{0,1:T(8,128)(2,1)}, bf16[256,1408]{0,1:T(8,128)(2,1)S(1)}, u32[]{:S(2)}, u32[]{:S(2)}) collective-permute-start(bf16[256,1408]{0,1:T(8,128)(2,1)} %bitcast.52), channel_id=1, source_target_pairs={{0,6},{1,7},{2,0},{3,1},{4,2},{5,3},{6,4},{7,5},{8,14},{9,15},{10,... | collective-permute-start | bytes 2162696 | tf_op jit(solution)/shard_map/ppermute | solution.py:31
  903.7 52.4 %collective-permute-start.49 = (bf16[256,1408]{0,1:T(8,128)(2,1)S(1)}, bf16[256,1408]{0,1:T(8,128)(2,1)}, u32[]{:S(2)}, u32[]{:S(2)}) collective-permute-start(bf16[256,1408]{0,1:T(8,128)(2,1)S(1)} %get-tuple-element.73), channel_id=1, source_target_pairs={{0,8},{8,0},{16,24},{24,16},{1,9},{9,1},{17,25},{25,17},{2,10},{10... | collective-permute-start | bytes 2162696 | tf_op jit(solution)/shard_map/ppermute | solution.py:95
  905.5 35.3 %collective-permute-start.50 = (bf16[256,1408]{0,1:T(8,128)(2,1)S(1)}, bf16[256,1408]{0,1:T(8,128)(2,1)}, u32[]{:S(2)}, u32[]{:S(2)}) collective-permute-start(bf16[256,1408]{0,1:T(8,128)(2,1)S(1)} %get-tuple-element.73), channel_id=1, source_target_pairs={{0,16},{8,24},{16,0},{24,8},{1,17},{9,25},{17,1},{25,9},{2,18},{10... | collective-permute-start | bytes 2162696 | tf_op jit(solution)/shard_map/ppermute | solution.py:100
  918.7 45.5 %collective-permute-start.55 = (bf16[256,1408]{0,1:T(8,128)(2,1)}, bf16[256,1408]{0,1:T(8,128)(2,1)S(1)}, u32[]{:S(2)}, u32[]{:S(2)}) collective-permute-start(bf16[256,1408]{0,1:T(8,128)(2,1)} %get-tuple-element.71), channel_id=1, source_target_pairs={{0,8},{8,0},{16,24},{24,16},{1,9},{9,1},{17,25},{25,17},{2,10},{10... | collective-permute-start | bytes 2162696 | tf_op jit(solution)/shard_map/ppermute | solution.py:95
  919.1 12.2 %collective-permute-start.43 = (bf16[64,2048]{1,0:T(8,128)(2,1)}, bf16[64,2048]{1,0:T(8,128)(2,1)S(1)}, u32[]{:S(2)}, u32[]{:S(2)}) collective-permute-start(bf16[64,2048]{1,0:T(8,128)(2,1)} %reduce-scatter.8.cloned.1.call-done), channel_id=1, source_target_pairs={{0,0},{4,1},{8,10},{12,11},{16,20},{20,21},{24,30},{28,31}} | collective-permute-start | bytes 786440 | tf_op jit(solution)/shard_map/ppermute | solution.py:172
  924.3 7.7 collective-permute-start.44
  932.0 8.0 collective-permute-start.46
  932.7 27.4 %collective-permute-start.56 = (bf16[256,1408]{0,1:T(8,128)(2,1)}, bf16[256,1408]{0,1:T(8,128)(2,1)S(1)}, u32[]{:S(2)}, u32[]{:S(2)}) collective-permute-start(bf16[256,1408]{0,1:T(8,128)(2,1)} %get-tuple-element.71), channel_id=1, source_target_pairs={{0,16},{8,24},{16,0},{24,8},{1,17},{9,25},{17,1},{25,9},{2,18},{10... | collective-permute-start | bytes 2162696 | tf_op jit(solution)/shard_map/ppermute | solution.py:100
  940.1 25.9 %collective-permute-start.47 = (bf16[256,2048]{1,0:T(8,128)(2,1)S(1)}, bf16[256,2048]{1,0:T(8,128)(2,1)S(1)}, u32[]{:S(2)}, u32[]{:S(2)}) collective-permute-start(bf16[256,2048]{1,0:T(8,128)(2,1)S(1)} %constant_dynamic-update-slice_fusion.5), channel_id=1, source_target_pairs={{0,16},{1,17},{10,26},{11,27},{20,4},{21,5},{30,14},{31,15}} | collective-permute-start | bytes 3145736 | tf_op jit(solution)/shard_map/ppermute | solution.py:176
  940.8 27.1 %collective-permute-start.51 = (bf16[256,1408]{0,1:T(8,128)(2,1)}, bf16[256,1408]{0,1:T(8,128)(2,1)S(1)}, u32[]{:S(2)}, u32[]{:S(2)}) collective-permute-start(bf16[256,1408]{0,1:T(8,128)(2,1)} %collective-permute-done.50), channel_id=1, source_target_pairs={{0,8},{8,0},{16,24},{24,16},{1,9},{9,1},{17,25},{25,17},{2,10},{10... | collective-permute-start | bytes 2162696 | tf_op jit(solution)/shard_map/ppermute | solution.py:95
  960.1 11.3 %collective-permute-start.57 = (bf16[256,1408]{0,1:T(8,128)(2,1)S(1)}, bf16[256,1408]{0,1:T(8,128)(2,1)S(1)}, u32[]{:S(2)}, u32[]{:S(2)}) collective-permute-start(bf16[256,1408]{0,1:T(8,128)(2,1)S(1)} %collective-permute-done.56), channel_id=1, source_target_pairs={{0,8},{8,0},{16,24},{24,16},{1,9},{9,1},{17,25},{25,17},{2,10},{10... | collective-permute-start | bytes 2162696 | tf_op jit(solution)/shard_map/ppermute | solution.py:95
  966.4 42.4 %collective-permute-start.48 = (bf16[256,2048]{1,0:T(8,128)(2,1)S(1)}, bf16[256,2048]{1,0:T(8,128)(2,1)S(1)}, u32[]{:S(2)}, u32[]{:S(2)}) collective-permute-start(bf16[256,2048]{1,0:T(8,128)(2,1)S(1)} %add.376), channel_id=1, source_target_pairs={{0,8},{16,24},{1,9},{17,25},{10,2},{26,18},{11,3},{27,19},{4,12},{... | collective-permute-start | bytes 3145736 | tf_op jit(solution)/shard_map/ppermute | solution.py:183
  997.4 22.0 %collective-permute-start.40 = (bf16[256,640]{1,0:T(8,128)(2,1)}, bf16[256,640]{1,0:T(8,128)(2,1)}, u32[]{:S(2)}, u32[]{:S(2)}) collective-permute-start(bf16[256,640]{1,0:T(8,128)(2,1)} %reduce-scatter.6.cloned.1.call-done), channel_id=1, source_target_pairs={{0,8},{8,0},{16,24},{24,16},{1,9},{9,1},{17,25},{25,17},{2,10},{10... | collective-permute-start | bytes 983048 | tf_op jit(solution)/shard_map/ppermute | solution.py:95
  1008.8 9.6 collective-permute-start.41
  (50 other events, 979.8 us)
Sparse Core Ops, SparseCore 0:
  11.0 62.9 all-gather.4
  76.8 47.8 all-gather.6
  126.7 143.9 all-gather.10
  296.2 110.4 all-gather.8
  584.8 131.5 reduce-scatter.3
  812.4 99.5 reduce-scatter.7
  915.6 81.4 reduce-scatter.5

commit v3 on v2

--- a/solution.py
+++ b/solution.py
@@ -40,35 +40,71 @@
     return me // 2, lax.rem(me, 2)
 
 
-def interleave(own, other):
-    n, m = lax.axis_size(F), lines()
-    line, side = line_and_side()
-    both = jnp.concatenate([own, other], axis=0)
-    size = both.shape[0] // n
-    places = [
-        lax.rem(j // 2 - line + m, m) + m * jnp.where(side == j % 2, 0, 1) for j in range(n)
-    ]
-    return jnp.concatenate(
-        [lax.dynamic_slice_in_dim(both, p * size, size, axis=0) for p in places], axis=0
-    )
-
-
-def scatter_sides(total):
-    m = lines()
-    _, side = line_and_side()
-    parts = total.reshape(m, 2, total.shape[0] // (2 * m), total.shape[1])
-    mine = lax.dynamic_index_in_dim(parts, side, 1, keepdims=False)
-    return mine, side_swap(lax.dynamic_index_in_dim(parts, 1 - side, 1, keepdims=False))
-
-
-def scatter_lines(total):
-    m = lines()
-    line, _ = line_and_side()
-
-    def part(k):
-        return lax.dynamic_index_in_dim(total, lax.rem(line + k, m), 0, keepdims=False)
-
-    return [part(0)] + [line_shift(part(k), k) for k in range(1, m)]
+class Arrivals:
+    def __init__(self, block):
+        self.own = [block] + [line_shift(block, -k) for k in range(1, lines())]
+        self.other = [side_swap(part) for part in self.own]
+
+    def first(self, own, other):
+        m = lines()
+        return self.own[1 : own * m // 4] + self.other[: other * m // 4]
+
+    def whole(self):
+        return assemble(self.own + self.other)
+
+
+def assemble_kernel(*refs, n):
+    m = n // 2
+    me = lax.axis_index(F)
+    line, side = me // 2, lax.rem(me, 2)
+    out, sems = refs[n], refs[n + 1]
+    copies = []
+    for a in range(2):
+        for k in range(m):
+            place = lax.rem(line + k, m) * 2 + (side if a == 0 else 1 - side)
+            i = a * m + k
+            copies.append(pltpu.make_async_copy(refs[i], out.at[place], sems.at[i]))
+    for copy in copies:
+        copy.start()
+    for copy in copies:
+        copy.wait()
+
+
+def assemble(parts):
+    n = len(parts)
+    shape = parts[0].shape
+    out = pl.pallas_call(
+        functools.partial(assemble_kernel, n=n),
+        out_shape=jax.ShapeDtypeStruct((n,) + shape, parts[0].dtype),
+        in_specs=[pl.BlockSpec(memory_space=pl.ANY)] * n,
+        out_specs=pl.BlockSpec(memory_space=pl.ANY),
+        scratch_shapes=[pltpu.SemaphoreType.DMA((n,))],
+        cost_estimate=pl.CostEstimate(flops=0, transcendentals=0, bytes_accessed=1024),
+        name="assemble",
+    )(*parts)
+    return out.reshape(n * shape[0], shape[1])
+
+
+class Departures:
+    def __init__(self, total):
+        m = lines()
+        line, side = line_and_side()
+        parts = total.reshape(2 * m, total.shape[0] // (2 * m), total.shape[1])
+
+        def part(k, s):
+            place = lax.rem(line + k, m) * 2 + s
+            return lax.dynamic_index_in_dim(parts, place, 0, keepdims=False)
+
+        self.order = list(range(1, m)) + [0]
+        self.mine = [part(k, side) for k in self.order]
+        self.sent = [side_swap(part(k, 1 - side)) for k in self.order]
+
+    def lines(self, marks):
+        out = []
+        for k, mine, sent, mark in zip(self.order, self.mine, self.sent, marks):
+            both = (mine.astype(F32) + after(sent, mark).astype(F32)).astype(BF)
+            out.append(line_shift(both, k) if k else both)
+        return out
 
 
 def gather_all(block):
@@ -100,12 +136,21 @@
     return lax.ppermute(value, C, [(i, (i + 2 * k) % n) for i in range(n)])
 
 
-def spread(block):
+def spread(block, marks=()):
     out = []
     for k in range(chips()):
-        near = chip_shift(block, k) if k else block
+        near = after(chip_shift(block, k), *marks) if k else block
         out += [near, core_swap(near)]
     return out
+
+
+def spread_direct(block):
+    n = lax.axis_size(C)
+    return [
+        lax.ppermute(block, C, [(i, (i + 2 * k) % n ^ h) for i in range(n)]) if k or h else block
+        for k in range(chips())
+        for h in range(2)
+    ]
 
 
 def spread_index():
@@ -448,7 +493,7 @@
     part_up = hidden_columns(w_up)
     part_down = lax.dynamic_slice_in_dim(w_down, c * seg_len, seg_len, axis=0)
 
-    seg_all = jnp.concatenate(spread(segment_ids[0]), axis=0)
+    seg_all = jnp.concatenate(spread_direct(segment_ids[0]), axis=0)
     nb = nc
     seg_row = seg_all.reshape(nb, 1, rows)
     seg_col = seg_all.reshape(nb * rows, 1)
@@ -456,84 +501,81 @@
         [jnp.stack(spread_index()), seg_row[:, 0, 0], seg_row[:, 0, rows - 1]]
     ).astype(jnp.int32)
 
-    full_qkv = gather_all(part_qkv)
-    full_out = gather_all(part_out)
-    full_gate = gather_all(part_gate)
-    full_up = gather_all(part_up)
-    down_lines = [line_shift(part_down, -k) for k in range(1, lax.axis_size(F) // 2)]
-
-    x_all = jnp.concatenate(spread(own), axis=0)
+    w_one, w_two = Arrivals(part_qkv), Arrivals(part_out)
+    w_three, w_four, w_five = Arrivals(part_down), Arrivals(part_gate), Arrivals(part_up)
+
+    x_all = jnp.concatenate(spread(own, w_one.first(4, 0)), axis=0)
     scale_one = inverse_rms(x_all.astype(F32))
-    qkv = (mm(after(x_all, *down_lines[:2]), full_qkv) * scale_one).astype(BF)
+    full_qkv = w_one.whole()
+    x_all = after(x_all, *w_two.first(3, 1))
+    qkv = (mm(x_all, full_qkv) * scale_one).astype(BF)
     g_parts = spread(grad_top)
-    qkv = after(qkv, *down_lines)
-    down_side = jnp.concatenate([part_down] + down_lines, axis=0)
-    down_other = side_swap(down_side)
+    qkv = after(qkv, *w_two.first(4, 3), *w_three.first(2, 0))
     mixed, den = attention_forward(meta, qkv, seg_col, seg_row, heads, rows)
 
     def blocks(value):
         return [value[i * rows : (i + 1) * rows] for i in range(nb)]
 
-    projected = mm(after(mixed, *g_parts), full_out).astype(BF)
-    residual = own.astype(F32) + gather_back(blocks(projected))
+    full_out = w_two.whole()
+    projected = mm(after(mixed, *g_parts, *w_three.first(3, 2)), full_out).astype(BF)
+    sums = add_cores(blocks(projected))
+    residual = own.astype(F32) + add_chips(sums)
+    residual = after(residual, *w_three.first(4, 4), *w_four.first(2, 2))
 
     scale_two = inverse_rms(residual)
     unit_two = residual * scale_two
-    n_all = jnp.concatenate(spread(unit_two.astype(BF)), axis=0)
-    full_down = interleave(down_side, down_other)
+    full_down = w_three.whole()
     g_all = jnp.concatenate(g_parts, axis=0)
-    grad_hidden = mm_nt(g_all, full_down)
-    gate = mm(after(n_all, grad_hidden), full_gate)
+    grad_hidden = mm_nt(after(g_all, unit_two), full_down)
+    n_parts = spread(unit_two.astype(BF), [grad_hidden] + w_four.first(4, 3))
+    n_all = jnp.concatenate(n_parts, axis=0)
+    full_gate = w_four.whole()
+    gate = mm(n_all, full_gate)
+    full_up = w_five.whole()
     up = mm(n_all, full_up)
     sigmoid = jax.nn.sigmoid(gate)
     silu = gate * sigmoid
     act = (silu * up).astype(BF)
     grad_gate = (grad_hidden * up * sigmoid * (1.0 + gate * (1.0 - sigmoid))).astype(BF)
     grad_up = (grad_hidden * silu).astype(BF)
-    projected_two = mm(act, full_down).astype(BF)
-    out_sums = add_cores(blocks(projected_two))
-    grad_gate = after(grad_gate, projected_two)
     back_two = (mm_nt(grad_gate, full_gate) + mm_nt(grad_up, full_up)).astype(BF)
-    block_out = residual + add_chips(out_sums)
-    back_sums = add_cores(blocks(after(back_two, block_out)))
-
-    total_down = mm_tn(after(act, back_two), g_all).astype(BF)
+    back_sums = add_cores(blocks(back_two))
+
+    total_gate = mm_tn(n_all, after(grad_gate, back_two)).astype(BF)
+    away_gate = Departures(total_gate)
+    total_up = mm_tn(n_all, after(grad_up, total_gate, *back_sums)).astype(BF)
+    away_up = Departures(total_up)
+    total_down = mm_tn(after(act, total_up, away_gate.sent[0]), g_all).astype(BF)
     sum_down = scatter_all(total_down)
-    total_gate = mm_tn(n_all, after(grad_gate, total_down, *back_sums)).astype(BF)
-    mine_gate, sent_gate = scatter_sides(total_gate)
-    total_up = mm_tn(n_all, after(grad_up, total_gate)).astype(BF)
-    mine_up, sent_up = scatter_sides(total_up)
-    grad_unit_two = add_chips([after(back_sums[0], total_up)] + back_sums[1:])
+    grad_unit_two = after(add_chips(back_sums), total_down, away_gate.sent[1])
 
     grad_residual = grad_top.astype(F32) + scale_two * (
         grad_unit_two - unit_two * jnp.mean(grad_unit_two * unit_two, axis=-1, keepdims=True)
     )
     branch = grad_residual.astype(BF)
-    b_all = jnp.concatenate(spread(branch), axis=0)
-
-    def both(mine, sent):
-        return (mine.astype(F32) + sent.astype(F32)).astype(BF)
-
-    both_gate = both(mine_gate, after(sent_gate, branch))
-    lines_gate = scatter_lines(both_gate)
-
-    b_all = after(b_all, both_gate)
+    projected_two = mm(after(act, branch), full_down).astype(BF)
+    m = nf // 2
+    lines_gate = away_gate.lines([branch] * m)
+    b_parts = spread(branch, [projected_two, away_up.sent[0]] + away_gate.sent)
+    b_all = jnp.concatenate(b_parts, axis=0)
+    out_sums = add_cores(blocks(after(projected_two, b_all)))
+    block_out = residual + add_chips(out_sums)
+
     total_out = mm_tn(mixed, b_all).astype(BF)
-    grad_mixed = mm_nt(after(b_all, total_out), full_out)
+    grad_mixed = mm_nt(after(b_all, total_out, away_up.sent[1 % m]), full_out)
+    sum_out = scatter_all(after(total_out, sum_down))
+    grad_mixed = after(grad_mixed, sum_down, away_up.sent[2 % m], *out_sums)
     grad_qkv = attention_backward(
         meta, qkv, seg_col, seg_row, grad_mixed, mixed, den, scale_one, heads, rows
     )
-    both_up = both(mine_up, after(sent_up, grad_qkv))
-    lines_up = scatter_lines(both_up)
-    grad_qkv = after(grad_qkv, sum_down, both_up, *lines_gate)
-    sum_out = scatter_all(after(total_out, grad_qkv))
-    back_one = mm_nt(grad_qkv, full_qkv).astype(BF)
+    lines_up = away_up.lines([branch, b_all, grad_mixed] + [grad_qkv] * (m - 3))
+    back_one = mm_nt(after(grad_qkv, block_out, *lines_gate), full_qkv).astype(BF)
     one_sums = add_cores(blocks(back_one))
     total_qkv = mm_tn(x_all, after(grad_qkv, *one_sums)).astype(BF)
     grad_unit_one = add_chips(one_sums)
     sum_qkv = scatter_all(total_qkv)
     sum_down = after(sum_down, total_qkv)
-    sum_gate = add_all([after(lines_gate[0], grad_unit_one)] + lines_gate[1:])
+    sum_gate = add_all([after(lines_gate[0], total_qkv)] + lines_gate[1:])
     sum_up = add_all([after(lines_up[0], grad_unit_one)] + lines_up[1:])
 
     unit_one = own.astype(F32) * inverse_rms(own.astype(F32))

time: 1060 us -> 1640 us (1.55); the launches traced: 1040 us -> 1640 us
  Pallas kernels: 39.8 us -> 722 us
  starting transfers between devices: 206 us -> 147 us
  waiting for transfers between devices: 331 us -> 304 us
    pallas_call x0 -> x5, Pallas kernels: none -> 673 us  [assemble(): pl.pallas_call(functools.partial(assemble_kernel, n=n), out_shape=jax.Sha...]
    ppermute x26 -> x24, starting transfers between devices: 126 us -> 58.8 us  [core_swap(): return lax.ppermute(value, C, [(i, i ^ 1) for i in range(n)])]
    ppermute x3 -> x28, waiting for transfers between devices: 90.5 us -> 52.9 us  [side_swap(): return lax.ppermute(value, F, [(j, j ^ 1) for j in range(lax.axis_size(F))])]
    ppermute x9 -> x21, waiting for transfers between devices: 91.4 us -> 82.5 us  [line_shift(): lax.ppermute(value, F, [(j, (j // 2 + k) % m * 2 + j % 2) for j in range(...]
    ppermute x13 -> x12, waiting for transfers between devices: 128 us -> 137 us  [chip_shift(): return lax.ppermute(value, C, [(i, (i + 2 * k) % n) for i in range(n)])]
    unnamed x114 -> x173, local copies, waits for them, and re-layouts: 45.3 us -> 48.6 us
  transfers between devices with their start and end apart: 68 -> 101, of which waited for: 18 -> 31; matrix products, arithmetic and copies ran while one was open for 34% -> 19% of each run, Pallas kernels for 4% -> 44%
where the time goes in v3:
time: 1640 us
  Pallas kernels  722 us (44%)
  waiting for transfers between devices  304 us (19%)
  matrix products  226 us (14%)
  starting transfers between devices  147 us (9%)
  local copies, waits for them, and re-layouts  114 us (7%)
  other arithmetic  109 us (7%)
    pallas_call x5, Pallas kernels, assemble(): pl.pallas_call(functools.partial(assemble_kernel, n=n), out_shape=jax.Sha...  673 us
    ppermute x12, waiting for transfers between devices, chip_shift(): return lax.ppermute(value, C, [(i, (i + 2 * k) % n) for i in range(n)])  137 us
    ppermute x21, waiting for transfers between devices, line_shift(): lax.ppermute(value, F, [(j, (j // 2 + k) % m * 2 + j % 2) for j in range(...  82.5 us
    dot_general x5, matrix products, mm(): return jnp.dot(a, b, preferred_element_type=F32)  80 us
    dot_general x5, matrix products, mm_nt(): lax.dot_general(a, b, (((1,), (1,)), ((), ())), preferred_element_type=F32)  76.8 us
    dot_general x5, matrix products, mm_tn(): lax.dot_general(a, b, (((0,), (0,)), ((), ())), preferred_element_type=F32)  69 us
    ppermute x24, starting transfers between devices, core_swap(): return lax.ppermute(value, C, [(i, i ^ 1) for i in range(n)])  58.8 us
    ppermute x28, waiting for transfers between devices, side_swap(): return lax.ppermute(value, F, [(j, j ^ 1) for j in range(lax.axis_size(F))])  52.9 us
  transfers between devices with their start and end apart: 101, of which 31 were waited for; matrix products, arithmetic and copies ran while one was open for 19% of the time, Pallas kernels for 44%

profile of v3, /device:TPU:17, one launch (start us, length us, event | category | flops | bytes accessed | tf_op | source)
XLA Modules:
  0.0 1636.9 jit_solution(11023667061621324104)
XLA Ops:
  20.5 18.3 %collective-permute-done.6.refs_2_ = bf16[256,640]{1,0:T(8,128)(2,1)} collective-permute-done((bf16[256,640]{1,0:T(8,128)(2,1)S(1)}, bf16[256,640]{1,0:T(8,128)(2,1)}, u32[]{:S(2)}, u32[]{:S(2)}) %collective-permute-start.6) | collective-permute-done | bytes 327712 | tf_op jit(solution)/shard_map/ppermute | solution.py:31
  44.0 10.2 collective-permute-done.4
  67.9 6.3 collective-permute-done.13.refs_1_
  74.2 9.2 collective-permute-done.14.refs_2_
  87.4 4.9 collective-permute-done.20.refs_3_
  96.7 6.1 collective-permute-done.18.refs_6_
  104.0 5.8 collective-permute-done.19.refs_7_
  110.3 5.1 collective-permute-done.21.refs_5_
  115.7 6.2 collective-permute-done.22.refs_6_
  124.4 80.6 %assemble.5 = bf16[8,256,640]{2,1,0:T(8,128)(2,1)} custom-call(bf16[256,640]{1,0:T(8,128)(2,1)} %copy-done.32, bf16[256,640]{1,0:T(8,128)(2,1)} %copy-done.41, bf16[256,640]{1,0:T(8,128)(2,1)} %collective-permute-done.6.refs_2_, bf16[256,640]{1,0:T(8,128)(2,1)} %collective-permute-done.7.refs_3_, bf16[256,640]{1,0:T(8,128)(2,1)} %copy-done.42, ...), custom_call_target="tpu_custom_call" | custom-call | bytes 1024 | tf_op jit(solution)/shard_map/assemble/pallas_call | solution.py:76
  205.1 64.7 %assemble.6 = bf16[8,64,2048]{2,1,0:T(8,128)(2,1)} custom-call(bf16[64,2048]{1,0:T(8,128)(2,1)} %copy-done.33, bf16[64,2048]{1,0:T(8,128)(2,1)} %copy-done.47, bf16[64,2048]{1,0:T(8,128)(2,1)} %copy-done.48, bf16[64,2048]{1,0:T(8,128)(2,1)} %copy-done.50, bf16[64,2048]{1,0:T(8,128)(2,1)} %copy-done.49, bf16[64,2048]{1,0:T(8,128)(2,1)} %collective-permute-done.21.refs_5_, ...), custom_call_target="tpu_custom_call" | custom-call | bytes 1024 | tf_op jit(solution)/shard_map/assemble/pallas_call | solution.py:76
  283.0 7.9 multiply_convert_fusion.3.qkv
  291.0 17.8 %attention_forward.1 = (bf16[2048,512]{1,0:T(8,128)(2,1)}, f32[2048,4]{1,0:T(8,128)}) custom-call(s32[12]{0:T(128)} %concatenate.40.meta, bf16[2048,640]{1,0:T(8,128)(2,1)} %multiply_convert_fusion.3.qkv, s32[2048,1]{1,0:T(8,128)} %copy.28.seg_col, s32[4,1,512]{2,1,0:T(1,128)} %copy-done.52), custom_call_target="tpu_custom_call" | custom-call | flops 4194304 | bytes 16384 | tf_op jit(solution)/shard_map/attention_forward/pallas_call | solution.py:373
  308.8 6.7 convolution_convert_fusion.2
  320.7 4.6 copy.29
  325.2 4.6 copy.31
  351.4 14.4 collective-permute-done.37.refs_1_
  370.4 12.5 collective-permute-done.36.refs_7_
  383.1 175.9 %assemble.7 = bf16[8,176,2048]{2,1,0:T(8,128)(2,1)} custom-call(bf16[176,2048]{1,0:T(8,128)(2,1)} %constant_dynamic-slice_fusion.18.refs_0_, bf16[176,2048]{1,0:T(8,128)(2,1)} %copy-done.36, bf16[176,2048]{1,0:T(8,128)(2,1)} %collective-permute-done.27.refs_2_, bf16[176,2048]{1,0:T(8,128)(2,1)} %collective-permute-done.34.refs_3_, ...), custom_call_target="tpu_custom_call" | custom-call | bytes 1024 | tf_op jit(solution)/shard_map/assemble/pallas_call | solution.py:76
  565.6 5.3 fusion.8
  570.8 5.0 collective-permute-start.48
  581.0 16.0 fusion.28
  597.0 18.8 %collective-permute-start.40 = (bf16[512,2048]{1,0:T(8,128)(2,1)S(1)}, bf16[512,2048]{1,0:T(8,128)(2,1)}, u32[]{:S(2)}, u32[]{:S(2)}) collective-permute-start(bf16[512,2048]{1,0:T(8,128)(2,1)S(1)} %get-tuple-element.96), channel_id=1, source_target_pairs={{0,8},{8,0},{16,24},{24,16},{1,9},{9,1},{17,25},{25,17},{2,10},{10... | collective-permute-start | bytes 6291464 | tf_op jit(solution)/shard_map/ppermute | solution.py:131
  615.8 8.0 collective-permute-done.41
  629.1 16.2 collective-permute-done.49.refs_3_
  646.8 13.9 collective-permute-done.46.refs_7_
  662.8 175.9 %assemble.8 = bf16[8,256,1408]{2,1,0:T(8,128)(2,1)} custom-call(bf16[256,1408]{1,0:T(8,128)(2,1)} %get-tuple-element.146.refs_0_, bf16[256,1408]{1,0:T(8,128)(2,1)} %collective-permute-done.37.refs_1_, bf16[256,1408]{1,0:T(8,128)(2,1)} %collective-permute-done.42.refs_2_, bf16[256,1408]{1,0:T(8,128)(2,1)} %copy-done.34, ...), custom_call_target="tpu_custom_call" | custom-call | bytes 1024 | tf_op jit(solution)/shard_map/assemble/pallas_call | solution.py:76
  839.6 175.9 %assemble.9 = bf16[8,256,1408]{2,1,0:T(8,128)(2,1)} custom-call(bf16[256,1408]{1,0:T(8,128)(2,1)} %copy-done.19, bf16[256,1408]{1,0:T(8,128)(2,1)} %collective-permute-done.47.refs_1_, bf16[256,1408]{1,0:T(8,128)(2,1)} %collective-permute-done.48.refs_2_, bf16[256,1408]{1,0:T(8,128)(2,1)} %collective-permute-done.49.refs_3_, bf16[256,1408]{1,0:T(8,128)(2,1)} %copy-done.37, ...), custom_call_target="tpu_custom_call" | custom-call | bytes 1024 | tf_op jit(solution)/shard_map/assemble/pallas_call | solution.py:76
  1015.5 21.2 %fusion.20 = f32[2048,1408]{1,0:T(8,128)} fusion(bf16[2048,1408]{1,0:T(8,128)(2,1)} %bitcast.190, bf16[512,2048]{1,0:T(8,128)(2,1)} %collective-permute-done.45, bf16[512,2048]{1,0:T(8,128)(2,1)} %collective-permute-done.41, bf16[512,2048]{1,0:T(8,128)(2,1)} %collective-permute-done.40, bf16[512,2048]{1,0:T(8,128)(2,1)S(1)} %get-tuple-element.96), kind=kOutput, calls=%fused_computation.140 | convolution fusion | flops 11844714496 | bytes 25690112 | tf_op jit(solution)/shard_map/dot_general | solution.py:431
  1036.6 29.0 %multiply_convert_fusion.1 = (bf16[2048,1408]{1,0:T(8,128)(2,1)}, bf16[2048,1408]{1,0:T(8,128)(2,1)}, bf16[2048,1408]{1,0:T(8,128)(2,1)}) fusion(f32[2048,1408]{1,0:T(8,128)} %fusion.28, f32[2048,1408]{1,0:T(8,128)} %fusion.20, bf16[2048,1408]{1,0:T(8,128)(2,1)} %bitcast.188, bf16[512,2048]{1,0:T(8,128)(2,1)} %collective-permute-done.45, ...), kind=kOutput, calls=%fused_computation.3 | convolution fusion | flops 11887968256 | bytes 54525952 | tf_op jit(solution)/shard_map/dot_general | solution.py:431
  1065.6 19.7 %fusion.29 = f32[2048,2048]{1,0:T(8,128)} fusion(bf16[2048,1408]{1,0:T(8,128)(2,1)} %get-tuple-element.52, bf16[2048,1408]{1,0:T(8,128)(2,1)} %bitcast.191), kind=kOutput, calls=%fused_computation.149 | convolution fusion | flops 11811160064 | bytes 28311552 | tf_op jit(solution)/shard_map/dot_general | solution.py:439
  1085.4 21.4 %add_convert_fusion = bf16[2048,2048]{1,0:T(8,128)(2,1)} fusion(f32[2048,2048]{1,0:T(8,128)} %fusion.29, bf16[2048,1408]{1,0:T(8,128)(2,1)} %get-tuple-element.51, bf16[2048,1408]{1,0:T(8,128)(2,1)} %bitcast.189), kind=kOutput, calls=%fused_computation | convolution fusion | flops 11819548672 | bytes 36700160 | tf_op jit(solution)/shard_map/dot_general | solution.py:439
  1106.8 4.8 fusion.25
  1113.2 17.3 %convolution_convert_fusion.5 = bf16[2048,1408]{1,0:T(8,128)(2,1)S(1)} fusion(bf16[2048,1408]{1,0:T(8,128)(2,1)} %get-tuple-element.51, bf16[512,2048]{1,0:T(8,128)(2,1)} %collective-permute-done.45, bf16[512,2048]{1,0:T(8,128)(2,1)} %collective-permute-done.41, bf16[512,2048]{1,0:T(8,128)(2,1)} %collective-permute-done.40, ...), kind=kOutput, calls=%fused_computation.16 | convolution fusion | flops 11847598080 | bytes 19922944 | tf_op jit(solution)/shard_map/dot_general | solution.py:435
  1141.7 4.6 add_convert_fusion.3
  1146.2 19.1 %convolution_convert_fusion.4 = bf16[2048,1408]{1,0:T(8,128)(2,1)} fusion(bf16[2048,1408]{1,0:T(8,128)(2,1)} %get-tuple-element.52, bf16[512,2048]{1,0:T(8,128)(2,1)} %collective-permute-done.45, bf16[512,2048]{1,0:T(8,128)(2,1)} %collective-permute-done.41, bf16[512,2048]{1,0:T(8,128)(2,1)} %collective-permute-done.40, bf16[512,2048]{1,0:T(8,128)(2,1)S(1)} %copy-done.31), kind=kOutput, calls=%fused_computation.15 | convolution fusion | flops 11847598080 | bytes 19922944 | tf_op jit(solution)/shard_map/dot_general | solution.py:435
  1166.5 16.2 convolution_convert_fusion.3
  1182.8 5.2 constant_dynamic-slice_fusion.4
  1190.7 21.5 %collective-permute-done.56 = bf16[512,2048]{1,0:T(8,128)(2,1)} collective-permute-done((bf16[512,2048]{1,0:T(8,128)(2,1)}, bf16[512,2048]{1,0:T(8,128)(2,1)}, u32[]{:S(2)}, u32[]{:S(2)}) %collective-permute-start.56) | collective-permute-done | bytes 2097184 | tf_op jit(solution)/shard_map/ppermute | solution.py:136
  1223.7 15.1 convolution_convert_fusion.1
  1238.8 28.1 %collective-permute-done.60 = bf16[512,2048]{1,0:T(8,128)(2,1)} collective-permute-done((bf16[512,2048]{1,0:T(8,128)(2,1)}, bf16[512,2048]{1,0:T(8,128)(2,1)}, u32[]{:S(2)}, u32[]{:S(2)}) %collective-permute-start.60) | collective-permute-done | bytes 2097184 | tf_op jit(solution)/shard_map/ppermute | solution.py:136
  1278.8 5.5 pad_maximum_fusion.3
  1299.9 6.0 convolution_convert_fusion.7
  1308.1 10.6 fusion.30.gm
  1318.7 27.1 %collective-permute-done.67 = bf16[512,2048]{1,0:T(8,128)(2,1)} collective-permute-done((bf16[512,2048]{1,0:T(8,128)(2,1)S(1)}, bf16[512,2048]{1,0:T(8,128)(2,1)}, u32[]{:S(2)}, u32[]{:S(2)}) %collective-permute-start.67) | collective-permute-done | bytes 2097184 | tf_op jit(solution)/shard_map/ppermute | solution.py:136
  1345.8 5.8 add_add_fusion
  1351.6 31.0 %attention_backward.1 = bf16[2048,640]{1,0:T(8,128)(2,1)} custom-call(s32[12]{0:T(128)} %concatenate.40.meta, bf16[2048,640]{1,0:T(8,128)(2,1)} %multiply_convert_fusion.3.qkv, s32[2048,1]{1,0:T(8,128)} %copy.28.seg_col, s32[4,1,512]{2,1,0:T(1,128)} %copy-done.52, f32[2048,512]{1,0:T(8,128)} %fusion.30.gm, bf16[2048,512]{1,0:T(8,128)(2,1)} %get-tuple-element.47.mixed, ...), custom_call_target="tpu_custom_call" | custom-call | flops 10485760 | bytes 32768 | tf_op jit(solution)/shard_map/attention_backward/pallas_call | solution.py:401
  1382.7 9.1 convolution_convert_fusion
  1409.2 4.4 add_convert_fusion.1
  1413.7 10.3 convolution_convert_fusion.6
  1437.4 10.7 collective-permute-done.86
  1449.2 14.3 collective-permute-done.96
  1476.3 5.1 bitcast_convert_fusion
  1485.2 12.3 reduce-scatter.8.cloned.1.call-done
  1497.5 18.3 %collective-permute-start.79 = (bf16[64,2048]{1,0:T(8,128)(2,1)}, bf16[64,2048]{1,0:T(8,128)(2,1)S(1)}, u32[]{:S(2)}, u32[]{:S(2)}) collective-permute-start(bf16[64,2048]{1,0:T(8,128)(2,1)} %reduce-scatter.8.cloned.1.call-done), channel_id=1, source_target_pairs={{0,0},{4,1},{8,10},{12,11},{16,20},{20,21},{24,30},{28,31}} | collective-permute-start | bytes 786440 | tf_op jit(solution)/shard_map/ppermute | solution.py:217
  1522.4 8.4 collective-permute-done.90
  1533.4 4.5 collective-permute-start.92
  1537.9 10.7 collective-permute-done.79
  1553.1 10.6 collective-permute-done.93
  1574.6 5.9 bitcast_multiply_fusion
  1580.5 6.3 copy.66
  1586.8 6.2 copy.67
  1596.7 9.2 collective-permute-start.76
  1609.1 6.3 collective-permute-done.77
  (443 shorter events, 263.1 us)
Async XLA Ops:
  7.2 1344.4 %reduce-scatter.4.cloned.1.call-start = ((), (), s32[]{:S(2)}) async-start(), calls=%async_computation.3 | async-start | bytes 6488064 | tf_op jit(solution)/shard_map/reduce_scatter | solution.py:115
  7.3 46.9 %collective-permute-start.4 = (bf16[512,2048]{1,0:T(8,128)(2,1)}, bf16[512,2048]{1,0:T(8,128)(2,1)}, u32[]{:S(2)}, u32[]{:S(2)}) collective-permute-start(bf16[512,2048]{1,0:T(8,128)(2,1)} %bitcast.166), channel_id=1, source_target_pairs={{0,16},{8,24},{16,0},{24,8},{1,17},{9,25},{17,1},{25,9},{2,18},{10... | collective-permute-start | bytes 6291464 | tf_op jit(solution)/shard_map/ppermute | solution.py:136
  11.6 27.2 %collective-permute-start.6 = (bf16[256,640]{1,0:T(8,128)(2,1)S(1)}, bf16[256,640]{1,0:T(8,128)(2,1)}, u32[]{:S(2)}, u32[]{:S(2)}) collective-permute-start(bf16[256,640]{1,0:T(8,128)(2,1)S(1)} %multiply_convert_fusion.6.refs_0_), channel_id=1, source_target_pairs={{0,4},{1,5},{2,6},{3,7},{4,0},{5,1},{6,2},{7,3},{8,12},{9,13},{10,... | collective-permute-start | bytes 983048 | tf_op jit(solution)/shard_map/ppermute | solution.py:31
  14.8 27.9 %collective-permute-start.7 = (bf16[256,640]{1,0:T(8,128)(2,1)S(1)}, bf16[256,640]{1,0:T(8,128)(2,1)}, u32[]{:S(2)}, u32[]{:S(2)}) collective-permute-start(bf16[256,640]{1,0:T(8,128)(2,1)S(1)} %multiply_convert_fusion.6.refs_0_), channel_id=1, source_target_pairs={{0,2},{1,3},{2,4},{3,5},{4,6},{5,7},{6,0},{7,1},{8,10},{9,11},{10,... | collective-permute-start | bytes 983048 | tf_op jit(solution)/shard_map/ppermute | solution.py:31
  17.6 41.0 %collective-permute-start.10 = (bf16[64,2048]{1,0:T(8,128)(2,1)S(1)}, bf16[64,2048]{1,0:T(8,128)(2,1)S(1)}, u32[]{:S(2)}, u32[]{:S(2)}) collective-permute-start(bf16[64,2048]{1,0:T(8,128)(2,1)S(1)} %get-tuple-element.139), channel_id=1, source_target_pairs={{0,1},{1,5},{10,9},{11,13},{20,17},{21,21},{30,25},{31,29}} | collective-permute-start | bytes 786440 | tf_op jit(solution)/shard_map/ppermute | solution.py:208
  19.8 42.2 %collective-permute-start.11 = (bf16[64,2048]{1,0:T(8,128)(2,1)S(1)}, bf16[64,2048]{1,0:T(8,128)(2,1)S(1)}, u32[]{:S(2)}, u32[]{:S(2)}) collective-permute-start(bf16[64,2048]{1,0:T(8,128)(2,1)S(1)} %get-tuple-element.142), channel_id=1, source_target_pairs={{0,2},{1,6},{10,10},{11,14},{20,18},{21,22},{30,26},{31,30}} | collective-permute-start | bytes 786440 | tf_op jit(solution)/shard_map/ppermute | solution.py:208
  58.6 216.7 %collective-permute-start.3 = (bf16[512,2048]{1,0:T(8,128)(2,1)}, bf16[512,2048]{1,0:T(8,128)(2,1)}, u32[]{:S(2)}, u32[]{:S(2)}) collective-permute-start(bf16[512,2048]{1,0:T(8,128)(2,1)} %bitcast.167), channel_id=1, source_target_pairs={{0,8},{8,0},{16,24},{24,16},{1,9},{9,1},{17,25},{25,17},{2,10},{10... | collective-permute-start | bytes 6291464 | tf_op jit(solution)/shard_map/ppermute | solution.py:131
  62.2 207.7 %collective-permute-start.25 = (bf16[512,2048]{1,0:T(8,128)(2,1)}, bf16[512,2048]{1,0:T(8,128)(2,1)}, u32[]{:S(2)}, u32[]{:S(2)}) collective-permute-start(bf16[512,2048]{1,0:T(8,128)(2,1)} %bitcast.171), channel_id=1, source_target_pairs={{0,16},{8,24},{16,0},{24,8},{1,17},{9,25},{17,1},{25,9},{2,18},{10... | collective-permute-start | bytes 6291464 | tf_op jit(solution)/shard_map/ppermute | solution.py:136
  66.6 208.6 %collective-permute-start.8 = (bf16[512,2048]{1,0:T(8,128)(2,1)}, bf16[512,2048]{1,0:T(8,128)(2,1)}, u32[]{:S(2)}, u32[]{:S(2)}) collective-permute-start(bf16[512,2048]{1,0:T(8,128)(2,1)} %collective-permute-done.4), channel_id=1, source_target_pairs={{0,8},{8,0},{16,24},{24,16},{1,9},{9,1},{17,25},{25,17},{2,10},{10... | collective-permute-start | bytes 6291464 | tf_op jit(solution)/shard_map/ppermute | solution.py:131
  109.8 161.3 %collective-permute-start.23 = (bf16[176,2048]{1,0:T(8,128)(2,1)}, bf16[176,2048]{1,0:T(8,128)(2,1)S(1)}, u32[]{:S(2)}, u32[]{:S(2)}) collective-permute-start(bf16[176,2048]{1,0:T(8,128)(2,1)} %constant_dynamic-slice_fusion.18.refs_0_), channel_id=1, source_target_pairs={{0,6},{1,7},{2,0},{3,1},{4,2},{5,3},{6,4},{7,5},{8,14},{9,15},{10,... | collective-permute-start | bytes 2162696 | tf_op jit(solution)/shard_map/ppermute | solution.py:31
  121.9 83.1 %collective-permute-start.30 = (bf16[64,2048]{1,0:T(8,128)(2,1)}, bf16[64,2048]{1,0:T(8,128)(2,1)}, u32[]{:S(2)}, u32[]{:S(2)}) collective-permute-start(bf16[64,2048]{1,0:T(8,128)(2,1)} %copy-done.50), channel_id=1, source_target_pairs={{0,1},{1,0},{2,3},{3,2},{4,5},{5,4},{6,7},{7,6},{8,9},{9,8},{10,11... | collective-permute-start | bytes 786440 | tf_op jit(solution)/shard_map/ppermute | solution.py:35
  205.0 103.8 %collective-permute-start.27 = (bf16[176,2048]{1,0:T(8,128)(2,1)}, bf16[176,2048]{1,0:T(8,128)(2,1)}, u32[]{:S(2)}, u32[]{:S(2)}) collective-permute-start(bf16[176,2048]{1,0:T(8,128)(2,1)} %constant_dynamic-slice_fusion.18.refs_0_), channel_id=1, source_target_pairs={{0,4},{1,5},{2,6},{3,7},{4,0},{5,1},{6,2},{7,3},{8,12},{9,13},{10,... | collective-permute-start | bytes 2162696 | tf_op jit(solution)/shard_map/ppermute | solution.py:31
  269.8 38.9 %collective-permute-start.28 = (bf16[176,2048]{1,0:T(8,128)(2,1)}, bf16[176,2048]{1,0:T(8,128)(2,1)}, u32[]{:S(2)}, u32[]{:S(2)}) collective-permute-start(bf16[176,2048]{1,0:T(8,128)(2,1)} %constant_dynamic-slice_fusion.18.refs_0_), channel_id=1, source_target_pairs={{0,1},{1,0},{2,3},{3,2},{4,5},{5,4},{6,7},{7,6},{8,9},{9,8},{10,11... | collective-permute-start | bytes 2162696 | tf_op jit(solution)/shard_map/ppermute | solution.py:35
  271.2 37.6 %collective-permute-start.24 = (bf16[512,2048]{1,0:T(8,128)(2,1)}, bf16[512,2048]{1,0:T(8,128)(2,1)}, u32[]{:S(2)}, u32[]{:S(2)}) collective-permute-start(bf16[512,2048]{1,0:T(8,128)(2,1)} %bitcast.172), channel_id=1, source_target_pairs={{0,8},{8,0},{16,24},{24,16},{1,9},{9,1},{17,25},{25,17},{2,10},{10... | collective-permute-start | bytes 6291464 | tf_op jit(solution)/shard_map/ppermute | solution.py:131
  275.2 33.6 %collective-permute-start.29 = (bf16[176,2048]{1,0:T(8,128)(2,1)S(1)}, bf16[176,2048]{1,0:T(8,128)(2,1)}, u32[]{:S(2)}, u32[]{:S(2)}) collective-permute-start(bf16[176,2048]{1,0:T(8,128)(2,1)S(1)} %collective-permute-done.23.refs_1_), channel_id=1, source_target_pairs={{0,1},{1,0},{2,3},{3,2},{4,5},{5,4},{6,7},{7,6},{8,9},{9,8},{10,11... | collective-permute-start | bytes 2162696 | tf_op jit(solution)/shard_map/ppermute | solution.py:35
  275.2 33.6 %collective-permute-start.26 = (bf16[512,2048]{1,0:T(8,128)(2,1)}, bf16[512,2048]{1,0:T(8,128)(2,1)}, u32[]{:S(2)}, u32[]{:S(2)}) collective-permute-start(bf16[512,2048]{1,0:T(8,128)(2,1)} %collective-permute-done.25), channel_id=1, source_target_pairs={{0,8},{8,0},{16,24},{24,16},{1,9},{9,1},{17,25},{25,17},{2,10},{10... | collective-permute-start | bytes 6291464 | tf_op jit(solution)/shard_map/ppermute | solution.py:131
  320.5 29.4 %collective-permute-start.34 = (bf16[176,2048]{1,0:T(8,128)(2,1)}, bf16[176,2048]{1,0:T(8,128)(2,1)}, u32[]{:S(2)}, u32[]{:S(2)}) collective-permute-start(bf16[176,2048]{1,0:T(8,128)(2,1)} %constant_dynamic-slice_fusion.18.refs_0_), channel_id=1, source_target_pairs={{0,2},{1,3},{2,4},{3,5},{4,6},{5,7},{6,0},{7,1},{8,10},{9,11},{10,... | collective-permute-start | bytes 2162696 | tf_op jit(solution)/shard_map/ppermute | solution.py:31
  332.5 230.9 %collective-permute-start.31 = (bf16[512,2048]{1,0:T(8,128)(2,1)}, bf16[512,2048]{1,0:T(8,128)(2,1)}, u32[]{:S(2)}, u32[]{:S(2)}) collective-permute-start(bf16[512,2048]{1,0:T(8,128)(2,1)} %get-tuple-element.109), channel_id=1, source_target_pairs={{0,8},{8,0},{16,24},{24,16},{1,9},{9,1},{17,25},{25,17},{2,10},{10... | collective-permute-start | bytes 6291464 | tf_op jit(solution)/shard_map/ppermute | solution.py:131
  337.1 228.5 %collective-permute-start.33 = (bf16[512,2048]{1,0:T(8,128)(2,1)}, bf16[512,2048]{1,0:T(8,128)(2,1)}, u32[]{:S(2)}, u32[]{:S(2)}) collective-permute-start(bf16[512,2048]{1,0:T(8,128)(2,1)} %add_convert_fusion.4), channel_id=1, source_target_pairs={{0,16},{8,24},{16,0},{24,8},{1,17},{9,25},{17,1},{25,9},{2,18},{10... | collective-permute-start | bytes 6291464 | tf_op jit(solution)/shard_map/ppermute | solution.py:136
  349.9 32.9 %collective-permute-start.36 = (bf16[176,2048]{1,0:T(8,128)(2,1)}, bf16[176,2048]{1,0:T(8,128)(2,1)}, u32[]{:S(2)}, u32[]{:S(2)}) collective-permute-start(bf16[176,2048]{1,0:T(8,128)(2,1)} %collective-permute-done.34.refs_3_), channel_id=1, source_target_pairs={{0,1},{1,0},{2,3},{3,2},{4,5},{5,4},{6,7},{7,6},{8,9},{9,8},{10,11... | collective-permute-start | bytes 2162696 | tf_op jit(solution)/shard_map/ppermute | solution.py:35
  365.8 205.1 %collective-permute-start.38 = (bf16[256,1408]{1,0:T(8,128)(2,1)}, bf16[256,1408]{1,0:T(8,128)(2,1)}, u32[]{:S(2)}, u32[]{:S(2)}) collective-permute-start(bf16[256,1408]{1,0:T(8,128)(2,1)} %get-tuple-element.146.refs_0_), channel_id=1, source_target_pairs={{0,1},{1,0},{2,3},{3,2},{4,5},{5,4},{6,7},{7,6},{8,9},{9,8},{10,11... | collective-permute-start | bytes 2162696 | tf_op jit(solution)/shard_map/ppermute | solution.py:35
  368.6 207.3 %collective-permute-start.42 = (bf16[256,1408]{1,0:T(8,128)(2,1)}, bf16[256,1408]{1,0:T(8,128)(2,1)}, u32[]{:S(2)}, u32[]{:S(2)}) collective-permute-start(bf16[256,1408]{1,0:T(8,128)(2,1)} %get-tuple-element.146.refs_0_), channel_id=1, source_target_pairs={{0,4},{1,5},{2,6},{3,7},{4,0},{5,1},{6,2},{7,3},{8,12},{9,13},{10,... | collective-permute-start | bytes 2162696 | tf_op jit(solution)/shard_map/ppermute | solution.py:31
  382.8 193.3 %collective-permute-start.39 = (bf16[256,1408]{1,0:T(8,128)(2,1)}, bf16[256,1408]{1,0:T(8,128)(2,1)}, u32[]{:S(2)}, u32[]{:S(2)}) collective-permute-start(bf16[256,1408]{1,0:T(8,128)(2,1)} %collective-permute-done.37.refs_1_), channel_id=1, source_target_pairs={{0,1},{1,0},{2,3},{3,2},{4,5},{5,4},{6,7},{7,6},{8,9},{9,8},{10,11... | collective-permute-start | bytes 2162696 | tf_op jit(solution)/shard_map/ppermute | solution.py:35
  563.4 33.6 %collective-permute-start.43 = (bf16[256,1408]{1,0:T(8,128)(2,1)}, bf16[256,1408]{1,0:T(8,128)(2,1)S(1)}, u32[]{:S(2)}, u32[]{:S(2)}) collective-permute-start(bf16[256,1408]{1,0:T(8,128)(2,1)} %get-tuple-element.146.refs_0_), channel_id=1, source_target_pairs={{0,2},{1,3},{2,4},{3,5},{4,6},{5,7},{6,0},{7,1},{8,10},{9,11},{10,... | collective-permute-start | bytes 2162696 | tf_op jit(solution)/shard_map/ppermute | solution.py:31
  565.6 62.0 %collective-permute-start.47 = (bf16[256,1408]{1,0:T(8,128)(2,1)S(1)}, bf16[256,1408]{1,0:T(8,128)(2,1)}, u32[]{:S(2)}, u32[]{:S(2)}) collective-permute-start(bf16[256,1408]{1,0:T(8,128)(2,1)S(1)} %get-tuple-element.145.refs_0_), channel_id=1, source_target_pairs={{0,6},{1,7},{2,0},{3,1},{4,2},{5,3},{6,4},{7,5},{8,14},{9,15},{10,... | collective-permute-start | bytes 2162696 | tf_op jit(solution)/shard_map/ppermute | solution.py:31
  570.8 58.0 %collective-permute-start.48 = (bf16[256,1408]{1,0:T(8,128)(2,1)S(1)}, bf16[256,1408]{1,0:T(8,128)(2,1)}, u32[]{:S(2)}, u32[]{:S(2)}) collective-permute-start(bf16[256,1408]{1,0:T(8,128)(2,1)S(1)} %get-tuple-element.145.refs_0_), channel_id=1, source_target_pairs={{0,4},{1,5},{2,6},{3,7},{4,0},{5,1},{6,2},{7,3},{8,12},{9,13},{10,... | collective-permute-start | bytes 2162696 | tf_op jit(solution)/shard_map/ppermute | solution.py:31
  575.9 39.9 %collective-permute-start.44 = (bf16[256,1408]{1,0:T(8,128)(2,1)}, bf16[256,1408]{1,0:T(8,128)(2,1)S(1)}, u32[]{:S(2)}, u32[]{:S(2)}) collective-permute-start(bf16[256,1408]{1,0:T(8,128)(2,1)} %collective-permute-done.42.refs_2_), channel_id=1, source_target_pairs={{0,1},{1,0},{2,3},{3,2},{4,5},{5,4},{6,7},{7,6},{8,9},{9,8},{10,11... | collective-permute-start | bytes 2162696 | tf_op jit(solution)/shard_map/ppermute | solution.py:35
  579.2 44.6 %collective-permute-start.41 = (bf16[512,2048]{1,0:T(8,128)(2,1)S(1)}, bf16[512,2048]{1,0:T(8,128)(2,1)}, u32[]{:S(2)}, u32[]{:S(2)}) collective-permute-start(bf16[512,2048]{1,0:T(8,128)(2,1)S(1)} %get-tuple-element.96), channel_id=1, source_target_pairs={{0,16},{8,24},{16,0},{24,8},{1,17},{9,25},{17,1},{25,9},{2,18},{10... | collective-permute-start | bytes 6291464 | tf_op jit(solution)/shard_map/ppermute | solution.py:136
  597.0 418.5 %collective-permute-start.40 = (bf16[512,2048]{1,0:T(8,128)(2,1)S(1)}, bf16[512,2048]{1,0:T(8,128)(2,1)}, u32[]{:S(2)}, u32[]{:S(2)}) collective-permute-start(bf16[512,2048]{1,0:T(8,128)(2,1)S(1)} %get-tuple-element.96), channel_id=1, source_target_pairs={{0,8},{8,0},{16,24},{24,16},{1,9},{9,1},{17,25},{25,17},{2,10},{10... | collective-permute-start | bytes 6291464 | tf_op jit(solution)/shard_map/ppermute | solution.py:131
  623.7 391.8 %collective-permute-start.45 = (bf16[512,2048]{1,0:T(8,128)(2,1)}, bf16[512,2048]{1,0:T(8,128)(2,1)}, u32[]{:S(2)}, u32[]{:S(2)}) collective-permute-start(bf16[512,2048]{1,0:T(8,128)(2,1)} %collective-permute-done.41), channel_id=1, source_target_pairs={{0,8},{8,0},{16,24},{24,16},{1,9},{9,1},{17,25},{25,17},{2,10},{10... | collective-permute-start | bytes 6291464 | tf_op jit(solution)/shard_map/ppermute | solution.py:131
  628.8 32.0 %collective-permute-start.46 = (bf16[256,1408]{1,0:T(8,128)(2,1)S(1)}, bf16[256,1408]{1,0:T(8,128)(2,1)S(1)}, u32[]{:S(2)}, u32[]{:S(2)}) collective-permute-start(bf16[256,1408]{1,0:T(8,128)(2,1)S(1)} %collective-permute-done.43.refs_3_), channel_id=1, source_target_pairs={{0,1},{1,0},{2,3},{3,2},{4,5},{5,4},{6,7},{7,6},{8,9},{9,8},{10,11... | collective-permute-start | bytes 2162696 | tf_op jit(solution)/shard_map/ppermute | solution.py:35
  645.3 193.4 %collective-permute-start.51 = (bf16[256,1408]{1,0:T(8,128)(2,1)}, bf16[256,1408]{1,0:T(8,128)(2,1)}, u32[]{:S(2)}, u32[]{:S(2)}) collective-permute-start(bf16[256,1408]{1,0:T(8,128)(2,1)} %collective-permute-done.47.refs_1_), channel_id=1, source_target_pairs={{0,1},{1,0},{2,3},{3,2},{4,5},{5,4},{6,7},{7,6},{8,9},{9,8},{10,11... | collective-permute-start | bytes 2162696 | tf_op jit(solution)/shard_map/ppermute | solution.py:35
  646.5 192.2 %collective-permute-start.52 = (bf16[256,1408]{1,0:T(8,128)(2,1)}, bf16[256,1408]{1,0:T(8,128)(2,1)S(1)}, u32[]{:S(2)}, u32[]{:S(2)}) collective-permute-start(bf16[256,1408]{1,0:T(8,128)(2,1)} %collective-permute-done.48.refs_2_), channel_id=1, source_target_pairs={{0,1},{1,0},{2,3},{3,2},{4,5},{5,4},{6,7},{7,6},{8,9},{9,8},{10,11... | collective-permute-start | bytes 2162696 | tf_op jit(solution)/shard_map/ppermute | solution.py:35
  661.6 177.1 %collective-permute-start.53 = (bf16[256,1408]{1,0:T(8,128)(2,1)}, bf16[256,1408]{1,0:T(8,128)(2,1)}, u32[]{:S(2)}, u32[]{:S(2)}) collective-permute-start(bf16[256,1408]{1,0:T(8,128)(2,1)} %collective-permute-done.49.refs_3_), channel_id=1, source_target_pairs={{0,1},{1,0},{2,3},{3,2},{4,5},{5,4},{6,7},{7,6},{8,9},{9,8},{10,11... | collective-permute-start | bytes 2162696 | tf_op jit(solution)/shard_map/ppermute | solution.py:35
  1111.6 28.9 %collective-permute-start.55 = (bf16[512,2048]{1,0:T(8,128)(2,1)}, bf16[512,2048]{1,0:T(8,128)(2,1)}, u32[]{:S(2)}, u32[]{:S(2)}) collective-permute-start(bf16[512,2048]{1,0:T(8,128)(2,1)} %get-tuple-element.108), channel_id=1, source_target_pairs={{0,8},{8,0},{16,24},{24,16},{1,9},{9,1},{17,25},{25,17},{2,10},{10... | collective-permute-start | bytes 6291464 | tf_op jit(solution)/shard_map/ppermute | solution.py:131
  1134.7 30.6 %collective-permute-start.57 = (bf16[256,1408]{0,1:T(8,128)(2,1)}, bf16[256,1408]{0,1:T(8,128)(2,1)}, u32[]{:S(2)}, u32[]{:S(2)}) collective-permute-start(bf16[256,1408]{0,1:T(8,128)(2,1)} %bitcast.204), channel_id=1, source_target_pairs={{0,1},{1,0},{2,3},{3,2},{4,5},{5,4},{6,7},{7,6},{8,9},{9,8},{10,11... | collective-permute-start | bytes 2162696 | tf_op jit(solution)/shard_map/ppermute | solution.py:35
  1136.1 80.3 %collective-permute-start.58 = (bf16[256,1408]{0,1:T(8,128)(2,1)}, bf16[256,1408]{0,1:T(8,128)(2,1)}, u32[]{:S(2)}, u32[]{:S(2)}) collective-permute-start(bf16[256,1408]{0,1:T(8,128)(2,1)} %bitcast.199), channel_id=1, source_target_pairs={{0,1},{1,0},{2,3},{3,2},{4,5},{5,4},{6,7},{7,6},{8,9},{9,8},{10,11... | collective-permute-start | bytes 2162696 | tf_op jit(solution)/shard_map/ppermute | solution.py:35
  1137.3 53.0 %collective-permute-start.54 = (bf16[512,2048]{1,0:T(8,128)(2,1)}, bf16[512,2048]{1,0:T(8,128)(2,1)}, u32[]{:S(2)}, u32[]{:S(2)}) collective-permute-start(bf16[512,2048]{1,0:T(8,128)(2,1)} %get-tuple-element.107), channel_id=1, source_target_pairs={{0,8},{8,0},{16,24},{24,16},{1,9},{9,1},{17,25},{25,17},{2,10},{10... | collective-permute-start | bytes 6291464 | tf_op jit(solution)/shard_map/ppermute | solution.py:131
  1139.0 99.8 %collective-permute-start.63 = (bf16[256,1408]{0,1:T(8,128)(2,1)}, bf16[256,1408]{0,1:T(8,128)(2,1)}, u32[]{:S(2)}, u32[]{:S(2)}) collective-permute-start(bf16[256,1408]{0,1:T(8,128)(2,1)} %bitcast.27), channel_id=1, source_target_pairs={{0,1},{1,0},{2,3},{3,2},{4,5},{5,4},{6,7},{7,6},{8,9},{9,8},{10,11... | collective-permute-start | bytes 2162696 | tf_op jit(solution)/shard_map/ppermute | solution.py:35
  1140.5 98.3 %collective-permute-start.62 = (bf16[256,1408]{0,1:T(8,128)(2,1)}, bf16[256,1408]{0,1:T(8,128)(2,1)}, u32[]{:S(2)}, u32[]{:S(2)}) collective-permute-start(bf16[256,1408]{0,1:T(8,128)(2,1)} %bitcast.26), channel_id=1, source_target_pairs={{0,1},{1,0},{2,3},{3,2},{4,5},{5,4},{6,7},{7,6},{8,9},{9,8},{10,11... | collective-permute-start | bytes 2162696 | tf_op jit(solution)/shard_map/ppermute | solution.py:35
  1165.3 46.9 %collective-permute-start.56 = (bf16[512,2048]{1,0:T(8,128)(2,1)}, bf16[512,2048]{1,0:T(8,128)(2,1)}, u32[]{:S(2)}, u32[]{:S(2)}) collective-permute-start(bf16[512,2048]{1,0:T(8,128)(2,1)} %add_convert_fusion.3), channel_id=1, source_target_pairs={{0,16},{8,24},{16,0},{24,8},{1,17},{9,25},{17,1},{25,9},{2,18},{10... | collective-permute-start | bytes 6291464 | tf_op jit(solution)/shard_map/ppermute | solution.py:136
  1190.3 307.3 %reduce-scatter.8.cloned.1.call-start = ((), (), s32[]{:S(2)}) async-start(), calls=%async_computation.5 | async-start | bytes 2359296 | tf_op jit(solution)/shard_map/reduce_scatter | solution.py:115
  1190.3 48.5 %collective-permute-start.61 = (bf16[256,1408]{0,1:T(8,128)(2,1)}, bf16[256,1408]{0,1:T(8,128)(2,1)}, u32[]{:S(2)}, u32[]{:S(2)}) collective-permute-start(bf16[256,1408]{0,1:T(8,128)(2,1)} %bitcast.203), channel_id=1, source_target_pairs={{0,1},{1,0},{2,3},{3,2},{4,5},{5,4},{6,7},{7,6},{8,9},{9,8},{10,11... | collective-permute-start | bytes 2162696 | tf_op jit(solution)/shard_map/ppermute | solution.py:35
  1220.8 46.1 %collective-permute-start.60 = (bf16[512,2048]{1,0:T(8,128)(2,1)}, bf16[512,2048]{1,0:T(8,128)(2,1)}, u32[]{:S(2)}, u32[]{:S(2)}) collective-permute-start(bf16[512,2048]{1,0:T(8,128)(2,1)} %fusion.19), channel_id=1, source_target_pairs={{0,16},{8,24},{16,0},{24,8},{1,17},{9,25},{17,1},{25,9},{2,18},{10... | collective-permute-start | bytes 6291464 | tf_op jit(solution)/shard_map/ppermute | solution.py:136
  1222.0 56.8 %collective-permute-start.59 = (bf16[512,2048]{1,0:T(8,128)(2,1)}, bf16[512,2048]{1,0:T(8,128)(2,1)}, u32[]{:S(2)}, u32[]{:S(2)}) collective-permute-start(bf16[512,2048]{1,0:T(8,128)(2,1)} %fusion.19), channel_id=1, source_target_pairs={{0,8},{8,0},{16,24},{24,16},{1,9},{9,1},{17,25},{25,17},{2,10},{10... | collective-permute-start | bytes 6291464 | tf_op jit(solution)/shard_map/ppermute | solution.py:131
  1275.0 30.8 %collective-permute-start.68 = (bf16[256,1408]{0,1:T(8,128)(2,1)}, bf16[256,1408]{0,1:T(8,128)(2,1)}, u32[]{:S(2)}, u32[]{:S(2)}) collective-permute-start(bf16[256,1408]{0,1:T(8,128)(2,1)} %bitcast.201), channel_id=1, source_target_pairs={{0,1},{1,0},{2,3},{3,2},{4,5},{5,4},{6,7},{7,6},{8,9},{9,8},{10,11... | collective-permute-start | bytes 2162696 | tf_op jit(solution)/shard_map/ppermute | solution.py:35
  1277.6 74.0 %collective-permute-start.69 = (bf16[256,1408]{0,1:T(8,128)(2,1)}, bf16[256,1408]{0,1:T(8,128)(2,1)}, u32[]{:S(2)}, u32[]{:S(2)}) collective-permute-start(bf16[256,1408]{0,1:T(8,128)(2,1)} %bitcast.200), channel_id=1, source_target_pairs={{0,1},{1,0},{2,3},{3,2},{4,5},{5,4},{6,7},{7,6},{8,9},{9,8},{10,11... | collective-permute-start | bytes 2162696 | tf_op jit(solution)/shard_map/ppermute | solution.py:35
  1289.6 93.1 %collective-permute-start.72 = (bf16[256,1408]{0,1:T(8,128)(2,1)}, bf16[256,1408]{0,1:T(8,128)(2,1)}, u32[]{:S(2)}, u32[]{:S(2)}) collective-permute-start(bf16[256,1408]{0,1:T(8,128)(2,1)} %fusion.14), channel_id=1, source_target_pairs={{0,6},{1,7},{2,0},{3,1},{4,2},{5,3},{6,4},{7,5},{8,14},{9,15},{10,... | collective-permute-start | bytes 2162696 | tf_op jit(solution)/shard_map/ppermute | solution.py:31
  1298.7 47.1 %collective-permute-start.67 = (bf16[512,2048]{1,0:T(8,128)(2,1)S(1)}, bf16[512,2048]{1,0:T(8,128)(2,1)}, u32[]{:S(2)}, u32[]{:S(2)}) collective-permute-start(bf16[512,2048]{1,0:T(8,128)(2,1)S(1)} %add_convert_fusion.2), channel_id=1, source_target_pairs={{0,16},{8,24},{16,0},{24,8},{1,17},{9,25},{17,1},{25,9},{2,18},{10... | collective-permute-start | bytes 6291464 | tf_op jit(solution)/shard_map/ppermute | solution.py:136
  1305.8 76.8 %collective-permute-start.71 = (bf16[256,1408]{0,1:T(8,128)(2,1)}, bf16[256,1408]{0,1:T(8,128)(2,1)}, u32[]{:S(2)}, u32[]{:S(2)}) collective-permute-start(bf16[256,1408]{0,1:T(8,128)(2,1)} %fusion.15), channel_id=1, source_target_pairs={{0,4},{1,5},{2,6},{3,7},{4,0},{5,1},{6,2},{7,3},{8,12},{9,13},{10,... | collective-permute-start | bytes 2162696 | tf_op jit(solution)/shard_map/ppermute | solution.py:31
  1318.7 63.9 %collective-permute-start.70 = (bf16[256,1408]{0,1:T(8,128)(2,1)}, bf16[256,1408]{0,1:T(8,128)(2,1)}, u32[]{:S(2)}, u32[]{:S(2)}) collective-permute-start(bf16[256,1408]{0,1:T(8,128)(2,1)} %fusion.16), channel_id=1, source_target_pairs={{0,2},{1,3},{2,4},{3,5},{4,6},{5,7},{6,0},{7,1},{8,10},{9,11},{10,... | collective-permute-start | bytes 2162696 | tf_op jit(solution)/shard_map/ppermute | solution.py:31
  1406.8 114.0 %collective-permute-start.88 = (bf16[256,1408]{0,1:T(8,128)(2,1)}, bf16[256,1408]{0,1:T(8,128)(2,1)}, u32[]{:S(2)}, u32[]{:S(2)}) collective-permute-start(bf16[256,1408]{0,1:T(8,128)(2,1)} %fusion.12), channel_id=1, source_target_pairs={{0,2},{1,3},{2,4},{3,5},{4,6},{5,7},{6,0},{7,1},{8,10},{9,11},{10,... | collective-permute-start | bytes 2162696 | tf_op jit(solution)/shard_map/ppermute | solution.py:31
  1406.8 189.9 %reduce-scatter.6.cloned.1.call-start = ((), (), s32[]{:S(2)}) async-start(), calls=%async_computation.4 | async-start | bytes 2949120 | tf_op jit(solution)/shard_map/reduce_scatter | solution.py:115
  1409.2 76.0 %collective-permute-start.73 = (bf16[512,2048]{1,0:T(8,128)(2,1)}, bf16[512,2048]{1,0:T(8,128)(2,1)}, u32[]{:S(2)}, u32[]{:S(2)}) collective-permute-start(bf16[512,2048]{1,0:T(8,128)(2,1)} %get-tuple-element.103), channel_id=1, source_target_pairs={{0,8},{8,0},{16,24},{24,16},{1,9},{9,1},{17,25},{25,17},{2,10},{10... | collective-permute-start | bytes 6291464 | tf_op jit(solution)/shard_map/ppermute | solution.py:131
  1431.2 32.3 %collective-permute-start.96 = (bf16[176,2048]{1,0:T(8,128)(2,1)}, bf16[176,2048]{1,0:T(8,128)(2,1)}, u32[]{:S(2)}, u32[]{:S(2)}) collective-permute-start(bf16[176,2048]{1,0:T(8,128)(2,1)} %reduce-scatter.4.cloned.1.call-done), channel_id=1, source_target_pairs={{0,16},{8,24},{16,0},{24,8},{1,17},{9,25},{17,1},{25,9},{2,18},{10... | collective-permute-start | bytes 2162696 | tf_op jit(solution)/shard_map/ppermute | solution.py:136
  1435.6 30.5 %collective-permute-start.95 = (bf16[176,2048]{1,0:T(8,128)(2,1)}, bf16[176,2048]{1,0:T(8,128)(2,1)S(1)}, u32[]{:S(2)}, u32[]{:S(2)}) collective-permute-start(bf16[176,2048]{1,0:T(8,128)(2,1)} %reduce-scatter.4.cloned.1.call-done), channel_id=1, source_target_pairs={{0,8},{8,0},{16,24},{24,16},{1,9},{9,1},{17,25},{25,17},{2,10},{10... | collective-permute-start | bytes 2162696 | tf_op jit(solution)/shard_map/ppermute | solution.py:131
  1448.1 67.7 %collective-permute-start.75 = (bf16[512,2048]{1,0:T(8,128)(2,1)}, bf16[512,2048]{1,0:T(8,128)(2,1)}, u32[]{:S(2)}, u32[]{:S(2)}) collective-permute-start(bf16[512,2048]{1,0:T(8,128)(2,1)} %add_convert_fusion.1), channel_id=1, source_target_pairs={{0,16},{8,24},{16,0},{24,8},{1,17},{9,25},{17,1},{25,9},{2,18},{10... | collective-permute-start | bytes 6291464 | tf_op jit(solution)/shard_map/ppermute | solution.py:136
  1469.1 52.4 %collective-permute-start.89 = (bf16[256,1408]{0,1:T(8,128)(2,1)}, bf16[256,1408]{0,1:T(8,128)(2,1)}, u32[]{:S(2)}, u32[]{:S(2)}) collective-permute-start(bf16[256,1408]{0,1:T(8,128)(2,1)} %fusion.11), channel_id=1, source_target_pairs={{0,4},{1,5},{2,6},{3,7},{4,0},{5,1},{6,2},{7,3},{8,12},{9,13},{10,... | collective-permute-start | bytes 2162696 | tf_op jit(solution)/shard_map/ppermute | solution.py:31
  1473.6 57.1 %collective-permute-start.90 = (bf16[256,1408]{0,1:T(8,128)(2,1)}, bf16[256,1408]{0,1:T(8,128)(2,1)}, u32[]{:S(2)}, u32[]{:S(2)}) collective-permute-start(bf16[256,1408]{0,1:T(8,128)(2,1)} %fusion.10), channel_id=1, source_target_pairs={{0,6},{1,7},{2,0},{3,1},{4,2},{5,3},{6,4},{7,5},{8,14},{9,15},{10,... | collective-permute-start | bytes 2162696 | tf_op jit(solution)/shard_map/ppermute | solution.py:31
  1497.5 51.0 %collective-permute-start.79 = (bf16[64,2048]{1,0:T(8,128)(2,1)}, bf16[64,2048]{1,0:T(8,128)(2,1)S(1)}, u32[]{:S(2)}, u32[]{:S(2)}) collective-permute-start(bf16[64,2048]{1,0:T(8,128)(2,1)} %reduce-scatter.8.cloned.1.call-done), channel_id=1, source_target_pairs={{0,0},{4,1},{8,10},{12,11},{16,20},{20,21},{24,30},{28,31}} | collective-permute-start | bytes 786440 | tf_op jit(solution)/shard_map/ppermute | solution.py:217
  1515.8 32.8 %collective-permute-start.80 = (bf16[64,2048]{1,0:T(8,128)(2,1)}, bf16[64,2048]{1,0:T(8,128)(2,1)S(1)}, u32[]{:S(2)}, u32[]{:S(2)}) collective-permute-start(bf16[64,2048]{1,0:T(8,128)(2,1)} %reduce-scatter.8.cloned.1.call-done), channel_id=1, source_target_pairs={{1,0},{5,1},{9,10},{13,11},{17,20},{21,21},{25,30},{29,31}} | collective-permute-start | bytes 786440 | tf_op jit(solution)/shard_map/ppermute | solution.py:217
  1520.8 27.8 %collective-permute-start.81 = (bf16[64,2048]{1,0:T(8,128)(2,1)S(1)}, bf16[64,2048]{1,0:T(8,128)(2,1)S(1)}, u32[]{:S(2)}, u32[]{:S(2)}) collective-permute-start(bf16[64,2048]{1,0:T(8,128)(2,1)S(1)} %copy-done.63), channel_id=1, source_target_pairs={{2,0},{6,1},{10,10},{14,11},{18,20},{22,21},{26,30},{30,31}} | collective-permute-start | bytes 786440 | tf_op jit(solution)/shard_map/ppermute | solution.py:217
  1533.4 33.7 %collective-permute-start.92 = (bf16[256,1408]{0,1:T(8,128)(2,1)S(1)}, bf16[256,1408]{0,1:T(8,128)(2,1)S(1)}, u32[]{:S(2)}, u32[]{:S(2)}) collective-permute-start(bf16[256,1408]{0,1:T(8,128)(2,1)S(1)} %get-tuple-element.91), channel_id=1, source_target_pairs={{0,8},{8,0},{16,24},{24,16},{1,9},{9,1},{17,25},{25,17},{2,10},{10... | collective-permute-start | bytes 2162696 | tf_op jit(solution)/shard_map/ppermute | solution.py:131
  1568.7 37.2 %collective-permute-start.84 = (bf16[256,2048]{1,0:T(8,128)(2,1)}, bf16[256,2048]{1,0:T(8,128)(2,1)}, u32[]{:S(2)}, u32[]{:S(2)}) collective-permute-start(bf16[256,2048]{1,0:T(8,128)(2,1)} %add.362), channel_id=1, source_target_pairs={{0,8},{16,24},{1,9},{17,25},{10,2},{26,18},{11,3},{27,19},{4,12},{... | collective-permute-start | bytes 3145736 | tf_op jit(solution)/shard_map/ppermute | solution.py:228
  (114 other events, 3268.0 us)
Sparse Core Ops, SparseCore 0:
  1190.4 128.2 reduce-scatter.3
  1406.9 90.5 reduce-scatter.7
  1501.0 95.6 reduce-scatter.5

commit v4 on v2

--- a/solution.py
+++ b/solution.py
@@ -40,19 +40,6 @@
     return me // 2, lax.rem(me, 2)
 
 
-def interleave(own, other):
-    n, m = lax.axis_size(F), lines()
-    line, side = line_and_side()
-    both = jnp.concatenate([own, other], axis=0)
-    size = both.shape[0] // n
-    places = [
-        lax.rem(j // 2 - line + m, m) + m * jnp.where(side == j % 2, 0, 1) for j in range(n)
-    ]
-    return jnp.concatenate(
-        [lax.dynamic_slice_in_dim(both, p * size, size, axis=0) for p in places], axis=0
-    )
-
-
 def scatter_sides(total):
     m = lines()
     _, side = line_and_side()
@@ -61,9 +48,10 @@
     return mine, side_swap(lax.dynamic_index_in_dim(parts, 1 - side, 1, keepdims=False))
 
 
-def scatter_lines(total):
+def scatter_lines(mine, sent):
     m = lines()
     line, _ = line_and_side()
+    total = (mine.astype(F32) + sent.astype(F32)).astype(BF)
 
     def part(k):
         return lax.dynamic_index_in_dim(total, lax.rem(line + k, m), 0, keepdims=False)
@@ -100,12 +88,21 @@
     return lax.ppermute(value, C, [(i, (i + 2 * k) % n) for i in range(n)])
 
 
-def spread(block):
+def spread(block, marks=()):
     out = []
     for k in range(chips()):
-        near = chip_shift(block, k) if k else block
+        near = after(chip_shift(block, k), *marks) if k else block
         out += [near, core_swap(near)]
     return out
+
+
+def spread_direct(block):
+    n = lax.axis_size(C)
+    return [
+        lax.ppermute(block, C, [(i, (i + 2 * k) % n ^ h) for i in range(n)]) if k or h else block
+        for k in range(chips())
+        for h in range(2)
+    ]
 
 
 def spread_index():
@@ -448,7 +445,7 @@
     part_up = hidden_columns(w_up)
     part_down = lax.dynamic_slice_in_dim(w_down, c * seg_len, seg_len, axis=0)
 
-    seg_all = jnp.concatenate(spread(segment_ids[0]), axis=0)
+    seg_all = jnp.concatenate(spread_direct(segment_ids[0]), axis=0)
     nb = nc
     seg_row = seg_all.reshape(nb, 1, rows)
     seg_col = seg_all.reshape(nb * rows, 1)
@@ -456,51 +453,42 @@
         [jnp.stack(spread_index()), seg_row[:, 0, 0], seg_row[:, 0, rows - 1]]
     ).astype(jnp.int32)
 
+    x_parts = spread(own)
     full_qkv = gather_all(part_qkv)
-    full_out = gather_all(part_out)
+    full_out = gather_all(after(part_out, x_parts[-2]))
     full_gate = gather_all(part_gate)
     full_up = gather_all(part_up)
-    down_lines = [line_shift(part_down, -k) for k in range(1, lax.axis_size(F) // 2)]
-
-    x_all = jnp.concatenate(spread(own), axis=0)
+    full_down = gather_all(part_down)
+
+    x_all = jnp.concatenate(x_parts, axis=0)
     scale_one = inverse_rms(x_all.astype(F32))
-    qkv = (mm(after(x_all, *down_lines[:2]), full_qkv) * scale_one).astype(BF)
+    qkv = (mm(x_all, full_qkv) * scale_one).astype(BF)
     g_parts = spread(grad_top)
-    qkv = after(qkv, *down_lines)
-    down_side = jnp.concatenate([part_down] + down_lines, axis=0)
-    down_other = side_swap(down_side)
     mixed, den = attention_forward(meta, qkv, seg_col, seg_row, heads, rows)
 
     def blocks(value):
         return [value[i * rows : (i + 1) * rows] for i in range(nb)]
 
     projected = mm(after(mixed, *g_parts), full_out).astype(BF)
-    residual = own.astype(F32) + gather_back(blocks(projected))
+    residual = own.astype(F32) + add_chips(add_cores(blocks(projected)))
 
     scale_two = inverse_rms(residual)
     unit_two = residual * scale_two
     n_all = jnp.concatenate(spread(unit_two.astype(BF)), axis=0)
-    full_down = interleave(down_side, down_other)
     g_all = jnp.concatenate(g_parts, axis=0)
-    grad_hidden = mm_nt(g_all, full_down)
-    gate = mm(after(n_all, grad_hidden), full_gate)
-    up = mm(n_all, full_up)
+    gate = mm(n_all, full_gate)
+    up = mm(after(n_all, gate), full_up)
+    grad_hidden = mm_nt(after(g_all, up), full_down)
     sigmoid = jax.nn.sigmoid(gate)
     silu = gate * sigmoid
     act = (silu * up).astype(BF)
     grad_gate = (grad_hidden * up * sigmoid * (1.0 + gate * (1.0 - sigmoid))).astype(BF)
     grad_up = (grad_hidden * silu).astype(BF)
-    projected_two = mm(act, full_down).astype(BF)
-    out_sums = add_cores(blocks(projected_two))
-    grad_gate = after(grad_gate, projected_two)
     back_two = (mm_nt(grad_gate, full_gate) + mm_nt(grad_up, full_up)).astype(BF)
-    block_out = residual + add_chips(out_sums)
-    back_sums = add_cores(blocks(after(back_two, block_out)))
-
-    total_down = mm_tn(after(act, back_two), g_all).astype(BF)
-    sum_down = scatter_all(total_down)
-    total_gate = mm_tn(n_all, after(grad_gate, total_down, *back_sums)).astype(BF)
-    mine_gate, sent_gate = scatter_sides(total_gate)
+    back_sums = add_cores(blocks(back_two))
+
+    total_gate = mm_tn(n_all, after(grad_gate, *back_sums)).astype(BF)
+    sum_gate = scatter_all(total_gate)
     total_up = mm_tn(n_all, after(grad_up, total_gate)).astype(BF)
     mine_up, sent_up = scatter_sides(total_up)
     grad_unit_two = add_chips([after(back_sums[0], total_up)] + back_sums[1:])
@@ -509,32 +497,31 @@
         grad_unit_two - unit_two * jnp.mean(grad_unit_two * unit_two, axis=-1, keepdims=True)
     )
     branch = grad_residual.astype(BF)
-    b_all = jnp.concatenate(spread(branch), axis=0)
-
-    def both(mine, sent):
-        return (mine.astype(F32) + sent.astype(F32)).astype(BF)
-
-    both_gate = both(mine_gate, after(sent_gate, branch))
-    lines_gate = scatter_lines(both_gate)
-
-    b_all = after(b_all, both_gate)
-    total_out = mm_tn(mixed, b_all).astype(BF)
-    grad_mixed = mm_nt(after(b_all, total_out), full_out)
+    total_down = mm_tn(after(act, branch), g_all).astype(BF)
+    sum_down = scatter_all(total_down)
+    projected_two = mm(after(act, total_down), full_down).astype(BF)
+    b_all = jnp.concatenate(spread(branch, [projected_two]), axis=0)
+    out_sums = add_cores(blocks(after(projected_two, b_all)))
+
+    grad_mixed = mm_nt(b_all, full_out)
+    lines_up = scatter_lines(mine_up, after(sent_up, grad_mixed))
+    total_out = mm_tn(mixed, after(b_all, lines_up[0])).astype(BF)
     grad_qkv = attention_backward(
-        meta, qkv, seg_col, seg_row, grad_mixed, mixed, den, scale_one, heads, rows
+        meta, qkv, seg_col, seg_row, after(grad_mixed, total_out, *out_sums), mixed, den, scale_one, heads, rows
     )
-    both_up = both(mine_up, after(sent_up, grad_qkv))
-    lines_up = scatter_lines(both_up)
-    grad_qkv = after(grad_qkv, sum_down, both_up, *lines_gate)
-    sum_out = scatter_all(after(total_out, grad_qkv))
-    back_one = mm_nt(grad_qkv, full_qkv).astype(BF)
+    sum_out = scatter_all(total_out)
+    block_out = residual + after(add_chips([jnp.zeros_like(out_sums[0])] + out_sums[1:]), grad_qkv) + out_sums[0]
+    back_one = mm_nt(after(grad_qkv, block_out), full_qkv).astype(BF)
     one_sums = add_cores(blocks(back_one))
-    total_qkv = mm_tn(x_all, after(grad_qkv, *one_sums)).astype(BF)
+    total_qkv = mm_tn(x_all, after(grad_qkv, *one_sums, *lines_up)).astype(BF)
+    mine_qkv, sent_qkv = scatter_sides(total_qkv)
     grad_unit_one = add_chips(one_sums)
-    sum_qkv = scatter_all(total_qkv)
-    sum_down = after(sum_down, total_qkv)
-    sum_gate = add_all([after(lines_gate[0], grad_unit_one)] + lines_gate[1:])
+    lines_qkv = scatter_lines(mine_qkv, sent_qkv)
+    sum_gate = after(sum_gate, lines_qkv[0])
     sum_up = add_all([after(lines_up[0], grad_unit_one)] + lines_up[1:])
+    sum_down = after(sum_down, grad_unit_one)
+    sum_out = after(sum_out, grad_unit_one)
+    sum_qkv = add_all(lines_qkv)
 
     unit_one = own.astype(F32) * inverse_rms(own.astype(F32))
     input_grad = grad_residual + grad_unit_one - unit_one * jnp.mean(

time: 1060 us -> 1070 us (level); the launches traced: 1040 us -> 1060 us
  waiting for transfers between devices: 331 us -> 488 us
  starting transfers between devices: 206 us -> 56.4 us
    ppermute x26 -> x24, starting transfers between devices: 126 us -> 19.2 us  [core_swap(): return lax.ppermute(value, C, [(i, i ^ 1) for i in range(n)])]
    all_gather x4 -> x5, waiting for transfers between devices: 0.03 us -> 82.8 us  [gather_all(): return lax.all_gather(block, F, axis=0, tiled=True)]
    ppermute x0 -> x3, waiting for transfers between devices: none -> 41.7 us  [spread_direct(): lax.ppermute(block, C, [(i, (i + 2 * k) % n ^ h) for i in range(n)])]
    ppermute x3 -> x2, starting transfers between devices: 23.7 us -> 0.63 us  [side_swap(): return lax.ppermute(value, F, [(j, j ^ 1) for j in range(lax.axis_size(F))])]
    ppermute x4, waiting for transfers between devices: 14.2 us -> 35.3 us  [group_pieces(): got = lax.ppermute(shard[q * rows:(q + 1) * rows], (C, F), pairs)]
    ppermute x9 -> x6, starting transfers between devices: 25.5 us -> 8.82 us  [line_shift(): lax.ppermute(value, F, [(j, (j // 2 + k) % m * 2 + j % 2) for j in range(...]
    dynamic_slice x10 -> x5, local copies, waits for them, and re-layouts: 18.1 us -> 7.37 us  [part(): lax.dynamic_index_in_dim(total, lax.rem(line + k, m), 0, keepdims=False)]
    unnamed x114 -> x107, local copies, waits for them, and re-layouts: 45.3 us -> 39.7 us
  transfers between devices with their start and end apart: 68 -> 65, of which waited for: 18 -> 26; matrix products, arithmetic and copies ran while one was open for 34% -> 35% of each run, Pallas kernels for 4% -> 4%
where the time goes in v4:
time: 1070 us; the launch traced here: 1060 us
  waiting for transfers between devices  488 us (46%)
  matrix products  236 us (22%)
  local copies, waits for them, and re-layouts  113 us (11%)
  other arithmetic  110 us (10%)
  starting transfers between devices  56.4 us (5%)
  Pallas kernels  40 us (4%)
  between operations  15.4 us (1%)
    ppermute x12, waiting for transfers between devices, chip_shift(): return lax.ppermute(value, C, [(i, (i + 2 * k) % n) for i in range(n)])  133 us
    ppermute x6, waiting for transfers between devices, line_shift(): lax.ppermute(value, F, [(j, (j // 2 + k) % m * 2 + j % 2) for j in range(...  94.4 us
    ppermute x2, waiting for transfers between devices, side_swap(): return lax.ppermute(value, F, [(j, j ^ 1) for j in range(lax.axis_size(F))])  89.9 us
    dot_general x5, matrix products, mm_nt(): lax.dot_general(a, b, (((1,), (1,)), ((), ())), preferred_element_type=F32)  82.9 us
    all_gather x5, waiting for transfers between devices, gather_all(): return lax.all_gather(block, F, axis=0, tiled=True)  82.8 us
    dot_general x5, matrix products, mm(): return jnp.dot(a, b, preferred_element_type=F32)  79.8 us
    dot_general x5, matrix products, mm_tn(): lax.dot_general(a, b, (((0,), (0,)), ((), ())), preferred_element_type=F32)  73.3 us
    ppermute x3, waiting for transfers between devices, spread_direct(): lax.ppermute(block, C, [(i, (i + 2 * k) % n ^ h) for i in range(n)])  41.7 us
  transfers between devices with their start and end apart: 65, of which 26 were waited for; matrix products, arithmetic and copies ran while one was open for 35% of the time, Pallas kernels for 4%

profile of v4, /device:TPU:17, one launch (start us, length us, event | category | flops | bytes accessed | tf_op | source)
XLA Modules:
  0.0 1058.6 jit_solution(8550877464990454211)
XLA Ops:
  17.0 35.3 %collective-permute-done.9 = bf16[64,2048]{1,0:T(8,128)(2,1)S(1)} collective-permute-done((bf16[64,2048]{1,0:T(8,128)(2,1)S(1)}, bf16[64,2048]{1,0:T(8,128)(2,1)S(1)}, u32[]{:S(2)}, u32[]{:S(2)}) %collective-permute-start.9) | collective-permute-done | bytes 262176 | tf_op jit(solution)/shard_map/ppermute | solution.py:160
  53.0 4.9 collective-permute-done.4
  58.0 4.6 copy.29
  62.5 4.6 copy.30
  74.0 6.4 collective-permute-done
  80.9 35.4 %collective-permute-done.1 = s32[512]{0:T(512)S(1)} collective-permute-done((s32[512]{0:T(512)S(1)}, s32[512]{0:T(512)S(1)}, u32[]{:S(2)}, u32[]{:S(2)}) %collective-permute-start.1) | collective-permute-done | bytes 2080 | tf_op jit(solution)/shard_map/ppermute | solution.py:102
  120.9 4.8 multiply_reduce_fusion
  125.9 14.4 %multiply_convert_fusion.3.qkv = bf16[2048,640]{1,0:T(8,128)(2,1)} fusion(bf16[2048,640]{1,0:T(8,128)(2,1)} %all-gather.6.cloned.1.call-done, f32[2048]{0:T(1024)S(1)} %add_rsqrt_fusion, bf16[512,2048]{1,0:T(8,128)(2,1)} %collective-permute-done.5, bf16[512,2048]{1,0:T(8,128)(2,1)} %collective-permute-done.4, bf16[512,2048]{1,0:T(8,128)(2,1)} %collective-permute-done.3, ...), kind=kOutput, calls=%fused_computation.30 | convolution fusion | flops 5404884992 | bytes 13639680 | tf_op jit(solution)/shard_map/dot_general | solution.py:383
  140.3 15.0 %attention_forward.1 = (bf16[2048,512]{1,0:T(8,128)(2,1)}, f32[2048,4]{1,0:T(8,128)}) custom-call(s32[12]{0:T(128)} %concatenate.40.meta, bf16[2048,640]{1,0:T(8,128)(2,1)} %multiply_convert_fusion.3.qkv, s32[2048,1]{1,0:T(8,128)} %copy.28.seg_col, s32[4,1,512]{2,1,0:T(1,128)} %copy-done.32), custom_call_target="tpu_custom_call" | custom-call | flops 4194304 | bytes 16384 | tf_op jit(solution)/shard_map/attention_forward/pallas_call | solution.py:325
  155.3 6.7 convolution_convert_fusion.2
  163.1 3.7 collective-permute-done.14
  169.8 44.9 %collective-permute-done.15 = bf16[512,2048]{1,0:T(8,128)(2,1)S(1)} collective-permute-done((bf16[512,2048]{1,0:T(8,128)(2,1)S(1)}, bf16[512,2048]{1,0:T(8,128)(2,1)S(1)}, u32[]{:S(2)}, u32[]{:S(2)}) %collective-permute-start.15) | collective-permute-done | bytes 2097184 | tf_op jit(solution)/shard_map/ppermute | solution.py:88
  224.6 42.7 %collective-permute-done.17 = bf16[512,2048]{1,0:T(8,128)(2,1)} collective-permute-done((bf16[512,2048]{1,0:T(8,128)(2,1)}, bf16[512,2048]{1,0:T(8,128)(2,1)}, u32[]{:S(2)}, u32[]{:S(2)}) %collective-permute-start.17) | collective-permute-done | bytes 2097184 | tf_op jit(solution)/shard_map/ppermute | solution.py:88
  269.2 7.2 pad_maximum_fusion.2
  277.9 6.2 pad_maximum_fusion.1
  284.0 21.5 %fusion.15 = f32[2048,1408]{1,0:T(8,128)} fusion(bf16[2048,1408]{0,1:T(8,128)(2,1)} %all-gather.10.cloned.1.call-done, bf16[512,2048]{1,0:T(8,128)(2,1)} %copy-done.23, bf16[512,2048]{1,0:T(8,128)(2,1)} %collective-permute-done.17, bf16[512,2048]{1,0:T(8,128)(2,1)S(1)} %collective-permute-done.16, bf16[512,2048]{1,0:T(8,128)(2,1)} %multiply_convert_fusion.4), kind=kOutput, calls=%fused_computation.121 | convolution fusion | flops 11844714496 | bytes 25690112 | tf_op jit(solution)/shard_map/dot_general | solution.py:383
  305.6 8.2 all-gather.12.cloned.1.call-done
  313.8 18.6 %fusion.22 = f32[2048,1408]{1,0:T(8,128)} fusion(bf16[2048,2048]{1,0:T(8,128)(2,1)} %pad_maximum_fusion.1, bf16[2048,1408]{0,1:T(8,128)(2,1)} %all-gather.12.cloned.1.call-done), kind=kOutput, calls=%fused_computation.128 | convolution fusion | flops 11811160064 | bytes 25690112 | tf_op jit(solution)/shard_map/dot_general | solution.py:383
  332.5 74.5 %all-gather.14.cloned.1.call-done = bf16[1408,2048]{1,0:T(8,128)(2,1)} async-done(((bf16[176,2048]{1,0:T(8,128)(2,1)}), bf16[1408,2048]{1,0:T(8,128)(2,1)}) %all-gather.14.cloned.1.call-update) | async-done | bytes 5767184 | tf_op jit(solution)/shard_map/all_gather | solution.py:63
  407.0 26.1 %multiply_convert_fusion = (bf16[2048,1408]{1,0:T(8,128)(2,1)}, bf16[2048,1408]{1,0:T(8,128)(2,1)}, bf16[2048,1408]{1,0:T(8,128)(2,1)}) fusion(f32[2048,1408]{1,0:T(8,128)} %fusion.15, f32[2048,1408]{1,0:T(8,128)} %fusion.22, bf16[2048,2048]{1,0:T(8,128)(2,1)} %pad_maximum_fusion.2, bf16[1408,2048]{1,0:T(8,128)(2,1)} %all-gather.14.cloned.1.call-done), kind=kOutput, calls=%fused_computation.2 | convolution fusion | flops 11854413824 | bytes 54525952 | tf_op jit(solution)/shard_map/dot_general | solution.py:391
  433.0 19.3 %fusion.23 = f32[2048,2048]{1,0:T(8,128)} fusion(bf16[2048,1408]{1,0:T(8,128)(2,1)} %get-tuple-element.39, bf16[2048,1408]{0,1:T(8,128)(2,1)} %all-gather.10.cloned.1.call-done), kind=kOutput, calls=%fused_computation.129 | convolution fusion | flops 11811160064 | bytes 28311552 | tf_op jit(solution)/shard_map/dot_general | solution.py:391
  452.4 19.6 %add_convert_fusion = bf16[2048,2048]{1,0:T(8,128)(2,1)} fusion(f32[2048,2048]{1,0:T(8,128)} %fusion.23, bf16[2048,1408]{1,0:T(8,128)(2,1)} %get-tuple-element.40, bf16[2048,1408]{0,1:T(8,128)(2,1)S(1)} %copy-done.43), kind=kOutput, calls=%fused_computation | convolution fusion | flops 11819548672 | bytes 36700160 | tf_op jit(solution)/shard_map/dot_general | solution.py:391
  476.5 3.7 collective-permute-done.19
  480.2 3.0 collective-permute-done.20
  483.2 4.7 add_convert_fusion.3
  489.1 16.7 %convolution_convert_fusion.5 = bf16[2048,1408]{1,0:T(8,128)(2,1)} fusion(bf16[2048,1408]{1,0:T(8,128)(2,1)S(1)} %bitcast.179, bf16[512,2048]{1,0:T(8,128)(2,1)S(1)} %copy-done.24, bf16[512,2048]{1,0:T(8,128)(2,1)} %collective-permute-done.17, bf16[512,2048]{1,0:T(8,128)(2,1)S(1)} %copy-done.22, bf16[512,2048]{1,0:T(8,128)(2,1)} %multiply_convert_fusion.4), kind=kOutput, calls=%fused_computation.16 | convolution fusion | flops 11847598080 | bytes 19922944 | tf_op jit(solution)/shard_map/dot_general | solution.py:387
  505.9 19.4 %convolution_convert_fusion.4 = bf16[2048,1408]{1,0:T(8,128)(2,1)} fusion(bf16[2048,1408]{1,0:T(8,128)(2,1)} %get-tuple-element.40, bf16[512,2048]{1,0:T(8,128)(2,1)} %copy-done.23, bf16[512,2048]{1,0:T(8,128)(2,1)} %collective-permute-done.17, bf16[512,2048]{1,0:T(8,128)(2,1)} %copy-done.21, bf16[512,2048]{1,0:T(8,128)(2,1)} %multiply_convert_fusion.4), kind=kOutput, calls=%fused_computation.15 | convolution fusion | flops 11847598080 | bytes 19922944 | tf_op jit(solution)/shard_map/dot_general | solution.py:387
  525.3 9.7 collective-permute-done.21
  535.8 4.0 fusion.16
  542.4 18.2 %convolution_convert_fusion.3 = bf16[1408,2048]{1,0:T(8,128)(2,1)} fusion(bf16[2048,1408]{1,0:T(8,128)(2,1)} %get-tuple-element.43, bf16[512,2048]{1,0:T(8,128)(2,1)} %collective-permute-done.8, bf16[512,2048]{1,0:T(8,128)(2,1)} %collective-permute-done.7, bf16[512,2048]{1,0:T(8,128)(2,1)} %collective-permute-done.6, bf16[512,2048]{1,0:T(8,128)(2,1)} %bitcast.156), kind=kOutput, calls=%fused_computation.14 | convolution fusion | flops 11847598080 | bytes 19922944 | tf_op jit(solution)/shard_map/dot_general | solution.py:387
  560.7 18.4 %convolution_convert_fusion.1 = bf16[2048,2048]{1,0:T(8,128)(2,1)} fusion(bf16[2048,1408]{1,0:T(8,128)(2,1)} %get-tuple-element.43, bf16[1408,2048]{1,0:T(8,128)(2,1)} %all-gather.14.cloned.1.call-done), kind=kOutput, calls=%fused_computation.12 | convolution fusion | flops 11815354368 | bytes 19922944 | tf_op jit(solution)/shard_map/dot_general | solution.py:383
  579.1 7.1 collective-permute-done.23
  588.2 3.8 dynamic-slice_bitcast_fusion
  592.6 7.5 pad_maximum_fusion.3
  600.1 4.9 fusion.18
  606.4 10.6 %fusion.24.gm = f32[2048,512]{1,0:T(8,128)} fusion(bf16[2048,2048]{1,0:T(8,128)(2,1)} %pad_maximum_fusion.3, bf16[512,2048]{1,0:T(8,128)(2,1)} %all-gather.8.cloned.1.call-done), kind=kOutput, calls=%fused_computation.130 | convolution fusion | flops 4294967296 | bytes 14680064 | tf_op jit(solution)/shard_map/dot_general | solution.py:391
  617.0 58.1 %collective-permute-done.27 = bf16[4,256,1408]{2,1,0:T(8,128)(2,1)S(1)} collective-permute-done((bf16[4,256,1408]{2,1,0:T(8,128)(2,1)}, bf16[4,256,1408]{2,1,0:T(8,128)(2,1)S(1)}, u32[]{:S(2)}, u32[]{:S(2)}) %collective-permute-start.27) | collective-permute-done | bytes 2883616 | tf_op jit(solution)/shard_map/ppermute | solution.py:35
  675.8 4.8 add_convert_fusion.2
  681.8 3.4 fusion.1
  689.1 10.0 convolution_convert_fusion.7
  699.2 25.1 %attention_backward.1 = bf16[2048,640]{1,0:T(8,128)(2,1)} custom-call(s32[12]{0:T(128)} %concatenate.40.meta, bf16[2048,640]{1,0:T(8,128)(2,1)} %multiply_convert_fusion.3.qkv, s32[2048,1]{1,0:T(8,128)} %copy.28.seg_col, s32[4,1,512]{2,1,0:T(1,128)} %copy-done.32, f32[2048,512]{1,0:T(8,128)} %fusion.24.gm, bf16[2048,512]{1,0:T(8,128)(2,1)} %get-tuple-element.35.mixed, ...), custom_call_target="tpu_custom_call" | custom-call | flops 10485760 | bytes 32768 | tf_op jit(solution)/shard_map/attention_backward/pallas_call | solution.py:353
  724.2 3.2 collective-permute-done.26
  729.6 5.3 add_add_fusion
  734.9 7.2 convolution_convert_fusion
  749.7 4.0 collective-permute-start.32
  757.4 4.6 add_convert_fusion.1
  762.0 13.2 %collective-permute-done.32 = bf16[256,1408]{0,1:T(8,128)(2,1)S(1)} collective-permute-done((bf16[256,1408]{0,1:T(8,128)(2,1)}, bf16[256,1408]{0,1:T(8,128)(2,1)S(1)}, u32[]{:S(2)}, u32[]{:S(2)}) %collective-permute-start.32) | collective-permute-done | bytes 720928 | tf_op jit(solution)/shard_map/ppermute | solution.py:31
  775.2 38.3 %collective-permute-done.33 = bf16[256,1408]{0,1:T(8,128)(2,1)} collective-permute-done((bf16[256,1408]{0,1:T(8,128)(2,1)}, bf16[256,1408]{0,1:T(8,128)(2,1)}, u32[]{:S(2)}, u32[]{:S(2)}) %collective-permute-start.33) | collective-permute-done | bytes 720928 | tf_op jit(solution)/shard_map/ppermute | solution.py:31
  813.5 19.3 %collective-permute-done.34 = bf16[256,1408]{0,1:T(8,128)(2,1)} collective-permute-done((bf16[256,1408]{0,1:T(8,128)(2,1)}, bf16[256,1408]{0,1:T(8,128)(2,1)}, u32[]{:S(2)}, u32[]{:S(2)}) %collective-permute-start.34) | collective-permute-done | bytes 720928 | tf_op jit(solution)/shard_map/ppermute | solution.py:31
  832.9 9.0 convolution_convert_fusion.6
  843.0 31.9 %collective-permute-done.35 = bf16[4,256,640]{2,1,0:T(8,128)(2,1)S(1)} collective-permute-done((bf16[4,256,640]{2,1,0:T(8,128)(2,1)S(1)}, bf16[4,256,640]{2,1,0:T(8,128)(2,1)S(1)}, u32[]{:S(2)}, u32[]{:S(2)}) %collective-permute-start.35) | collective-permute-done | bytes 1310752 | tf_op jit(solution)/shard_map/ppermute | solution.py:35
  882.9 3.5 collective-permute-done.36
  886.5 13.7 %collective-permute-done.37 = bf16[256,640]{1,0:T(8,128)(2,1)S(1)} collective-permute-done((bf16[256,640]{1,0:T(8,128)(2,1)S(1)}, bf16[256,640]{1,0:T(8,128)(2,1)S(1)}, u32[]{:S(2)}, u32[]{:S(2)}) %collective-permute-start.37) | collective-permute-done | bytes 327712 | tf_op jit(solution)/shard_map/ppermute | solution.py:31
  900.9 6.3 collective-permute-done.38
  922.0 6.1 fusion.6
  928.1 5.3 collective-permute-start.42
  933.4 6.4 fusion.8
  953.6 3.5 broadcast_multiply_fusion
  977.5 6.2 collective-permute-done.55
  985.3 13.8 %collective-permute-done.52 = bf16[256,1408]{0,1:T(8,128)(2,1)} collective-permute-done((bf16[256,1408]{0,1:T(8,128)(2,1)}, bf16[256,1408]{0,1:T(8,128)(2,1)}, u32[]{:S(2)}, u32[]{:S(2)}) %collective-permute-start.52) | collective-permute-done | bytes 720928 | tf_op jit(solution)/shard_map/ppermute | solution.py:88
  1022.2 5.9 bitcast_multiply_fusion
  1028.0 6.2 copy.56
  1034.3 6.2 copy.57
  1043.1 5.3 bitcast_convert_fusion
  (294 shorter events, 161.0 us)
Async XLA Ops:
  7.2 118.7 %all-gather.6.cloned.1.call-start = ((), (), s32[]{:S(2)}) async-start(), calls=%async_computation.3 | async-start | bytes 2949120 | tf_op jit(solution)/shard_map/all_gather | solution.py:63
  10.9 144.3 %all-gather.8.cloned.1.call-start = ((), (), s32[]{:S(2)}) async-start(), calls=%async_computation.4 | async-start | bytes 2359296 | tf_op jit(solution)/shard_map/all_gather | solution.py:63
  11.0 46.9 %collective-permute-start.4 = (bf16[512,2048]{1,0:T(8,128)(2,1)}, bf16[512,2048]{1,0:T(8,128)(2,1)}, u32[]{:S(2)}, u32[]{:S(2)}) collective-permute-start(bf16[512,2048]{1,0:T(8,128)(2,1)} %bitcast.144), channel_id=1, source_target_pairs={{0,16},{8,24},{16,0},{24,8},{1,17},{9,25},{17,1},{25,9},{2,18},{10... | collective-permute-start | bytes 6291464 | tf_op jit(solution)/shard_map/ppermute | solution.py:88
  13.6 3.4 collective-permute-start.10
  14.2 2.7 collective-permute-start.11
  15.6 36.6 %collective-permute-start.9 = (bf16[64,2048]{1,0:T(8,128)(2,1)S(1)}, bf16[64,2048]{1,0:T(8,128)(2,1)S(1)}, u32[]{:S(2)}, u32[]{:S(2)}) collective-permute-start(bf16[64,2048]{1,0:T(8,128)(2,1)S(1)} %get-tuple-element.114), channel_id=1, source_target_pairs={{0,0},{1,4},{10,8},{11,12},{20,16},{21,20},{30,24},{31,28}} | collective-permute-start | bytes 786440 | tf_op jit(solution)/shard_map/ppermute | solution.py:160
  57.9 226.1 %all-gather.10.cloned.1.call-start = ((), (), s32[]{:S(2)}) async-start(), calls=%async_computation.5 | async-start | bytes 6488064 | tf_op jit(solution)/shard_map/all_gather | solution.py:63
  70.1 243.7 %all-gather.12.cloned.1.call-start = ((), (), s32[]{:S(2)}) async-start(), calls=%async_computation.6 | async-start | bytes 6488064 | tf_op jit(solution)/shard_map/all_gather | solution.py:63
  70.1 50.8 %collective-permute-start.7 = (bf16[512,2048]{1,0:T(8,128)(2,1)}, bf16[512,2048]{1,0:T(8,128)(2,1)}, u32[]{:S(2)}, u32[]{:S(2)}) collective-permute-start(bf16[512,2048]{1,0:T(8,128)(2,1)} %bitcast.153), channel_id=1, source_target_pairs={{0,16},{8,24},{16,0},{24,8},{1,17},{9,25},{17,1},{25,9},{2,18},{10... | collective-permute-start | bytes 6291464 | tf_op jit(solution)/shard_map/ppermute | solution.py:88
  71.4 49.5 %collective-permute-start.3 = (bf16[512,2048]{1,0:T(8,128)(2,1)}, bf16[512,2048]{1,0:T(8,128)(2,1)}, u32[]{:S(2)}, u32[]{:S(2)}) collective-permute-start(bf16[512,2048]{1,0:T(8,128)(2,1)} %bitcast.145), channel_id=1, source_target_pairs={{0,8},{8,0},{16,24},{24,16},{1,9},{9,1},{17,25},{25,17},{2,10},{10... | collective-permute-start | bytes 6291464 | tf_op jit(solution)/shard_map/ppermute | solution.py:83
  73.2 47.8 %collective-permute-start.5 = (bf16[512,2048]{1,0:T(8,128)(2,1)}, bf16[512,2048]{1,0:T(8,128)(2,1)}, u32[]{:S(2)}, u32[]{:S(2)}) collective-permute-start(bf16[512,2048]{1,0:T(8,128)(2,1)} %collective-permute-done.4), channel_id=1, source_target_pairs={{0,8},{8,0},{16,24},{24,16},{1,9},{9,1},{17,25},{25,17},{2,10},{10... | collective-permute-start | bytes 6291464 | tf_op jit(solution)/shard_map/ppermute | solution.py:83
  73.2 7.1 collective-permute-start
  73.7 42.6 %collective-permute-start.1 = (s32[512]{0:T(512)S(1)}, s32[512]{0:T(512)S(1)}, u32[]{:S(2)}, u32[]{:S(2)}) collective-permute-start(s32[512]{0:T(512)S(1)} %bitcast.171), channel_id=1, source_target_pairs={{0,16},{8,24},{16,0},{24,8},{1,17},{9,25},{17,1},{25,9},{2,18},{10... | collective-permute-start | bytes 6152 | tf_op jit(solution)/shard_map/ppermute | solution.py:102
  80.3 38.3 %collective-permute-start.2 = (s32[512]{0:T(512)S(1)}, s32[512]{0:T(512)S(1)}, u32[]{:S(2)}, u32[]{:S(2)}) collective-permute-start(s32[512]{0:T(512)S(1)} %bitcast.172), channel_id=1, source_target_pairs={{0,24},{8,16},{16,8},{24,0},{1,25},{9,17},{17,9},{25,1},{2,26},{10... | collective-permute-start | bytes 6152 | tf_op jit(solution)/shard_map/ppermute | solution.py:102
  80.9 326.1 %all-gather.14.cloned.1.call-start = ((), (), s32[]{:S(2)}) async-start(), calls=%async_computation.7 | async-start | bytes 6488064 | tf_op jit(solution)/shard_map/all_gather | solution.py:63
  116.3 39.0 %collective-permute-start.6 = (bf16[512,2048]{1,0:T(8,128)(2,1)}, bf16[512,2048]{1,0:T(8,128)(2,1)}, u32[]{:S(2)}, u32[]{:S(2)}) collective-permute-start(bf16[512,2048]{1,0:T(8,128)(2,1)} %bitcast.154), channel_id=1, source_target_pairs={{0,8},{8,0},{16,24},{24,16},{1,9},{9,1},{17,25},{25,17},{2,10},{10... | collective-permute-start | bytes 6291464 | tf_op jit(solution)/shard_map/ppermute | solution.py:83
  120.9 34.3 %collective-permute-start.8 = (bf16[512,2048]{1,0:T(8,128)(2,1)}, bf16[512,2048]{1,0:T(8,128)(2,1)}, u32[]{:S(2)}, u32[]{:S(2)}) collective-permute-start(bf16[512,2048]{1,0:T(8,128)(2,1)} %collective-permute-done.7), channel_id=1, source_target_pairs={{0,8},{8,0},{16,24},{24,16},{1,9},{9,1},{17,25},{25,17},{2,10},{10... | collective-permute-start | bytes 6291464 | tf_op jit(solution)/shard_map/ppermute | solution.py:83
  162.5 4.3 collective-permute-start.14
  163.1 6.8 collective-permute-start.13
  167.8 47.0 %collective-permute-start.15 = (bf16[512,2048]{1,0:T(8,128)(2,1)S(1)}, bf16[512,2048]{1,0:T(8,128)(2,1)S(1)}, u32[]{:S(2)}, u32[]{:S(2)}) collective-permute-start(bf16[512,2048]{1,0:T(8,128)(2,1)S(1)} %add_convert_fusion.4), channel_id=1, source_target_pairs={{0,16},{8,24},{16,0},{24,8},{1,17},{9,25},{17,1},{25,9},{2,18},{10... | collective-permute-start | bytes 6291464 | tf_op jit(solution)/shard_map/ppermute | solution.py:88
  220.9 46.4 %collective-permute-start.17 = (bf16[512,2048]{1,0:T(8,128)(2,1)}, bf16[512,2048]{1,0:T(8,128)(2,1)}, u32[]{:S(2)}, u32[]{:S(2)}) collective-permute-start(bf16[512,2048]{1,0:T(8,128)(2,1)} %multiply_convert_fusion.4), channel_id=1, source_target_pairs={{0,16},{8,24},{16,0},{24,8},{1,17},{9,25},{17,1},{25,9},{2,18},{10... | collective-permute-start | bytes 6291464 | tf_op jit(solution)/shard_map/ppermute | solution.py:88
  223.0 687.1 %reduce-scatter.6.cloned.1.call-start = ((), (), s32[]{:S(2)}) async-start(), calls=%async_computation.9 | async-start | bytes 6488064 | tf_op jit(solution)/shard_map/reduce_scatter | solution.py:67
  223.1 53.4 %collective-permute-start.16 = (bf16[512,2048]{1,0:T(8,128)(2,1)}, bf16[512,2048]{1,0:T(8,128)(2,1)S(1)}, u32[]{:S(2)}, u32[]{:S(2)}) collective-permute-start(bf16[512,2048]{1,0:T(8,128)(2,1)} %multiply_convert_fusion.4), channel_id=1, source_target_pairs={{0,8},{8,0},{16,24},{24,16},{1,9},{9,1},{17,25},{25,17},{2,10},{10... | collective-permute-start | bytes 6291464 | tf_op jit(solution)/shard_map/ppermute | solution.py:83
  267.3 9.2 collective-permute-start.18
  474.9 5.2 collective-permute-start.19
  476.4 6.8 collective-permute-start.20
  487.9 47.1 %collective-permute-start.21 = (bf16[512,2048]{1,0:T(8,128)(2,1)}, bf16[512,2048]{1,0:T(8,128)(2,1)S(1)}, u32[]{:S(2)}, u32[]{:S(2)}) collective-permute-start(bf16[512,2048]{1,0:T(8,128)(2,1)} %get-tuple-element.89), channel_id=1, source_target_pairs={{0,16},{8,24},{16,0},{24,8},{1,17},{9,25},{17,1},{25,9},{2,18},{10... | collective-permute-start | bytes 6291464 | tf_op jit(solution)/shard_map/ppermute | solution.py:88
  505.8 422.2 %reduce-scatter.8.cloned.1.call-start = ((), (), s32[]{:S(2)}) async-start(), calls=%async_computation.10 | async-start | bytes 6488064 | tf_op jit(solution)/shard_map/reduce_scatter | solution.py:67
  539.8 46.4 %collective-permute-start.23 = (bf16[512,2048]{1,0:T(8,128)(2,1)}, bf16[512,2048]{1,0:T(8,128)(2,1)}, u32[]{:S(2)}, u32[]{:S(2)}) collective-permute-start(bf16[512,2048]{1,0:T(8,128)(2,1)} %get-tuple-element.78), channel_id=1, source_target_pairs={{0,16},{8,24},{16,0},{24,8},{1,17},{9,25},{17,1},{25,9},{2,18},{10... | collective-permute-start | bytes 6291464 | tf_op jit(solution)/shard_map/ppermute | solution.py:88
  541.0 51.6 %collective-permute-start.22 = (bf16[512,2048]{1,0:T(8,128)(2,1)}, bf16[512,2048]{1,0:T(8,128)(2,1)}, u32[]{:S(2)}, u32[]{:S(2)}) collective-permute-start(bf16[512,2048]{1,0:T(8,128)(2,1)} %get-tuple-element.78), channel_id=1, source_target_pairs={{0,8},{8,0},{16,24},{24,16},{1,9},{9,1},{17,25},{25,17},{2,10},{10... | collective-permute-start | bytes 6291464 | tf_op jit(solution)/shard_map/ppermute | solution.py:83
  586.2 6.4 collective-permute-start.24
  592.0 83.1 %collective-permute-start.27 = (bf16[4,256,1408]{2,1,0:T(8,128)(2,1)}, bf16[4,256,1408]{2,1,0:T(8,128)(2,1)S(1)}, u32[]{:S(2)}, u32[]{:S(2)}) collective-permute-start(bf16[4,256,1408]{2,1,0:T(8,128)(2,1)} %dynamic-slice_bitcast_fusion), channel_id=1, source_target_pairs={{0,1},{1,0},{2,3},{3,2},{4,5},{5,4},{6,7},{7,6},{8,9},{9,8},{10,11... | collective-permute-start | bytes 8650760 | tf_op jit(solution)/shard_map/ppermute | solution.py:35
  592.6 335.5 %reduce-scatter.4.cloned.1.call-start = ((), (), s32[]{:S(2)}) async-start(), calls=%async_computation.8 | async-start | bytes 2359296 | tf_op jit(solution)/shard_map/reduce_scatter | solution.py:67
  605.0 70.7 %collective-permute-start.25 = (bf16[512,2048]{1,0:T(8,128)(2,1)}, bf16[512,2048]{1,0:T(8,128)(2,1)}, u32[]{:S(2)}, u32[]{:S(2)}) collective-permute-start(bf16[512,2048]{1,0:T(8,128)(2,1)} %get-tuple-element.88), channel_id=1, source_target_pairs={{0,8},{8,0},{16,24},{24,16},{1,9},{9,1},{17,25},{25,17},{2,10},{10... | collective-permute-start | bytes 6291464 | tf_op jit(solution)/shard_map/ppermute | solution.py:83
  675.1 54.5 %collective-permute-start.28 = (bf16[512,2048]{1,0:T(8,128)(2,1)}, bf16[512,2048]{1,0:T(8,128)(2,1)}, u32[]{:S(2)}, u32[]{:S(2)}) collective-permute-start(bf16[512,2048]{1,0:T(8,128)(2,1)} %get-tuple-element.87), channel_id=1, source_target_pairs={{0,8},{8,0},{16,24},{24,16},{1,9},{9,1},{17,25},{25,17},{2,10},{10... | collective-permute-start | bytes 6291464 | tf_op jit(solution)/shard_map/ppermute | solution.py:83
  680.6 46.8 %collective-permute-start.26 = (bf16[512,2048]{1,0:T(8,128)(2,1)}, bf16[512,2048]{1,0:T(8,128)(2,1)}, u32[]{:S(2)}, u32[]{:S(2)}) collective-permute-start(bf16[512,2048]{1,0:T(8,128)(2,1)} %add_convert_fusion.2), channel_id=1, source_target_pairs={{0,16},{8,24},{16,0},{24,8},{1,17},{9,25},{17,1},{25,9},{2,18},{10... | collective-permute-start | bytes 6291464 | tf_op jit(solution)/shard_map/ppermute | solution.py:88
  747.0 10.5 collective-permute-start.30
  749.7 25.5 %collective-permute-start.32 = (bf16[256,1408]{0,1:T(8,128)(2,1)}, bf16[256,1408]{0,1:T(8,128)(2,1)S(1)}, u32[]{:S(2)}, u32[]{:S(2)}) collective-permute-start(bf16[256,1408]{0,1:T(8,128)(2,1)} %bitcast.164), channel_id=1, source_target_pairs={{0,2},{1,3},{2,4},{3,5},{4,6},{5,7},{6,0},{7,1},{8,10},{9,11},{10,... | collective-permute-start | bytes 2162696 | tf_op jit(solution)/shard_map/ppermute | solution.py:31
  754.8 58.7 %collective-permute-start.33 = (bf16[256,1408]{0,1:T(8,128)(2,1)}, bf16[256,1408]{0,1:T(8,128)(2,1)}, u32[]{:S(2)}, u32[]{:S(2)}) collective-permute-start(bf16[256,1408]{0,1:T(8,128)(2,1)} %bitcast.165), channel_id=1, source_target_pairs={{0,4},{1,5},{2,6},{3,7},{4,0},{5,1},{6,2},{7,3},{8,12},{9,13},{10,... | collective-permute-start | bytes 2162696 | tf_op jit(solution)/shard_map/ppermute | solution.py:31
  756.1 76.8 %collective-permute-start.34 = (bf16[256,1408]{0,1:T(8,128)(2,1)}, bf16[256,1408]{0,1:T(8,128)(2,1)}, u32[]{:S(2)}, u32[]{:S(2)}) collective-permute-start(bf16[256,1408]{0,1:T(8,128)(2,1)} %bitcast.166), channel_id=1, source_target_pairs={{0,6},{1,7},{2,0},{3,1},{4,2},{5,3},{6,4},{7,5},{8,14},{9,15},{10,... | collective-permute-start | bytes 2162696 | tf_op jit(solution)/shard_map/ppermute | solution.py:31
  842.1 32.8 %collective-permute-start.35 = (bf16[4,256,640]{2,1,0:T(8,128)(2,1)S(1)}, bf16[4,256,640]{2,1,0:T(8,128)(2,1)S(1)}, u32[]{:S(2)}, u32[]{:S(2)}) collective-permute-start(bf16[4,256,640]{2,1,0:T(8,128)(2,1)S(1)} %dynamic-slice_bitcast_fusion.1), channel_id=1, source_target_pairs={{0,1},{1,0},{2,3},{3,2},{4,5},{5,4},{6,7},{7,6},{8,9},{9,8},{10,11... | collective-permute-start | bytes 3932168 | tf_op jit(solution)/shard_map/ppermute | solution.py:35
  842.1 79.8 %collective-permute-start.29 = (bf16[512,2048]{1,0:T(8,128)(2,1)}, bf16[512,2048]{1,0:T(8,128)(2,1)}, u32[]{:S(2)}, u32[]{:S(2)}) collective-permute-start(bf16[512,2048]{1,0:T(8,128)(2,1)} %get-tuple-element.85), channel_id=1, source_target_pairs={{0,8},{8,0},{16,24},{24,16},{1,9},{9,1},{17,25},{25,17},{2,10},{10... | collective-permute-start | bytes 6291464 | tf_op jit(solution)/shard_map/ppermute | solution.py:83
  842.7 79.2 %collective-permute-start.31 = (bf16[512,2048]{1,0:T(8,128)(2,1)}, bf16[512,2048]{1,0:T(8,128)(2,1)}, u32[]{:S(2)}, u32[]{:S(2)}) collective-permute-start(bf16[512,2048]{1,0:T(8,128)(2,1)} %add_convert_fusion.1), channel_id=1, source_target_pairs={{0,16},{8,24},{16,0},{24,8},{1,17},{9,25},{17,1},{25,9},{2,18},{10... | collective-permute-start | bytes 6291464 | tf_op jit(solution)/shard_map/ppermute | solution.py:88
  877.1 9.4 collective-permute-start.36
  878.7 21.4 %collective-permute-start.37 = (bf16[256,640]{1,0:T(8,128)(2,1)S(1)}, bf16[256,640]{1,0:T(8,128)(2,1)S(1)}, u32[]{:S(2)}, u32[]{:S(2)}) collective-permute-start(bf16[256,640]{1,0:T(8,128)(2,1)S(1)} %get-tuple-element.112), channel_id=1, source_target_pairs={{0,4},{1,5},{2,6},{3,7},{4,0},{5,1},{6,2},{7,3},{8,12},{9,13},{10,... | collective-permute-start | bytes 983048 | tf_op jit(solution)/shard_map/ppermute | solution.py:31
  880.5 26.7 %collective-permute-start.38 = (bf16[256,640]{1,0:T(8,128)(2,1)S(1)}, bf16[256,640]{1,0:T(8,128)(2,1)}, u32[]{:S(2)}, u32[]{:S(2)}) collective-permute-start(bf16[256,640]{1,0:T(8,128)(2,1)S(1)} %get-tuple-element.111), channel_id=1, source_target_pairs={{0,6},{1,7},{2,0},{3,1},{4,2},{5,3},{6,4},{7,5},{8,14},{9,15},{10,... | collective-permute-start | bytes 983048 | tf_op jit(solution)/shard_map/ppermute | solution.py:31
  908.5 8.1 collective-permute-start.39
  909.1 9.3 collective-permute-start.40
  910.2 55.0 %collective-permute-start.48 = (bf16[256,1408]{1,0:T(8,128)(2,1)}, bf16[256,1408]{1,0:T(8,128)(2,1)}, u32[]{:S(2)}, u32[]{:S(2)}) collective-permute-start(bf16[256,1408]{1,0:T(8,128)(2,1)} %reduce-scatter.6.cloned.1.call-done), channel_id=1, source_target_pairs={{0,8},{8,0},{16,24},{24,16},{1,9},{9,1},{17,25},{25,17},{2,10},{10... | collective-permute-start | bytes 2162696 | tf_op jit(solution)/shard_map/ppermute | solution.py:83
  916.6 51.8 %collective-permute-start.49 = (bf16[256,1408]{1,0:T(8,128)(2,1)}, bf16[256,1408]{1,0:T(8,128)(2,1)}, u32[]{:S(2)}, u32[]{:S(2)}) collective-permute-start(bf16[256,1408]{1,0:T(8,128)(2,1)} %reduce-scatter.6.cloned.1.call-done), channel_id=1, source_target_pairs={{0,16},{8,24},{16,0},{24,8},{1,17},{9,25},{17,1},{25,9},{2,18},{10... | collective-permute-start | bytes 2162696 | tf_op jit(solution)/shard_map/ppermute | solution.py:88
  918.4 27.1 %collective-permute-start.41 = (bf16[256,640]{1,0:T(8,128)(2,1)}, bf16[256,640]{1,0:T(8,128)(2,1)S(1)}, u32[]{:S(2)}, u32[]{:S(2)}) collective-permute-start(bf16[256,640]{1,0:T(8,128)(2,1)} %collective-permute-done.40), channel_id=1, source_target_pairs={{0,8},{8,0},{16,24},{24,16},{1,9},{9,1},{17,25},{25,17},{2,10},{10... | collective-permute-start | bytes 983048 | tf_op jit(solution)/shard_map/ppermute | solution.py:83
  928.1 73.9 %collective-permute-start.54 = (bf16[176,2048]{1,0:T(8,128)(2,1)}, bf16[176,2048]{1,0:T(8,128)(2,1)}, u32[]{:S(2)}, u32[]{:S(2)}) collective-permute-start(bf16[176,2048]{1,0:T(8,128)(2,1)} %reduce-scatter.8.cloned.1.call-done), channel_id=1, source_target_pairs={{0,8},{8,0},{16,24},{24,16},{1,9},{9,1},{17,25},{25,17},{2,10},{10... | collective-permute-start | bytes 2162696 | tf_op jit(solution)/shard_map/ppermute | solution.py:83
  928.1 32.4 %collective-permute-start.42 = (bf16[64,2048]{1,0:T(8,128)(2,1)}, bf16[64,2048]{1,0:T(8,128)(2,1)}, u32[]{:S(2)}, u32[]{:S(2)}) collective-permute-start(bf16[64,2048]{1,0:T(8,128)(2,1)} %reduce-scatter.4.cloned.1.call-done), channel_id=1, source_target_pairs={{0,0},{4,1},{8,10},{12,11},{16,20},{20,21},{24,30},{28,31}} | collective-permute-start | bytes 786440 | tf_op jit(solution)/shard_map/ppermute | solution.py:169
  945.4 17.4 %collective-permute-start.43 = (bf16[64,2048]{1,0:T(8,128)(2,1)}, bf16[64,2048]{1,0:T(8,128)(2,1)}, u32[]{:S(2)}, u32[]{:S(2)}) collective-permute-start(bf16[64,2048]{1,0:T(8,128)(2,1)} %reduce-scatter.4.cloned.1.call-done), channel_id=1, source_target_pairs={{1,0},{5,1},{9,10},{13,11},{17,20},{21,21},{25,30},{29,31}} | collective-permute-start | bytes 786440 | tf_op jit(solution)/shard_map/ppermute | solution.py:169
  960.5 10.3 collective-permute-start.44
  962.8 9.1 collective-permute-start.45
  965.2 18.5 %collective-permute-start.55 = (bf16[176,2048]{1,0:T(8,128)(2,1)}, bf16[176,2048]{1,0:T(8,128)(2,1)}, u32[]{:S(2)}, u32[]{:S(2)}) collective-permute-start(bf16[176,2048]{1,0:T(8,128)(2,1)} %reduce-scatter.8.cloned.1.call-done), channel_id=1, source_target_pairs={{0,16},{8,24},{16,0},{24,8},{1,17},{9,25},{17,1},{25,9},{2,18},{10... | collective-permute-start | bytes 2162696 | tf_op jit(solution)/shard_map/ppermute | solution.py:88
  968.5 30.7 %collective-permute-start.51 = (bf16[256,1408]{0,1:T(8,128)(2,1)}, bf16[256,1408]{0,1:T(8,128)(2,1)}, u32[]{:S(2)}, u32[]{:S(2)}) collective-permute-start(bf16[256,1408]{0,1:T(8,128)(2,1)} %get-tuple-element.73), channel_id=1, source_target_pairs={{0,8},{8,0},{16,24},{24,16},{1,9},{9,1},{17,25},{25,17},{2,10},{10... | collective-permute-start | bytes 2162696 | tf_op jit(solution)/shard_map/ppermute | solution.py:83
  970.8 28.4 %collective-permute-start.52 = (bf16[256,1408]{0,1:T(8,128)(2,1)}, bf16[256,1408]{0,1:T(8,128)(2,1)}, u32[]{:S(2)}, u32[]{:S(2)}) collective-permute-start(bf16[256,1408]{0,1:T(8,128)(2,1)} %get-tuple-element.73), channel_id=1, source_target_pairs={{0,16},{8,24},{16,0},{24,8},{1,17},{9,25},{17,1},{25,9},{2,18},{10... | collective-permute-start | bytes 2162696 | tf_op jit(solution)/shard_map/ppermute | solution.py:88
  971.9 34.1 %collective-permute-start.50 = (bf16[256,1408]{1,0:T(8,128)(2,1)}, bf16[256,1408]{1,0:T(8,128)(2,1)}, u32[]{:S(2)}, u32[]{:S(2)}) collective-permute-start(bf16[256,1408]{1,0:T(8,128)(2,1)} %collective-permute-done.49), channel_id=1, source_target_pairs={{0,8},{8,0},{16,24},{24,16},{1,9},{9,1},{17,25},{25,17},{2,10},{10... | collective-permute-start | bytes 2162696 | tf_op jit(solution)/shard_map/ppermute | solution.py:83
  983.7 29.7 %collective-permute-start.46 = (bf16[256,2048]{1,0:T(8,128)(2,1)}, bf16[256,2048]{1,0:T(8,128)(2,1)}, u32[]{:S(2)}, u32[]{:S(2)}) collective-permute-start(bf16[256,2048]{1,0:T(8,128)(2,1)} %constant_dynamic-update-slice_fusion), channel_id=1, source_target_pairs={{0,16},{1,17},{10,26},{11,27},{20,4},{21,5},{30,14},{31,15}} | collective-permute-start | bytes 3145736 | tf_op jit(solution)/shard_map/ppermute | solution.py:173
  999.1 41.9 %collective-permute-start.56 = (bf16[176,2048]{1,0:T(8,128)(2,1)}, bf16[176,2048]{1,0:T(8,128)(2,1)}, u32[]{:S(2)}, u32[]{:S(2)}) collective-permute-start(bf16[176,2048]{1,0:T(8,128)(2,1)} %collective-permute-done.55), channel_id=1, source_target_pairs={{0,8},{8,0},{16,24},{24,16},{1,9},{9,1},{17,25},{25,17},{2,10},{10... | collective-permute-start | bytes 2162696 | tf_op jit(solution)/shard_map/ppermute | solution.py:83
  999.1 18.5 %collective-permute-start.53 = (bf16[256,1408]{0,1:T(8,128)(2,1)}, bf16[256,1408]{0,1:T(8,128)(2,1)}, u32[]{:S(2)}, u32[]{:S(2)}) collective-permute-start(bf16[256,1408]{0,1:T(8,128)(2,1)} %collective-permute-done.52), channel_id=1, source_target_pairs={{0,8},{8,0},{16,24},{24,16},{1,9},{9,1},{17,25},{25,17},{2,10},{10... | collective-permute-start | bytes 2162696 | tf_op jit(solution)/shard_map/ppermute | solution.py:83
  1016.3 32.0 %collective-permute-start.47 = (bf16[256,2048]{1,0:T(8,128)(2,1)}, bf16[256,2048]{1,0:T(8,128)(2,1)}, u32[]{:S(2)}, u32[]{:S(2)}) collective-permute-start(bf16[256,2048]{1,0:T(8,128)(2,1)} %add.293), channel_id=1, source_target_pairs={{0,8},{16,24},{1,9},{17,25},{10,2},{26,18},{11,3},{27,19},{4,12},{... | collective-permute-start | bytes 3145736 | tf_op jit(solution)/shard_map/ppermute | solution.py:180
  (49 other events, 1012.0 us)
Sparse Core Ops, SparseCore 0:
  11.1 64.5 all-gather.5
  78.4 47.6 all-gather.7
  128.7 91.2 all-gather.9
  222.5 91.2 all-gather.11
  316.4 90.4 all-gather.13
  505.9 106.9 reduce-scatter.5
  617.2 114.4 reduce-scatter.7
  757.5 113.8 reduce-scatter.3

commit v5 on v4

--- a/solution.py
+++ b/solution.py
@@ -26,9 +26,9 @@
     return lax.axis_size(F) // 2
 
 
-def line_shift(value, k):
-    n, m = lax.axis_size(F), lines()
-    return lax.ppermute(value, F, [(j, (j // 2 + k) % m * 2 + j % 2) for j in range(n)])
+def line_groups():
+    m = lines()
+    return [[2 * line + side for line in range(m)] for side in range(2)]
 
 
 def side_swap(value):
@@ -48,30 +48,43 @@
     return mine, side_swap(lax.dynamic_index_in_dim(parts, 1 - side, 1, keepdims=False))
 
 
-def scatter_lines(mine, sent):
-    m = lines()
-    line, _ = line_and_side()
-    total = (mine.astype(F32) + sent.astype(F32)).astype(BF)
-
-    def part(k):
-        return lax.dynamic_index_in_dim(total, lax.rem(line + k, m), 0, keepdims=False)
-
-    return [part(0)] + [line_shift(part(k), k) for k in range(1, m)]
-
-
-def gather_all(block):
-    return lax.all_gather(block, F, axis=0, tiled=True)
-
-
-def scatter_all(total):
-    return lax.psum_scatter(total, F, scatter_dimension=0, tiled=True)
-
-
-def add_all(parts):
-    total = parts[0].astype(F32)
-    for part in parts[1:]:
-        total = total + part.astype(F32)
-    return total
+def add_sides(mine, sent):
+    both = (mine.astype(F32) + sent.astype(F32)).astype(BF)
+    return both.reshape(-1, both.shape[-1])
+
+
+def scatter_lines(total):
+    return lax.psum_scatter(total, F, scatter_dimension=0, axis_index_groups=line_groups(), tiled=True)
+
+
+def gather_lines(block):
+    return lax.all_gather(block, F, axis=0, axis_index_groups=line_groups())
+
+
+def assemble_kernel(own, other, out, sems, *, m):
+    side = lax.rem(lax.axis_index(F), 2)
+    copies = []
+    for k in range(m):
+        copies.append(pltpu.make_async_copy(own.at[k], out.at[2 * k + side], sems.at[k]))
+        copies.append(pltpu.make_async_copy(other.at[k], out.at[2 * k + 1 - side], sems.at[m + k]))
+    for copy in copies:
+        copy.start()
+    for copy in copies:
+        copy.wait()
+
+
+def assemble(own, other):
+    m, rows, width = own.shape
+    out = pl.pallas_call(
+        functools.partial(assemble_kernel, m=m),
+        out_shape=jax.ShapeDtypeStruct((2 * m, rows, width), own.dtype),
+        in_specs=[pl.BlockSpec(memory_space=pl.ANY)] * 2,
+        out_specs=pl.BlockSpec(memory_space=pltpu.VMEM),
+        scratch_shapes=[pltpu.SemaphoreType.DMA((2 * m,))],
+        cost_estimate=pl.CostEstimate(flops=0, transcendentals=0, bytes_accessed=1024),
+        name="assemble",
+    )(own, other)
+    return out.reshape(2 * m * rows, width)
 
 
 def chips():
@@ -379,6 +392,73 @@
     )(meta, qkv, seg_col, seg_row, gm, mixed, den, scale)
 
 
+def of_context(parts, c, nc):
+    me = lax.axis_index(C)
+    out = parts[0][...]
+    for i in range(1, nc):
+        near = lax.rem(me - 2 * (i // 2) + nc, nc)
+        index = near if i % 2 == 0 else near + 1 - 2 * lax.rem(near, 2)
+        out = jnp.where(index == c, parts[i][...], out)
+    return out
+
+
+def columns_kernel(*refs, nc, seg, groups):
+    parts, weight, gain, out, along = refs[:nc], refs[nc], refs[nc + 1], refs[nc + 2], refs[nc + 3]
+    total = jnp.zeros(along.shape, F32)
+    for c in range(nc):
+        part = of_context(parts, c, nc)
+        for j in range(groups):
+            place = slice((j * nc + c) * seg, (j * nc + c + 1) * seg)
+            value = part[:, j * seg : (j + 1) * seg].astype(F32)
+            total += jnp.sum(value * weight[:, place].astype(F32), axis=1, keepdims=True)
+            out[:, place] = value * gain[...]
+    along[...] = total
+
+
+def finish_columns(parts, weight, gain, seg, groups):
+    nc = len(parts)
+    rows, width = weight.shape
+    tile = next(t for t in (64, 32, 16, 8) if rows % t == 0)
+
+    def spec(size):
+        return pl.BlockSpec((tile, size), lambda i: (i, 0))
+
+    return pl.pallas_call(
+        functools.partial(columns_kernel, nc=nc, seg=seg, groups=groups),
+        out_shape=(
+            jax.ShapeDtypeStruct((rows, width), F32),
+            jax.ShapeDtypeStruct((rows, 1), F32),
+        ),
+        grid=(rows // tile,),
+        in_specs=[spec(parts[0].shape[1])] * nc + [spec(width), spec(1)],
+        out_specs=[spec(width), spec(1)],
+        cost_estimate=pl.CostEstimate(flops=0, transcendentals=0, bytes_accessed=1024),
+        name="finish_columns",
+    )(*parts, weight, gain)
+
+
+def rows_kernel(*refs, nc):
+    out = refs[nc]
+    size = refs[0].shape[0]
+    for c in range(nc):
+        out[c * size : (c + 1) * size, :] = of_context(refs[:nc], c, nc).astype(F32)
+
+
+def finish_rows(parts):
+    nc = len(parts)
+    rows, width = parts[0].shape
+    tile = next(t for t in (512, 256, 128) if width % t == 0)
+    return pl.pallas_call(
+        functools.partial(rows_kernel, nc=nc),
+        out_shape=jax.ShapeDtypeStruct((nc * rows, width), F32),
+        grid=(width // tile,),
+        in_specs=[pl.BlockSpec((rows, tile), lambda i: (0, i))] * nc,
+        out_specs=pl.BlockSpec((nc * rows, tile), lambda i: (0, i)),
+        cost_estimate=pl.CostEstimate(flops=0, transcendentals=0, bytes_accessed=1024),
+        name="finish_rows",
+    )(*parts)
+
+
 def mm(a, b):
     return jnp.dot(a, b, preferred_element_type=F32)
 
@@ -453,30 +533,35 @@
         [jnp.stack(spread_index()), seg_row[:, 0, 0], seg_row[:, 0, rows - 1]]
     ).astype(jnp.int32)
 
-    x_parts = spread(own)
-    full_qkv = gather_all(part_qkv)
-    full_out = gather_all(after(part_out, x_parts[-2]))
-    full_gate = gather_all(part_gate)
-    full_up = gather_all(part_up)
-    full_down = gather_all(part_down)
-
+    line_qkv = gather_lines(part_qkv)
+    x_parts = spread(own, [line_qkv])
+    line_out = gather_lines(after(part_out, x_parts[-2]))
+    line_gate = gather_lines(part_gate)
+    line_up = gather_lines(part_up)
+    line_down = gather_lines(part_down)
     x_all = jnp.concatenate(x_parts, axis=0)
     scale_one = inverse_rms(x_all.astype(F32))
+    full_qkv = assemble(line_qkv, side_swap(line_qkv))
+    g_parts = spread(after(grad_top, seg_all, x_all))
     qkv = (mm(x_all, full_qkv) * scale_one).astype(BF)
-    g_parts = spread(grad_top)
     mixed, den = attention_forward(meta, qkv, seg_col, seg_row, heads, rows)
 
     def blocks(value):
         return [value[i * rows : (i + 1) * rows] for i in range(nb)]
 
+    full_out = assemble(line_out, side_swap(line_out))
     projected = mm(after(mixed, *g_parts), full_out).astype(BF)
-    residual = own.astype(F32) + add_chips(add_cores(blocks(projected)))
+    sums = add_cores(blocks(projected))
+    residual = own.astype(F32) + add_chips(sums)
 
     scale_two = inverse_rms(residual)
     unit_two = residual * scale_two
+    full_gate = assemble(line_gate, side_swap(after(line_gate, *sums)))
     n_all = jnp.concatenate(spread(unit_two.astype(BF)), axis=0)
     g_all = jnp.concatenate(g_parts, axis=0)
+    full_up = assemble(line_up, side_swap(after(line_up, unit_two)))
     gate = mm(n_all, full_gate)
+    full_down = assemble(line_down, side_swap(after(line_down, n_all)))
     up = mm(after(n_all, gate), full_up)
     grad_hidden = mm_nt(after(g_all, up), full_down)
     sigmoid = jax.nn.sigmoid(gate)
@@ -488,7 +573,7 @@
     back_sums = add_cores(blocks(back_two))
 
     total_gate = mm_tn(n_all, after(grad_gate, *back_sums)).astype(BF)
-    sum_gate = scatter_all(total_gate)
+    mine_gate, sent_gate = scatter_sides(total_gate)
     total_up = mm_tn(n_all, after(grad_up, total_gate)).astype(BF)
     mine_up, sent_up = scatter_sides(total_up)
     grad_unit_two = add_chips([after(back_sums[0], total_up)] + back_sums[1:])
@@ -498,30 +583,35 @@
     )
     branch = grad_residual.astype(BF)
     total_down = mm_tn(after(act, branch), g_all).astype(BF)
-    sum_down = scatter_all(total_down)
+    mine_down, sent_down = scatter_sides(total_down)
     projected_two = mm(after(act, total_down), full_down).astype(BF)
-    b_all = jnp.concatenate(spread(branch, [projected_two]), axis=0)
+    both_gate = add_sides(mine_gate, after(sent_gate, total_down))
+    sum_gate = scatter_lines(both_gate)
+    b_all = jnp.concatenate(spread(branch, [projected_two, both_gate]), axis=0)
     out_sums = add_cores(blocks(after(projected_two, b_all)))
 
     grad_mixed = mm_nt(b_all, full_out)
-    lines_up = scatter_lines(mine_up, after(sent_up, grad_mixed))
-    total_out = mm_tn(mixed, after(b_all, lines_up[0])).astype(BF)
+    total_out = mm_tn(mixed, after(b_all, grad_mixed)).astype(BF)
+    mine_out, sent_out = scatter_sides(total_out)
+    both_up = add_sides(mine_up, after(sent_up, total_out))
+    sum_up = scatter_lines(both_up)
     grad_qkv = attention_backward(
-        meta, qkv, seg_col, seg_row, after(grad_mixed, total_out, *out_sums), mixed, den, scale_one, heads, rows
+        meta, qkv, seg_col, seg_row, after(grad_mixed, both_up, *out_sums), mixed, den, scale_one, heads, rows
     )
-    sum_out = scatter_all(total_out)
     block_out = residual + after(add_chips([jnp.zeros_like(out_sums[0])] + out_sums[1:]), grad_qkv) + out_sums[0]
     back_one = mm_nt(after(grad_qkv, block_out), full_qkv).astype(BF)
     one_sums = add_cores(blocks(back_one))
-    total_qkv = mm_tn(x_all, after(grad_qkv, *one_sums, *lines_up)).astype(BF)
+    both_down = add_sides(mine_down, after(sent_down, *one_sums))
+    total_qkv = mm_tn(x_all, after(grad_qkv, both_down)).astype(BF)
     mine_qkv, sent_qkv = scatter_sides(total_qkv)
     grad_unit_one = add_chips(one_sums)
-    lines_qkv = scatter_lines(mine_qkv, sent_qkv)
-    sum_gate = after(sum_gate, lines_qkv[0])
-    sum_up = add_all([after(lines_up[0], grad_unit_one)] + lines_up[1:])
-    sum_down = after(sum_down, grad_unit_one)
-    sum_out = after(sum_out, grad_unit_one)
-    sum_qkv = add_all(lines_qkv)
+    sum_down = scatter_lines(both_down)
+    both_out = add_sides(mine_out, after(sent_out, both_down))
+    sum_out = scatter_lines(both_out)
+    both_qkv = add_sides(mine_qkv, after(sent_qkv, both_out, grad_unit_one))
+    sum_qkv = scatter_lines(both_qkv)
+    sum_gate = after(sum_gate, both_qkv)
+    sum_up = after(sum_up, both_qkv, grad_unit_one)
 
     unit_one = own.astype(F32) * inverse_rms(own.astype(F32))
     input_grad = grad_residual + grad_unit_one - unit_one * jnp.mean(
@@ -529,45 +619,39 @@
     )
 
     def over_context(value):
-        return in_order(spread(value.astype(BF)))
-
-    def from_hidden(stacked):
-        return (
-            stacked.reshape(nc, shard, nf, seg_len)
-            .transpose(1, 2, 0, 3)
-            .reshape(shard, hidden_all)
-            .astype(F32)
-        )
-
-    def side_by_side(stacked):
-        return stacked.transpose(1, 0, 2).reshape(stacked.shape[1], -1).astype(F32)
-
-    all_down = over_context(sum_down).reshape(nc * seg_len, width).astype(F32)
-    all_gate = from_hidden(over_context(sum_gate))
-    all_up = from_hidden(over_context(sum_up))
-    all_qkv = over_context(sum_qkv)
-    all_query = side_by_side(all_qkv[:, :, :qk])
-    all_key = side_by_side(all_qkv[:, :, qk : 2 * qk])
-    all_value = side_by_side(all_qkv[:, :, 2 * qk :])
-    all_out = ungroup_pieces(sum_out.astype(BF)).astype(F32)
-
-    def along(weight, grad):
-        return jnp.sum(weight.astype(F32) * grad, axis=1)
-
-    grad_gain_one = along(w_query, all_query) + along(w_key, all_key) + along(w_value, all_value)
-    grad_gain_two = along(w_gate, all_gate) + along(w_up, all_up)
+        return spread(value.astype(BF))
+
+    def from_hidden(value, weight):
+        stacked = in_order(over_context(value)).reshape(nc, shard, nf, seg_len)
+        grad = stacked.transpose(1, 2, 0, 3).reshape(shard, hidden_all).astype(F32)
+        return grad * gain_two, jnp.sum(weight.astype(F32) * grad, axis=1, keepdims=True)
+
+    grad_w_gate, along_gate = from_hidden(sum_gate, w_gate)
+    grad_w_up, along_up = from_hidden(sum_up, w_up)
+    qkv_parts = over_context(sum_qkv)
+
+    def columns_of(first, size):
+        return [part[:, first : first + size] for part in qkv_parts]
+
+    grad_w_query, along_query = finish_columns(columns_of(0, qk), w_query, gain_one, qk, 1)
+    grad_w_key, along_key = finish_columns(columns_of(qk, qk), w_key, gain_one, qk, 1)
+    grad_w_value, along_value = finish_columns(
+        columns_of(2 * qk, heads * VH), w_value, gain_one, heads * VH, 1
+    )
+    grad_w_down = finish_rows(over_context(sum_down))
+    grad_w_out = ungroup_pieces(sum_out.astype(BF)).astype(F32)
     return (
         block_out.astype(BF)[None],
         input_grad[None],
-        grad_gain_one,
-        all_query * gain_one,
-        all_key * gain_one,
-        all_value * gain_one,
-        all_out,
-        grad_gain_two,
-        all_gate * gain_two,
-        all_up * gain_two,
-        all_down,
+        (along_query + along_key + along_value)[:, 0],
+        grad_w_query,
+        grad_w_key,
+        grad_w_value,
+        grad_w_out,
+        (along_gate + along_up)[:, 0],
+        grad_w_gate,
+        grad_w_up,
+        grad_w_down,
     )
 
 

time: 1070 us -> 1020 us (0.953)
  waiting for transfers between devices: 488 us -> 406 us
  Pallas kernels: 40 us -> 87.4 us
  local copies, waits for them, and re-layouts: 113 us -> 87.7 us
  starting transfers between devices: 56.4 us -> 71.7 us
    ppermute x2 -> x10, waiting for transfers between devices: 89.9 us -> 199 us  [side_swap(): return lax.ppermute(value, F, [(j, j ^ 1) for j in range(lax.axis_size(F))])]
    ppermute x6 -> x0, waiting for transfers between devices: 94.4 us -> none  [line_shift(): lax.ppermute(value, F, [(j, (j // 2 + k) % m * 2 + j % 2) for j in range(...]
    all_gather x5, waiting for transfers between devices: 82.8 us -> 38.4 us  [gather_lines(): return lax.all_gather(block, F, axis=0, axis_index_groups=line_groups())]
    ppermute x3, waiting for transfers between devices: 41.7 us -> 0.6 us  [spread_direct(): lax.ppermute(block, C, [(i, (i + 2 * k) % n ^ h) for i in range(n)])]
    pallas_call x0 -> x9, Pallas kernels: none -> 38.7 us  [the longest x5 21.9 us: assemble(): pl.pallas_call(functools.partial(assemble_kernel, m=m), out_shape=jax.Sha...]
    ppermute x4, waiting for transfers between devices: 35.3 us -> 6.94 us  [group_pieces(): got = lax.ppermute(shard[q * rows:(q + 1) * rows], (C, F), pairs)]
    ppermute x12, waiting for transfers between devices: 133 us -> 115 us  [chip_shift(): return lax.ppermute(value, C, [(i, (i + 2 * k) % n) for i in range(n)])]
    ppermute x4, waiting for transfers between devices: 0.01 us -> 17 us  [ungroup_pieces(): lax.ppermute(piece, (C, F), pairs)]
  transfers between devices with their start and end apart: 65 -> 69, of which waited for: 26 -> 26; matrix products, arithmetic and copies ran while one was open for 35% -> 34% of each run, Pallas kernels for 4% -> 8%
where the time goes in v5:
time: 1020 us; the launch traced here: 1010 us
  waiting for transfers between devices  406 us (40%)
  matrix products  229 us (22%)
  other arithmetic  115 us (11%)
  local copies, waits for them, and re-layouts  87.7 us (9%)
  Pallas kernels  87.4 us (9%)
  starting transfers between devices  71.7 us (7%)
  between operations  15.5 us (2%)
    ppermute x10, waiting for transfers between devices, side_swap(): return lax.ppermute(value, F, [(j, j ^ 1) for j in range(lax.axis_size(F))])  199 us
    ppermute x12, waiting for transfers between devices, chip_shift(): return lax.ppermute(value, C, [(i, (i + 2 * k) % n) for i in range(n)])  115 us
    dot_general x5, matrix products, mm_nt(): lax.dot_general(a, b, (((1,), (1,)), ((), ())), preferred_element_type=F32)  81.1 us
    dot_general x5, matrix products, mm(): return jnp.dot(a, b, preferred_element_type=F32)  74.9 us
    dot_general x5, matrix products, mm_tn(): lax.dot_general(a, b, (((0,), (0,)), ((), ())), preferred_element_type=F32)  73.2 us
    all_gather x5, waiting for transfers between devices, gather_lines(): return lax.all_gather(block, F, axis=0, axis_index_groups=line_groups())  38.4 us
    pallas_call x1, Pallas kernels, attention_backward(): pl.pallas_call(functools.partial(backward_kernel, heads=heads, rows=rows,...  30.9 us
    unnamed x85, local copies, waits for them, and re-layouts  26.4 us
  transfers between devices with their start and end apart: 69, of which 26 were waited for; matrix products, arithmetic and copies ran while one was open for 34% of the time, Pallas kernels for 8%

profile of v5, /device:TPU:17, one launch (start us, length us, event | category | flops | bytes accessed | tf_op | source)
XLA Modules:
  0.0 1012.8 jit_solution(3145893284238755315)
XLA Ops:
  13.1 31.2 %all-gather.8.cloned.1.call-done.own = bf16[4,256,640]{2,1,0:T(8,128)(2,1)} async-done(((bf16[1,256,640]{2,1,0:T(8,128)(2,1)}), bf16[4,256,640]{2,1,0:T(8,128)(2,1)}) %all-gather.8.cloned.1.call-update) | async-done | bytes 1310736 | tf_op jit(solution)/shard_map/all_gather | solution.py:61
  44.3 9.9 collective-permute-done.4
  63.8 7.0 multiply_reduce_fusion
  72.0 6.9 collective-permute-done.10
  83.3 4.6 copy.50
  87.9 4.6 copy.52
  100.1 8.2 collective-permute-done.6.other
  119.7 11.1 %multiply_convert_fusion.3.qkv = bf16[2048,640]{1,0:T(8,128)(2,1)} fusion(bf16[2048,2048]{1,0:T(8,128)(2,1)} %get-tuple-element.116, bf16[2048,640]{1,0:T(8,128)(2,1)} %bitcast.183, f32[2048]{0:T(1024)S(1)} %add_rsqrt_fusion), kind=kOutput, calls=%fused_computation.34 | convolution fusion | flops 5371330560 | bytes 13639680 | tf_op jit(solution)/shard_map/dot_general | solution.py:463
  130.9 17.8 %attention_forward.1 = (bf16[2048,512]{1,0:T(8,128)(2,1)}, f32[2048,4]{1,0:T(8,128)}) custom-call(s32[12]{0:T(128)} %concatenate.53.meta, bf16[2048,640]{1,0:T(8,128)(2,1)} %multiply_convert_fusion.3.qkv, s32[2048,1]{1,0:T(8,128)} %copy.49.seg_col, s32[4,1,512]{2,1,0:T(1,128)} %copy-done.20), custom_call_target="tpu_custom_call" | custom-call | flops 4194304 | bytes 16384 | tf_op jit(solution)/shard_map/attention_forward/pallas_call | solution.py:338
  151.6 6.8 convolution_convert_fusion.2
  170.4 43.6 %collective-permute-done.17 = bf16[512,2048]{1,0:T(8,128)(2,1)} collective-permute-done((bf16[512,2048]{1,0:T(8,128)(2,1)}, bf16[512,2048]{1,0:T(8,128)(2,1)}, u32[]{:S(2)}, u32[]{:S(2)}) %collective-permute-start.17) | collective-permute-done | bytes 2097184 | tf_op jit(solution)/shard_map/ppermute | solution.py:101
  214.0 5.7 fusion.11
  219.7 7.7 fusion.18
  229.9 4.4 all-gather.12.cloned.1.call-done.own
  236.5 37.4 %collective-permute-done.19 = bf16[512,2048]{1,0:T(8,128)(2,1)} collective-permute-done((bf16[512,2048]{1,0:T(8,128)(2,1)}, bf16[512,2048]{1,0:T(8,128)(2,1)}, u32[]{:S(2)}, u32[]{:S(2)}) %collective-permute-start.19) | collective-permute-done | bytes 2097184 | tf_op jit(solution)/shard_map/ppermute | solution.py:101
  276.8 7.1 pad_maximum_fusion.2
  283.8 7.8 collective-permute-done.21.other
  291.7 5.3 assemble.7
  297.0 56.5 %collective-permute-done.22.other = bf16[4,256,1408]{2,1,0:T(8,128)(2,1)} collective-permute-done((bf16[4,256,1408]{2,1,0:T(8,128)(2,1)}, bf16[4,256,1408]{2,1,0:T(8,128)(2,1)}, u32[]{:S(2)}, u32[]{:S(2)}) %collective-permute-start.22) | collective-permute-done | bytes 2883616 | tf_op jit(solution)/shard_map/ppermute | solution.py:35
  353.5 5.2 assemble.8
  358.7 7.0 pad_maximum_fusion.1
  365.8 21.7 %fusion.16 = f32[2048,1408]{1,0:T(8,128)} fusion(bf16[2048,1408]{1,0:T(8,128)(2,1)} %bitcast.173, bf16[512,2048]{1,0:T(8,128)(2,1)} %collective-permute-done.20, bf16[512,2048]{1,0:T(8,128)(2,1)} %collective-permute-done.19, bf16[512,2048]{1,0:T(8,128)(2,1)} %collective-permute-done.18, bf16[512,2048]{1,0:T(8,128)(2,1)} %get-tuple-element.113), kind=kOutput, calls=%fused_computation.103 | convolution fusion | flops 11844714496 | bytes 25690112 | tf_op jit(solution)/shard_map/dot_general | solution.py:463
  388.8 18.5 %fusion.28 = f32[2048,1408]{1,0:T(8,128)} fusion(bf16[2048,2048]{1,0:T(8,128)(2,1)} %pad_maximum_fusion.1, bf16[2048,1408]{1,0:T(8,128)(2,1)} %bitcast.175), kind=kOutput, calls=%fused_computation.115 | convolution fusion | flops 11811160064 | bytes 25690112 | tf_op jit(solution)/shard_map/dot_general | solution.py:463
  407.3 42.4 %collective-permute-done.23.other = bf16[4,176,2048]{2,1,0:T(8,128)(2,1)S(1)} collective-permute-done((bf16[4,176,2048]{2,1,0:T(8,128)(2,1)}, bf16[4,176,2048]{2,1,0:T(8,128)(2,1)S(1)}, u32[]{:S(2)}, u32[]{:S(2)}) %collective-permute-start.23) | collective-permute-done | bytes 2883616 | tf_op jit(solution)/shard_map/ppermute | solution.py:35
  451.3 5.2 assemble.9
  456.6 26.4 %multiply_convert_fusion.1 = (bf16[2048,1408]{1,0:T(8,128)(2,1)}, bf16[2048,1408]{1,0:T(8,128)(2,1)}, bf16[2048,1408]{1,0:T(8,128)(2,1)}) fusion(f32[2048,1408]{1,0:T(8,128)} %fusion.16, f32[2048,1408]{1,0:T(8,128)} %fusion.28, bf16[2048,2048]{1,0:T(8,128)(2,1)} %pad_maximum_fusion.2, bf16[1408,2048]{1,0:T(8,128)(2,1)} %bitcast.167), kind=kOutput, calls=%fused_computation.3 | convolution fusion | flops 11854413824 | bytes 54525952 | tf_op jit(solution)/shard_map/dot_general | solution.py:471
  483.0 19.3 %fusion.29 = f32[2048,2048]{1,0:T(8,128)} fusion(bf16[2048,1408]{1,0:T(8,128)(2,1)} %get-tuple-element.58, bf16[2048,1408]{1,0:T(8,128)(2,1)} %bitcast.176), kind=kOutput, calls=%fused_computation.116 | convolution fusion | flops 11811160064 | bytes 28311552 | tf_op jit(solution)/shard_map/dot_general | solution.py:471
  502.3 21.6 %add_convert_fusion = bf16[2048,2048]{1,0:T(8,128)(2,1)} fusion(f32[2048,2048]{1,0:T(8,128)} %fusion.29, bf16[2048,1408]{1,0:T(8,128)(2,1)} %get-tuple-element.57, bf16[2048,1408]{1,0:T(8,128)(2,1)} %bitcast.174), kind=kOutput, calls=%fused_computation | convolution fusion | flops 11819548672 | bytes 36700160 | tf_op jit(solution)/shard_map/dot_general | solution.py:471
  523.9 4.8 fusion.21
  531.7 4.0 collective-permute-done.24
  538.8 6.2 add_convert_fusion.3
  545.3 17.7 %convolution_convert_fusion.5 = bf16[2048,1408]{1,0:T(8,128)(2,1)S(1)} fusion(bf16[2048,1408]{1,0:T(8,128)(2,1)} %get-tuple-element.57, bf16[512,2048]{1,0:T(8,128)(2,1)} %collective-permute-done.20, bf16[512,2048]{1,0:T(8,128)(2,1)} %collective-permute-done.19, bf16[512,2048]{1,0:T(8,128)(2,1)} %collective-permute-done.18, ...), kind=kOutput, calls=%fused_computation.16 | convolution fusion | flops 11847598080 | bytes 19922944 | tf_op jit(solution)/shard_map/dot_general | solution.py:467
  563.0 21.1 %convolution_convert_fusion.4 = bf16[2048,1408]{1,0:T(8,128)(2,1)} fusion(bf16[2048,1408]{1,0:T(8,128)(2,1)} %get-tuple-element.58, bf16[512,2048]{1,0:T(8,128)(2,1)} %collective-permute-done.20, bf16[512,2048]{1,0:T(8,128)(2,1)} %collective-permute-done.19, bf16[512,2048]{1,0:T(8,128)(2,1)} %collective-permute-done.18, ...), kind=kOutput, calls=%fused_computation.15 | convolution fusion | flops 11847598080 | bytes 19922944 | tf_op jit(solution)/shard_map/dot_general | solution.py:467
  587.2 4.9 collective-permute-done.26
  592.9 5.6 fusion.17
  600.2 18.6 %convolution_convert_fusion.3 = bf16[1408,2048]{1,0:T(8,128)(2,1)} fusion(bf16[2048,1408]{1,0:T(8,128)(2,1)} %get-tuple-element.61, bf16[512,2048]{1,0:T(8,128)(2,1)} %collective-permute-done.9, bf16[512,2048]{1,0:T(8,128)(2,1)} %collective-permute-done.8, bf16[512,2048]{1,0:T(8,128)(2,1)} %collective-permute-done.7, bf16[512,2048]{1,0:T(8,128)(2,1)} %bitcast.15), kind=kOutput, calls=%fused_computation.14 | convolution fusion | flops 11847598080 | bytes 19922944 | tf_op jit(solution)/shard_map/dot_general | solution.py:467
  618.9 16.8 %convolution_convert_fusion.1 = bf16[2048,2048]{1,0:T(8,128)(2,1)} fusion(bf16[2048,1408]{1,0:T(8,128)(2,1)} %get-tuple-element.61, bf16[1408,2048]{1,0:T(8,128)(2,1)S(1)} %bitcast.170), kind=kOutput, calls=%fused_computation.12 | convolution fusion | flops 11815354368 | bytes 19922944 | tf_op jit(solution)/shard_map/dot_general | solution.py:463
  635.6 13.9 %collective-permute-done.29 = bf16[4,256,1408]{2,1,0:T(8,128)(2,1)S(1)} collective-permute-done((bf16[4,256,1408]{2,1,0:T(8,128)(2,1)}, bf16[4,256,1408]{2,1,0:T(8,128)(2,1)S(1)}, u32[]{:S(2)}, u32[]{:S(2)}) %collective-permute-start.29) | collective-permute-done | bytes 2883616 | tf_op jit(solution)/shard_map/ppermute | solution.py:35
  660.4 6.8 pad_maximum_fusion.3
  667.2 4.8 fusion.20
  677.3 4.1 dynamic-slice_bitcast_fusion
  682.1 6.3 fusion.30.gm
  689.2 4.6 add_convert_fusion.2
  695.0 5.8 convolution_convert_fusion.7
  700.7 39.3 %collective-permute-done.33 = bf16[4,256,1408]{2,1,0:T(8,128)(2,1)S(1)} collective-permute-done((bf16[4,256,1408]{2,1,0:T(8,128)(2,1)S(1)}, bf16[4,256,1408]{2,1,0:T(8,128)(2,1)S(1)}, u32[]{:S(2)}, u32[]{:S(2)}) %collective-permute-start.33) | collective-permute-done | bytes 2883616 | tf_op jit(solution)/shard_map/ppermute | solution.py:35
  743.6 30.9 %attention_backward.1 = bf16[2048,640]{1,0:T(8,128)(2,1)} custom-call(s32[12]{0:T(128)} %concatenate.53.meta, bf16[2048,640]{1,0:T(8,128)(2,1)} %multiply_convert_fusion.3.qkv, s32[2048,1]{1,0:T(8,128)} %copy.49.seg_col, s32[4,1,512]{2,1,0:T(1,128)} %copy-done.20, f32[2048,512]{1,0:T(8,128)} %fusion.30.gm, bf16[2048,512]{1,0:T(8,128)(2,1)} %get-tuple-element.50.mixed, ...), custom_call_target="tpu_custom_call" | custom-call | flops 10485760 | bytes 32768 | tf_op jit(solution)/shard_map/attention_backward/pallas_call | solution.py:366
  776.8 6.6 add_add_fusion
  783.4 7.5 convolution_convert_fusion
  801.8 4.6 fusion.1
  806.3 17.9 %collective-permute-done.40 = bf16[4,64,2048]{2,1,0:T(8,128)(2,1)} collective-permute-done((bf16[4,64,2048]{2,1,0:T(8,128)(2,1)}, bf16[4,64,2048]{2,1,0:T(8,128)(2,1)}, u32[]{:S(2)}, u32[]{:S(2)}) %collective-permute-start.40) | collective-permute-done | bytes 1048608 | tf_op jit(solution)/shard_map/ppermute | solution.py:35
  827.2 10.0 convolution_convert_fusion.6
  838.7 8.8 collective-permute-done.37
  847.6 6.1 fusion.8
  853.7 13.1 %collective-permute-done.39 = bf16[4,256,640]{2,1,0:T(8,128)(2,1)S(1)} collective-permute-done((bf16[4,256,640]{2,1,0:T(8,128)(2,1)S(1)}, bf16[4,256,640]{2,1,0:T(8,128)(2,1)S(1)}, u32[]{:S(2)}, u32[]{:S(2)}) %collective-permute-start.39) | collective-permute-done | bytes 1310752 | tf_op jit(solution)/shard_map/ppermute | solution.py:35
  876.6 5.0 fusion.10
  885.1 17.0 %collective-permute-done.44 = bf16[64,2048]{1,0:T(8,128)(2,1)S(1)} collective-permute-done((bf16[64,2048]{1,0:T(8,128)(2,1)}, bf16[64,2048]{1,0:T(8,128)(2,1)S(1)}, u32[]{:S(2)}, u32[]{:S(2)}) %collective-permute-start.44) | collective-permute-done | bytes 262176 | tf_op jit(solution)/shard_map/ppermute | solution.py:182
  921.4 6.0 bitcast_multiply_fusion
  927.4 6.3 copy.68
  933.7 6.2 copy.69
  940.5 8.9 collective-permute-start.42
  949.4 14.1 %reduce-scatter.14.cloned.1.call-done.refs_0_ = bf16[176,2048]{1,0:T(8,128)(2,1)} async-done(((bf16[704,2048]{1,0:T(8,128)(2,1)}), bf16[176,2048]{1,0:T(8,128)(2,1)}) %reduce-scatter.14.cloned.1.call-update) | async-done | bytes 720912 | tf_op jit(solution)/shard_map/reduce_scatter | solution.py:57
  970.7 10.1 collective-permute-done.57.refs_2_
  994.1 4.3 finish_columns.5
  1000.3 5.2 finish_rows.1
  (282 shorter events, 172.6 us)
Async XLA Ops:
  7.2 37.1 %all-gather.8.cloned.1.call-start = ((), (), s32[]{:S(2)}) async-start(), calls=%async_computation.5 | async-start | bytes 1638400 | tf_op jit(solution)/shard_map/all_gather | solution.py:61
  7.2 46.9 %collective-permute-start.4 = (bf16[512,2048]{1,0:T(8,128)(2,1)}, bf16[512,2048]{1,0:T(8,128)(2,1)}, u32[]{:S(2)}, u32[]{:S(2)}) collective-permute-start(bf16[512,2048]{1,0:T(8,128)(2,1)} %bitcast.150), channel_id=1, source_target_pairs={{0,16},{8,24},{16,0},{24,8},{1,17},{9,25},{17,1},{25,9},{2,18},{10... | collective-permute-start | bytes 6291464 | tf_op jit(solution)/shard_map/ppermute | solution.py:101
  12.1 102.3 %all-gather.14.cloned.1.call-start = ((), (), s32[]{:S(2)}) async-start(), calls=%async_computation.13 | async-start | bytes 1310720 | tf_op jit(solution)/shard_map/all_gather | solution.py:61
  12.1 51.0 %collective-permute-start.3 = (bf16[512,2048]{1,0:T(8,128)(2,1)}, bf16[512,2048]{1,0:T(8,128)(2,1)}, u32[]{:S(2)}, u32[]{:S(2)}) collective-permute-start(bf16[512,2048]{1,0:T(8,128)(2,1)} %bitcast.151), channel_id=1, source_target_pairs={{0,8},{8,0},{16,24},{24,16},{1,9},{9,1},{17,25},{25,17},{2,10},{10... | collective-permute-start | bytes 6291464 | tf_op jit(solution)/shard_map/ppermute | solution.py:96
  54.1 9.6 collective-permute-start.5
  55.7 5.3 collective-permute-start.1
  59.7 19.2 %collective-permute-start.10 = (bf16[64,2048]{1,0:T(8,128)(2,1)S(1)}, bf16[64,2048]{1,0:T(8,128)(2,1)S(1)}, u32[]{:S(2)}, u32[]{:S(2)}) collective-permute-start(bf16[64,2048]{1,0:T(8,128)(2,1)S(1)} %get-tuple-element.135), channel_id=1, source_target_pairs={{0,0},{1,4},{10,8},{11,12},{20,16},{21,20},{30,24},{31,28}} | collective-permute-start | bytes 786440 | tf_op jit(solution)/shard_map/ppermute | solution.py:173
  61.0 17.9 %collective-permute-start.11 = (bf16[64,2048]{1,0:T(8,128)(2,1)S(1)}, bf16[64,2048]{1,0:T(8,128)(2,1)S(1)}, u32[]{:S(2)}, u32[]{:S(2)}) collective-permute-start(bf16[64,2048]{1,0:T(8,128)(2,1)S(1)} %get-tuple-element.134), channel_id=1, source_target_pairs={{0,1},{1,5},{10,9},{11,13},{20,17},{21,21},{30,25},{31,29}} | collective-permute-start | bytes 786440 | tf_op jit(solution)/shard_map/ppermute | solution.py:173
  61.7 17.2 %collective-permute-start.12 = (bf16[64,2048]{1,0:T(8,128)(2,1)S(1)}, bf16[64,2048]{1,0:T(8,128)(2,1)S(1)}, u32[]{:S(2)}, u32[]{:S(2)}) collective-permute-start(bf16[64,2048]{1,0:T(8,128)(2,1)S(1)} %get-tuple-element.137), channel_id=1, source_target_pairs={{0,2},{1,6},{10,10},{11,14},{20,18},{21,22},{30,26},{31,30}} | collective-permute-start | bytes 786440 | tf_op jit(solution)/shard_map/ppermute | solution.py:173
  63.1 15.9 %collective-permute-start.13 = (bf16[64,2048]{1,0:T(8,128)(2,1)S(1)}, bf16[64,2048]{1,0:T(8,128)(2,1)S(1)}, u32[]{:S(2)}, u32[]{:S(2)}) collective-permute-start(bf16[64,2048]{1,0:T(8,128)(2,1)S(1)} %get-tuple-element.136), channel_id=1, source_target_pairs={{0,3},{1,7},{10,11},{11,15},{20,19},{21,23},{30,27},{31,31}} | collective-permute-start | bytes 786440 | tf_op jit(solution)/shard_map/ppermute | solution.py:173
  70.8 46.0 %collective-permute-start.8 = (bf16[512,2048]{1,0:T(8,128)(2,1)}, bf16[512,2048]{1,0:T(8,128)(2,1)}, u32[]{:S(2)}, u32[]{:S(2)}) collective-permute-start(bf16[512,2048]{1,0:T(8,128)(2,1)} %bitcast.15), channel_id=1, source_target_pairs={{0,16},{8,24},{16,0},{24,8},{1,17},{9,25},{17,1},{25,9},{2,18},{10... | collective-permute-start | bytes 6291464 | tf_op jit(solution)/shard_map/ppermute | solution.py:101
  79.7 148.9 %all-gather.10.cloned.1.call-start = ((), (), s32[]{:S(2)}) async-start(), calls=%async_computation.6 | async-start | bytes 3604480 | tf_op jit(solution)/shard_map/all_gather | solution.py:61
  79.8 28.5 %collective-permute-start.6 = (bf16[4,256,640]{2,1,0:T(8,128)(2,1)}, bf16[4,256,640]{2,1,0:T(8,128)(2,1)}, u32[]{:S(2)}, u32[]{:S(2)}) collective-permute-start(bf16[4,256,640]{2,1,0:T(8,128)(2,1)} %all-gather.8.cloned.1.call-done.own), channel_id=1, source_target_pairs={{0,1},{1,0},{2,3},{3,2},{4,5},{5,4},{6,7},{7,6},{8,9},{9,8},{10,11... | collective-permute-start | bytes 3932168 | tf_op jit(solution)/shard_map/ppermute | solution.py:35
  97.6 136.6 %all-gather.12.cloned.1.call-start = ((), (), s32[]{:S(2)}) async-start(), calls=%async_computation.7 | async-start | bytes 3604480 | tf_op jit(solution)/shard_map/all_gather | solution.py:61
  114.4 34.3 %collective-permute-start.14 = (bf16[4,64,2048]{2,1,0:T(8,128)(2,1)}, bf16[4,64,2048]{2,1,0:T(8,128)(2,1)}, u32[]{:S(2)}, u32[]{:S(2)}) collective-permute-start(bf16[4,64,2048]{2,1,0:T(8,128)(2,1)} %bitcast.192), channel_id=1, source_target_pairs={{0,1},{1,0},{2,3},{3,2},{4,5},{5,4},{6,7},{7,6},{8,9},{9,8},{10,11... | collective-permute-start | bytes 3145736 | tf_op jit(solution)/shard_map/ppermute | solution.py:35
  115.6 36.0 %collective-permute-start.7 = (bf16[512,2048]{1,0:T(8,128)(2,1)}, bf16[512,2048]{1,0:T(8,128)(2,1)}, u32[]{:S(2)}, u32[]{:S(2)}) collective-permute-start(bf16[512,2048]{1,0:T(8,128)(2,1)} %bitcast.15), channel_id=1, source_target_pairs={{0,8},{8,0},{16,24},{24,16},{1,9},{9,1},{17,25},{25,17},{2,10},{10... | collective-permute-start | bytes 6291464 | tf_op jit(solution)/shard_map/ppermute | solution.py:96
  116.7 34.9 %collective-permute-start.9 = (bf16[512,2048]{1,0:T(8,128)(2,1)}, bf16[512,2048]{1,0:T(8,128)(2,1)}, u32[]{:S(2)}, u32[]{:S(2)}) collective-permute-start(bf16[512,2048]{1,0:T(8,128)(2,1)} %collective-permute-done.8), channel_id=1, source_target_pairs={{0,8},{8,0},{16,24},{24,16},{1,9},{9,1},{17,25},{25,17},{2,10},{10... | collective-permute-start | bytes 6291464 | tf_op jit(solution)/shard_map/ppermute | solution.py:96
  160.3 10.1 collective-permute-start.15
  166.6 47.4 %collective-permute-start.17 = (bf16[512,2048]{1,0:T(8,128)(2,1)}, bf16[512,2048]{1,0:T(8,128)(2,1)}, u32[]{:S(2)}, u32[]{:S(2)}) collective-permute-start(bf16[512,2048]{1,0:T(8,128)(2,1)} %add_convert_fusion.4), channel_id=1, source_target_pairs={{0,16},{8,24},{16,0},{24,8},{1,17},{9,25},{17,1},{25,9},{2,18},{10... | collective-permute-start | bytes 6291464 | tf_op jit(solution)/shard_map/ppermute | solution.py:101
  170.1 217.4 %all-gather.16.cloned.1.call-start = ((), (), s32[]{:S(2)}) async-start(), calls=%async_computation.14 | async-start | bytes 3604480 | tf_op jit(solution)/shard_map/all_gather | solution.py:61
  227.4 46.5 %collective-permute-start.19 = (bf16[512,2048]{1,0:T(8,128)(2,1)}, bf16[512,2048]{1,0:T(8,128)(2,1)}, u32[]{:S(2)}, u32[]{:S(2)}) collective-permute-start(bf16[512,2048]{1,0:T(8,128)(2,1)} %get-tuple-element.113), channel_id=1, source_target_pairs={{0,16},{8,24},{16,0},{24,8},{1,17},{9,25},{17,1},{25,9},{2,18},{10... | collective-permute-start | bytes 6291464 | tf_op jit(solution)/shard_map/ppermute | solution.py:101
  228.6 63.1 %collective-permute-start.21 = (bf16[4,256,1408]{2,1,0:T(8,128)(2,1)}, bf16[4,256,1408]{2,1,0:T(8,128)(2,1)}, u32[]{:S(2)}, u32[]{:S(2)}) collective-permute-start(bf16[4,256,1408]{2,1,0:T(8,128)(2,1)} %all-gather.10.cloned.1.call-done.own), channel_id=1, source_target_pairs={{0,1},{1,0},{2,3},{3,2},{4,5},{5,4},{6,7},{7,6},{8,9},{9,8},{10,11... | collective-permute-start | bytes 8650760 | tf_op jit(solution)/shard_map/ppermute | solution.py:35
  234.2 119.3 %collective-permute-start.22 = (bf16[4,256,1408]{2,1,0:T(8,128)(2,1)}, bf16[4,256,1408]{2,1,0:T(8,128)(2,1)}, u32[]{:S(2)}, u32[]{:S(2)}) collective-permute-start(bf16[4,256,1408]{2,1,0:T(8,128)(2,1)} %all-gather.12.cloned.1.call-done.own), channel_id=1, source_target_pairs={{0,1},{1,0},{2,3},{3,2},{4,5},{5,4},{6,7},{7,6},{8,9},{9,8},{10,11... | collective-permute-start | bytes 8650760 | tf_op jit(solution)/shard_map/ppermute | solution.py:35
  235.4 123.3 %collective-permute-start.18 = (bf16[512,2048]{1,0:T(8,128)(2,1)}, bf16[512,2048]{1,0:T(8,128)(2,1)}, u32[]{:S(2)}, u32[]{:S(2)}) collective-permute-start(bf16[512,2048]{1,0:T(8,128)(2,1)} %get-tuple-element.113), channel_id=1, source_target_pairs={{0,8},{8,0},{16,24},{24,16},{1,9},{9,1},{17,25},{25,17},{2,10},{10... | collective-permute-start | bytes 6291464 | tf_op jit(solution)/shard_map/ppermute | solution.py:96
  273.9 84.9 %collective-permute-start.20 = (bf16[512,2048]{1,0:T(8,128)(2,1)}, bf16[512,2048]{1,0:T(8,128)(2,1)}, u32[]{:S(2)}, u32[]{:S(2)}) collective-permute-start(bf16[512,2048]{1,0:T(8,128)(2,1)} %collective-permute-done.19), channel_id=1, source_target_pairs={{0,8},{8,0},{16,24},{24,16},{1,9},{9,1},{17,25},{25,17},{2,10},{10... | collective-permute-start | bytes 6291464 | tf_op jit(solution)/shard_map/ppermute | solution.py:96
  276.7 592.4 %reduce-scatter.10.cloned.1.call-start = ((), (), s32[]{:S(2)}) async-start(), calls=%async_computation.10 | async-start | bytes 3604480 | tf_op jit(solution)/shard_map/reduce_scatter | solution.py:57
  387.5 62.1 %collective-permute-start.23 = (bf16[4,176,2048]{2,1,0:T(8,128)(2,1)}, bf16[4,176,2048]{2,1,0:T(8,128)(2,1)S(1)}, u32[]{:S(2)}, u32[]{:S(2)}) collective-permute-start(bf16[4,176,2048]{2,1,0:T(8,128)(2,1)} %bitcast.179), channel_id=1, source_target_pairs={{0,1},{1,0},{2,3},{3,2},{4,5},{5,4},{6,7},{7,6},{8,9},{9,8},{10,11... | collective-permute-start | bytes 8650760 | tf_op jit(solution)/shard_map/ppermute | solution.py:35
  528.7 7.0 collective-permute-start.24
  531.7 7.1 collective-permute-start.25
  545.0 47.0 %collective-permute-start.26 = (bf16[512,2048]{1,0:T(8,128)(2,1)}, bf16[512,2048]{1,0:T(8,128)(2,1)S(1)}, u32[]{:S(2)}, u32[]{:S(2)}) collective-permute-start(bf16[512,2048]{1,0:T(8,128)(2,1)} %get-tuple-element.124), channel_id=1, source_target_pairs={{0,16},{8,24},{16,0},{24,8},{1,17},{9,25},{17,1},{25,9},{2,18},{10... | collective-permute-start | bytes 6291464 | tf_op jit(solution)/shard_map/ppermute | solution.py:101
  585.9 63.6 %collective-permute-start.29 = (bf16[4,256,1408]{2,1,0:T(8,128)(2,1)}, bf16[4,256,1408]{2,1,0:T(8,128)(2,1)S(1)}, u32[]{:S(2)}, u32[]{:S(2)}) collective-permute-start(bf16[4,256,1408]{2,1,0:T(8,128)(2,1)} %dynamic-slice_bitcast_fusion.2), channel_id=1, source_target_pairs={{0,1},{1,0},{2,3},{3,2},{4,5},{5,4},{6,7},{7,6},{8,9},{9,8},{10,11... | collective-permute-start | bytes 8650760 | tf_op jit(solution)/shard_map/ppermute | solution.py:35
  598.5 56.4 %collective-permute-start.28 = (bf16[512,2048]{1,0:T(8,128)(2,1)}, bf16[512,2048]{1,0:T(8,128)(2,1)}, u32[]{:S(2)}, u32[]{:S(2)}) collective-permute-start(bf16[512,2048]{1,0:T(8,128)(2,1)} %get-tuple-element.111), channel_id=1, source_target_pairs={{0,16},{8,24},{16,0},{24,8},{1,17},{9,25},{17,1},{25,9},{2,18},{10... | collective-permute-start | bytes 6291464 | tf_op jit(solution)/shard_map/ppermute | solution.py:101
  598.7 57.8 %collective-permute-start.27 = (bf16[512,2048]{1,0:T(8,128)(2,1)}, bf16[512,2048]{1,0:T(8,128)(2,1)}, u32[]{:S(2)}, u32[]{:S(2)}) collective-permute-start(bf16[512,2048]{1,0:T(8,128)(2,1)} %get-tuple-element.111), channel_id=1, source_target_pairs={{0,8},{8,0},{16,24},{24,16},{1,9},{9,1},{17,25},{25,17},{2,10},{10... | collective-permute-start | bytes 6291464 | tf_op jit(solution)/shard_map/ppermute | solution.py:96
  654.9 5.5 collective-permute-start.30
  656.4 215.9 %reduce-scatter.12.cloned.1.call-start = ((), (), s32[]{:S(2)}) async-start(), calls=%async_computation.11 | async-start | bytes 3604480 | tf_op jit(solution)/shard_map/reduce_scatter | solution.py:57
  672.0 17.1 %collective-permute-start.31 = (bf16[512,2048]{1,0:T(8,128)(2,1)}, bf16[512,2048]{1,0:T(8,128)(2,1)}, u32[]{:S(2)}, u32[]{:S(2)}) collective-permute-start(bf16[512,2048]{1,0:T(8,128)(2,1)} %get-tuple-element.123), channel_id=1, source_target_pairs={{0,8},{8,0},{16,24},{24,16},{1,9},{9,1},{17,25},{25,17},{2,10},{10... | collective-permute-start | bytes 6291464 | tf_op jit(solution)/shard_map/ppermute | solution.py:96
  676.0 64.0 %collective-permute-start.33 = (bf16[4,256,1408]{2,1,0:T(8,128)(2,1)S(1)}, bf16[4,256,1408]{2,1,0:T(8,128)(2,1)S(1)}, u32[]{:S(2)}, u32[]{:S(2)}) collective-permute-start(bf16[4,256,1408]{2,1,0:T(8,128)(2,1)S(1)} %dynamic-slice_bitcast_fusion.1), channel_id=1, source_target_pairs={{0,1},{1,0},{2,3},{3,2},{4,5},{5,4},{6,7},{7,6},{8,9},{9,8},{10,11... | collective-permute-start | bytes 8650760 | tf_op jit(solution)/shard_map/ppermute | solution.py:35
  681.4 120.4 %collective-permute-start.38 = (bf16[4,176,2048]{2,1,0:T(8,128)(2,1)}, bf16[4,176,2048]{2,1,0:T(8,128)(2,1)}, u32[]{:S(2)}, u32[]{:S(2)}) collective-permute-start(bf16[4,176,2048]{2,1,0:T(8,128)(2,1)} %dynamic-slice_bitcast_fusion), channel_id=1, source_target_pairs={{0,1},{1,0},{2,3},{3,2},{4,5},{5,4},{6,7},{7,6},{8,9},{9,8},{10,11... | collective-permute-start | bytes 8650760 | tf_op jit(solution)/shard_map/ppermute | solution.py:35
  688.4 88.4 %collective-permute-start.34 = (bf16[512,2048]{1,0:T(8,128)(2,1)}, bf16[512,2048]{1,0:T(8,128)(2,1)}, u32[]{:S(2)}, u32[]{:S(2)}) collective-permute-start(bf16[512,2048]{1,0:T(8,128)(2,1)} %get-tuple-element.122), channel_id=1, source_target_pairs={{0,8},{8,0},{16,24},{24,16},{1,9},{9,1},{17,25},{25,17},{2,10},{10... | collective-permute-start | bytes 6291464 | tf_op jit(solution)/shard_map/ppermute | solution.py:96
  693.8 80.7 %collective-permute-start.32 = (bf16[512,2048]{1,0:T(8,128)(2,1)}, bf16[512,2048]{1,0:T(8,128)(2,1)}, u32[]{:S(2)}, u32[]{:S(2)}) collective-permute-start(bf16[512,2048]{1,0:T(8,128)(2,1)} %add_convert_fusion.2), channel_id=1, source_target_pairs={{0,16},{8,24},{16,0},{24,8},{1,17},{9,25},{17,1},{25,9},{2,18},{10... | collective-permute-start | bytes 6291464 | tf_op jit(solution)/shard_map/ppermute | solution.py:101
  743.5 138.1 %reduce-scatter.8.cloned.1.call-start = ((), (), s32[]{:S(2)}) async-start(), calls=%async_computation.9 | async-start | bytes 1310720 | tf_op jit(solution)/shard_map/reduce_scatter | solution.py:57
  792.6 5.5 collective-permute-start.36
  795.3 28.9 %collective-permute-start.40 = (bf16[4,64,2048]{2,1,0:T(8,128)(2,1)}, bf16[4,64,2048]{2,1,0:T(8,128)(2,1)}, u32[]{:S(2)}, u32[]{:S(2)}) collective-permute-start(bf16[4,64,2048]{2,1,0:T(8,128)(2,1)} %dynamic-slice_bitcast_fusion.4), channel_id=1, source_target_pairs={{0,1},{1,0},{2,3},{3,2},{4,5},{5,4},{6,7},{7,6},{8,9},{9,8},{10,11... | collective-permute-start | bytes 3145736 | tf_op jit(solution)/shard_map/ppermute | solution.py:35
  796.6 42.2 %collective-permute-start.35 = (bf16[512,2048]{1,0:T(8,128)(2,1)}, bf16[512,2048]{1,0:T(8,128)(2,1)}, u32[]{:S(2)}, u32[]{:S(2)}) collective-permute-start(bf16[512,2048]{1,0:T(8,128)(2,1)} %get-tuple-element.120), channel_id=1, source_target_pairs={{0,8},{8,0},{16,24},{24,16},{1,9},{9,1},{17,25},{25,17},{2,10},{10... | collective-permute-start | bytes 6291464 | tf_op jit(solution)/shard_map/ppermute | solution.py:96
  800.3 47.3 %collective-permute-start.37 = (bf16[512,2048]{1,0:T(8,128)(2,1)}, bf16[512,2048]{1,0:T(8,128)(2,1)}, u32[]{:S(2)}, u32[]{:S(2)}) collective-permute-start(bf16[512,2048]{1,0:T(8,128)(2,1)} %add_convert_fusion.1), channel_id=1, source_target_pairs={{0,16},{8,24},{16,0},{24,8},{1,17},{9,25},{17,1},{25,9},{2,18},{10... | collective-permute-start | bytes 6291464 | tf_op jit(solution)/shard_map/ppermute | solution.py:101
  827.2 113.3 %reduce-scatter.6.cloned.1.call-start = ((), (), s32[]{:S(2)}) async-start(), calls=%async_computation.8 | async-start | bytes 1638400 | tf_op jit(solution)/shard_map/reduce_scatter | solution.py:57
  837.4 29.4 %collective-permute-start.39 = (bf16[4,256,640]{2,1,0:T(8,128)(2,1)S(1)}, bf16[4,256,640]{2,1,0:T(8,128)(2,1)S(1)}, u32[]{:S(2)}, u32[]{:S(2)}) collective-permute-start(bf16[4,256,640]{2,1,0:T(8,128)(2,1)S(1)} %dynamic-slice_bitcast_fusion.3), channel_id=1, source_target_pairs={{0,1},{1,0},{2,3},{3,2},{4,5},{5,4},{6,7},{7,6},{8,9},{9,8},{10,11... | collective-permute-start | bytes 3932168 | tf_op jit(solution)/shard_map/ppermute | solution.py:35
  868.2 95.3 %reduce-scatter.14.cloned.1.call-start = ((), (), s32[]{:S(2)}) async-start(), calls=%async_computation.12 | async-start | bytes 3604480 | tf_op jit(solution)/shard_map/reduce_scatter | solution.py:57
  869.1 36.5 %collective-permute-start.50 = (bf16[256,1408]{0,1:T(8,128)(2,1)}, bf16[256,1408]{0,1:T(8,128)(2,1)}, u32[]{:S(2)}, u32[]{:S(2)}) collective-permute-start(bf16[256,1408]{0,1:T(8,128)(2,1)} %reduce-scatter.10.cloned.1.call-done), channel_id=1, source_target_pairs={{0,8},{8,0},{16,24},{24,16},{1,9},{9,1},{17,25},{25,17},{2,10},{10... | collective-permute-start | bytes 2162696 | tf_op jit(solution)/shard_map/ppermute | solution.py:96
  871.1 33.8 %collective-permute-start.51 = (bf16[256,1408]{0,1:T(8,128)(2,1)}, bf16[256,1408]{0,1:T(8,128)(2,1)}, u32[]{:S(2)}, u32[]{:S(2)}) collective-permute-start(bf16[256,1408]{0,1:T(8,128)(2,1)} %reduce-scatter.10.cloned.1.call-done), channel_id=1, source_target_pairs={{0,16},{8,24},{16,0},{24,8},{1,17},{9,25},{17,1},{25,9},{2,18},{10... | collective-permute-start | bytes 2162696 | tf_op jit(solution)/shard_map/ppermute | solution.py:101
  872.3 33.3 %collective-permute-start.54 = (bf16[256,1408]{0,1:T(8,128)(2,1)}, bf16[256,1408]{0,1:T(8,128)(2,1)}, u32[]{:S(2)}, u32[]{:S(2)}) collective-permute-start(bf16[256,1408]{0,1:T(8,128)(2,1)} %reduce-scatter.12.cloned.1.call-done), channel_id=1, source_target_pairs={{0,16},{8,24},{16,0},{24,8},{1,17},{9,25},{17,1},{25,9},{2,18},{10... | collective-permute-start | bytes 2162696 | tf_op jit(solution)/shard_map/ppermute | solution.py:101
  881.6 20.5 %collective-permute-start.44 = (bf16[64,2048]{1,0:T(8,128)(2,1)}, bf16[64,2048]{1,0:T(8,128)(2,1)S(1)}, u32[]{:S(2)}, u32[]{:S(2)}) collective-permute-start(bf16[64,2048]{1,0:T(8,128)(2,1)} %reduce-scatter.8.cloned.1.call-done), channel_id=1, source_target_pairs={{0,0},{4,1},{8,10},{12,11},{16,20},{20,21},{24,30},{28,31}} | collective-permute-start | bytes 786440 | tf_op jit(solution)/shard_map/ppermute | solution.py:182
  883.1 19.7 %collective-permute-start.45 = (bf16[64,2048]{1,0:T(8,128)(2,1)}, bf16[64,2048]{1,0:T(8,128)(2,1)S(1)}, u32[]{:S(2)}, u32[]{:S(2)}) collective-permute-start(bf16[64,2048]{1,0:T(8,128)(2,1)} %reduce-scatter.8.cloned.1.call-done), channel_id=1, source_target_pairs={{1,0},{5,1},{9,10},{13,11},{17,20},{21,21},{25,30},{29,31}} | collective-permute-start | bytes 786440 | tf_op jit(solution)/shard_map/ppermute | solution.py:182
  903.5 6.1 collective-permute-start.53
  904.2 6.7 collective-permute-start.48
  904.9 9.0 collective-permute-start.52
  905.6 11.8 %collective-permute-start.55 = (bf16[256,1408]{0,1:T(8,128)(2,1)}, bf16[256,1408]{0,1:T(8,128)(2,1)S(1)}, u32[]{:S(2)}, u32[]{:S(2)}) collective-permute-start(bf16[256,1408]{0,1:T(8,128)(2,1)} %collective-permute-done.54), channel_id=1, source_target_pairs={{0,8},{8,0},{16,24},{24,16},{1,9},{9,1},{17,25},{25,17},{2,10},{10... | collective-permute-start | bytes 2162696 | tf_op jit(solution)/shard_map/ppermute | solution.py:96
  912.3 52.4 %collective-permute-start.49 = (bf16[256,2048]{1,0:T(8,128)(2,1)}, bf16[256,2048]{1,0:T(8,128)(2,1)}, u32[]{:S(2)}, u32[]{:S(2)}) collective-permute-start(bf16[256,2048]{1,0:T(8,128)(2,1)} %add.243), channel_id=1, source_target_pairs={{0,8},{16,24},{1,9},{17,25},{10,2},{26,18},{11,3},{27,19},{4,12},{... | collective-permute-start | bytes 3145736 | tf_op jit(solution)/shard_map/ppermute | solution.py:193
  940.5 29.7 %collective-permute-start.42 = (bf16[256,640]{1,0:T(8,128)(2,1)}, bf16[256,640]{1,0:T(8,128)(2,1)S(1)}, u32[]{:S(2)}, u32[]{:S(2)}) collective-permute-start(bf16[256,640]{1,0:T(8,128)(2,1)} %reduce-scatter.6.cloned.1.call-done), channel_id=1, source_target_pairs={{0,16},{8,24},{16,0},{24,8},{1,17},{9,25},{17,1},{25,9},{2,18},{10... | collective-permute-start | bytes 983048 | tf_op jit(solution)/shard_map/ppermute | solution.py:101
  963.5 17.3 %collective-permute-start.57 = (bf16[176,2048]{1,0:T(8,128)(2,1)}, bf16[176,2048]{1,0:T(8,128)(2,1)}, u32[]{:S(2)}, u32[]{:S(2)}) collective-permute-start(bf16[176,2048]{1,0:T(8,128)(2,1)} %reduce-scatter.14.cloned.1.call-done.refs_0_), channel_id=1, source_target_pairs={{0,16},{8,24},{16,0},{24,8},{1,17},{9,25},{17,1},{25,9},{2,18},{10... | collective-permute-start | bytes 2162696 | tf_op jit(solution)/shard_map/ppermute | solution.py:101
  967.7 16.1 %collective-permute-start.41 = (bf16[256,640]{1,0:T(8,128)(2,1)S(1)}, bf16[256,640]{1,0:T(8,128)(2,1)S(1)}, u32[]{:S(2)}, u32[]{:S(2)}) collective-permute-start(bf16[256,640]{1,0:T(8,128)(2,1)S(1)} %copy-done.19), channel_id=1, source_target_pairs={{0,8},{8,0},{16,24},{24,16},{1,9},{9,1},{17,25},{25,17},{2,10},{10... | collective-permute-start | bytes 983048 | tf_op jit(solution)/shard_map/ppermute | solution.py:96
  970.2 15.1 %collective-permute-start.43 = (bf16[256,640]{1,0:T(8,128)(2,1)S(1)}, bf16[256,640]{1,0:T(8,128)(2,1)S(1)}, u32[]{:S(2)}, u32[]{:S(2)}) collective-permute-start(bf16[256,640]{1,0:T(8,128)(2,1)S(1)} %collective-permute-done.42), channel_id=1, source_target_pairs={{0,8},{8,0},{16,24},{24,16},{1,9},{9,1},{17,25},{25,17},{2,10},{10... | collective-permute-start | bytes 983048 | tf_op jit(solution)/shard_map/ppermute | solution.py:96
  970.2 30.1 %collective-permute-start.56 = (bf16[176,2048]{1,0:T(8,128)(2,1)}, bf16[176,2048]{1,0:T(8,128)(2,1)}, u32[]{:S(2)}, u32[]{:S(2)}) collective-permute-start(bf16[176,2048]{1,0:T(8,128)(2,1)} %reduce-scatter.14.cloned.1.call-done.refs_0_), channel_id=1, source_target_pairs={{0,8},{8,0},{16,24},{24,16},{1,9},{9,1},{17,25},{25,17},{2,10},{10... | collective-permute-start | bytes 2162696 | tf_op jit(solution)/shard_map/ppermute | solution.py:96
  980.8 19.5 %collective-permute-start.58 = (bf16[176,2048]{1,0:T(8,128)(2,1)}, bf16[176,2048]{1,0:T(8,128)(2,1)}, u32[]{:S(2)}, u32[]{:S(2)}) collective-permute-start(bf16[176,2048]{1,0:T(8,128)(2,1)} %collective-permute-done.57.refs_2_), channel_id=1, source_target_pairs={{0,8},{8,0},{16,24},{24,16},{1,9},{9,1},{17,25},{25,17},{2,10},{10... | collective-permute-start | bytes 2162696 | tf_op jit(solution)/shard_map/ppermute | solution.py:96
  (44 other events, 816.2 us)
Sparse Core Ops, SparseCore 0:
  12.2 32.0 all-gather.7
  79.8 34.5 all-gather.13
  116.5 57.7 all-gather.9
  176.4 57.7 all-gather.11
  276.8 57.1 all-gather.15
  656.6 55.5 reduce-scatter.9
  743.7 56.9 reduce-scatter.11
  827.3 26.1 reduce-scatter.7
  868.3 35.0 reduce-scatter.5
  905.6 57.9 reduce-scatter.13

commit v6 on v5

--- a/solution.py
+++ b/solution.py
@@ -35,20 +35,26 @@
     return lax.ppermute(value, F, [(j, j ^ 1) for j in range(lax.axis_size(F))])
 
 
+def swap_pieces(value, pieces):
+    size = value.shape[0] // pieces
+    return [side_swap(value[i * size : (i + 1) * size]) for i in range(pieces)]
+
+
 def line_and_side():
     me = lax.axis_index(F)
     return me // 2, lax.rem(me, 2)
 
 
-def scatter_sides(total):
+def scatter_sides(total, pieces=1):
     m = lines()
     _, side = line_and_side()
     parts = total.reshape(m, 2, total.shape[0] // (2 * m), total.shape[1])
     mine = lax.dynamic_index_in_dim(parts, side, 1, keepdims=False)
-    return mine, side_swap(lax.dynamic_index_in_dim(parts, 1 - side, 1, keepdims=False))
-
-
-def add_sides(mine, sent):
+    return mine, swap_pieces(lax.dynamic_index_in_dim(parts, 1 - side, 1, keepdims=False), pieces)
+
+
+def add_sides(mine, sent, *marks):
+    sent = jnp.concatenate([after(sent[0], *marks)] + sent[1:], axis=0)
     both = (mine.astype(F32) + sent.astype(F32)).astype(BF)
     return both.reshape(-1, both.shape[-1])
 
@@ -61,12 +67,15 @@
     return lax.all_gather(block, F, axis=0, axis_index_groups=line_groups())
 
 
-def assemble_kernel(own, other, out, sems, *, m):
+def assemble_kernel(own, *refs, m, pieces):
     side = lax.rem(lax.axis_index(F), 2)
+    out, sems = refs[pieces], refs[pieces + 1]
+    size = m // pieces
     copies = []
     for k in range(m):
+        other = refs[k // size].at[k % size]
         copies.append(pltpu.make_async_copy(own.at[k], out.at[2 * k + side], sems.at[k]))
-        copies.append(pltpu.make_async_copy(other.at[k], out.at[2 * k + 1 - side], sems.at[m + k]))
+        copies.append(pltpu.make_async_copy(other, out.at[2 * k + 1 - side], sems.at[m + k]))
     for copy in copies:
         copy.start()
     for copy in copies:
@@ -76,14 +85,14 @@
 def assemble(own, other):
     m, rows, width = own.shape
     out = pl.pallas_call(
-        functools.partial(assemble_kernel, m=m),
+        functools.partial(assemble_kernel, m=m, pieces=len(other)),
         out_shape=jax.ShapeDtypeStruct((2 * m, rows, width), own.dtype),
-        in_specs=[pl.BlockSpec(memory_space=pl.ANY)] * 2,
+        in_specs=[pl.BlockSpec(memory_space=pl.ANY)] * (1 + len(other)),
         out_specs=pl.BlockSpec(memory_space=pltpu.VMEM),
         scratch_shapes=[pltpu.SemaphoreType.DMA((2 * m,))],
         cost_estimate=pl.CostEstimate(flops=0, transcendentals=0, bytes_accessed=1024),
         name="assemble",
-    )(own, other)
+    )(own, *other)
     return out.reshape(2 * m * rows, width)
 
 
@@ -534,35 +543,39 @@
     ).astype(jnp.int32)
 
     line_qkv = gather_lines(part_qkv)
-    x_parts = spread(own, [line_qkv])
-    line_out = gather_lines(after(part_out, x_parts[-2]))
+    other_qkv = swap_pieces(line_qkv, 1)
+    x_parts = spread(own, [line_qkv, part_out])
+    line_out = gather_lines(part_out)
     line_gate = gather_lines(part_gate)
     line_up = gather_lines(part_up)
     line_down = gather_lines(part_down)
     x_all = jnp.concatenate(x_parts, axis=0)
     scale_one = inverse_rms(x_all.astype(F32))
-    full_qkv = assemble(line_qkv, side_swap(line_qkv))
-    g_parts = spread(after(grad_top, seg_all, x_all))
+    full_qkv = assemble(line_qkv, other_qkv)
+    g_parts = spread(after(grad_top, seg_all, x_all, *other_qkv))
     qkv = (mm(x_all, full_qkv) * scale_one).astype(BF)
     mixed, den = attention_forward(meta, qkv, seg_col, seg_row, heads, rows)
 
     def blocks(value):
         return [value[i * rows : (i + 1) * rows] for i in range(nb)]
 
-    full_out = assemble(line_out, side_swap(line_out))
+    full_out = assemble(line_out, swap_pieces(line_out, 1))
     projected = mm(after(mixed, *g_parts), full_out).astype(BF)
     sums = add_cores(blocks(projected))
-    residual = own.astype(F32) + add_chips(sums)
+    other_gate = swap_pieces(after(line_gate, *sums), 2)
+    residual = after(own.astype(F32) + add_chips(sums), other_gate[0])
 
     scale_two = inverse_rms(residual)
     unit_two = residual * scale_two
-    full_gate = assemble(line_gate, side_swap(after(line_gate, *sums)))
-    n_all = jnp.concatenate(spread(unit_two.astype(BF)), axis=0)
+    full_gate = assemble(line_gate, other_gate)
+    n_all = jnp.concatenate(spread(unit_two.astype(BF), other_gate), axis=0)
     g_all = jnp.concatenate(g_parts, axis=0)
-    full_up = assemble(line_up, side_swap(after(line_up, unit_two)))
-    gate = mm(n_all, full_gate)
-    full_down = assemble(line_down, side_swap(after(line_down, n_all)))
-    up = mm(after(n_all, gate), full_up)
+    other_up = swap_pieces(after(line_up, unit_two), 1)
+    other_down = swap_pieces(line_down, 2)
+    gate = mm(after(n_all, line_down), full_gate)
+    full_up = assemble(line_up, [after(part, gate) for part in other_up])
+    up = mm(after(n_all, gate, other_down[0]), full_up)
+    full_down = assemble(line_down, [after(part, up) for part in other_down])
     grad_hidden = mm_nt(after(g_all, up), full_down)
     sigmoid = jax.nn.sigmoid(gate)
     silu = gate * sigmoid
@@ -573,45 +586,46 @@
     back_sums = add_cores(blocks(back_two))
 
     total_gate = mm_tn(n_all, after(grad_gate, *back_sums)).astype(BF)
-    mine_gate, sent_gate = scatter_sides(total_gate)
+    mine_gate, sent_gate = scatter_sides(total_gate, 2)
     total_up = mm_tn(n_all, after(grad_up, total_gate)).astype(BF)
-    mine_up, sent_up = scatter_sides(total_up)
-    grad_unit_two = add_chips([after(back_sums[0], total_up)] + back_sums[1:])
+    mine_up, sent_up = scatter_sides(total_up, 2)
+    grad_unit_two = add_chips([after(back_sums[0], total_up, sent_gate[0])] + back_sums[1:])
 
     grad_residual = grad_top.astype(F32) + scale_two * (
         grad_unit_two - unit_two * jnp.mean(grad_unit_two * unit_two, axis=-1, keepdims=True)
     )
     branch = grad_residual.astype(BF)
     total_down = mm_tn(after(act, branch), g_all).astype(BF)
-    mine_down, sent_down = scatter_sides(total_down)
+    mine_down, sent_down = scatter_sides(total_down, 2)
     projected_two = mm(after(act, total_down), full_down).astype(BF)
-    both_gate = add_sides(mine_gate, after(sent_gate, total_down))
+    both_gate = add_sides(mine_gate, sent_gate, total_down)
     sum_gate = scatter_lines(both_gate)
     b_all = jnp.concatenate(spread(branch, [projected_two, both_gate]), axis=0)
     out_sums = add_cores(blocks(after(projected_two, b_all)))
 
     grad_mixed = mm_nt(b_all, full_out)
-    total_out = mm_tn(mixed, after(b_all, grad_mixed)).astype(BF)
+    total_out = mm_tn(mixed, after(b_all, grad_mixed, sent_up[0])).astype(BF)
     mine_out, sent_out = scatter_sides(total_out)
-    both_up = add_sides(mine_up, after(sent_up, total_out))
-    sum_up = scatter_lines(both_up)
     grad_qkv = attention_backward(
-        meta, qkv, seg_col, seg_row, after(grad_mixed, both_up, *out_sums), mixed, den, scale_one, heads, rows
+        meta, qkv, seg_col, seg_row, after(grad_mixed, total_out, *out_sums), mixed, den, scale_one, heads, rows
     )
     block_out = residual + after(add_chips([jnp.zeros_like(out_sums[0])] + out_sums[1:]), grad_qkv) + out_sums[0]
-    back_one = mm_nt(after(grad_qkv, block_out), full_qkv).astype(BF)
+    back_one = mm_nt(after(grad_qkv, block_out, *sent_up), full_qkv).astype(BF)
     one_sums = add_cores(blocks(back_one))
-    both_down = add_sides(mine_down, after(sent_down, *one_sums))
-    total_qkv = mm_tn(x_all, after(grad_qkv, both_down)).astype(BF)
+    both_up = add_sides(mine_up, sent_up, *one_sums)
+    sum_up = scatter_lines(both_up)
+    total_qkv = mm_tn(x_all, after(grad_qkv, both_up, sum_gate, sent_down[0])).astype(BF)
+    both_down = add_sides(mine_down, sent_down, total_qkv)
     mine_qkv, sent_qkv = scatter_sides(total_qkv)
-    grad_unit_one = add_chips(one_sums)
+    grad_unit_one = after(add_chips(one_sums), sum_up)
     sum_down = scatter_lines(both_down)
-    both_out = add_sides(mine_out, after(sent_out, both_down))
+    both_out = add_sides(mine_out, sent_out, both_down, grad_unit_one)
     sum_out = scatter_lines(both_out)
-    both_qkv = add_sides(mine_qkv, after(sent_qkv, both_out, grad_unit_one))
+    both_qkv = add_sides(mine_qkv, sent_qkv, both_out, grad_unit_one)
     sum_qkv = scatter_lines(both_qkv)
     sum_gate = after(sum_gate, both_qkv)
-    sum_up = after(sum_up, both_qkv, grad_unit_one)
+    sum_up = after(sum_up, both_qkv)
+    sum_out = after(sum_out, both_qkv)
 
     unit_one = own.astype(F32) * inverse_rms(own.astype(F32))
     input_grad = grad_residual + grad_unit_one - unit_one * jnp.mean(

time: 1020 us -> 1110 us (1.088)
  local copies, waits for them, and re-layouts: 87.7 us -> 137 us
  other arithmetic: 115 us -> 152 us
  starting transfers between devices: 71.7 us -> 104 us
  waiting for transfers between devices: 406 us -> 393 us
    convert_element_type x0 -> x4, local copies, waits for them, and re-layouts: none -> 25.1 us  [add_sides(): both = (mine.astype(F32) + sent.astype(F32)).astype(BF)]
    convert_element_type x5 -> x9, other arithmetic: 12.1 us -> 35.3 us  [add_sides(): both = (mine.astype(F32) + sent.astype(F32)).astype(BF)]
    ppermute x12, waiting for transfers between devices: 115 us -> 135 us  [chip_shift(): return lax.ppermute(value, C, [(i, (i + 2 * k) % n) for i in range(n)])]
    slice x0 -> x7, local copies, waits for them, and re-layouts: none -> 16.8 us  [swap_pieces(): return [side_swap(value[i * size:(i + 1) * size]) for i in range(pieces)]]
    ppermute x4, waiting for transfers between devices: 17 us -> 2 us  [ungroup_pieces(): lax.ppermute(piece, (C, F), pairs)]
    reduce_scatter x5, waiting for transfers between devices: 14.2 us -> 0.03 us  [scatter_lines(): lax.psum_scatter(total, F, scatter_dimension=0, axis_index_groups=line_gr...]
    all_gather x5, waiting for transfers between devices: 38.4 us -> 24.3 us  [gather_lines(): return lax.all_gather(block, F, axis=0, axis_index_groups=line_groups())]
    ppermute x10 -> x15, starting transfers between devices: 14.2 us -> 28.2 us  [side_swap(): return lax.ppermute(value, F, [(j, j ^ 1) for j in range(lax.axis_size(F))])]
  transfers between devices with their start and end apart: 69 -> 74, of which waited for: 26 -> 24; matrix products, arithmetic and copies ran while one was open for 34% -> 38% of each run, Pallas kernels for 8% -> 7%
where the time goes in v6:
time: 1110 us
  waiting for transfers between devices  393 us (35%)
  matrix products  225 us (20%)
  other arithmetic  152 us (14%)
  local copies, waits for them, and re-layouts  137 us (12%)
  starting transfers between devices  104 us (9%)
  Pallas kernels  78.9 us (7%)
  between operations  15.1 us (1%)
    ppermute x15, waiting for transfers between devices, side_swap(): return lax.ppermute(value, F, [(j, j ^ 1) for j in range(lax.axis_size(F))])  205 us
    ppermute x12, waiting for transfers between devices, chip_shift(): return lax.ppermute(value, C, [(i, (i + 2 * k) % n) for i in range(n)])  135 us
    dot_general x5, matrix products, mm_nt(): lax.dot_general(a, b, (((1,), (1,)), ((), ())), preferred_element_type=F32)  84.2 us
    dot_general x5, matrix products, mm_tn(): lax.dot_general(a, b, (((0,), (0,)), ((), ())), preferred_element_type=F32)  71.9 us
    dot_general x5, matrix products, mm(): return jnp.dot(a, b, preferred_element_type=F32)  68.9 us
    ppermute x24, starting transfers between devices, core_swap(): return lax.ppermute(value, C, [(i, i ^ 1) for i in range(n)])  36.7 us
    convert_element_type x9, other arithmetic, add_sides(): both = (mine.astype(F32) + sent.astype(F32)).astype(BF)  35.3 us
    unnamed x93, local copies, waits for them, and re-layouts  31.2 us
  transfers between devices with their start and end apart: 74, of which 24 were waited for; matrix products, arithmetic and copies ran while one was open for 38% of the time, Pallas kernels for 7%

profile of v6, /device:TPU:17, one launch (start us, length us, event | category | flops | bytes accessed | tf_op | source)
XLA Modules:
  0.0 1105.5 jit_solution(14735998693509751576)
XLA Ops:
  16.8 10.7 collective-permute-done.5
  28.3 19.7 %all-gather.8.cloned.1.call-done.own = bf16[4,256,640]{2,1,0:T(8,128)(2,1)} async-done(((bf16[1,256,640]{2,1,0:T(8,128)(2,1)}), bf16[4,256,640]{2,1,0:T(8,128)(2,1)}) %all-gather.8.cloned.1.call-update) | async-done | bytes 1310736 | tf_op jit(solution)/shard_map/all_gather | solution.py:67
  48.0 6.2 collective-permute-done.4
  67.8 7.5 multiply_reduce_fusion
  75.3 12.5 %collective-permute-done.10.refs_0_ = bf16[4,256,640]{2,1,0:T(8,128)(2,1)} collective-permute-done((bf16[4,256,640]{2,1,0:T(8,128)(2,1)}, bf16[4,256,640]{2,1,0:T(8,128)(2,1)}, u32[]{:S(2)}, u32[]{:S(2)}) %collective-permute-start.10) | collective-permute-done | bytes 1310752 | tf_op jit(solution)/shard_map/ppermute | solution.py:35
  92.2 4.6 all-gather.14.cloned.1.call-done
  98.0 4.6 copy.56
  102.6 4.6 copy.58
  114.8 6.2 collective-permute-done.14.refs_0_
  128.9 8.7 collective-permute-done.12
  139.7 10.9 multiply_convert_fusion.3.qkv
  150.7 14.5 %attention_forward.1 = (bf16[2048,512]{1,0:T(8,128)(2,1)}, f32[2048,4]{1,0:T(8,128)}) custom-call(s32[12]{0:T(128)} %concatenate.62.meta, bf16[2048,640]{1,0:T(8,128)(2,1)} %multiply_convert_fusion.3.qkv, s32[2048,1]{1,0:T(8,128)} %copy.55.seg_col, s32[4,1,512]{2,1,0:T(1,128)} %copy-done.27), custom_call_target="tpu_custom_call" | custom-call | flops 4194304 | bytes 16384 | tf_op jit(solution)/shard_map/attention_forward/pallas_call | solution.py:347
  165.2 6.7 convolution_convert_fusion.2
  181.0 4.4 add_convert_fusion.6
  195.6 37.2 %collective-permute-done.17 = bf16[512,2048]{1,0:T(8,128)(2,1)} collective-permute-done((bf16[512,2048]{1,0:T(8,128)(2,1)}, bf16[512,2048]{1,0:T(8,128)(2,1)}, u32[]{:S(2)}, u32[]{:S(2)}) %collective-permute-start.17) | collective-permute-done | bytes 2097184 | tf_op jit(solution)/shard_map/ppermute | solution.py:110
  232.8 5.3 fusion.9
  248.0 29.2 %collective-permute-done.21.refs_1_ = bf16[2,256,1408]{2,1,0:T(8,128)(2,1)S(1)} collective-permute-done((bf16[2,256,1408]{2,1,0:T(8,128)(2,1)S(1)}, bf16[2,256,1408]{2,1,0:T(8,128)(2,1)S(1)}, u32[]{:S(2)}, u32[]{:S(2)}) %collective-permute-start.21) | collective-permute-done | bytes 1441824 | tf_op jit(solution)/shard_map/ppermute | solution.py:35
  277.2 10.4 collective-permute-done.20
  296.9 7.0 pad_maximum_fusion.2
  303.9 5.2 assemble.7
  315.0 15.8 %fusion.27 = f32[2048,1408]{1,0:T(8,128)} fusion(bf16[2048,2048]{1,0:T(8,128)(2,1)S(1)} %pad_maximum_fusion.1, bf16[2048,1408]{1,0:T(8,128)(2,1)S(1)} %bitcast.186), kind=kOutput, calls=%fused_computation.129 | convolution fusion | flops 11811160064 | bytes 25690112 | tf_op jit(solution)/shard_map/dot_general | solution.py:472
  330.8 90.9 %collective-permute-done.24.refs_0_ = bf16[4,256,1408]{2,1,0:T(8,128)(2,1)S(1)} collective-permute-done((bf16[4,256,1408]{2,1,0:T(8,128)(2,1)}, bf16[4,256,1408]{2,1,0:T(8,128)(2,1)S(1)}, u32[]{:S(2)}, u32[]{:S(2)}) %collective-permute-start.24) | collective-permute-done | bytes 2883616 | tf_op jit(solution)/shard_map/ppermute | solution.py:35
  423.3 5.2 assemble.8
  428.6 18.5 %fusion.28 = f32[2048,1408]{1,0:T(8,128)} fusion(bf16[2048,2048]{1,0:T(8,128)(2,1)} %copy-done.12, bf16[2048,1408]{1,0:T(8,128)(2,1)} %bitcast.187), kind=kOutput, calls=%fused_computation.130 | convolution fusion | flops 11811160064 | bytes 25690112 | tf_op jit(solution)/shard_map/dot_general | solution.py:472
  447.1 5.2 assemble.9
  452.3 26.1 %multiply_convert_fusion.1 = (bf16[2048,1408]{1,0:T(8,128)(2,1)}, bf16[2048,1408]{1,0:T(8,128)(2,1)}, bf16[2048,1408]{1,0:T(8,128)(2,1)}) fusion(f32[2048,1408]{1,0:T(8,128)} %fusion.27, f32[2048,1408]{1,0:T(8,128)} %fusion.28, bf16[2048,2048]{1,0:T(8,128)(2,1)} %pad_maximum_fusion.2, bf16[1408,2048]{1,0:T(8,128)(2,1)} %bitcast.181), kind=kOutput, calls=%fused_computation.3 | convolution fusion | flops 11854413824 | bytes 54525952 | tf_op jit(solution)/shard_map/dot_general | solution.py:480
  478.4 19.5 %fusion.29 = f32[2048,2048]{1,0:T(8,128)} fusion(bf16[2048,1408]{1,0:T(8,128)(2,1)} %get-tuple-element.68, bf16[2048,1408]{1,0:T(8,128)(2,1)} %bitcast.188), kind=kOutput, calls=%fused_computation.131 | convolution fusion | flops 11811160064 | bytes 28311552 | tf_op jit(solution)/shard_map/dot_general | solution.py:480
  497.8 21.5 %add_convert_fusion = bf16[2048,2048]{1,0:T(8,128)(2,1)} fusion(f32[2048,2048]{1,0:T(8,128)} %fusion.29, bf16[2048,1408]{1,0:T(8,128)(2,1)} %get-tuple-element.67, bf16[2048,1408]{1,0:T(8,128)(2,1)} %bitcast.183), kind=kOutput, calls=%fused_computation | convolution fusion | flops 11819548672 | bytes 36700160 | tf_op jit(solution)/shard_map/dot_general | solution.py:480
  519.3 4.8 fusion.18
  531.8 8.2 add_convert_fusion.5
  541.5 17.4 %convolution_convert_fusion.5 = bf16[2048,1408]{1,0:T(8,128)(2,1)S(1)} fusion(bf16[2048,1408]{1,0:T(8,128)(2,1)} %get-tuple-element.67, bf16[512,2048]{1,0:T(8,128)(2,1)} %collective-permute-done.22, bf16[512,2048]{1,0:T(8,128)(2,1)} %collective-permute-done.20, bf16[512,2048]{1,0:T(8,128)(2,1)} %collective-permute-done.19, bf16[512,2048]{1,0:T(8,128)(2,1)S(1)} %copy-done.14), kind=kOutput, calls=%fused_computation.16 | convolution fusion | flops 11847598080 | bytes 19922944 | tf_op jit(solution)/shard_map/dot_general | solution.py:476
  566.4 6.4 copy.80
  572.8 19.4 %convolution_convert_fusion.4 = bf16[2048,1408]{1,0:T(8,128)(2,1)} fusion(bf16[2048,1408]{1,0:T(8,128)(2,1)} %get-tuple-element.68, bf16[512,2048]{1,0:T(8,128)(2,1)} %collective-permute-done.22, bf16[512,2048]{1,0:T(8,128)(2,1)} %collective-permute-done.20, bf16[512,2048]{1,0:T(8,128)(2,1)} %collective-permute-done.19, bf16[512,2048]{1,0:T(8,128)(2,1)S(1)} %copy-done.15), kind=kOutput, calls=%fused_computation.15 | convolution fusion | flops 11847598080 | bytes 19922944 | tf_op jit(solution)/shard_map/dot_general | solution.py:476
  595.7 6.0 fusion.14
  604.6 18.2 %convolution_convert_fusion.3 = bf16[1408,2048]{1,0:T(8,128)(2,1)} fusion(bf16[2048,1408]{1,0:T(8,128)(2,1)} %get-tuple-element.71, bf16[512,2048]{1,0:T(8,128)(2,1)} %collective-permute-done.13, bf16[512,2048]{1,0:T(8,128)(2,1)} %collective-permute-done.12, bf16[512,2048]{1,0:T(8,128)(2,1)} %collective-permute-done.11, bf16[512,2048]{1,0:T(8,128)(2,1)} %bitcast.15), kind=kOutput, calls=%fused_computation.14 | convolution fusion | flops 11847598080 | bytes 19922944 | tf_op jit(solution)/shard_map/dot_general | solution.py:476
  629.5 6.3 copy.81
  635.7 7.0 add_convert_fusion.2
  642.7 16.9 %convolution_convert_fusion.1 = bf16[2048,2048]{1,0:T(8,128)(2,1)S(1)} fusion(bf16[2048,1408]{1,0:T(8,128)(2,1)} %get-tuple-element.71, bf16[1408,2048]{1,0:T(8,128)(2,1)} %bitcast.182), kind=kOutput, calls=%fused_computation.12 | convolution fusion | flops 11815354368 | bytes 19922944 | tf_op jit(solution)/shard_map/dot_general | solution.py:472
  665.2 6.5 pad_maximum_fusion.3
  685.1 4.6 add_convert_fusion.4
  689.7 10.0 fusion.30.gm
  699.7 13.8 %collective-permute-done.36 = bf16[2,256,1408]{2,1,0:T(8,128)(2,1)} collective-permute-done((bf16[2,256,1408]{2,1,0:T(8,128)(2,1)}, bf16[2,256,1408]{2,1,0:T(8,128)(2,1)}, u32[]{:S(2)}, u32[]{:S(2)}) %collective-permute-start.36) | collective-permute-done | bytes 1441824 | tf_op jit(solution)/shard_map/ppermute | solution.py:35
  713.6 5.8 convolution_convert_fusion.7
  719.3 25.3 %attention_backward.1 = bf16[2048,640]{1,0:T(8,128)(2,1)} custom-call(s32[12]{0:T(128)} %concatenate.62.meta, bf16[2048,640]{1,0:T(8,128)(2,1)} %multiply_convert_fusion.3.qkv, s32[2048,1]{1,0:T(8,128)} %copy.55.seg_col, s32[4,1,512]{2,1,0:T(1,128)} %copy-done.27, f32[2048,512]{1,0:T(8,128)} %fusion.30.gm, bf16[2048,512]{1,0:T(8,128)(2,1)} %get-tuple-element.56.mixed, ...), custom_call_target="tpu_custom_call" | custom-call | flops 10485760 | bytes 32768 | tf_op jit(solution)/shard_map/attention_backward/pallas_call | solution.py:375
  747.4 5.4 add_add_fusion
  752.8 7.2 convolution_convert_fusion
  769.3 6.2 copy.82
  775.6 4.4 add_convert_fusion.3
  785.2 6.2 copy.83
  791.4 6.9 add_convert_fusion.1
  801.6 7.2 collective-permute-start.42
  811.0 29.9 %collective-permute-done.42 = bf16[2,176,2048]{2,1,0:T(8,128)(2,1)} collective-permute-done((bf16[2,176,2048]{2,1,0:T(8,128)(2,1)S(1)}, bf16[2,176,2048]{2,1,0:T(8,128)(2,1)}, u32[]{:S(2)}, u32[]{:S(2)}) %collective-permute-start.42) | collective-permute-done | bytes 1441824 | tf_op jit(solution)/shard_map/ppermute | solution.py:35
  840.9 11.3 %convolution_convert_fusion.6 = bf16[2048,640]{1,0:T(8,128)(2,1)} fusion(bf16[2048,2048]{1,0:T(8,128)(2,1)} %get-tuple-element.124, bf16[2048,640]{1,0:T(8,128)(2,1)} %attention_backward.1), kind=kOutput, calls=%fused_computation.53 | convolution fusion | flops 5370019840 | bytes 13631488 | tf_op jit(solution)/shard_map/dot_general | solution.py:476
  852.2 19.6 %collective-permute-done.45 = bf16[2,176,2048]{2,1,0:T(8,128)(2,1)} collective-permute-done((bf16[2,176,2048]{2,1,0:T(8,128)(2,1)}, bf16[2,176,2048]{2,1,0:T(8,128)(2,1)}, u32[]{:S(2)}, u32[]{:S(2)}) %collective-permute-start.45) | collective-permute-done | bytes 1441824 | tf_op jit(solution)/shard_map/ppermute | solution.py:35
  883.0 42.4 %collective-permute-done.41 = bf16[512,2048]{1,0:T(8,128)(2,1)S(1)} collective-permute-done((bf16[512,2048]{1,0:T(8,128)(2,1)}, bf16[512,2048]{1,0:T(8,128)(2,1)S(1)}, u32[]{:S(2)}, u32[]{:S(2)}) %collective-permute-start.41) | collective-permute-done | bytes 2097184 | tf_op jit(solution)/shard_map/ppermute | solution.py:110
  925.4 4.7 convert_add_fusion.2
  949.8 6.3 fusion.8
  956.1 30.3 %collective-permute-done.62.refs_2_ = bf16[176,2048]{1,0:T(8,128)(2,1)} collective-permute-done((bf16[176,2048]{1,0:T(8,128)(2,1)}, bf16[176,2048]{1,0:T(8,128)(2,1)}, u32[]{:S(2)}, u32[]{:S(2)}) %collective-permute-start.62) | collective-permute-done | bytes 720928 | tf_op jit(solution)/shard_map/ppermute | solution.py:110
  995.9 6.1 collective-permute-start.49
  1031.5 9.2 bitcast_multiply_fusion
  1040.7 6.2 copy.78
  1046.9 6.2 copy.79
  1053.7 5.2 finish_rows.1
  1058.9 17.2 %collective-permute-start.46 = (bf16[256,640]{1,0:T(8,128)(2,1)S(1)}, bf16[256,640]{1,0:T(8,128)(2,1)S(1)}, u32[]{:S(2)}, u32[]{:S(2)}) collective-permute-start(bf16[256,640]{1,0:T(8,128)(2,1)S(1)} %copy-done.26), channel_id=1, source_target_pairs={{0,8},{8,0},{16,24},{24,16},{1,9},{9,1},{17,25},{25,17},{2,10},{10... | collective-permute-start | bytes 983048 | tf_op jit(solution)/shard_map/ppermute | solution.py:105
  (317 shorter events, 256.6 us)
Async XLA Ops:
  7.2 40.8 %all-gather.8.cloned.1.call-start = ((), (), s32[]{:S(2)}) async-start(), calls=%async_computation.5 | async-start | bytes 1638400 | tf_op jit(solution)/shard_map/all_gather | solution.py:67
  7.3 46.9 %collective-permute-start.4 = (bf16[512,2048]{1,0:T(8,128)(2,1)}, bf16[512,2048]{1,0:T(8,128)(2,1)}, u32[]{:S(2)}, u32[]{:S(2)}) collective-permute-start(bf16[512,2048]{1,0:T(8,128)(2,1)} %bitcast.167), channel_id=1, source_target_pairs={{0,16},{8,24},{16,0},{24,8},{1,17},{9,25},{17,1},{25,9},{2,18},{10... | collective-permute-start | bytes 6291464 | tf_op jit(solution)/shard_map/ppermute | solution.py:110
  12.1 84.7 %all-gather.14.cloned.1.call-start = ((), (), s32[]{:S(2)}) async-start(), calls=%async_computation.13 | async-start | bytes 1310720 | tf_op jit(solution)/shard_map/all_gather | solution.py:67
  13.4 14.1 %collective-permute-start.5 = (bf16[64,2048]{1,0:T(8,128)(2,1)S(1)}, bf16[64,2048]{1,0:T(8,128)(2,1)S(1)}, u32[]{:S(2)}, u32[]{:S(2)}) collective-permute-start(bf16[64,2048]{1,0:T(8,128)(2,1)S(1)} %get-tuple-element.155), channel_id=1, source_target_pairs={{0,0},{1,4},{10,8},{11,12},{20,16},{21,20},{30,24},{31,28}} | collective-permute-start | bytes 786440 | tf_op jit(solution)/shard_map/ppermute | solution.py:182
  14.7 12.8 %collective-permute-start.6 = (bf16[64,2048]{1,0:T(8,128)(2,1)S(1)}, bf16[64,2048]{1,0:T(8,128)(2,1)S(1)}, u32[]{:S(2)}, u32[]{:S(2)}) collective-permute-start(bf16[64,2048]{1,0:T(8,128)(2,1)S(1)} %get-tuple-element.154), channel_id=1, source_target_pairs={{0,1},{1,5},{10,9},{11,13},{20,17},{21,21},{30,25},{31,29}} | collective-permute-start | bytes 786440 | tf_op jit(solution)/shard_map/ppermute | solution.py:182
  15.4 12.1 %collective-permute-start.7 = (bf16[64,2048]{1,0:T(8,128)(2,1)S(1)}, bf16[64,2048]{1,0:T(8,128)(2,1)S(1)}, u32[]{:S(2)}, u32[]{:S(2)}) collective-permute-start(bf16[64,2048]{1,0:T(8,128)(2,1)S(1)} %get-tuple-element.157), channel_id=1, source_target_pairs={{0,2},{1,6},{10,10},{11,14},{20,18},{21,22},{30,26},{31,30}} | collective-permute-start | bytes 786440 | tf_op jit(solution)/shard_map/ppermute | solution.py:182
  16.1 11.4 %collective-permute-start.8 = (bf16[64,2048]{1,0:T(8,128)(2,1)S(1)}, bf16[64,2048]{1,0:T(8,128)(2,1)S(1)}, u32[]{:S(2)}, u32[]{:S(2)}) collective-permute-start(bf16[64,2048]{1,0:T(8,128)(2,1)S(1)} %get-tuple-element.156), channel_id=1, source_target_pairs={{0,3},{1,7},{10,11},{11,15},{20,19},{21,23},{30,27},{31,31}} | collective-permute-start | bytes 786440 | tf_op jit(solution)/shard_map/ppermute | solution.py:182
  27.5 40.3 %collective-permute-start.3 = (bf16[512,2048]{1,0:T(8,128)(2,1)}, bf16[512,2048]{1,0:T(8,128)(2,1)}, u32[]{:S(2)}, u32[]{:S(2)}) collective-permute-start(bf16[512,2048]{1,0:T(8,128)(2,1)} %bitcast.168), channel_id=1, source_target_pairs={{0,8},{8,0},{16,24},{24,16},{1,9},{9,1},{17,25},{25,17},{2,10},{10... | collective-permute-start | bytes 6291464 | tf_op jit(solution)/shard_map/ppermute | solution.py:105
  54.1 13.6 %collective-permute-start.9 = (bf16[512,2048]{1,0:T(8,128)(2,1)}, bf16[512,2048]{1,0:T(8,128)(2,1)}, u32[]{:S(2)}, u32[]{:S(2)}) collective-permute-start(bf16[512,2048]{1,0:T(8,128)(2,1)} %collective-permute-done.4), channel_id=1, source_target_pairs={{0,8},{8,0},{16,24},{24,16},{1,9},{9,1},{17,25},{25,17},{2,10},{10... | collective-permute-start | bytes 6291464 | tf_op jit(solution)/shard_map/ppermute | solution.py:105
  55.7 32.1 %collective-permute-start.10 = (bf16[4,256,640]{2,1,0:T(8,128)(2,1)}, bf16[4,256,640]{2,1,0:T(8,128)(2,1)}, u32[]{:S(2)}, u32[]{:S(2)}) collective-permute-start(bf16[4,256,640]{2,1,0:T(8,128)(2,1)} %all-gather.8.cloned.1.call-done.own), channel_id=1, source_target_pairs={{0,1},{1,0},{2,3},{3,2},{4,5},{5,4},{6,7},{7,6},{8,9},{9,8},{10,11... | collective-permute-start | bytes 3932168 | tf_op jit(solution)/shard_map/ppermute | solution.py:35
  58.6 7.4 collective-permute-start.1
  67.7 119.2 %all-gather.10.cloned.1.call-start = ((), (), s32[]{:S(2)}) async-start(), calls=%async_computation.6 | async-start | bytes 3604480 | tf_op jit(solution)/shard_map/all_gather | solution.py:67
  87.8 49.8 %collective-permute-start.12 = (bf16[512,2048]{1,0:T(8,128)(2,1)}, bf16[512,2048]{1,0:T(8,128)(2,1)}, u32[]{:S(2)}, u32[]{:S(2)}) collective-permute-start(bf16[512,2048]{1,0:T(8,128)(2,1)} %bitcast.15), channel_id=1, source_target_pairs={{0,16},{8,24},{16,0},{24,8},{1,17},{9,25},{17,1},{25,9},{2,18},{10... | collective-permute-start | bytes 6291464 | tf_op jit(solution)/shard_map/ppermute | solution.py:110
  96.8 24.2 %collective-permute-start.14 = (bf16[4,64,2048]{2,1,0:T(8,128)(2,1)}, bf16[4,64,2048]{2,1,0:T(8,128)(2,1)}, u32[]{:S(2)}, u32[]{:S(2)}) collective-permute-start(bf16[4,64,2048]{2,1,0:T(8,128)(2,1)} %bitcast.202), channel_id=1, source_target_pairs={{0,1},{1,0},{2,3},{3,2},{4,5},{5,4},{6,7},{7,6},{8,9},{9,8},{10,11... | collective-permute-start | bytes 3145736 | tf_op jit(solution)/shard_map/ppermute | solution.py:35
  112.2 177.3 %all-gather.16.cloned.1.call-start = ((), (), s32[]{:S(2)}) async-start(), calls=%async_computation.14 | async-start | bytes 3604480 | tf_op jit(solution)/shard_map/all_gather | solution.py:67
  127.4 37.9 %collective-permute-start.11 = (bf16[512,2048]{1,0:T(8,128)(2,1)}, bf16[512,2048]{1,0:T(8,128)(2,1)}, u32[]{:S(2)}, u32[]{:S(2)}) collective-permute-start(bf16[512,2048]{1,0:T(8,128)(2,1)} %bitcast.15), channel_id=1, source_target_pairs={{0,8},{8,0},{16,24},{24,16},{1,9},{9,1},{17,25},{25,17},{2,10},{10... | collective-permute-start | bytes 6291464 | tf_op jit(solution)/shard_map/ppermute | solution.py:105
  137.6 27.6 %collective-permute-start.13 = (bf16[512,2048]{1,0:T(8,128)(2,1)}, bf16[512,2048]{1,0:T(8,128)(2,1)}, u32[]{:S(2)}, u32[]{:S(2)}) collective-permute-start(bf16[512,2048]{1,0:T(8,128)(2,1)} %collective-permute-done.12), channel_id=1, source_target_pairs={{0,8},{8,0},{16,24},{24,16},{1,9},{9,1},{17,25},{25,17},{2,10},{10... | collective-permute-start | bytes 6291464 | tf_op jit(solution)/shard_map/ppermute | solution.py:105
  177.6 131.6 %all-gather.12.cloned.1.call-start = ((), (), s32[]{:S(2)}) async-start(), calls=%async_computation.7 | async-start | bytes 3604480 | tf_op jit(solution)/shard_map/all_gather | solution.py:67
  178.0 17.6 %collective-permute-start.15 = (bf16[512,2048]{1,0:T(8,128)(2,1)}, bf16[512,2048]{1,0:T(8,128)(2,1)}, u32[]{:S(2)}, u32[]{:S(2)}) collective-permute-start(bf16[512,2048]{1,0:T(8,128)(2,1)} %get-tuple-element.136), channel_id=1, source_target_pairs={{0,8},{8,0},{16,24},{24,16},{1,9},{9,1},{17,25},{25,17},{2,10},{10... | collective-permute-start | bytes 6291464 | tf_op jit(solution)/shard_map/ppermute | solution.py:105
  185.5 47.4 %collective-permute-start.17 = (bf16[512,2048]{1,0:T(8,128)(2,1)}, bf16[512,2048]{1,0:T(8,128)(2,1)}, u32[]{:S(2)}, u32[]{:S(2)}) collective-permute-start(bf16[512,2048]{1,0:T(8,128)(2,1)} %add_convert_fusion.6), channel_id=1, source_target_pairs={{0,16},{8,24},{16,0},{24,8},{1,17},{9,25},{17,1},{25,9},{2,18},{10... | collective-permute-start | bytes 6291464 | tf_op jit(solution)/shard_map/ppermute | solution.py:110
  190.5 47.6 %collective-permute-start.18 = (bf16[2,256,1408]{2,1,0:T(8,128)(2,1)}, bf16[2,256,1408]{2,1,0:T(8,128)(2,1)}, u32[]{:S(2)}, u32[]{:S(2)}) collective-permute-start(bf16[2,256,1408]{2,1,0:T(8,128)(2,1)} %get-tuple-element.151), channel_id=1, source_target_pairs={{0,1},{1,0},{2,3},{3,2},{4,5},{5,4},{6,7},{7,6},{8,9},{9,8},{10,11... | collective-permute-start | bytes 4325384 | tf_op jit(solution)/shard_map/ppermute | solution.py:35
  195.5 645.4 %reduce-scatter.8.cloned.1.call-start = ((), (), s32[]{:S(2)}) async-start(), calls=%async_computation.9 | async-start | bytes 3604480 | tf_op jit(solution)/shard_map/reduce_scatter | solution.py:63
  241.4 46.3 %collective-permute-start.20 = (bf16[512,2048]{1,0:T(8,128)(2,1)S(1)}, bf16[512,2048]{1,0:T(8,128)(2,1)}, u32[]{:S(2)}, u32[]{:S(2)}) collective-permute-start(bf16[512,2048]{1,0:T(8,128)(2,1)S(1)} %get-tuple-element.121), channel_id=1, source_target_pairs={{0,16},{8,24},{16,0},{24,8},{1,17},{9,25},{17,1},{25,9},{2,18},{10... | collective-permute-start | bytes 6291464 | tf_op jit(solution)/shard_map/ppermute | solution.py:110
  242.8 34.4 %collective-permute-start.21 = (bf16[2,256,1408]{2,1,0:T(8,128)(2,1)S(1)}, bf16[2,256,1408]{2,1,0:T(8,128)(2,1)S(1)}, u32[]{:S(2)}, u32[]{:S(2)}) collective-permute-start(bf16[2,256,1408]{2,1,0:T(8,128)(2,1)S(1)} %copy-done.23), channel_id=1, source_target_pairs={{0,1},{1,0},{2,3},{3,2},{4,5},{5,4},{6,7},{7,6},{8,9},{9,8},{10,11... | collective-permute-start | bytes 4325384 | tf_op jit(solution)/shard_map/ppermute | solution.py:35
  246.5 64.3 %collective-permute-start.19 = (bf16[512,2048]{1,0:T(8,128)(2,1)S(1)}, bf16[512,2048]{1,0:T(8,128)(2,1)}, u32[]{:S(2)}, u32[]{:S(2)}) collective-permute-start(bf16[512,2048]{1,0:T(8,128)(2,1)S(1)} %get-tuple-element.121), channel_id=1, source_target_pairs={{0,8},{8,0},{16,24},{24,16},{1,9},{9,1},{17,25},{25,17},{2,10},{10... | collective-permute-start | bytes 6291464 | tf_op jit(solution)/shard_map/ppermute | solution.py:105
  287.7 23.1 %collective-permute-start.22 = (bf16[512,2048]{1,0:T(8,128)(2,1)}, bf16[512,2048]{1,0:T(8,128)(2,1)}, u32[]{:S(2)}, u32[]{:S(2)}) collective-permute-start(bf16[512,2048]{1,0:T(8,128)(2,1)} %collective-permute-done.20), channel_id=1, source_target_pairs={{0,8},{8,0},{16,24},{24,16},{1,9},{9,1},{17,25},{25,17},{2,10},{10... | collective-permute-start | bytes 6291464 | tf_op jit(solution)/shard_map/ppermute | solution.py:105
  293.3 130.1 %collective-permute-start.23 = (bf16[2,176,2048]{2,1,0:T(8,128)(2,1)}, bf16[2,176,2048]{2,1,0:T(8,128)(2,1)}, u32[]{:S(2)}, u32[]{:S(2)}) collective-permute-start(bf16[2,176,2048]{2,1,0:T(8,128)(2,1)} %bitcast.22), channel_id=1, source_target_pairs={{0,1},{1,0},{2,3},{3,2},{4,5},{5,4},{6,7},{7,6},{8,9},{9,8},{10,11... | collective-permute-start | bytes 4325384 | tf_op jit(solution)/shard_map/ppermute | solution.py:35
  296.9 150.2 %collective-permute-start.25 = (bf16[2,176,2048]{2,1,0:T(8,128)(2,1)}, bf16[2,176,2048]{2,1,0:T(8,128)(2,1)}, u32[]{:S(2)}, u32[]{:S(2)}) collective-permute-start(bf16[2,176,2048]{2,1,0:T(8,128)(2,1)} %bitcast.26), channel_id=1, source_target_pairs={{0,1},{1,0},{2,3},{3,2},{4,5},{5,4},{6,7},{7,6},{8,9},{9,8},{10,11... | collective-permute-start | bytes 4325384 | tf_op jit(solution)/shard_map/ppermute | solution.py:35
  309.2 112.5 %collective-permute-start.24 = (bf16[4,256,1408]{2,1,0:T(8,128)(2,1)}, bf16[4,256,1408]{2,1,0:T(8,128)(2,1)S(1)}, u32[]{:S(2)}, u32[]{:S(2)}) collective-permute-start(bf16[4,256,1408]{2,1,0:T(8,128)(2,1)} %all-gather.12.cloned.1.call-done.own), channel_id=1, source_target_pairs={{0,1},{1,0},{2,3},{3,2},{4,5},{5,4},{6,7},{7,6},{8,9},{9,8},{10,11... | collective-permute-start | bytes 8650760 | tf_op jit(solution)/shard_map/ppermute | solution.py:35
  524.7 7.1 collective-permute-start.27
  540.0 53.4 %collective-permute-start.29 = (bf16[512,2048]{1,0:T(8,128)(2,1)}, bf16[512,2048]{1,0:T(8,128)(2,1)}, u32[]{:S(2)}, u32[]{:S(2)}) collective-permute-start(bf16[512,2048]{1,0:T(8,128)(2,1)} %get-tuple-element.132), channel_id=1, source_target_pairs={{0,16},{8,24},{16,0},{24,8},{1,17},{9,25},{17,1},{25,9},{2,18},{10... | collective-permute-start | bytes 6291464 | tf_op jit(solution)/shard_map/ppermute | solution.py:110
  560.6 32.8 %collective-permute-start.28 = (bf16[2,256,1408]{2,1,0:T(8,128)(2,1)}, bf16[2,256,1408]{2,1,0:T(8,128)(2,1)}, u32[]{:S(2)}, u32[]{:S(2)}) collective-permute-start(bf16[2,256,1408]{2,1,0:T(8,128)(2,1)} %slice_bitcast_fusion.1), channel_id=1, source_target_pairs={{0,1},{1,0},{2,3},{3,2},{4,5},{5,4},{6,7},{7,6},{8,9},{9,8},{10,11... | collective-permute-start | bytes 4325384 | tf_op jit(solution)/shard_map/ppermute | solution.py:35
  563.3 61.0 %collective-permute-start.32 = (bf16[2,256,1408]{2,1,0:T(8,128)(2,1)}, bf16[2,256,1408]{2,1,0:T(8,128)(2,1)}, u32[]{:S(2)}, u32[]{:S(2)}) collective-permute-start(bf16[2,256,1408]{2,1,0:T(8,128)(2,1)} %dynamic-slice_bitcast_fusion.5), channel_id=1, source_target_pairs={{0,1},{1,0},{2,3},{3,2},{4,5},{5,4},{6,7},{7,6},{8,9},{9,8},{10,11... | collective-permute-start | bytes 4325384 | tf_op jit(solution)/shard_map/ppermute | solution.py:35
  601.7 57.9 %collective-permute-start.31 = (bf16[512,2048]{1,0:T(8,128)(2,1)}, bf16[512,2048]{1,0:T(8,128)(2,1)}, u32[]{:S(2)}, u32[]{:S(2)}) collective-permute-start(bf16[512,2048]{1,0:T(8,128)(2,1)} %get-tuple-element.119), channel_id=1, source_target_pairs={{0,16},{8,24},{16,0},{24,8},{1,17},{9,25},{17,1},{25,9},{2,18},{10... | collective-permute-start | bytes 6291464 | tf_op jit(solution)/shard_map/ppermute | solution.py:110
  601.8 59.4 %collective-permute-start.30 = (bf16[512,2048]{1,0:T(8,128)(2,1)}, bf16[512,2048]{1,0:T(8,128)(2,1)}, u32[]{:S(2)}, u32[]{:S(2)}) collective-permute-start(bf16[512,2048]{1,0:T(8,128)(2,1)} %get-tuple-element.119), channel_id=1, source_target_pairs={{0,8},{8,0},{16,24},{24,16},{1,9},{9,1},{17,25},{25,17},{2,10},{10... | collective-permute-start | bytes 6291464 | tf_op jit(solution)/shard_map/ppermute | solution.py:105
  674.0 11.1 %collective-permute-start.34 = (bf16[512,2048]{1,0:T(8,128)(2,1)}, bf16[512,2048]{1,0:T(8,128)(2,1)}, u32[]{:S(2)}, u32[]{:S(2)}) collective-permute-start(bf16[512,2048]{1,0:T(8,128)(2,1)} %get-tuple-element.131), channel_id=1, source_target_pairs={{0,8},{8,0},{16,24},{24,16},{1,9},{9,1},{17,25},{25,17},{2,10},{10... | collective-permute-start | bytes 6291464 | tf_op jit(solution)/shard_map/ppermute | solution.py:105
  680.2 33.3 %collective-permute-start.36 = (bf16[2,256,1408]{2,1,0:T(8,128)(2,1)}, bf16[2,256,1408]{2,1,0:T(8,128)(2,1)}, u32[]{:S(2)}, u32[]{:S(2)}) collective-permute-start(bf16[2,256,1408]{2,1,0:T(8,128)(2,1)} %slice_bitcast_fusion), channel_id=1, source_target_pairs={{0,1},{1,0},{2,3},{3,2},{4,5},{5,4},{6,7},{7,6},{8,9},{9,8},{10,11... | collective-permute-start | bytes 4325384 | tf_op jit(solution)/shard_map/ppermute | solution.py:35
  684.2 68.5 %collective-permute-start.38 = (bf16[2,256,1408]{2,1,0:T(8,128)(2,1)}, bf16[2,256,1408]{2,1,0:T(8,128)(2,1)}, u32[]{:S(2)}, u32[]{:S(2)}) collective-permute-start(bf16[2,256,1408]{2,1,0:T(8,128)(2,1)} %dynamic-slice_bitcast_fusion.4), channel_id=1, source_target_pairs={{0,1},{1,0},{2,3},{3,2},{4,5},{5,4},{6,7},{7,6},{8,9},{9,8},{10,11... | collective-permute-start | bytes 4325384 | tf_op jit(solution)/shard_map/ppermute | solution.py:35
  684.3 245.8 %reduce-scatter.6.cloned.1.call-start = ((), (), s32[]{:S(2)}) async-start(), calls=%async_computation.8 | async-start | bytes 3604480 | tf_op jit(solution)/shard_map/reduce_scatter | solution.py:63
  684.3 62.6 %collective-permute-start.37 = (bf16[512,2048]{1,0:T(8,128)(2,1)}, bf16[512,2048]{1,0:T(8,128)(2,1)}, u32[]{:S(2)}, u32[]{:S(2)}) collective-permute-start(bf16[512,2048]{1,0:T(8,128)(2,1)} %get-tuple-element.130), channel_id=1, source_target_pairs={{0,8},{8,0},{16,24},{24,16},{1,9},{9,1},{17,25},{25,17},{2,10},{10... | collective-permute-start | bytes 6291464 | tf_op jit(solution)/shard_map/ppermute | solution.py:105
  689.7 54.9 %collective-permute-start.35 = (bf16[512,2048]{1,0:T(8,128)(2,1)}, bf16[512,2048]{1,0:T(8,128)(2,1)}, u32[]{:S(2)}, u32[]{:S(2)}) collective-permute-start(bf16[512,2048]{1,0:T(8,128)(2,1)} %add_convert_fusion.4), channel_id=1, source_target_pairs={{0,16},{8,24},{16,0},{24,8},{1,17},{9,25},{17,1},{25,9},{2,18},{10... | collective-permute-start | bytes 6291464 | tf_op jit(solution)/shard_map/ppermute | solution.py:110
  764.6 10.9 collective-permute-start.40
  798.4 150.4 %reduce-scatter.14.cloned.1.call-start = ((), (), s32[]{:S(2)}) async-start(), calls=%async_computation.12 | async-start | bytes 3604480 | tf_op jit(solution)/shard_map/reduce_scatter | solution.py:63
  801.6 39.3 %collective-permute-start.42 = (bf16[2,176,2048]{2,1,0:T(8,128)(2,1)S(1)}, bf16[2,176,2048]{2,1,0:T(8,128)(2,1)}, u32[]{:S(2)}, u32[]{:S(2)}) collective-permute-start(bf16[2,176,2048]{2,1,0:T(8,128)(2,1)S(1)} %get-tuple-element.143), channel_id=1, source_target_pairs={{0,1},{1,0},{2,3},{3,2},{4,5},{5,4},{6,7},{7,6},{8,9},{9,8},{10,11... | collective-permute-start | bytes 4325384 | tf_op jit(solution)/shard_map/ppermute | solution.py:35
  808.8 63.0 %collective-permute-start.45 = (bf16[2,176,2048]{2,1,0:T(8,128)(2,1)}, bf16[2,176,2048]{2,1,0:T(8,128)(2,1)}, u32[]{:S(2)}, u32[]{:S(2)}) collective-permute-start(bf16[2,176,2048]{2,1,0:T(8,128)(2,1)} %get-tuple-element.142), channel_id=1, source_target_pairs={{0,1},{1,0},{2,3},{3,2},{4,5},{5,4},{6,7},{7,6},{8,9},{9,8},{10,11... | collective-permute-start | bytes 4325384 | tf_op jit(solution)/shard_map/ppermute | solution.py:35
  877.2 118.7 %reduce-scatter.12.cloned.1.call-start = ((), (), s32[]{:S(2)}) async-start(), calls=%async_computation.11 | async-start | bytes 1310720 | tf_op jit(solution)/shard_map/reduce_scatter | solution.py:63
  877.9 47.4 %collective-permute-start.41 = (bf16[512,2048]{1,0:T(8,128)(2,1)}, bf16[512,2048]{1,0:T(8,128)(2,1)S(1)}, u32[]{:S(2)}, u32[]{:S(2)}) collective-permute-start(bf16[512,2048]{1,0:T(8,128)(2,1)} %add_convert_fusion.3), channel_id=1, source_target_pairs={{0,16},{8,24},{16,0},{24,8},{1,17},{9,25},{17,1},{25,9},{2,18},{10... | collective-permute-start | bytes 6291464 | tf_op jit(solution)/shard_map/ppermute | solution.py:110
  880.3 49.8 %collective-permute-start.44 = (bf16[4,64,2048]{2,1,0:T(8,128)(2,1)}, bf16[4,64,2048]{2,1,0:T(8,128)(2,1)}, u32[]{:S(2)}, u32[]{:S(2)}) collective-permute-start(bf16[4,64,2048]{2,1,0:T(8,128)(2,1)} %dynamic-slice_bitcast_fusion.7), channel_id=1, source_target_pairs={{0,1},{1,0},{2,3},{3,2},{4,5},{5,4},{6,7},{7,6},{8,9},{9,8},{10,11... | collective-permute-start | bytes 3145736 | tf_op jit(solution)/shard_map/ppermute | solution.py:35
  883.0 51.0 %collective-permute-start.43 = (bf16[4,256,640]{2,1,0:T(8,128)(2,1)}, bf16[4,256,640]{2,1,0:T(8,128)(2,1)}, u32[]{:S(2)}, u32[]{:S(2)}) collective-permute-start(bf16[4,256,640]{2,1,0:T(8,128)(2,1)} %dynamic-slice_bitcast_fusion.6), channel_id=1, source_target_pairs={{0,1},{1,0},{2,3},{3,2},{4,5},{5,4},{6,7},{7,6},{8,9},{9,8},{10,11... | collective-permute-start | bytes 3932168 | tf_op jit(solution)/shard_map/ppermute | solution.py:35
  933.1 90.8 %reduce-scatter.10.cloned.1.call-start = ((), (), s32[]{:S(2)}) async-start(), calls=%async_computation.10 | async-start | bytes 1638400 | tf_op jit(solution)/shard_map/reduce_scatter | solution.py:63
  936.6 51.1 %collective-permute-start.55 = (bf16[256,1408]{0,1:T(8,128)(2,1)}, bf16[256,1408]{0,1:T(8,128)(2,1)}, u32[]{:S(2)}, u32[]{:S(2)}) collective-permute-start(bf16[256,1408]{0,1:T(8,128)(2,1)} %reduce-scatter.8.cloned.1.call-done), channel_id=1, source_target_pairs={{0,8},{8,0},{16,24},{24,16},{1,9},{9,1},{17,25},{25,17},{2,10},{10... | collective-permute-start | bytes 2162696 | tf_op jit(solution)/shard_map/ppermute | solution.py:105
  937.5 49.8 %collective-permute-start.56 = (bf16[256,1408]{0,1:T(8,128)(2,1)}, bf16[256,1408]{0,1:T(8,128)(2,1)}, u32[]{:S(2)}, u32[]{:S(2)}) collective-permute-start(bf16[256,1408]{0,1:T(8,128)(2,1)} %reduce-scatter.8.cloned.1.call-done), channel_id=1, source_target_pairs={{0,16},{8,24},{16,0},{24,8},{1,17},{9,25},{17,1},{25,9},{2,18},{10... | collective-permute-start | bytes 2162696 | tf_op jit(solution)/shard_map/ppermute | solution.py:110
  938.4 53.5 %collective-permute-start.58 = (bf16[256,1408]{0,1:T(8,128)(2,1)}, bf16[256,1408]{0,1:T(8,128)(2,1)}, u32[]{:S(2)}, u32[]{:S(2)}) collective-permute-start(bf16[256,1408]{0,1:T(8,128)(2,1)} %reduce-scatter.6.cloned.1.call-done), channel_id=1, source_target_pairs={{0,8},{8,0},{16,24},{24,16},{1,9},{9,1},{17,25},{25,17},{2,10},{10... | collective-permute-start | bytes 2162696 | tf_op jit(solution)/shard_map/ppermute | solution.py:105
  938.7 48.6 %collective-permute-start.59 = (bf16[256,1408]{0,1:T(8,128)(2,1)}, bf16[256,1408]{0,1:T(8,128)(2,1)}, u32[]{:S(2)}, u32[]{:S(2)}) collective-permute-start(bf16[256,1408]{0,1:T(8,128)(2,1)} %reduce-scatter.6.cloned.1.call-done), channel_id=1, source_target_pairs={{0,16},{8,24},{16,0},{24,8},{1,17},{9,25},{17,1},{25,9},{2,18},{10... | collective-permute-start | bytes 2162696 | tf_op jit(solution)/shard_map/ppermute | solution.py:110
  948.8 37.6 %collective-permute-start.62 = (bf16[176,2048]{1,0:T(8,128)(2,1)}, bf16[176,2048]{1,0:T(8,128)(2,1)}, u32[]{:S(2)}, u32[]{:S(2)}) collective-permute-start(bf16[176,2048]{1,0:T(8,128)(2,1)} %reduce-scatter.14.cloned.1.call-done.refs_0_), channel_id=1, source_target_pairs={{0,16},{8,24},{16,0},{24,8},{1,17},{9,25},{17,1},{25,9},{2,18},{10... | collective-permute-start | bytes 2162696 | tf_op jit(solution)/shard_map/ppermute | solution.py:110
  986.4 67.3 %collective-permute-start.61 = (bf16[176,2048]{1,0:T(8,128)(2,1)}, bf16[176,2048]{1,0:T(8,128)(2,1)}, u32[]{:S(2)}, u32[]{:S(2)}) collective-permute-start(bf16[176,2048]{1,0:T(8,128)(2,1)} %reduce-scatter.14.cloned.1.call-done.refs_0_), channel_id=1, source_target_pairs={{0,8},{8,0},{16,24},{24,16},{1,9},{9,1},{17,25},{25,17},{2,10},{10... | collective-permute-start | bytes 2162696 | tf_op jit(solution)/shard_map/ppermute | solution.py:105
  987.2 66.4 %collective-permute-start.63 = (bf16[176,2048]{1,0:T(8,128)(2,1)}, bf16[176,2048]{1,0:T(8,128)(2,1)}, u32[]{:S(2)}, u32[]{:S(2)}) collective-permute-start(bf16[176,2048]{1,0:T(8,128)(2,1)} %collective-permute-done.62.refs_2_), channel_id=1, source_target_pairs={{0,8},{8,0},{16,24},{24,16},{1,9},{9,1},{17,25},{25,17},{2,10},{10... | collective-permute-start | bytes 2162696 | tf_op jit(solution)/shard_map/ppermute | solution.py:105
  987.3 14.8 %collective-permute-start.57 = (bf16[256,1408]{0,1:T(8,128)(2,1)}, bf16[256,1408]{0,1:T(8,128)(2,1)S(1)}, u32[]{:S(2)}, u32[]{:S(2)}) collective-permute-start(bf16[256,1408]{0,1:T(8,128)(2,1)} %collective-permute-done.56), channel_id=1, source_target_pairs={{0,8},{8,0},{16,24},{24,16},{1,9},{9,1},{17,25},{25,17},{2,10},{10... | collective-permute-start | bytes 2162696 | tf_op jit(solution)/shard_map/ppermute | solution.py:105
  987.8 29.6 %collective-permute-start.60 = (bf16[256,1408]{0,1:T(8,128)(2,1)}, bf16[256,1408]{0,1:T(8,128)(2,1)S(1)}, u32[]{:S(2)}, u32[]{:S(2)}) collective-permute-start(bf16[256,1408]{0,1:T(8,128)(2,1)} %collective-permute-done.59), channel_id=1, source_target_pairs={{0,8},{8,0},{16,24},{24,16},{1,9},{9,1},{17,25},{25,17},{2,10},{10... | collective-permute-start | bytes 2162696 | tf_op jit(solution)/shard_map/ppermute | solution.py:105
  995.9 9.8 collective-permute-start.49
  1009.9 17.3 %collective-permute-start.53 = (bf16[256,2048]{1,0:T(8,128)(2,1)}, bf16[256,2048]{1,0:T(8,128)(2,1)}, u32[]{:S(2)}, u32[]{:S(2)}) collective-permute-start(bf16[256,2048]{1,0:T(8,128)(2,1)} %constant_dynamic-update-slice_fusion), channel_id=1, source_target_pairs={{0,16},{1,17},{10,26},{11,27},{20,4},{21,5},{30,14},{31,15}} | collective-permute-start | bytes 3145736 | tf_op jit(solution)/shard_map/ppermute | solution.py:195
  1023.9 53.6 %collective-permute-start.47 = (bf16[256,640]{1,0:T(8,128)(2,1)}, bf16[256,640]{1,0:T(8,128)(2,1)S(1)}, u32[]{:S(2)}, u32[]{:S(2)}) collective-permute-start(bf16[256,640]{1,0:T(8,128)(2,1)} %reduce-scatter.10.cloned.1.call-done), channel_id=1, source_target_pairs={{0,16},{8,24},{16,0},{24,8},{1,17},{9,25},{17,1},{25,9},{2,18},{10... | collective-permute-start | bytes 983048 | tf_op jit(solution)/shard_map/ppermute | solution.py:110
  1030.1 65.3 %collective-permute-start.54 = (bf16[256,2048]{1,0:T(8,128)(2,1)}, bf16[256,2048]{1,0:T(8,128)(2,1)}, u32[]{:S(2)}, u32[]{:S(2)}) collective-permute-start(bf16[256,2048]{1,0:T(8,128)(2,1)} %add.246), channel_id=1, source_target_pairs={{0,8},{16,24},{1,9},{17,25},{10,2},{26,18},{11,3},{27,19},{4,12},{... | collective-permute-start | bytes 3145736 | tf_op jit(solution)/shard_map/ppermute | solution.py:202
  1058.9 20.1 %collective-permute-start.46 = (bf16[256,640]{1,0:T(8,128)(2,1)S(1)}, bf16[256,640]{1,0:T(8,128)(2,1)S(1)}, u32[]{:S(2)}, u32[]{:S(2)}) collective-permute-start(bf16[256,640]{1,0:T(8,128)(2,1)S(1)} %copy-done.26), channel_id=1, source_target_pairs={{0,8},{8,0},{16,24},{24,16},{1,9},{9,1},{17,25},{25,17},{2,10},{10... | collective-permute-start | bytes 983048 | tf_op jit(solution)/shard_map/ppermute | solution.py:105
  (53 other events, 774.3 us)
Sparse Core Ops, SparseCore 0:
  12.2 35.7 all-gather.7
  67.8 28.8 all-gather.13
  112.4 57.1 all-gather.9
  177.7 62.2 all-gather.15
  241.9 57.7 all-gather.11
  684.4 58.4 reduce-scatter.7
  798.5 63.6 reduce-scatter.5
  877.4 58.3 reduce-scatter.13
  938.6 25.7 reduce-scatter.11
  967.1 30.0 reduce-scatter.9

commit v7 on v5

--- a/solution.py
+++ b/solution.py
@@ -61,29 +61,32 @@
     return lax.all_gather(block, F, axis=0, axis_index_groups=line_groups())
 
 
-def assemble_kernel(own, other, out, sems, *, m):
+def assemble_kernel(own, *refs, m, pieces):
     side = lax.rem(lax.axis_index(F), 2)
+    out, sems = refs[pieces], refs[pieces + 1]
+    size = m // pieces
     copies = []
     for k in range(m):
+        other = refs[k // size].at[k % size]
         copies.append(pltpu.make_async_copy(own.at[k], out.at[2 * k + side], sems.at[k]))
-        copies.append(pltpu.make_async_copy(other.at[k], out.at[2 * k + 1 - side], sems.at[m + k]))
+        copies.append(pltpu.make_async_copy(other, out.at[2 * k + 1 - side], sems.at[m + k]))
     for copy in copies:
         copy.start()
     for copy in copies:
         copy.wait()
 
 
-def assemble(own, other):
+def assemble(own, *other):
     m, rows, width = own.shape
     out = pl.pallas_call(
-        functools.partial(assemble_kernel, m=m),
+        functools.partial(assemble_kernel, m=m, pieces=len(other)),
         out_shape=jax.ShapeDtypeStruct((2 * m, rows, width), own.dtype),
-        in_specs=[pl.BlockSpec(memory_space=pl.ANY)] * 2,
+        in_specs=[pl.BlockSpec(memory_space=pl.ANY)] * (1 + len(other)),
         out_specs=pl.BlockSpec(memory_space=pltpu.VMEM),
         scratch_shapes=[pltpu.SemaphoreType.DMA((2 * m,))],
         cost_estimate=pl.CostEstimate(flops=0, transcendentals=0, bytes_accessed=1024),
         name="assemble",
-    )(own, other)
+    )(own, *other)
     return out.reshape(2 * m * rows, width)
 
 
@@ -552,15 +555,18 @@
     full_out = assemble(line_out, side_swap(line_out))
     projected = mm(after(mixed, *g_parts), full_out).astype(BF)
     sums = add_cores(blocks(projected))
-    residual = own.astype(F32) + add_chips(sums)
+    low, high = jnp.split(after(line_gate, *sums), 2)
+    other_gate = [side_swap(low), side_swap(high)]
+    residual = after(own.astype(F32) + add_chips(sums), other_gate[0])
 
     scale_two = inverse_rms(residual)
     unit_two = residual * scale_two
-    full_gate = assemble(line_gate, side_swap(after(line_gate, *sums)))
+    full_gate = assemble(line_gate, *other_gate)
     n_all = jnp.concatenate(spread(unit_two.astype(BF)), axis=0)
     g_all = jnp.concatenate(g_parts, axis=0)
-    full_up = assemble(line_up, side_swap(after(line_up, unit_two)))
+    other_up = side_swap(after(line_up, unit_two))
     gate = mm(n_all, full_gate)
+    full_up = assemble(line_up, after(other_up, gate))
     full_down = assemble(line_down, side_swap(after(line_down, n_all)))
     up = mm(after(n_all, gate), full_up)
     grad_hidden = mm_nt(after(g_all, up), full_down)
@@ -593,25 +599,26 @@
     grad_mixed = mm_nt(b_all, full_out)
     total_out = mm_tn(mixed, after(b_all, grad_mixed)).astype(BF)
     mine_out, sent_out = scatter_sides(total_out)
-    both_up = add_sides(mine_up, after(sent_up, total_out))
-    sum_up = scatter_lines(both_up)
     grad_qkv = attention_backward(
-        meta, qkv, seg_col, seg_row, after(grad_mixed, both_up, *out_sums), mixed, den, scale_one, heads, rows
+        meta, qkv, seg_col, seg_row, after(grad_mixed, total_out, *out_sums), mixed, den, scale_one, heads, rows
     )
     block_out = residual + after(add_chips([jnp.zeros_like(out_sums[0])] + out_sums[1:]), grad_qkv) + out_sums[0]
-    back_one = mm_nt(after(grad_qkv, block_out), full_qkv).astype(BF)
+    both_up = add_sides(mine_up, after(sent_up, grad_qkv))
+    sum_up = scatter_lines(both_up)
+    back_one = mm_nt(after(grad_qkv, block_out, both_up), full_qkv).astype(BF)
     one_sums = add_cores(blocks(back_one))
-    both_down = add_sides(mine_down, after(sent_down, *one_sums))
-    total_qkv = mm_tn(x_all, after(grad_qkv, both_down)).astype(BF)
+    total_qkv = mm_tn(x_all, after(grad_qkv, sum_gate, *one_sums)).astype(BF)
     mine_qkv, sent_qkv = scatter_sides(total_qkv)
     grad_unit_one = add_chips(one_sums)
+    both_down = add_sides(mine_down, after(sent_down, total_qkv, grad_unit_one))
     sum_down = scatter_lines(both_down)
-    both_out = add_sides(mine_out, after(sent_out, both_down))
+    both_out = add_sides(mine_out, after(sent_out, both_down, sum_up))
     sum_out = scatter_lines(both_out)
-    both_qkv = add_sides(mine_qkv, after(sent_qkv, both_out, grad_unit_one))
+    both_qkv = add_sides(mine_qkv, after(sent_qkv, both_out, sum_down))
     sum_qkv = scatter_lines(both_qkv)
-    sum_gate = after(sum_gate, both_qkv)
-    sum_up = after(sum_up, both_qkv, grad_unit_one)
+    sum_gate = after(sum_gate, both_out)
+    sum_up = after(sum_up, both_out)
+    sum_out = after(sum_out, both_qkv)
 
     unit_one = own.astype(F32) * inverse_rms(own.astype(F32))
     input_grad = grad_residual + grad_unit_one - unit_one * jnp.mean(

time: 1020 us -> 1050 us (1.029)
  starting transfers between devices: 71.7 us -> 99.8 us
  waiting for transfers between devices: 406 us -> 382 us
  matrix products: 229 us -> 249 us
    ppermute x10 -> x11, waiting for transfers between devices: 199 us -> 151 us  [side_swap(): return lax.ppermute(value, F, [(j, j ^ 1) for j in range(lax.axis_size(F))])]
    ppermute x12, waiting for transfers between devices: 115 us -> 149 us  [chip_shift(): return lax.ppermute(value, C, [(i, (i + 2 * k) % n) for i in range(n)])]
    ppermute x24, starting transfers between devices: 26.3 us -> 57.7 us  [core_swap(): return lax.ppermute(value, C, [(i, i ^ 1) for i in range(n)])]
    ppermute x4, waiting for transfers between devices: 17 us -> 0.35 us  [ungroup_pieces(): lax.ppermute(piece, (C, F), pairs)]
    dot_general x5, matrix products: 73.2 us -> 89 us  [mm_tn(): lax.dot_general(a, b, (((0,), (0,)), ((), ())), preferred_element_type=F32)]
    unnamed x85 -> x73, local copies, waits for them, and re-layouts: 26.4 us -> 27.6 us
  transfers between devices with their start and end apart: 69 -> 70, of which waited for: 26 -> 27; matrix products, arithmetic and copies ran while one was open for 34% -> 35% of each run, Pallas kernels for 8% -> 6%
where the time goes in v7:
time: 1050 us; the launch traced here: 1040 us
  waiting for transfers between devices  382 us (36%)
  matrix products  249 us (24%)
  other arithmetic  120 us (11%)
  starting transfers between devices  99.8 us (10%)
  local copies, waits for them, and re-layouts  94.7 us (9%)
  Pallas kernels  78.4 us (7%)
  between operations  15.1 us (1%)
    ppermute x11, waiting for transfers between devices, side_swap(): return lax.ppermute(value, F, [(j, j ^ 1) for j in range(lax.axis_size(F))])  151 us
    ppermute x12, waiting for transfers between devices, chip_shift(): return lax.ppermute(value, C, [(i, (i + 2 * k) % n) for i in range(n)])  149 us
    dot_general x5, matrix products, mm_tn(): lax.dot_general(a, b, (((0,), (0,)), ((), ())), preferred_element_type=F32)  89 us
    dot_general x5, matrix products, mm_nt(): lax.dot_general(a, b, (((1,), (1,)), ((), ())), preferred_element_type=F32)  85.2 us
    dot_general x5, matrix products, mm(): return jnp.dot(a, b, preferred_element_type=F32)  74.7 us
    ppermute x24, starting transfers between devices, core_swap(): return lax.ppermute(value, C, [(i, i ^ 1) for i in range(n)])  57.7 us
    all_gather x5, waiting for transfers between devices, gather_lines(): return lax.all_gather(block, F, axis=0, axis_index_groups=line_groups())  44 us
    unnamed x73, local copies, waits for them, and re-layouts  27.6 us
  transfers between devices with their start and end apart: 70, of which 27 were waited for; matrix products, arithmetic and copies ran while one was open for 35% of the time, Pallas kernels for 6%

profile of v7, /device:TPU:17, one launch (start us, length us, event | category | flops | bytes accessed | tf_op | source)
XLA Modules:
  0.0 1038.5 jit_solution(13553811868260560279)
XLA Ops:
  13.1 31.2 %all-gather.8.cloned.1.call-done.own = bf16[4,256,640]{2,1,0:T(8,128)(2,1)} async-done(((bf16[1,256,640]{2,1,0:T(8,128)(2,1)}), bf16[4,256,640]{2,1,0:T(8,128)(2,1)}) %all-gather.8.cloned.1.call-update) | async-done | bytes 1310736 | tf_op jit(solution)/shard_map/all_gather | solution.py:61
  44.3 9.9 collective-permute-done.4
  63.8 7.0 multiply_reduce_fusion
  71.9 7.0 collective-permute-done.10
  83.3 4.6 copy.50
  87.9 4.6 copy.52
  100.0 8.3 collective-permute-done.6.refs_0_
  119.7 10.9 %multiply_convert_fusion.3.qkv = bf16[2048,640]{1,0:T(8,128)(2,1)} fusion(bf16[2048,2048]{1,0:T(8,128)(2,1)} %get-tuple-element.120, bf16[2048,640]{1,0:T(8,128)(2,1)} %bitcast.173, f32[2048]{0:T(1024)S(1)} %add_rsqrt_fusion), kind=kOutput, calls=%fused_computation.34 | convolution fusion | flops 5371330560 | bytes 13639680 | tf_op jit(solution)/shard_map/dot_general | solution.py:466
  130.6 14.7 %attention_forward.1 = (bf16[2048,512]{1,0:T(8,128)(2,1)}, f32[2048,4]{1,0:T(8,128)}) custom-call(s32[12]{0:T(128)} %concatenate.53.meta, bf16[2048,640]{1,0:T(8,128)(2,1)} %multiply_convert_fusion.3.qkv, s32[2048,1]{1,0:T(8,128)} %copy.49.seg_col, s32[4,1,512]{2,1,0:T(1,128)} %copy-done.19), custom_call_target="tpu_custom_call" | custom-call | flops 4194304 | bytes 16384 | tf_op jit(solution)/shard_map/attention_forward/pallas_call | solution.py:341
  148.3 6.8 convolution_convert_fusion.2
  164.5 9.9 all-gather.10.cloned.1.call-done.own
  181.5 29.1 %collective-permute-done.17 = bf16[512,2048]{1,0:T(8,128)(2,1)} collective-permute-done((bf16[512,2048]{1,0:T(8,128)(2,1)}, bf16[512,2048]{1,0:T(8,128)(2,1)}, u32[]{:S(2)}, u32[]{:S(2)}) %collective-permute-start.17) | collective-permute-done | bytes 2097184 | tf_op jit(solution)/shard_map/ppermute | solution.py:104
  210.6 5.9 fusion.11
  222.9 44.0 %collective-permute-done.20 = bf16[512,2048]{1,0:T(8,128)(2,1)} collective-permute-done((bf16[512,2048]{1,0:T(8,128)(2,1)}, bf16[512,2048]{1,0:T(8,128)(2,1)}, u32[]{:S(2)}, u32[]{:S(2)}) %collective-permute-start.20) | collective-permute-done | bytes 2097184 | tf_op jit(solution)/shard_map/ppermute | solution.py:104
  271.0 7.3 pad_maximum_fusion.2
  278.3 23.9 %collective-permute-done.22.refs_1_ = bf16[2,256,1408]{2,1,0:T(8,128)(2,1)} collective-permute-done((bf16[2,256,1408]{2,1,0:T(8,128)(2,1)}, bf16[2,256,1408]{2,1,0:T(8,128)(2,1)}, u32[]{:S(2)}, u32[]{:S(2)}) %collective-permute-start.22) | collective-permute-done | bytes 1441824 | tf_op jit(solution)/shard_map/ppermute | solution.py:35
  302.2 5.2 assemble.7
  308.8 21.8 %fusion.16 = f32[2048,1408]{1,0:T(8,128)} fusion(bf16[2048,1408]{1,0:T(8,128)(2,1)} %bitcast.161, bf16[512,2048]{1,0:T(8,128)(2,1)} %collective-permute-done.21, bf16[512,2048]{1,0:T(8,128)(2,1)} %collective-permute-done.20, bf16[512,2048]{1,0:T(8,128)(2,1)} %collective-permute-done.19, bf16[512,2048]{1,0:T(8,128)(2,1)} %get-tuple-element.117), kind=kOutput, calls=%fused_computation.103 | convolution fusion | flops 11844714496 | bytes 25690112 | tf_op jit(solution)/shard_map/dot_general | solution.py:466
  330.6 40.4 %collective-permute-done.23.refs_0_ = bf16[4,256,1408]{2,1,0:T(8,128)(2,1)S(1)} collective-permute-done((bf16[4,256,1408]{2,1,0:T(8,128)(2,1)}, bf16[4,256,1408]{2,1,0:T(8,128)(2,1)S(1)}, u32[]{:S(2)}, u32[]{:S(2)}) %collective-permute-start.23) | collective-permute-done | bytes 2883616 | tf_op jit(solution)/shard_map/ppermute | solution.py:35
  371.0 8.0 pad_maximum_fusion.1
  380.3 5.2 assemble.8
  385.5 18.5 %fusion.29 = f32[2048,1408]{1,0:T(8,128)} fusion(bf16[2048,2048]{1,0:T(8,128)(2,1)} %pad_maximum_fusion.1, bf16[2048,1408]{1,0:T(8,128)(2,1)} %bitcast.165), kind=kOutput, calls=%fused_computation.116 | convolution fusion | flops 11811160064 | bytes 25690112 | tf_op jit(solution)/shard_map/dot_general | solution.py:466
  404.1 37.6 %collective-permute-done.24.refs_0_ = bf16[4,176,2048]{2,1,0:T(8,128)(2,1)S(1)} collective-permute-done((bf16[4,176,2048]{2,1,0:T(8,128)(2,1)}, bf16[4,176,2048]{2,1,0:T(8,128)(2,1)S(1)}, u32[]{:S(2)}, u32[]{:S(2)}) %collective-permute-start.24) | collective-permute-done | bytes 2883616 | tf_op jit(solution)/shard_map/ppermute | solution.py:35
  443.2 5.2 assemble.9
  448.4 26.4 %multiply_convert_fusion.1 = (bf16[2048,1408]{1,0:T(8,128)(2,1)}, bf16[2048,1408]{1,0:T(8,128)(2,1)}, bf16[2048,1408]{1,0:T(8,128)(2,1)}) fusion(f32[2048,1408]{1,0:T(8,128)} %fusion.16, f32[2048,1408]{1,0:T(8,128)} %fusion.29, bf16[2048,2048]{1,0:T(8,128)(2,1)} %pad_maximum_fusion.2, bf16[1408,2048]{1,0:T(8,128)(2,1)} %bitcast.157), kind=kOutput, calls=%fused_computation.3 | convolution fusion | flops 11854413824 | bytes 54525952 | tf_op jit(solution)/shard_map/dot_general | solution.py:474
  474.9 19.3 %fusion.30 = f32[2048,2048]{1,0:T(8,128)} fusion(bf16[2048,1408]{1,0:T(8,128)(2,1)} %get-tuple-element.63, bf16[2048,1408]{1,0:T(8,128)(2,1)} %bitcast.166), kind=kOutput, calls=%fused_computation.117 | convolution fusion | flops 11811160064 | bytes 28311552 | tf_op jit(solution)/shard_map/dot_general | solution.py:474
  494.1 21.6 %add_convert_fusion = bf16[2048,2048]{1,0:T(8,128)(2,1)} fusion(f32[2048,2048]{1,0:T(8,128)} %fusion.30, bf16[2048,1408]{1,0:T(8,128)(2,1)} %get-tuple-element.62, bf16[2048,1408]{1,0:T(8,128)(2,1)} %bitcast.162), kind=kOutput, calls=%fused_computation | convolution fusion | flops 11819548672 | bytes 36700160 | tf_op jit(solution)/shard_map/dot_general | solution.py:474
  515.7 4.8 fusion.21
  523.1 4.0 collective-permute-done.25
  530.3 6.2 add_convert_fusion.3
  537.7 17.7 %convolution_convert_fusion.5 = bf16[2048,1408]{1,0:T(8,128)(2,1)S(1)} fusion(bf16[2048,1408]{1,0:T(8,128)(2,1)} %get-tuple-element.62, bf16[512,2048]{1,0:T(8,128)(2,1)} %collective-permute-done.21, bf16[512,2048]{1,0:T(8,128)(2,1)} %collective-permute-done.20, bf16[512,2048]{1,0:T(8,128)(2,1)} %collective-permute-done.19, ...), kind=kOutput, calls=%fused_computation.16 | convolution fusion | flops 11847598080 | bytes 19922944 | tf_op jit(solution)/shard_map/dot_general | solution.py:470
  555.4 21.1 %convolution_convert_fusion.4 = bf16[2048,1408]{1,0:T(8,128)(2,1)} fusion(bf16[2048,1408]{1,0:T(8,128)(2,1)} %get-tuple-element.63, bf16[512,2048]{1,0:T(8,128)(2,1)} %collective-permute-done.21, bf16[512,2048]{1,0:T(8,128)(2,1)} %collective-permute-done.20, bf16[512,2048]{1,0:T(8,128)(2,1)} %collective-permute-done.19, ...), kind=kOutput, calls=%fused_computation.15 | convolution fusion | flops 11847598080 | bytes 19922944 | tf_op jit(solution)/shard_map/dot_general | solution.py:470
  579.5 4.0 collective-permute-done.27
  584.3 5.6 fusion.17
  592.6 29.1 %convolution_convert_fusion.3 = bf16[1408,2048]{1,0:T(8,128)(2,1)} fusion(bf16[2048,1408]{1,0:T(8,128)(2,1)} %get-tuple-element.66, bf16[512,2048]{1,0:T(8,128)(2,1)} %collective-permute-done.9, bf16[512,2048]{1,0:T(8,128)(2,1)} %collective-permute-done.8, bf16[512,2048]{1,0:T(8,128)(2,1)} %collective-permute-done.7, bf16[512,2048]{1,0:T(8,128)(2,1)} %bitcast.15), kind=kOutput, calls=%fused_computation.14 | convolution fusion | flops 11847598080 | bytes 19922944 | tf_op jit(solution)/shard_map/dot_general | solution.py:470
  621.8 16.7 %convolution_convert_fusion.1 = bf16[2048,2048]{1,0:T(8,128)(2,1)} fusion(bf16[2048,1408]{1,0:T(8,128)(2,1)} %get-tuple-element.66, bf16[1408,2048]{1,0:T(8,128)(2,1)S(1)} %bitcast.160), kind=kOutput, calls=%fused_computation.12 | convolution fusion | flops 11815354368 | bytes 19922944 | tf_op jit(solution)/shard_map/dot_general | solution.py:466
  648.7 4.0 collective-permute-done.31
  652.7 6.6 pad_maximum_fusion.3
  659.2 4.9 fusion.20
  669.3 10.6 %fusion.31.gm = f32[2048,512]{1,0:T(8,128)} fusion(bf16[2048,2048]{1,0:T(8,128)(2,1)} %pad_maximum_fusion.3, bf16[512,2048]{1,0:T(8,128)(2,1)} %bitcast.181), kind=kOutput, calls=%fused_computation.118 | convolution fusion | flops 4294967296 | bytes 14680064 | tf_op jit(solution)/shard_map/dot_general | solution.py:474
  680.3 4.6 add_convert_fusion.2
  685.2 9.6 convolution_convert_fusion.7
  694.8 24.9 %attention_backward.1 = bf16[2048,640]{1,0:T(8,128)(2,1)} custom-call(s32[12]{0:T(128)} %concatenate.53.meta, bf16[2048,640]{1,0:T(8,128)(2,1)} %multiply_convert_fusion.3.qkv, s32[2048,1]{1,0:T(8,128)} %copy.49.seg_col, s32[4,1,512]{2,1,0:T(1,128)} %copy-done.19, f32[2048,512]{1,0:T(8,128)} %fusion.31.gm, bf16[2048,512]{1,0:T(8,128)(2,1)} %get-tuple-element.53.mixed, ...), custom_call_target="tpu_custom_call" | custom-call | flops 10485760 | bytes 32768 | tf_op jit(solution)/shard_map/attention_backward/pallas_call | solution.py:369
  719.8 12.2 %collective-permute-done.35 = bf16[4,256,1408]{2,1,0:T(8,128)(2,1)} collective-permute-done((bf16[4,256,1408]{2,1,0:T(8,128)(2,1)S(1)}, bf16[4,256,1408]{2,1,0:T(8,128)(2,1)}, u32[]{:S(2)}, u32[]{:S(2)}) %collective-permute-start.35) | collective-permute-done | bytes 2883616 | tf_op jit(solution)/shard_map/ppermute | solution.py:35
  740.9 5.4 add_add_fusion
  746.3 7.4 convolution_convert_fusion
  768.8 11.5 %convolution_convert_fusion.6 = bf16[2048,640]{1,0:T(8,128)(2,1)} fusion(bf16[2048,2048]{1,0:T(8,128)(2,1)} %get-tuple-element.120, bf16[2048,640]{1,0:T(8,128)(2,1)} %attention_backward.1), kind=kOutput, calls=%fused_computation.55 | convolution fusion | flops 5370019840 | bytes 13631488 | tf_op jit(solution)/shard_map/dot_general | solution.py:470
  780.3 35.5 %collective-permute-done.38 = bf16[512,2048]{1,0:T(8,128)(2,1)} collective-permute-done((bf16[512,2048]{1,0:T(8,128)(2,1)}, bf16[512,2048]{1,0:T(8,128)(2,1)}, u32[]{:S(2)}, u32[]{:S(2)}) %collective-permute-start.38) | collective-permute-done | bytes 2097184 | tf_op jit(solution)/shard_map/ppermute | solution.py:104
  815.8 6.1 fusion.8
  821.9 5.6 collective-permute-done.41
  827.5 5.7 fusion.1
  840.3 19.4 %collective-permute-done.40 = bf16[4,64,2048]{2,1,0:T(8,128)(2,1)} collective-permute-done((bf16[4,64,2048]{2,1,0:T(8,128)(2,1)}, bf16[4,64,2048]{2,1,0:T(8,128)(2,1)}, u32[]{:S(2)}, u32[]{:S(2)}) %collective-permute-start.40) | collective-permute-done | bytes 1048608 | tf_op jit(solution)/shard_map/ppermute | solution.py:35
  867.7 6.4 fusion.10
  875.8 7.9 collective-permute-done.52
  885.0 14.1 %collective-permute-done.55 = bf16[256,1408]{0,1:T(8,128)(2,1)} collective-permute-done((bf16[256,1408]{0,1:T(8,128)(2,1)}, bf16[256,1408]{0,1:T(8,128)(2,1)}, u32[]{:S(2)}, u32[]{:S(2)}) %collective-permute-start.55) | collective-permute-done | bytes 720928 | tf_op jit(solution)/shard_map/ppermute | solution.py:104
  907.3 14.8 %reduce-scatter.14.cloned.1.call-done = bf16[64,2048]{1,0:T(8,128)(2,1)} async-done(((bf16[256,2048]{1,0:T(8,128)(2,1)}), bf16[64,2048]{1,0:T(8,128)(2,1)}) %reduce-scatter.14.cloned.1.call-update) | async-done | bytes 262160 | tf_op jit(solution)/shard_map/reduce_scatter | solution.py:57
  933.5 4.6 collective-permute-start.58
  945.3 31.7 %collective-permute-start.57 = (bf16[176,2048]{1,0:T(8,128)(2,1)}, bf16[176,2048]{1,0:T(8,128)(2,1)}, u32[]{:S(2)}, u32[]{:S(2)}) collective-permute-start(bf16[176,2048]{1,0:T(8,128)(2,1)} %reduce-scatter.10.cloned.1.call-done.refs_0_), channel_id=1, source_target_pairs={{0,8},{8,0},{16,24},{24,16},{1,9},{9,1},{17,25},{25,17},{2,10},{10... | collective-permute-start | bytes 2162696 | tf_op jit(solution)/shard_map/ppermute | solution.py:99
  979.3 5.9 bitcast_multiply_fusion
  985.1 6.2 copy.68
  991.3 6.2 copy.69
  998.1 5.2 finish_rows.1
  1008.0 4.8 collective-permute-done.43
  1025.5 4.3 finish_columns.5
  (272 shorter events, 194.0 us)
Async XLA Ops:
  7.2 37.1 %all-gather.8.cloned.1.call-start = ((), (), s32[]{:S(2)}) async-start(), calls=%async_computation.5 | async-start | bytes 1638400 | tf_op jit(solution)/shard_map/all_gather | solution.py:61
  7.2 46.9 %collective-permute-start.4 = (bf16[512,2048]{1,0:T(8,128)(2,1)}, bf16[512,2048]{1,0:T(8,128)(2,1)}, u32[]{:S(2)}, u32[]{:S(2)}) collective-permute-start(bf16[512,2048]{1,0:T(8,128)(2,1)} %bitcast.143), channel_id=1, source_target_pairs={{0,16},{8,24},{16,0},{24,8},{1,17},{9,25},{17,1},{25,9},{2,18},{10... | collective-permute-start | bytes 6291464 | tf_op jit(solution)/shard_map/ppermute | solution.py:104
  12.1 102.3 %all-gather.14.cloned.1.call-start = ((), (), s32[]{:S(2)}) async-start(), calls=%async_computation.13 | async-start | bytes 1310720 | tf_op jit(solution)/shard_map/all_gather | solution.py:61
  12.1 51.0 %collective-permute-start.3 = (bf16[512,2048]{1,0:T(8,128)(2,1)}, bf16[512,2048]{1,0:T(8,128)(2,1)}, u32[]{:S(2)}, u32[]{:S(2)}) collective-permute-start(bf16[512,2048]{1,0:T(8,128)(2,1)} %bitcast.144), channel_id=1, source_target_pairs={{0,8},{8,0},{16,24},{24,16},{1,9},{9,1},{17,25},{25,17},{2,10},{10... | collective-permute-start | bytes 6291464 | tf_op jit(solution)/shard_map/ppermute | solution.py:99
  54.1 9.6 collective-permute-start.5
  55.7 5.3 collective-permute-start.1
  56.9 4.8 collective-permute-start.2
  59.7 19.2 %collective-permute-start.10 = (bf16[64,2048]{1,0:T(8,128)(2,1)S(1)}, bf16[64,2048]{1,0:T(8,128)(2,1)S(1)}, u32[]{:S(2)}, u32[]{:S(2)}) collective-permute-start(bf16[64,2048]{1,0:T(8,128)(2,1)S(1)} %get-tuple-element.143), channel_id=1, source_target_pairs={{0,0},{1,4},{10,8},{11,12},{20,16},{21,20},{30,24},{31,28}} | collective-permute-start | bytes 786440 | tf_op jit(solution)/shard_map/ppermute | solution.py:176
  61.0 17.9 %collective-permute-start.11 = (bf16[64,2048]{1,0:T(8,128)(2,1)S(1)}, bf16[64,2048]{1,0:T(8,128)(2,1)S(1)}, u32[]{:S(2)}, u32[]{:S(2)}) collective-permute-start(bf16[64,2048]{1,0:T(8,128)(2,1)S(1)} %get-tuple-element.142), channel_id=1, source_target_pairs={{0,1},{1,5},{10,9},{11,13},{20,17},{21,21},{30,25},{31,29}} | collective-permute-start | bytes 786440 | tf_op jit(solution)/shard_map/ppermute | solution.py:176
  61.7 17.2 %collective-permute-start.12 = (bf16[64,2048]{1,0:T(8,128)(2,1)S(1)}, bf16[64,2048]{1,0:T(8,128)(2,1)S(1)}, u32[]{:S(2)}, u32[]{:S(2)}) collective-permute-start(bf16[64,2048]{1,0:T(8,128)(2,1)S(1)} %get-tuple-element.145), channel_id=1, source_target_pairs={{0,2},{1,6},{10,10},{11,14},{20,18},{21,22},{30,26},{31,30}} | collective-permute-start | bytes 786440 | tf_op jit(solution)/shard_map/ppermute | solution.py:176
  63.1 15.9 %collective-permute-start.13 = (bf16[64,2048]{1,0:T(8,128)(2,1)S(1)}, bf16[64,2048]{1,0:T(8,128)(2,1)S(1)}, u32[]{:S(2)}, u32[]{:S(2)}) collective-permute-start(bf16[64,2048]{1,0:T(8,128)(2,1)S(1)} %get-tuple-element.144), channel_id=1, source_target_pairs={{0,3},{1,7},{10,11},{11,15},{20,19},{21,23},{30,27},{31,31}} | collective-permute-start | bytes 786440 | tf_op jit(solution)/shard_map/ppermute | solution.py:176
  70.7 46.0 %collective-permute-start.8 = (bf16[512,2048]{1,0:T(8,128)(2,1)}, bf16[512,2048]{1,0:T(8,128)(2,1)}, u32[]{:S(2)}, u32[]{:S(2)}) collective-permute-start(bf16[512,2048]{1,0:T(8,128)(2,1)} %bitcast.15), channel_id=1, source_target_pairs={{0,16},{8,24},{16,0},{24,8},{1,17},{9,25},{17,1},{25,9},{2,18},{10... | collective-permute-start | bytes 6291464 | tf_op jit(solution)/shard_map/ppermute | solution.py:104
  79.7 94.7 %all-gather.10.cloned.1.call-start = ((), (), s32[]{:S(2)}) async-start(), calls=%async_computation.6 | async-start | bytes 3604480 | tf_op jit(solution)/shard_map/all_gather | solution.py:61
  79.8 28.5 %collective-permute-start.6 = (bf16[4,256,640]{2,1,0:T(8,128)(2,1)}, bf16[4,256,640]{2,1,0:T(8,128)(2,1)}, u32[]{:S(2)}, u32[]{:S(2)}) collective-permute-start(bf16[4,256,640]{2,1,0:T(8,128)(2,1)} %all-gather.8.cloned.1.call-done.own), channel_id=1, source_target_pairs={{0,1},{1,0},{2,3},{3,2},{4,5},{5,4},{6,7},{7,6},{8,9},{9,8},{10,11... | collective-permute-start | bytes 3932168 | tf_op jit(solution)/shard_map/ppermute | solution.py:35
  97.6 209.9 %all-gather.12.cloned.1.call-start = ((), (), s32[]{:S(2)}) async-start(), calls=%async_computation.7 | async-start | bytes 3604480 | tf_op jit(solution)/shard_map/all_gather | solution.py:61
  114.4 31.0 %collective-permute-start.14 = (bf16[4,64,2048]{2,1,0:T(8,128)(2,1)}, bf16[4,64,2048]{2,1,0:T(8,128)(2,1)}, u32[]{:S(2)}, u32[]{:S(2)}) collective-permute-start(bf16[4,64,2048]{2,1,0:T(8,128)(2,1)} %bitcast.182), channel_id=1, source_target_pairs={{0,1},{1,0},{2,3},{3,2},{4,5},{5,4},{6,7},{7,6},{8,9},{9,8},{10,11... | collective-permute-start | bytes 3145736 | tf_op jit(solution)/shard_map/ppermute | solution.py:35
  115.6 32.7 %collective-permute-start.7 = (bf16[512,2048]{1,0:T(8,128)(2,1)}, bf16[512,2048]{1,0:T(8,128)(2,1)}, u32[]{:S(2)}, u32[]{:S(2)}) collective-permute-start(bf16[512,2048]{1,0:T(8,128)(2,1)} %bitcast.15), channel_id=1, source_target_pairs={{0,8},{8,0},{16,24},{24,16},{1,9},{9,1},{17,25},{25,17},{2,10},{10... | collective-permute-start | bytes 6291464 | tf_op jit(solution)/shard_map/ppermute | solution.py:99
  116.7 31.6 %collective-permute-start.9 = (bf16[512,2048]{1,0:T(8,128)(2,1)}, bf16[512,2048]{1,0:T(8,128)(2,1)}, u32[]{:S(2)}, u32[]{:S(2)}) collective-permute-start(bf16[512,2048]{1,0:T(8,128)(2,1)} %collective-permute-done.8), channel_id=1, source_target_pairs={{0,8},{8,0},{16,24},{24,16},{1,9},{9,1},{17,25},{25,17},{2,10},{10... | collective-permute-start | bytes 6291464 | tf_op jit(solution)/shard_map/ppermute | solution.py:99
  157.0 24.5 %collective-permute-start.15 = (bf16[512,2048]{1,0:T(8,128)(2,1)}, bf16[512,2048]{1,0:T(8,128)(2,1)}, u32[]{:S(2)}, u32[]{:S(2)}) collective-permute-start(bf16[512,2048]{1,0:T(8,128)(2,1)} %get-tuple-element.132), channel_id=1, source_target_pairs={{0,8},{8,0},{16,24},{24,16},{1,9},{9,1},{17,25},{25,17},{2,10},{10... | collective-permute-start | bytes 6291464 | tf_op jit(solution)/shard_map/ppermute | solution.py:99
  163.2 47.4 %collective-permute-start.17 = (bf16[512,2048]{1,0:T(8,128)(2,1)}, bf16[512,2048]{1,0:T(8,128)(2,1)}, u32[]{:S(2)}, u32[]{:S(2)}) collective-permute-start(bf16[512,2048]{1,0:T(8,128)(2,1)} %add_convert_fusion.4), channel_id=1, source_target_pairs={{0,16},{8,24},{16,0},{24,8},{1,17},{9,25},{17,1},{25,9},{2,18},{10... | collective-permute-start | bytes 6291464 | tf_op jit(solution)/shard_map/ppermute | solution.py:104
  178.0 38.6 %collective-permute-start.18 = (bf16[2,256,1408]{2,1,0:T(8,128)(2,1)}, bf16[2,256,1408]{2,1,0:T(8,128)(2,1)}, u32[]{:S(2)}, u32[]{:S(2)}) collective-permute-start(bf16[2,256,1408]{2,1,0:T(8,128)(2,1)} %get-tuple-element.139), channel_id=1, source_target_pairs={{0,1},{1,0},{2,3},{3,2},{4,5},{5,4},{6,7},{7,6},{8,9},{9,8},{10,11... | collective-permute-start | bytes 4325384 | tf_op jit(solution)/shard_map/ppermute | solution.py:35
  181.5 197.5 %all-gather.16.cloned.1.call-start = ((), (), s32[]{:S(2)}) async-start(), calls=%async_computation.14 | async-start | bytes 3604480 | tf_op jit(solution)/shard_map/all_gather | solution.py:61
  220.4 46.5 %collective-permute-start.20 = (bf16[512,2048]{1,0:T(8,128)(2,1)}, bf16[512,2048]{1,0:T(8,128)(2,1)}, u32[]{:S(2)}, u32[]{:S(2)}) collective-permute-start(bf16[512,2048]{1,0:T(8,128)(2,1)} %get-tuple-element.117), channel_id=1, source_target_pairs={{0,16},{8,24},{16,0},{24,8},{1,17},{9,25},{17,1},{25,9},{2,18},{10... | collective-permute-start | bytes 6291464 | tf_op jit(solution)/shard_map/ppermute | solution.py:104
  221.6 87.2 %collective-permute-start.19 = (bf16[512,2048]{1,0:T(8,128)(2,1)}, bf16[512,2048]{1,0:T(8,128)(2,1)}, u32[]{:S(2)}, u32[]{:S(2)}) collective-permute-start(bf16[512,2048]{1,0:T(8,128)(2,1)} %get-tuple-element.117), channel_id=1, source_target_pairs={{0,8},{8,0},{16,24},{24,16},{1,9},{9,1},{17,25},{25,17},{2,10},{10... | collective-permute-start | bytes 6291464 | tf_op jit(solution)/shard_map/ppermute | solution.py:99
  266.9 41.9 %collective-permute-start.21 = (bf16[512,2048]{1,0:T(8,128)(2,1)}, bf16[512,2048]{1,0:T(8,128)(2,1)}, u32[]{:S(2)}, u32[]{:S(2)}) collective-permute-start(bf16[512,2048]{1,0:T(8,128)(2,1)} %collective-permute-done.20), channel_id=1, source_target_pairs={{0,8},{8,0},{16,24},{24,16},{1,9},{9,1},{17,25},{25,17},{2,10},{10... | collective-permute-start | bytes 6291464 | tf_op jit(solution)/shard_map/ppermute | solution.py:99
  268.8 33.5 %collective-permute-start.22 = (bf16[2,256,1408]{2,1,0:T(8,128)(2,1)}, bf16[2,256,1408]{2,1,0:T(8,128)(2,1)}, u32[]{:S(2)}, u32[]{:S(2)}) collective-permute-start(bf16[2,256,1408]{2,1,0:T(8,128)(2,1)} %get-tuple-element.138), channel_id=1, source_target_pairs={{0,1},{1,0},{2,3},{3,2},{4,5},{5,4},{6,7},{7,6},{8,9},{9,8},{10,11... | collective-permute-start | bytes 4325384 | tf_op jit(solution)/shard_map/ppermute | solution.py:35
  271.0 497.8 %reduce-scatter.6.cloned.1.call-start = ((), (), s32[]{:S(2)}) async-start(), calls=%async_computation.8 | async-start | bytes 3604480 | tf_op jit(solution)/shard_map/reduce_scatter | solution.py:57
  307.5 63.5 %collective-permute-start.23 = (bf16[4,256,1408]{2,1,0:T(8,128)(2,1)}, bf16[4,256,1408]{2,1,0:T(8,128)(2,1)S(1)}, u32[]{:S(2)}, u32[]{:S(2)}) collective-permute-start(bf16[4,256,1408]{2,1,0:T(8,128)(2,1)} %all-gather.12.cloned.1.call-done.own), channel_id=1, source_target_pairs={{0,1},{1,0},{2,3},{3,2},{4,5},{5,4},{6,7},{7,6},{8,9},{9,8},{10,11... | collective-permute-start | bytes 8650760 | tf_op jit(solution)/shard_map/ppermute | solution.py:35
  379.0 62.6 %collective-permute-start.24 = (bf16[4,176,2048]{2,1,0:T(8,128)(2,1)}, bf16[4,176,2048]{2,1,0:T(8,128)(2,1)S(1)}, u32[]{:S(2)}, u32[]{:S(2)}) collective-permute-start(bf16[4,176,2048]{2,1,0:T(8,128)(2,1)} %bitcast.169), channel_id=1, source_target_pairs={{0,1},{1,0},{2,3},{3,2},{4,5},{5,4},{6,7},{7,6},{8,9},{9,8},{10,11... | collective-permute-start | bytes 8650760 | tf_op jit(solution)/shard_map/ppermute | solution.py:35
  520.5 6.6 collective-permute-start.25
  523.1 7.1 collective-permute-start.26
  536.5 47.0 %collective-permute-start.27 = (bf16[512,2048]{1,0:T(8,128)(2,1)}, bf16[512,2048]{1,0:T(8,128)(2,1)S(1)}, u32[]{:S(2)}, u32[]{:S(2)}) collective-permute-start(bf16[512,2048]{1,0:T(8,128)(2,1)} %get-tuple-element.128), channel_id=1, source_target_pairs={{0,16},{8,24},{16,0},{24,8},{1,17},{9,25},{17,1},{25,9},{2,18},{10... | collective-permute-start | bytes 6291464 | tf_op jit(solution)/shard_map/ppermute | solution.py:104
  578.3 63.6 %collective-permute-start.30 = (bf16[4,256,1408]{2,1,0:T(8,128)(2,1)}, bf16[4,256,1408]{2,1,0:T(8,128)(2,1)S(1)}, u32[]{:S(2)}, u32[]{:S(2)}) collective-permute-start(bf16[4,256,1408]{2,1,0:T(8,128)(2,1)} %dynamic-slice_bitcast_fusion.2), channel_id=1, source_target_pairs={{0,1},{1,0},{2,3},{3,2},{4,5},{5,4},{6,7},{7,6},{8,9},{9,8},{10,11... | collective-permute-start | bytes 8650760 | tf_op jit(solution)/shard_map/ppermute | solution.py:35
  589.9 57.2 %collective-permute-start.29 = (bf16[512,2048]{1,0:T(8,128)(2,1)}, bf16[512,2048]{1,0:T(8,128)(2,1)}, u32[]{:S(2)}, u32[]{:S(2)}) collective-permute-start(bf16[512,2048]{1,0:T(8,128)(2,1)} %get-tuple-element.115), channel_id=1, source_target_pairs={{0,16},{8,24},{16,0},{24,8},{1,17},{9,25},{17,1},{25,9},{2,18},{10... | collective-permute-start | bytes 6291464 | tf_op jit(solution)/shard_map/ppermute | solution.py:104
  591.1 57.5 %collective-permute-start.28 = (bf16[512,2048]{1,0:T(8,128)(2,1)}, bf16[512,2048]{1,0:T(8,128)(2,1)}, u32[]{:S(2)}, u32[]{:S(2)}) collective-permute-start(bf16[512,2048]{1,0:T(8,128)(2,1)} %get-tuple-element.115), channel_id=1, source_target_pairs={{0,8},{8,0},{16,24},{24,16},{1,9},{9,1},{17,25},{25,17},{2,10},{10... | collective-permute-start | bytes 6291464 | tf_op jit(solution)/shard_map/ppermute | solution.py:99
  647.1 5.5 collective-permute-start.31
  664.1 16.1 %collective-permute-start.32 = (bf16[512,2048]{1,0:T(8,128)(2,1)}, bf16[512,2048]{1,0:T(8,128)(2,1)}, u32[]{:S(2)}, u32[]{:S(2)}) collective-permute-start(bf16[512,2048]{1,0:T(8,128)(2,1)} %get-tuple-element.127), channel_id=1, source_target_pairs={{0,8},{8,0},{16,24},{24,16},{1,9},{9,1},{17,25},{25,17},{2,10},{10... | collective-permute-start | bytes 6291464 | tf_op jit(solution)/shard_map/ppermute | solution.py:99
  667.9 64.1 %collective-permute-start.35 = (bf16[4,256,1408]{2,1,0:T(8,128)(2,1)S(1)}, bf16[4,256,1408]{2,1,0:T(8,128)(2,1)}, u32[]{:S(2)}, u32[]{:S(2)}) collective-permute-start(bf16[4,256,1408]{2,1,0:T(8,128)(2,1)S(1)} %dynamic-slice_bitcast_fusion.1), channel_id=1, source_target_pairs={{0,1},{1,0},{2,3},{3,2},{4,5},{5,4},{6,7},{7,6},{8,9},{9,8},{10,11... | collective-permute-start | bytes 8650760 | tf_op jit(solution)/shard_map/ppermute | solution.py:35
  669.2 190.5 %reduce-scatter.8.cloned.1.call-start = ((), (), s32[]{:S(2)}) async-start(), calls=%async_computation.9 | async-start | bytes 3604480 | tf_op jit(solution)/shard_map/reduce_scatter | solution.py:57
  679.8 60.5 %collective-permute-start.34 = (bf16[512,2048]{1,0:T(8,128)(2,1)}, bf16[512,2048]{1,0:T(8,128)(2,1)}, u32[]{:S(2)}, u32[]{:S(2)}) collective-permute-start(bf16[512,2048]{1,0:T(8,128)(2,1)} %get-tuple-element.126), channel_id=1, source_target_pairs={{0,8},{8,0},{16,24},{24,16},{1,9},{9,1},{17,25},{25,17},{2,10},{10... | collective-permute-start | bytes 6291464 | tf_op jit(solution)/shard_map/ppermute | solution.py:99
  684.9 53.2 %collective-permute-start.33 = (bf16[512,2048]{1,0:T(8,128)(2,1)}, bf16[512,2048]{1,0:T(8,128)(2,1)}, u32[]{:S(2)}, u32[]{:S(2)}) collective-permute-start(bf16[512,2048]{1,0:T(8,128)(2,1)} %add_convert_fusion.2), channel_id=1, source_target_pairs={{0,16},{8,24},{16,0},{24,8},{1,17},{9,25},{17,1},{25,9},{2,18},{10... | collective-permute-start | bytes 6291464 | tf_op jit(solution)/shard_map/ppermute | solution.py:104
  758.3 6.4 collective-permute-start.37
  759.3 144.8 %reduce-scatter.10.cloned.1.call-start = ((), (), s32[]{:S(2)}) async-start(), calls=%async_computation.10 | async-start | bytes 3604480 | tf_op jit(solution)/shard_map/reduce_scatter | solution.py:57
  763.2 64.4 %collective-permute-start.41 = (bf16[4,176,2048]{2,1,0:T(8,128)(2,1)}, bf16[4,176,2048]{2,1,0:T(8,128)(2,1)}, u32[]{:S(2)}, u32[]{:S(2)}) collective-permute-start(bf16[4,176,2048]{2,1,0:T(8,128)(2,1)} %dynamic-slice_bitcast_fusion), channel_id=1, source_target_pairs={{0,1},{1,0},{2,3},{3,2},{4,5},{5,4},{6,7},{7,6},{8,9},{9,8},{10,11... | collective-permute-start | bytes 8650760 | tf_op jit(solution)/shard_map/ppermute | solution.py:35
  764.4 15.9 %collective-permute-start.36 = (bf16[512,2048]{1,0:T(8,128)(2,1)}, bf16[512,2048]{1,0:T(8,128)(2,1)}, u32[]{:S(2)}, u32[]{:S(2)}) collective-permute-start(bf16[512,2048]{1,0:T(8,128)(2,1)} %get-tuple-element.124), channel_id=1, source_target_pairs={{0,8},{8,0},{16,24},{24,16},{1,9},{9,1},{17,25},{25,17},{2,10},{10... | collective-permute-start | bytes 6291464 | tf_op jit(solution)/shard_map/ppermute | solution.py:99
  768.5 47.3 %collective-permute-start.38 = (bf16[512,2048]{1,0:T(8,128)(2,1)}, bf16[512,2048]{1,0:T(8,128)(2,1)}, u32[]{:S(2)}, u32[]{:S(2)}) collective-permute-start(bf16[512,2048]{1,0:T(8,128)(2,1)} %add_convert_fusion.1), channel_id=1, source_target_pairs={{0,16},{8,24},{16,0},{24,8},{1,17},{9,25},{17,1},{25,9},{2,18},{10... | collective-permute-start | bytes 6291464 | tf_op jit(solution)/shard_map/ppermute | solution.py:104
  833.2 88.8 %reduce-scatter.14.cloned.1.call-start = ((), (), s32[]{:S(2)}) async-start(), calls=%async_computation.12 | async-start | bytes 1310720 | tf_op jit(solution)/shard_map/reduce_scatter | solution.py:57
  835.6 24.2 %collective-permute-start.40 = (bf16[4,64,2048]{2,1,0:T(8,128)(2,1)}, bf16[4,64,2048]{2,1,0:T(8,128)(2,1)}, u32[]{:S(2)}, u32[]{:S(2)}) collective-permute-start(bf16[4,64,2048]{2,1,0:T(8,128)(2,1)} %dynamic-slice_bitcast_fusion.4), channel_id=1, source_target_pairs={{0,1},{1,0},{2,3},{3,2},{4,5},{5,4},{6,7},{7,6},{8,9},{9,8},{10,11... | collective-permute-start | bytes 3145736 | tf_op jit(solution)/shard_map/ppermute | solution.py:35
  840.1 64.0 %collective-permute-start.39 = (bf16[4,256,640]{2,1,0:T(8,128)(2,1)}, bf16[4,256,640]{2,1,0:T(8,128)(2,1)}, u32[]{:S(2)}, u32[]{:S(2)}) collective-permute-start(bf16[4,256,640]{2,1,0:T(8,128)(2,1)} %dynamic-slice_bitcast_fusion.3), channel_id=1, source_target_pairs={{0,1},{1,0},{2,3},{3,2},{4,5},{5,4},{6,7},{7,6},{8,9},{9,8},{10,11... | collective-permute-start | bytes 3932168 | tf_op jit(solution)/shard_map/ppermute | solution.py:35
  862.7 37.4 %collective-permute-start.51 = (bf16[256,1408]{0,1:T(8,128)(2,1)}, bf16[256,1408]{0,1:T(8,128)(2,1)}, u32[]{:S(2)}, u32[]{:S(2)}) collective-permute-start(bf16[256,1408]{0,1:T(8,128)(2,1)} %reduce-scatter.6.cloned.1.call-done), channel_id=1, source_target_pairs={{0,8},{8,0},{16,24},{24,16},{1,9},{9,1},{17,25},{25,17},{2,10},{10... | collective-permute-start | bytes 2162696 | tf_op jit(solution)/shard_map/ppermute | solution.py:99
  865.7 18.0 %collective-permute-start.52 = (bf16[256,1408]{0,1:T(8,128)(2,1)}, bf16[256,1408]{0,1:T(8,128)(2,1)}, u32[]{:S(2)}, u32[]{:S(2)}) collective-permute-start(bf16[256,1408]{0,1:T(8,128)(2,1)} %reduce-scatter.6.cloned.1.call-done), channel_id=1, source_target_pairs={{0,16},{8,24},{16,0},{24,8},{1,17},{9,25},{17,1},{25,9},{2,18},{10... | collective-permute-start | bytes 2162696 | tf_op jit(solution)/shard_map/ppermute | solution.py:104
  866.0 36.4 %collective-permute-start.54 = (bf16[256,1408]{0,1:T(8,128)(2,1)}, bf16[256,1408]{0,1:T(8,128)(2,1)}, u32[]{:S(2)}, u32[]{:S(2)}) collective-permute-start(bf16[256,1408]{0,1:T(8,128)(2,1)} %reduce-scatter.8.cloned.1.call-done), channel_id=1, source_target_pairs={{0,8},{8,0},{16,24},{24,16},{1,9},{9,1},{17,25},{25,17},{2,10},{10... | collective-permute-start | bytes 2162696 | tf_op jit(solution)/shard_map/ppermute | solution.py:99
  866.2 32.9 %collective-permute-start.55 = (bf16[256,1408]{0,1:T(8,128)(2,1)}, bf16[256,1408]{0,1:T(8,128)(2,1)}, u32[]{:S(2)}, u32[]{:S(2)}) collective-permute-start(bf16[256,1408]{0,1:T(8,128)(2,1)} %reduce-scatter.8.cloned.1.call-done), channel_id=1, source_target_pairs={{0,16},{8,24},{16,0},{24,8},{1,17},{9,25},{17,1},{25,9},{2,18},{10... | collective-permute-start | bytes 2162696 | tf_op jit(solution)/shard_map/ppermute | solution.py:104
  867.5 135.8 %reduce-scatter.12.cloned.1.call-start = ((), (), s32[]{:S(2)}) async-start(), calls=%async_computation.11 | async-start | bytes 1638400 | tf_op jit(solution)/shard_map/reduce_scatter | solution.py:57
  883.7 46.6 %collective-permute-start.53 = (bf16[256,1408]{0,1:T(8,128)(2,1)}, bf16[256,1408]{0,1:T(8,128)(2,1)}, u32[]{:S(2)}, u32[]{:S(2)}) collective-permute-start(bf16[256,1408]{0,1:T(8,128)(2,1)} %collective-permute-done.52), channel_id=1, source_target_pairs={{0,8},{8,0},{16,24},{24,16},{1,9},{9,1},{17,25},{25,17},{2,10},{10... | collective-permute-start | bytes 2162696 | tf_op jit(solution)/shard_map/ppermute | solution.py:99
  899.2 33.2 %collective-permute-start.56 = (bf16[256,1408]{0,1:T(8,128)(2,1)}, bf16[256,1408]{0,1:T(8,128)(2,1)}, u32[]{:S(2)}, u32[]{:S(2)}) collective-permute-start(bf16[256,1408]{0,1:T(8,128)(2,1)} %collective-permute-done.55), channel_id=1, source_target_pairs={{0,8},{8,0},{16,24},{24,16},{1,9},{9,1},{17,25},{25,17},{2,10},{10... | collective-permute-start | bytes 2162696 | tf_op jit(solution)/shard_map/ppermute | solution.py:99
  922.0 5.8 collective-permute-start.45
  929.6 11.2 %collective-permute-start.49 = (bf16[256,2048]{1,0:T(8,128)(2,1)S(1)}, bf16[256,2048]{1,0:T(8,128)(2,1)S(1)}, u32[]{:S(2)}, u32[]{:S(2)}) collective-permute-start(bf16[256,2048]{1,0:T(8,128)(2,1)S(1)} %constant_dynamic-update-slice_fusion), channel_id=1, source_target_pairs={{0,16},{1,17},{10,26},{11,27},{20,4},{21,5},{30,14},{31,15}} | collective-permute-start | bytes 3145736 | tf_op jit(solution)/shard_map/ppermute | solution.py:189
  933.5 43.4 %collective-permute-start.58 = (bf16[176,2048]{1,0:T(8,128)(2,1)}, bf16[176,2048]{1,0:T(8,128)(2,1)}, u32[]{:S(2)}, u32[]{:S(2)}) collective-permute-start(bf16[176,2048]{1,0:T(8,128)(2,1)} %reduce-scatter.10.cloned.1.call-done.refs_0_), channel_id=1, source_target_pairs={{0,16},{8,24},{16,0},{24,8},{1,17},{9,25},{17,1},{25,9},{2,18},{10... | collective-permute-start | bytes 2162696 | tf_op jit(solution)/shard_map/ppermute | solution.py:104
  942.2 61.2 %collective-permute-start.50 = (bf16[256,2048]{1,0:T(8,128)(2,1)}, bf16[256,2048]{1,0:T(8,128)(2,1)}, u32[]{:S(2)}, u32[]{:S(2)}) collective-permute-start(bf16[256,2048]{1,0:T(8,128)(2,1)} %add.243), channel_id=1, source_target_pairs={{0,8},{16,24},{1,9},{17,25},{10,2},{26,18},{11,3},{27,19},{4,12},{... | collective-permute-start | bytes 3145736 | tf_op jit(solution)/shard_map/ppermute | solution.py:196
  945.3 52.9 %collective-permute-start.57 = (bf16[176,2048]{1,0:T(8,128)(2,1)}, bf16[176,2048]{1,0:T(8,128)(2,1)}, u32[]{:S(2)}, u32[]{:S(2)}) collective-permute-start(bf16[176,2048]{1,0:T(8,128)(2,1)} %reduce-scatter.10.cloned.1.call-done.refs_0_), channel_id=1, source_target_pairs={{0,8},{8,0},{16,24},{24,16},{1,9},{9,1},{17,25},{25,17},{2,10},{10... | collective-permute-start | bytes 2162696 | tf_op jit(solution)/shard_map/ppermute | solution.py:99
  977.0 21.2 %collective-permute-start.59 = (bf16[176,2048]{1,0:T(8,128)(2,1)}, bf16[176,2048]{1,0:T(8,128)(2,1)}, u32[]{:S(2)}, u32[]{:S(2)}) collective-permute-start(bf16[176,2048]{1,0:T(8,128)(2,1)} %collective-permute-done.58.refs_2_), channel_id=1, source_target_pairs={{0,8},{8,0},{16,24},{24,16},{1,9},{9,1},{17,25},{25,17},{2,10},{10... | collective-permute-start | bytes 2162696 | tf_op jit(solution)/shard_map/ppermute | solution.py:99
  1003.3 9.5 collective-permute-start.43
  1006.6 8.6 collective-permute-start.42
  (39 other events, 734.0 us)
Sparse Core Ops, SparseCore 0:
  12.2 32.0 all-gather.7
  79.8 34.5 all-gather.13
  116.5 57.7 all-gather.9
  181.6 57.1 all-gather.11
  271.1 60.9 all-gather.15
  669.3 58.8 reduce-scatter.5
  759.5 59.2 reduce-scatter.7
  833.3 59.9 reduce-scatter.9
  896.2 25.7 reduce-scatter.13
  927.6 34.4 reduce-scatter.11

commit v8 on v7

--- a/solution.py
+++ b/solution.py
@@ -40,15 +40,17 @@
     return me // 2, lax.rem(me, 2)
 
 
-def scatter_sides(total):
+def scatter_sides(total, pieces=1):
     m = lines()
     _, side = line_and_side()
     parts = total.reshape(m, 2, total.shape[0] // (2 * m), total.shape[1])
     mine = lax.dynamic_index_in_dim(parts, side, 1, keepdims=False)
-    return mine, side_swap(lax.dynamic_index_in_dim(parts, 1 - side, 1, keepdims=False))
-
-
-def add_sides(mine, sent):
+    theirs = lax.dynamic_index_in_dim(parts, 1 - side, 1, keepdims=False)
+    return mine, [side_swap(part) for part in jnp.split(theirs, pieces)]
+
+
+def add_sides(mine, sent, *marks):
+    sent = jnp.concatenate([after(sent[0], *marks)] + sent[1:], axis=0)
     both = (mine.astype(F32) + sent.astype(F32)).astype(BF)
     return both.reshape(-1, both.shape[-1])
 
@@ -542,17 +544,18 @@
     line_gate = gather_lines(part_gate)
     line_up = gather_lines(part_up)
     line_down = gather_lines(part_down)
-    x_all = jnp.concatenate(x_parts, axis=0)
+    other_qkv = side_swap(line_qkv)
+    x_all = after(jnp.concatenate(x_parts, axis=0), other_qkv)
     scale_one = inverse_rms(x_all.astype(F32))
-    full_qkv = assemble(line_qkv, side_swap(line_qkv))
-    g_parts = spread(after(grad_top, seg_all, x_all))
+    full_qkv = assemble(line_qkv, other_qkv)
     qkv = (mm(x_all, full_qkv) * scale_one).astype(BF)
+    g_parts = spread(after(grad_top, seg_all, x_all), [qkv])
     mixed, den = attention_forward(meta, qkv, seg_col, seg_row, heads, rows)
 
     def blocks(value):
         return [value[i * rows : (i + 1) * rows] for i in range(nb)]
 
-    full_out = assemble(line_out, side_swap(line_out))
+    full_out = assemble(line_out, side_swap(after(line_out, qkv)))
     projected = mm(after(mixed, *g_parts), full_out).astype(BF)
     sums = add_cores(blocks(projected))
     low, high = jnp.split(after(line_gate, *sums), 2)
@@ -562,11 +565,12 @@
     scale_two = inverse_rms(residual)
     unit_two = residual * scale_two
     full_gate = assemble(line_gate, *other_gate)
-    n_all = jnp.concatenate(spread(unit_two.astype(BF)), axis=0)
+    n_all = jnp.concatenate(spread(unit_two.astype(BF), other_gate), axis=0)
     g_all = jnp.concatenate(g_parts, axis=0)
-    other_up = side_swap(after(line_up, unit_two))
-    gate = mm(n_all, full_gate)
-    full_up = assemble(line_up, after(other_up, gate))
+    low, high = jnp.split(after(line_up, unit_two), 2)
+    other_up = [side_swap(low), side_swap(high)]
+    gate = mm(after(n_all, other_up[0]), full_gate)
+    full_up = assemble(line_up, other_up[0], after(other_up[1], gate))
     full_down = assemble(line_down, side_swap(after(line_down, n_all)))
     up = mm(after(n_all, gate), full_up)
     grad_hidden = mm_nt(after(g_all, up), full_down)
@@ -589,9 +593,9 @@
     )
     branch = grad_residual.astype(BF)
     total_down = mm_tn(after(act, branch), g_all).astype(BF)
-    mine_down, sent_down = scatter_sides(total_down)
+    mine_down, sent_down = scatter_sides(total_down, 2)
     projected_two = mm(after(act, total_down), full_down).astype(BF)
-    both_gate = add_sides(mine_gate, after(sent_gate, total_down))
+    both_gate = add_sides(mine_gate, sent_gate, total_down)
     sum_gate = scatter_lines(both_gate)
     b_all = jnp.concatenate(spread(branch, [projected_two, both_gate]), axis=0)
     out_sums = add_cores(blocks(after(projected_two, b_all)))
@@ -603,18 +607,18 @@
         meta, qkv, seg_col, seg_row, after(grad_mixed, total_out, *out_sums), mixed, den, scale_one, heads, rows
     )
     block_out = residual + after(add_chips([jnp.zeros_like(out_sums[0])] + out_sums[1:]), grad_qkv) + out_sums[0]
-    both_up = add_sides(mine_up, after(sent_up, grad_qkv))
+    both_up = add_sides(mine_up, sent_up, grad_qkv)
     sum_up = scatter_lines(both_up)
-    back_one = mm_nt(after(grad_qkv, block_out, both_up), full_qkv).astype(BF)
+    back_one = mm_nt(after(grad_qkv, block_out, both_up, sent_down[0]), full_qkv).astype(BF)
     one_sums = add_cores(blocks(back_one))
     total_qkv = mm_tn(x_all, after(grad_qkv, sum_gate, *one_sums)).astype(BF)
     mine_qkv, sent_qkv = scatter_sides(total_qkv)
     grad_unit_one = add_chips(one_sums)
-    both_down = add_sides(mine_down, after(sent_down, total_qkv, grad_unit_one))
+    both_down = add_sides(mine_down, sent_down, total_qkv)
     sum_down = scatter_lines(both_down)
-    both_out = add_sides(mine_out, after(sent_out, both_down, sum_up))
+    both_out = add_sides(mine_out, sent_out, both_down, sum_up)
     sum_out = scatter_lines(both_out)
-    both_qkv = add_sides(mine_qkv, after(sent_qkv, both_out, sum_down))
+    both_qkv = add_sides(mine_qkv, sent_qkv, both_out, grad_unit_one, sum_down)
     sum_qkv = scatter_lines(both_qkv)
     sum_gate = after(sum_gate, both_out)
     sum_up = after(sum_up, both_out)

time: 1050 us -> 1040 us (level)
  matrix products: 249 us -> 221 us
  starting transfers between devices: 99.8 us -> 120 us
  other arithmetic: 120 us -> 101 us
  local copies, waits for them, and re-layouts: 94.7 us -> 113 us
    ppermute x12, waiting for transfers between devices: 149 us -> 103 us  [chip_shift(): return lax.ppermute(value, C, [(i, (i + 2 * k) % n) for i in range(n)])]
    ppermute x11 -> x13, waiting for transfers between devices: 151 us -> 185 us  [side_swap(): return lax.ppermute(value, F, [(j, j ^ 1) for j in range(lax.axis_size(F))])]
    ppermute x24, starting transfers between devices: 57.7 us -> 87.7 us  [core_swap(): return lax.ppermute(value, C, [(i, i ^ 1) for i in range(n)])]
    dot_general x5, matrix products: 89 us -> 73.9 us  [mm_tn(): lax.dot_general(a, b, (((0,), (0,)), ((), ())), preferred_element_type=F32)]
    reduce_scatter x5, waiting for transfers between devices: 14.8 us -> 0.01 us  [scatter_lines(): lax.psum_scatter(total, F, scatter_dimension=0, axis_index_groups=line_gr...]
    unnamed x73 -> x106, local copies, waits for them, and re-layouts: 27.6 us -> 33.6 us
  transfers between devices with their start and end apart: 70 -> 72, of which waited for: 27 -> 30; matrix products, arithmetic and copies ran while one was open for 35% -> 34% of each run, Pallas kernels for 6% -> 7%
where the time goes in v8:
time: 1040 us; the launch traced here: 1030 us
  waiting for transfers between devices  373 us (36%)
  matrix products  221 us (21%)
  starting transfers between devices  120 us (12%)
  local copies, waits for them, and re-layouts  113 us (11%)
  other arithmetic  101 us (10%)
  Pallas kernels  87.4 us (8%)
  between operations  15.4 us (1%)
    ppermute x13, waiting for transfers between devices, side_swap(): return lax.ppermute(value, F, [(j, j ^ 1) for j in range(lax.axis_size(F))])  185 us
    ppermute x12, waiting for transfers between devices, chip_shift(): return lax.ppermute(value, C, [(i, (i + 2 * k) % n) for i in range(n)])  103 us
    ppermute x24, starting transfers between devices, core_swap(): return lax.ppermute(value, C, [(i, i ^ 1) for i in range(n)])  87.7 us
    dot_general x5, matrix products, mm_nt(): lax.dot_general(a, b, (((1,), (1,)), ((), ())), preferred_element_type=F32)  80.9 us
    dot_general x5, matrix products, mm_tn(): lax.dot_general(a, b, (((0,), (0,)), ((), ())), preferred_element_type=F32)  73.9 us
    dot_general x5, matrix products, mm(): return jnp.dot(a, b, preferred_element_type=F32)  66 us
    all_gather x5, waiting for transfers between devices, gather_lines(): return lax.all_gather(block, F, axis=0, axis_index_groups=line_groups())  50.7 us
    unnamed x106, local copies, waits for them, and re-layouts  33.6 us
  transfers between devices with their start and end apart: 72, of which 30 were waited for; matrix products, arithmetic and copies ran while one was open for 34% of the time, Pallas kernels for 7%

profile of v8, /device:TPU:17, one launch (start us, length us, event | category | flops | bytes accessed | tf_op | source)
XLA Modules:
  0.0 1030.3 jit_solution(12197417290952499602)
XLA Ops:
  13.1 31.2 %all-gather.8.cloned.1.call-done.own = bf16[4,256,640]{2,1,0:T(8,128)(2,1)} async-done(((bf16[1,256,640]{2,1,0:T(8,128)(2,1)}), bf16[4,256,640]{2,1,0:T(8,128)(2,1)}) %all-gather.8.cloned.1.call-update) | async-done | bytes 1310736 | tf_op jit(solution)/shard_map/all_gather | solution.py:63
  44.3 9.9 collective-permute-done.4
  64.3 14.6 %collective-permute-done.10 = bf16[64,2048]{1,0:T(8,128)(2,1)S(1)} collective-permute-done((bf16[64,2048]{1,0:T(8,128)(2,1)S(1)}, bf16[64,2048]{1,0:T(8,128)(2,1)S(1)}, u32[]{:S(2)}, u32[]{:S(2)}) %collective-permute-start.10) | collective-permute-done | bytes 262176 | tf_op jit(solution)/shard_map/ppermute | solution.py:178
  81.8 13.8 %collective-permute-done.6.refs_0_ = bf16[4,256,640]{2,1,0:T(8,128)(2,1)} collective-permute-done((bf16[4,256,640]{2,1,0:T(8,128)(2,1)}, bf16[4,256,640]{2,1,0:T(8,128)(2,1)}, u32[]{:S(2)}, u32[]{:S(2)}) %collective-permute-start.6) | collective-permute-done | bytes 1310752 | tf_op jit(solution)/shard_map/ppermute | solution.py:35
  99.0 4.4 pad_maximum_fusion
  105.2 11.4 %collective-permute-start.7 = (bf16[512,2048]{1,0:T(8,128)(2,1)}, bf16[512,2048]{1,0:T(8,128)(2,1)}, u32[]{:S(2)}, u32[]{:S(2)}) collective-permute-start(bf16[512,2048]{1,0:T(8,128)(2,1)} %bitcast.15), channel_id=1, source_target_pairs={{0,8},{8,0},{16,24},{24,16},{1,9},{9,1},{17,25},{25,17},{2,10},{10... | collective-permute-start | bytes 6291464 | tf_op jit(solution)/shard_map/ppermute | solution.py:101
  116.7 7.9 multiply_convert_fusion.3.qkv
  124.6 18.7 %collective-permute-done.8 = bf16[512,2048]{1,0:T(8,128)(2,1)} collective-permute-done((bf16[512,2048]{1,0:T(8,128)(2,1)}, bf16[512,2048]{1,0:T(8,128)(2,1)}, u32[]{:S(2)}, u32[]{:S(2)}) %collective-permute-start.8) | collective-permute-done | bytes 2097184 | tf_op jit(solution)/shard_map/ppermute | solution.py:106
  143.3 10.3 collective-permute-start.9
  153.6 4.6 copy.52
  158.1 4.6 copy.54
  170.3 17.8 %attention_forward.1 = (bf16[2048,512]{1,0:T(8,128)(2,1)}, f32[2048,4]{1,0:T(8,128)}) custom-call(s32[12]{0:T(128)} %concatenate.56.meta, bf16[2048,640]{1,0:T(8,128)(2,1)} %multiply_convert_fusion.3.qkv, s32[2048,1]{1,0:T(8,128)} %copy.51.seg_col, s32[4,1,512]{2,1,0:T(1,128)} %copy-done.28), custom_call_target="tpu_custom_call" | custom-call | flops 4194304 | bytes 16384 | tf_op jit(solution)/shard_map/attention_forward/pallas_call | solution.py:343
  191.1 6.8 convolution_convert_fusion.2
  206.0 19.6 %all-gather.10.cloned.1.call-done.own = bf16[4,256,1408]{2,1,0:T(8,128)(2,1)} async-done(((bf16[1,256,1408]{2,1,0:T(8,128)(2,1)}), bf16[4,256,1408]{2,1,0:T(8,128)(2,1)}) %all-gather.10.cloned.1.call-update) | async-done | bytes 2883600 | tf_op jit(solution)/shard_map/all_gather | solution.py:63
  232.7 20.7 %collective-permute-done.17 = bf16[512,2048]{1,0:T(8,128)(2,1)} collective-permute-done((bf16[512,2048]{1,0:T(8,128)(2,1)}, bf16[512,2048]{1,0:T(8,128)(2,1)}, u32[]{:S(2)}, u32[]{:S(2)}) %collective-permute-start.17) | collective-permute-done | bytes 2097184 | tf_op jit(solution)/shard_map/ppermute | solution.py:106
  253.4 5.9 fusion.11
  270.0 27.8 %collective-permute-done.21.refs_1_ = bf16[2,256,1408]{2,1,0:T(8,128)(2,1)} collective-permute-done((bf16[2,256,1408]{2,1,0:T(8,128)(2,1)S(1)}, bf16[2,256,1408]{2,1,0:T(8,128)(2,1)}, u32[]{:S(2)}, u32[]{:S(2)}) %collective-permute-start.21) | collective-permute-done | bytes 1441824 | tf_op jit(solution)/shard_map/ppermute | solution.py:35
  297.8 13.3 %collective-permute-done.20 = bf16[512,2048]{1,0:T(8,128)(2,1)} collective-permute-done((bf16[512,2048]{1,0:T(8,128)(2,1)}, bf16[512,2048]{1,0:T(8,128)(2,1)}, u32[]{:S(2)}, u32[]{:S(2)}) %collective-permute-start.20) | collective-permute-done | bytes 2097184 | tf_op jit(solution)/shard_map/ppermute | solution.py:106
  331.9 5.2 assemble.7
  337.5 5.3 pad_maximum_fusion.1
  342.8 11.6 %collective-permute-done.23.refs_0_ = bf16[2,256,1408]{2,1,0:T(8,128)(2,1)S(1)} collective-permute-done((bf16[2,256,1408]{2,1,0:T(8,128)(2,1)}, bf16[2,256,1408]{2,1,0:T(8,128)(2,1)S(1)}, u32[]{:S(2)}, u32[]{:S(2)}) %collective-permute-start.23) | collective-permute-done | bytes 1441824 | tf_op jit(solution)/shard_map/ppermute | solution.py:35
  354.4 15.8 %fusion.29 = f32[2048,1408]{1,0:T(8,128)} fusion(bf16[2048,2048]{1,0:T(8,128)(2,1)S(1)} %pad_maximum_fusion.1, bf16[2048,1408]{1,0:T(8,128)(2,1)S(1)} %bitcast.174), kind=kOutput, calls=%fused_computation.122 | convolution fusion | flops 11811160064 | bytes 25690112 | tf_op jit(solution)/shard_map/dot_general | solution.py:468
  370.2 15.2 %collective-permute-done.24.refs_1_ = bf16[2,256,1408]{2,1,0:T(8,128)(2,1)} collective-permute-done((bf16[2,256,1408]{2,1,0:T(8,128)(2,1)S(1)}, bf16[2,256,1408]{2,1,0:T(8,128)(2,1)}, u32[]{:S(2)}, u32[]{:S(2)}) %collective-permute-start.24) | collective-permute-done | bytes 1441824 | tf_op jit(solution)/shard_map/ppermute | solution.py:35
  386.6 5.2 assemble.8
  391.8 18.5 %fusion.30 = f32[2048,1408]{1,0:T(8,128)} fusion(bf16[2048,2048]{1,0:T(8,128)(2,1)} %copy-done.13, bf16[2048,1408]{1,0:T(8,128)(2,1)} %bitcast.179), kind=kOutput, calls=%fused_computation.123 | convolution fusion | flops 11811160064 | bytes 25690112 | tf_op jit(solution)/shard_map/dot_general | solution.py:468
  410.3 38.4 %collective-permute-done.25.refs_0_ = bf16[4,176,2048]{2,1,0:T(8,128)(2,1)S(1)} collective-permute-done((bf16[4,176,2048]{2,1,0:T(8,128)(2,1)}, bf16[4,176,2048]{2,1,0:T(8,128)(2,1)S(1)}, u32[]{:S(2)}, u32[]{:S(2)}) %collective-permute-start.25) | collective-permute-done | bytes 2883616 | tf_op jit(solution)/shard_map/ppermute | solution.py:35
  450.3 5.2 assemble.9
  455.5 26.0 %multiply_convert_fusion.1 = (bf16[2048,1408]{1,0:T(8,128)(2,1)}, bf16[2048,1408]{1,0:T(8,128)(2,1)}, bf16[2048,1408]{1,0:T(8,128)(2,1)}) fusion(f32[2048,1408]{1,0:T(8,128)} %fusion.29, f32[2048,1408]{1,0:T(8,128)} %fusion.30, bf16[2048,2048]{1,0:T(8,128)(2,1)} %constant_dynamic-update-slice_fusion, bf16[1408,2048]{1,0:T(8,128)(2,1)} %bitcast.167), kind=kOutput, calls=%fused_computation.3 | convolution fusion | flops 11854413824 | bytes 54525952 | tf_op jit(solution)/shard_map/dot_general | solution.py:476
  481.6 19.7 %fusion.31 = f32[2048,2048]{1,0:T(8,128)} fusion(bf16[2048,1408]{1,0:T(8,128)(2,1)} %get-tuple-element.73, bf16[2048,1408]{1,0:T(8,128)(2,1)} %bitcast.180), kind=kOutput, calls=%fused_computation.124 | convolution fusion | flops 11811160064 | bytes 28311552 | tf_op jit(solution)/shard_map/dot_general | solution.py:476
  501.2 21.4 %add_convert_fusion = bf16[2048,2048]{1,0:T(8,128)(2,1)} fusion(f32[2048,2048]{1,0:T(8,128)} %fusion.31, bf16[2048,1408]{1,0:T(8,128)(2,1)} %get-tuple-element.72, bf16[2048,1408]{1,0:T(8,128)(2,1)} %bitcast.171), kind=kOutput, calls=%fused_computation | convolution fusion | flops 11819548672 | bytes 36700160 | tf_op jit(solution)/shard_map/dot_general | solution.py:476
  522.7 4.8 fusion.20
  529.2 4.0 collective-permute-done.26
  536.3 6.2 add_convert_fusion.3
  543.7 17.7 %convolution_convert_fusion.5 = bf16[2048,1408]{1,0:T(8,128)(2,1)S(1)} fusion(bf16[2048,1408]{1,0:T(8,128)(2,1)} %get-tuple-element.72, bf16[512,2048]{1,0:T(8,128)(2,1)} %collective-permute-done.22, bf16[512,2048]{1,0:T(8,128)(2,1)} %collective-permute-done.20, bf16[512,2048]{1,0:T(8,128)(2,1)} %collective-permute-done.19, ...), kind=kOutput, calls=%fused_computation.15 | convolution fusion | flops 11847598080 | bytes 19922944 | tf_op jit(solution)/shard_map/dot_general | solution.py:472
  561.4 21.1 %convolution_convert_fusion.4 = bf16[2048,1408]{1,0:T(8,128)(2,1)} fusion(bf16[2048,1408]{1,0:T(8,128)(2,1)} %get-tuple-element.73, bf16[512,2048]{1,0:T(8,128)(2,1)} %collective-permute-done.22, bf16[512,2048]{1,0:T(8,128)(2,1)} %collective-permute-done.20, bf16[512,2048]{1,0:T(8,128)(2,1)} %collective-permute-done.19, ...), kind=kOutput, calls=%fused_computation.14 | convolution fusion | flops 11847598080 | bytes 19922944 | tf_op jit(solution)/shard_map/dot_general | solution.py:472
  585.5 4.1 collective-permute-done.28
  590.4 5.6 fusion.16
  598.7 18.3 %convolution_convert_fusion.3 = bf16[1408,2048]{1,0:T(8,128)(2,1)} fusion(bf16[2048,1408]{1,0:T(8,128)(2,1)} %get-tuple-element.76, bf16[2048,2048]{1,0:T(8,128)(2,1)} %constant_dynamic-update-slice_fusion), kind=kOutput, calls=%fused_computation.13 | convolution fusion | flops 11814043648 | bytes 19922944 | tf_op jit(solution)/shard_map/dot_general | solution.py:472
  617.0 16.9 %convolution_convert_fusion.1 = bf16[2048,2048]{1,0:T(8,128)(2,1)} fusion(bf16[2048,1408]{1,0:T(8,128)(2,1)} %get-tuple-element.76, bf16[1408,2048]{1,0:T(8,128)(2,1)S(1)} %bitcast.170), kind=kOutput, calls=%fused_computation.11 | convolution fusion | flops 11815354368 | bytes 19922944 | tf_op jit(solution)/shard_map/dot_general | solution.py:468
  633.9 14.0 %collective-permute-done.31 = bf16[4,256,1408]{2,1,0:T(8,128)(2,1)S(1)} collective-permute-done((bf16[4,256,1408]{2,1,0:T(8,128)(2,1)}, bf16[4,256,1408]{2,1,0:T(8,128)(2,1)S(1)}, u32[]{:S(2)}, u32[]{:S(2)}) %collective-permute-start.31) | collective-permute-done | bytes 2883616 | tf_op jit(solution)/shard_map/ppermute | solution.py:35
  656.9 7.1 pad_maximum_fusion.2
  664.0 4.9 fusion.19
  674.1 4.2 dynamic-slice_bitcast_fusion.2
  678.9 6.3 fusion.32.gm
  686.0 4.4 add_convert_fusion.2
  690.8 5.7 convolution_convert_fusion.7
  696.5 30.8 %attention_backward.1 = bf16[2048,640]{1,0:T(8,128)(2,1)} custom-call(s32[12]{0:T(128)} %concatenate.56.meta, bf16[2048,640]{1,0:T(8,128)(2,1)} %multiply_convert_fusion.3.qkv, s32[2048,1]{1,0:T(8,128)} %copy.51.seg_col, s32[4,1,512]{2,1,0:T(1,128)} %copy-done.28, f32[2048,512]{1,0:T(8,128)} %fusion.32.gm, bf16[2048,512]{1,0:T(8,128)(2,1)} %get-tuple-element.60.mixed, ...), custom_call_target="tpu_custom_call" | custom-call | flops 10485760 | bytes 32768 | tf_op jit(solution)/shard_map/attention_backward/pallas_call | solution.py:371
  727.3 9.5 collective-permute-done.36
  745.8 5.4 add_add_fusion
  751.2 16.5 %collective-permute-done.37 = bf16[2,176,2048]{2,1,0:T(8,128)(2,1)} collective-permute-done((bf16[2,176,2048]{2,1,0:T(8,128)(2,1)}, bf16[2,176,2048]{2,1,0:T(8,128)(2,1)}, u32[]{:S(2)}, u32[]{:S(2)}) %collective-permute-start.37) | collective-permute-done | bytes 1441824 | tf_op jit(solution)/shard_map/ppermute | solution.py:35
  767.7 7.4 convolution_convert_fusion
  784.2 11.1 %convolution_convert_fusion.6 = bf16[2048,640]{1,0:T(8,128)(2,1)} fusion(bf16[2048,2048]{1,0:T(8,128)(2,1)} %copy-done.5, bf16[2048,640]{1,0:T(8,128)(2,1)} %attention_backward.1), kind=kOutput, calls=%fused_computation.54 | convolution fusion | flops 5370019840 | bytes 13631488 | tf_op jit(solution)/shard_map/dot_general | solution.py:472
  795.3 16.4 %collective-permute-done.43 = bf16[2,176,2048]{2,1,0:T(8,128)(2,1)} collective-permute-done((bf16[2,176,2048]{2,1,0:T(8,128)(2,1)}, bf16[2,176,2048]{2,1,0:T(8,128)(2,1)}, u32[]{:S(2)}, u32[]{:S(2)}) %collective-permute-start.43) | collective-permute-done | bytes 1441824 | tf_op jit(solution)/shard_map/ppermute | solution.py:35
  824.6 19.2 %collective-permute-done.42 = bf16[4,64,2048]{2,1,0:T(8,128)(2,1)} collective-permute-done((bf16[4,64,2048]{2,1,0:T(8,128)(2,1)}, bf16[4,64,2048]{2,1,0:T(8,128)(2,1)}, u32[]{:S(2)}, u32[]{:S(2)}) %collective-permute-start.42) | collective-permute-done | bytes 1048608 | tf_op jit(solution)/shard_map/ppermute | solution.py:35
  857.3 12.2 %collective-permute-done.40 = bf16[512,2048]{1,0:T(8,128)(2,1)} collective-permute-done((bf16[512,2048]{1,0:T(8,128)(2,1)}, bf16[512,2048]{1,0:T(8,128)(2,1)}, u32[]{:S(2)}, u32[]{:S(2)}) %collective-permute-start.40) | collective-permute-done | bytes 2097184 | tf_op jit(solution)/shard_map/ppermute | solution.py:106
  869.8 4.2 fusion.8
  876.8 8.1 collective-permute-done.54
  886.2 14.1 %collective-permute-done.57 = bf16[256,1408]{0,1:T(8,128)(2,1)} collective-permute-done((bf16[256,1408]{0,1:T(8,128)(2,1)S(1)}, bf16[256,1408]{0,1:T(8,128)(2,1)}, u32[]{:S(2)}, u32[]{:S(2)}) %collective-permute-start.57) | collective-permute-done | bytes 720928 | tf_op jit(solution)/shard_map/ppermute | solution.py:106
  930.4 40.0 %collective-permute-start.59 = (bf16[176,2048]{1,0:T(8,128)(2,1)}, bf16[176,2048]{1,0:T(8,128)(2,1)}, u32[]{:S(2)}, u32[]{:S(2)}) collective-permute-start(bf16[176,2048]{1,0:T(8,128)(2,1)} %reduce-scatter.10.cloned.1.call-done.refs_0_), channel_id=1, source_target_pairs={{0,8},{8,0},{16,24},{24,16},{1,9},{9,1},{17,25},{25,17},{2,10},{10... | collective-permute-start | bytes 2162696 | tf_op jit(solution)/shard_map/ppermute | solution.py:101
  970.9 5.9 bitcast_multiply_fusion
  976.7 6.2 copy.71
  983.0 6.2 copy.72
  989.7 5.2 finish_rows.1
  1017.1 4.3 finish_columns.5
  (316 shorter events, 216.0 us)
Async XLA Ops:
  7.2 37.1 %all-gather.8.cloned.1.call-start = ((), (), s32[]{:S(2)}) async-start(), calls=%async_computation.5 | async-start | bytes 1638400 | tf_op jit(solution)/shard_map/all_gather | solution.py:63
  7.2 46.9 %collective-permute-start.4 = (bf16[512,2048]{1,0:T(8,128)(2,1)}, bf16[512,2048]{1,0:T(8,128)(2,1)}, u32[]{:S(2)}, u32[]{:S(2)}) collective-permute-start(bf16[512,2048]{1,0:T(8,128)(2,1)} %bitcast.154), channel_id=1, source_target_pairs={{0,16},{8,24},{16,0},{24,8},{1,17},{9,25},{17,1},{25,9},{2,18},{10... | collective-permute-start | bytes 6291464 | tf_op jit(solution)/shard_map/ppermute | solution.py:106
  12.1 141.5 %all-gather.14.cloned.1.call-start = ((), (), s32[]{:S(2)}) async-start(), calls=%async_computation.13 | async-start | bytes 1310720 | tf_op jit(solution)/shard_map/all_gather | solution.py:63
  12.1 86.9 %collective-permute-start.3 = (bf16[512,2048]{1,0:T(8,128)(2,1)}, bf16[512,2048]{1,0:T(8,128)(2,1)}, u32[]{:S(2)}, u32[]{:S(2)}) collective-permute-start(bf16[512,2048]{1,0:T(8,128)(2,1)} %bitcast.155), channel_id=1, source_target_pairs={{0,8},{8,0},{16,24},{24,16},{1,9},{9,1},{17,25},{25,17},{2,10},{10... | collective-permute-start | bytes 6291464 | tf_op jit(solution)/shard_map/ppermute | solution.py:101
  54.1 44.9 %collective-permute-start.5 = (bf16[512,2048]{1,0:T(8,128)(2,1)}, bf16[512,2048]{1,0:T(8,128)(2,1)}, u32[]{:S(2)}, u32[]{:S(2)}) collective-permute-start(bf16[512,2048]{1,0:T(8,128)(2,1)} %collective-permute-done.4), channel_id=1, source_target_pairs={{0,8},{8,0},{16,24},{24,16},{1,9},{9,1},{17,25},{25,17},{2,10},{10... | collective-permute-start | bytes 6291464 | tf_op jit(solution)/shard_map/ppermute | solution.py:101
  55.7 6.7 collective-permute-start.1
  56.9 6.8 collective-permute-start.2
  59.8 35.9 %collective-permute-start.6 = (bf16[4,256,640]{2,1,0:T(8,128)(2,1)}, bf16[4,256,640]{2,1,0:T(8,128)(2,1)}, u32[]{:S(2)}, u32[]{:S(2)}) collective-permute-start(bf16[4,256,640]{2,1,0:T(8,128)(2,1)} %all-gather.8.cloned.1.call-done.own), channel_id=1, source_target_pairs={{0,1},{1,0},{2,3},{3,2},{4,5},{5,4},{6,7},{7,6},{8,9},{9,8},{10,11... | collective-permute-start | bytes 3932168 | tf_op jit(solution)/shard_map/ppermute | solution.py:35
  62.3 16.6 %collective-permute-start.10 = (bf16[64,2048]{1,0:T(8,128)(2,1)S(1)}, bf16[64,2048]{1,0:T(8,128)(2,1)S(1)}, u32[]{:S(2)}, u32[]{:S(2)}) collective-permute-start(bf16[64,2048]{1,0:T(8,128)(2,1)S(1)} %get-tuple-element.155), channel_id=1, source_target_pairs={{0,0},{1,4},{10,8},{11,12},{20,16},{21,20},{30,24},{31,28}} | collective-permute-start | bytes 786440 | tf_op jit(solution)/shard_map/ppermute | solution.py:178
  63.7 16.0 %collective-permute-start.11 = (bf16[64,2048]{1,0:T(8,128)(2,1)S(1)}, bf16[64,2048]{1,0:T(8,128)(2,1)S(1)}, u32[]{:S(2)}, u32[]{:S(2)}) collective-permute-start(bf16[64,2048]{1,0:T(8,128)(2,1)S(1)} %get-tuple-element.154), channel_id=1, source_target_pairs={{0,1},{1,5},{10,9},{11,13},{20,17},{21,21},{30,25},{31,29}} | collective-permute-start | bytes 786440 | tf_op jit(solution)/shard_map/ppermute | solution.py:178
  81.8 143.8 %all-gather.10.cloned.1.call-start = ((), (), s32[]{:S(2)}) async-start(), calls=%async_computation.6 | async-start | bytes 3604480 | tf_op jit(solution)/shard_map/all_gather | solution.py:63
  105.1 38.2 %collective-permute-start.8 = (bf16[512,2048]{1,0:T(8,128)(2,1)}, bf16[512,2048]{1,0:T(8,128)(2,1)}, u32[]{:S(2)}, u32[]{:S(2)}) collective-permute-start(bf16[512,2048]{1,0:T(8,128)(2,1)} %bitcast.15), channel_id=1, source_target_pairs={{0,16},{8,24},{16,0},{24,8},{1,17},{9,25},{17,1},{25,9},{2,18},{10... | collective-permute-start | bytes 6291464 | tf_op jit(solution)/shard_map/ppermute | solution.py:106
  105.2 85.9 %collective-permute-start.7 = (bf16[512,2048]{1,0:T(8,128)(2,1)}, bf16[512,2048]{1,0:T(8,128)(2,1)}, u32[]{:S(2)}, u32[]{:S(2)}) collective-permute-start(bf16[512,2048]{1,0:T(8,128)(2,1)} %bitcast.15), channel_id=1, source_target_pairs={{0,8},{8,0},{16,24},{24,16},{1,9},{9,1},{17,25},{25,17},{2,10},{10... | collective-permute-start | bytes 6291464 | tf_op jit(solution)/shard_map/ppermute | solution.py:101
  143.3 47.8 %collective-permute-start.9 = (bf16[512,2048]{1,0:T(8,128)(2,1)}, bf16[512,2048]{1,0:T(8,128)(2,1)}, u32[]{:S(2)}, u32[]{:S(2)}) collective-permute-start(bf16[512,2048]{1,0:T(8,128)(2,1)} %collective-permute-done.8), channel_id=1, source_target_pairs={{0,8},{8,0},{16,24},{24,16},{1,9},{9,1},{17,25},{25,17},{2,10},{10... | collective-permute-start | bytes 6291464 | tf_op jit(solution)/shard_map/ppermute | solution.py:101
  153.6 34.6 %collective-permute-start.14 = (bf16[4,64,2048]{2,1,0:T(8,128)(2,1)}, bf16[4,64,2048]{2,1,0:T(8,128)(2,1)}, u32[]{:S(2)}, u32[]{:S(2)}) collective-permute-start(bf16[4,64,2048]{2,1,0:T(8,128)(2,1)} %bitcast.196), channel_id=1, source_target_pairs={{0,1},{1,0},{2,3},{3,2},{4,5},{5,4},{6,7},{7,6},{8,9},{9,8},{10,11... | collective-permute-start | bytes 3145736 | tf_op jit(solution)/shard_map/ppermute | solution.py:35
  167.8 150.1 %all-gather.12.cloned.1.call-start = ((), (), s32[]{:S(2)}) async-start(), calls=%async_computation.7 | async-start | bytes 3604480 | tf_op jit(solution)/shard_map/all_gather | solution.py:63
  199.8 32.9 %collective-permute-start.15 = (bf16[512,2048]{1,0:T(8,128)(2,1)}, bf16[512,2048]{1,0:T(8,128)(2,1)}, u32[]{:S(2)}, u32[]{:S(2)}) collective-permute-start(bf16[512,2048]{1,0:T(8,128)(2,1)} %get-tuple-element.140), channel_id=1, source_target_pairs={{0,8},{8,0},{16,24},{24,16},{1,9},{9,1},{17,25},{25,17},{2,10},{10... | collective-permute-start | bytes 6291464 | tf_op jit(solution)/shard_map/ppermute | solution.py:101
  206.0 47.4 %collective-permute-start.17 = (bf16[512,2048]{1,0:T(8,128)(2,1)}, bf16[512,2048]{1,0:T(8,128)(2,1)}, u32[]{:S(2)}, u32[]{:S(2)}) collective-permute-start(bf16[512,2048]{1,0:T(8,128)(2,1)} %add_convert_fusion.4), channel_id=1, source_target_pairs={{0,16},{8,24},{16,0},{24,8},{1,17},{9,25},{17,1},{25,9},{2,18},{10... | collective-permute-start | bytes 6291464 | tf_op jit(solution)/shard_map/ppermute | solution.py:106
  229.2 32.6 %collective-permute-start.18 = (bf16[2,256,1408]{2,1,0:T(8,128)(2,1)}, bf16[2,256,1408]{2,1,0:T(8,128)(2,1)}, u32[]{:S(2)}, u32[]{:S(2)}) collective-permute-start(bf16[2,256,1408]{2,1,0:T(8,128)(2,1)} %get-tuple-element.151), channel_id=1, source_target_pairs={{0,1},{1,0},{2,3},{3,2},{4,5},{5,4},{6,7},{7,6},{8,9},{9,8},{10,11... | collective-permute-start | bytes 4325384 | tf_op jit(solution)/shard_map/ppermute | solution.py:35
  232.6 152.7 %all-gather.16.cloned.1.call-start = ((), (), s32[]{:S(2)}) async-start(), calls=%async_computation.14 | async-start | bytes 3604480 | tf_op jit(solution)/shard_map/all_gather | solution.py:63
  265.3 45.8 %collective-permute-start.20 = (bf16[512,2048]{1,0:T(8,128)(2,1)}, bf16[512,2048]{1,0:T(8,128)(2,1)}, u32[]{:S(2)}, u32[]{:S(2)}) collective-permute-start(bf16[512,2048]{1,0:T(8,128)(2,1)} %get-tuple-element.127), channel_id=1, source_target_pairs={{0,16},{8,24},{16,0},{24,8},{1,17},{9,25},{17,1},{25,9},{2,18},{10... | collective-permute-start | bytes 6291464 | tf_op jit(solution)/shard_map/ppermute | solution.py:106
  266.5 31.3 %collective-permute-start.21 = (bf16[2,256,1408]{2,1,0:T(8,128)(2,1)S(1)}, bf16[2,256,1408]{2,1,0:T(8,128)(2,1)}, u32[]{:S(2)}, u32[]{:S(2)}) collective-permute-start(bf16[2,256,1408]{2,1,0:T(8,128)(2,1)S(1)} %copy-done.23), channel_id=1, source_target_pairs={{0,1},{1,0},{2,3},{3,2},{4,5},{5,4},{6,7},{7,6},{8,9},{9,8},{10,11... | collective-permute-start | bytes 4325384 | tf_op jit(solution)/shard_map/ppermute | solution.py:35
  267.7 69.7 %collective-permute-start.19 = (bf16[512,2048]{1,0:T(8,128)(2,1)}, bf16[512,2048]{1,0:T(8,128)(2,1)}, u32[]{:S(2)}, u32[]{:S(2)}) collective-permute-start(bf16[512,2048]{1,0:T(8,128)(2,1)} %get-tuple-element.127), channel_id=1, source_target_pairs={{0,8},{8,0},{16,24},{24,16},{1,9},{9,1},{17,25},{25,17},{2,10},{10... | collective-permute-start | bytes 6291464 | tf_op jit(solution)/shard_map/ppermute | solution.py:101
  311.2 26.3 %collective-permute-start.22 = (bf16[512,2048]{1,0:T(8,128)(2,1)}, bf16[512,2048]{1,0:T(8,128)(2,1)}, u32[]{:S(2)}, u32[]{:S(2)}) collective-permute-start(bf16[512,2048]{1,0:T(8,128)(2,1)} %collective-permute-done.20), channel_id=1, source_target_pairs={{0,8},{8,0},{16,24},{24,16},{1,9},{9,1},{17,25},{25,17},{2,10},{10... | collective-permute-start | bytes 6291464 | tf_op jit(solution)/shard_map/ppermute | solution.py:101
  314.7 469.5 %reduce-scatter.6.cloned.1.call-start = ((), (), s32[]{:S(2)}) async-start(), calls=%async_computation.8 | async-start | bytes 3604480 | tf_op jit(solution)/shard_map/reduce_scatter | solution.py:59
  321.0 33.4 %collective-permute-start.23 = (bf16[2,256,1408]{2,1,0:T(8,128)(2,1)}, bf16[2,256,1408]{2,1,0:T(8,128)(2,1)S(1)}, u32[]{:S(2)}, u32[]{:S(2)}) collective-permute-start(bf16[2,256,1408]{2,1,0:T(8,128)(2,1)} %get-tuple-element.149), channel_id=1, source_target_pairs={{0,1},{1,0},{2,3},{3,2},{4,5},{5,4},{6,7},{7,6},{8,9},{9,8},{10,11... | collective-permute-start | bytes 4325384 | tf_op jit(solution)/shard_map/ppermute | solution.py:35
  337.1 48.2 %collective-permute-start.24 = (bf16[2,256,1408]{2,1,0:T(8,128)(2,1)S(1)}, bf16[2,256,1408]{2,1,0:T(8,128)(2,1)}, u32[]{:S(2)}, u32[]{:S(2)}) collective-permute-start(bf16[2,256,1408]{2,1,0:T(8,128)(2,1)S(1)} %get-tuple-element.148), channel_id=1, source_target_pairs={{0,1},{1,0},{2,3},{3,2},{4,5},{5,4},{6,7},{7,6},{8,9},{9,8},{10,11... | collective-permute-start | bytes 4325384 | tf_op jit(solution)/shard_map/ppermute | solution.py:35
  385.4 63.4 %collective-permute-start.25 = (bf16[4,176,2048]{2,1,0:T(8,128)(2,1)}, bf16[4,176,2048]{2,1,0:T(8,128)(2,1)S(1)}, u32[]{:S(2)}, u32[]{:S(2)}) collective-permute-start(bf16[4,176,2048]{2,1,0:T(8,128)(2,1)} %bitcast.183), channel_id=1, source_target_pairs={{0,1},{1,0},{2,3},{3,2},{4,5},{5,4},{6,7},{7,6},{8,9},{9,8},{10,11... | collective-permute-start | bytes 8650760 | tf_op jit(solution)/shard_map/ppermute | solution.py:35
  527.5 5.7 collective-permute-start.26
  529.2 7.1 collective-permute-start.27
  542.5 47.0 %collective-permute-start.28 = (bf16[512,2048]{1,0:T(8,128)(2,1)}, bf16[512,2048]{1,0:T(8,128)(2,1)S(1)}, u32[]{:S(2)}, u32[]{:S(2)}) collective-permute-start(bf16[512,2048]{1,0:T(8,128)(2,1)} %get-tuple-element.136), channel_id=1, source_target_pairs={{0,16},{8,24},{16,0},{24,8},{1,17},{9,25},{17,1},{25,9},{2,18},{10... | collective-permute-start | bytes 6291464 | tf_op jit(solution)/shard_map/ppermute | solution.py:106
  584.3 63.6 %collective-permute-start.31 = (bf16[4,256,1408]{2,1,0:T(8,128)(2,1)}, bf16[4,256,1408]{2,1,0:T(8,128)(2,1)S(1)}, u32[]{:S(2)}, u32[]{:S(2)}) collective-permute-start(bf16[4,256,1408]{2,1,0:T(8,128)(2,1)} %dynamic-slice_bitcast_fusion.1), channel_id=1, source_target_pairs={{0,1},{1,0},{2,3},{3,2},{4,5},{5,4},{6,7},{7,6},{8,9},{9,8},{10,11... | collective-permute-start | bytes 8650760 | tf_op jit(solution)/shard_map/ppermute | solution.py:35
  596.0 55.4 %collective-permute-start.30 = (bf16[512,2048]{1,0:T(8,128)(2,1)}, bf16[512,2048]{1,0:T(8,128)(2,1)}, u32[]{:S(2)}, u32[]{:S(2)}) collective-permute-start(bf16[512,2048]{1,0:T(8,128)(2,1)} %get-tuple-element.125), channel_id=1, source_target_pairs={{0,16},{8,24},{16,0},{24,8},{1,17},{9,25},{17,1},{25,9},{2,18},{10... | collective-permute-start | bytes 6291464 | tf_op jit(solution)/shard_map/ppermute | solution.py:106
  597.1 55.8 %collective-permute-start.29 = (bf16[512,2048]{1,0:T(8,128)(2,1)}, bf16[512,2048]{1,0:T(8,128)(2,1)}, u32[]{:S(2)}, u32[]{:S(2)}) collective-permute-start(bf16[512,2048]{1,0:T(8,128)(2,1)} %get-tuple-element.125), channel_id=1, source_target_pairs={{0,8},{8,0},{16,24},{24,16},{1,9},{9,1},{17,25},{25,17},{2,10},{10... | collective-permute-start | bytes 6291464 | tf_op jit(solution)/shard_map/ppermute | solution.py:101
  651.4 5.5 collective-permute-start.32
  652.9 190.9 %reduce-scatter.8.cloned.1.call-start = ((), (), s32[]{:S(2)}) async-start(), calls=%async_computation.9 | async-start | bytes 3604480 | tf_op jit(solution)/shard_map/reduce_scatter | solution.py:59
  668.9 17.1 %collective-permute-start.33 = (bf16[512,2048]{1,0:T(8,128)(2,1)}, bf16[512,2048]{1,0:T(8,128)(2,1)}, u32[]{:S(2)}, u32[]{:S(2)}) collective-permute-start(bf16[512,2048]{1,0:T(8,128)(2,1)} %get-tuple-element.135), channel_id=1, source_target_pairs={{0,8},{8,0},{16,24},{24,16},{1,9},{9,1},{17,25},{25,17},{2,10},{10... | collective-permute-start | bytes 6291464 | tf_op jit(solution)/shard_map/ppermute | solution.py:101
  672.8 64.0 %collective-permute-start.36 = (bf16[4,256,1408]{2,1,0:T(8,128)(2,1)S(1)}, bf16[4,256,1408]{2,1,0:T(8,128)(2,1)}, u32[]{:S(2)}, u32[]{:S(2)}) collective-permute-start(bf16[4,256,1408]{2,1,0:T(8,128)(2,1)S(1)} %dynamic-slice_bitcast_fusion), channel_id=1, source_target_pairs={{0,1},{1,0},{2,3},{3,2},{4,5},{5,4},{6,7},{7,6},{8,9},{9,8},{10,11... | collective-permute-start | bytes 8650760 | tf_op jit(solution)/shard_map/ppermute | solution.py:35
  678.3 89.4 %collective-permute-start.37 = (bf16[2,176,2048]{2,1,0:T(8,128)(2,1)}, bf16[2,176,2048]{2,1,0:T(8,128)(2,1)}, u32[]{:S(2)}, u32[]{:S(2)}) collective-permute-start(bf16[2,176,2048]{2,1,0:T(8,128)(2,1)} %get-tuple-element.147), channel_id=1, source_target_pairs={{0,1},{1,0},{2,3},{3,2},{4,5},{5,4},{6,7},{7,6},{8,9},{9,8},{10,11... | collective-permute-start | bytes 4325384 | tf_op jit(solution)/shard_map/ppermute | solution.py:35
  685.2 60.1 %collective-permute-start.35 = (bf16[512,2048]{1,0:T(8,128)(2,1)}, bf16[512,2048]{1,0:T(8,128)(2,1)}, u32[]{:S(2)}, u32[]{:S(2)}) collective-permute-start(bf16[512,2048]{1,0:T(8,128)(2,1)} %get-tuple-element.134), channel_id=1, source_target_pairs={{0,8},{8,0},{16,24},{24,16},{1,9},{9,1},{17,25},{25,17},{2,10},{10... | collective-permute-start | bytes 6291464 | tf_op jit(solution)/shard_map/ppermute | solution.py:101
  690.5 52.5 %collective-permute-start.34 = (bf16[512,2048]{1,0:T(8,128)(2,1)}, bf16[512,2048]{1,0:T(8,128)(2,1)}, u32[]{:S(2)}, u32[]{:S(2)}) collective-permute-start(bf16[512,2048]{1,0:T(8,128)(2,1)} %add_convert_fusion.2), channel_id=1, source_target_pairs={{0,16},{8,24},{16,0},{24,8},{1,17},{9,25},{17,1},{25,9},{2,18},{10... | collective-permute-start | bytes 6291464 | tf_op jit(solution)/shard_map/ppermute | solution.py:106
  742.9 163.2 %reduce-scatter.10.cloned.1.call-start = ((), (), s32[]{:S(2)}) async-start(), calls=%async_computation.10 | async-start | bytes 3604480 | tf_op jit(solution)/shard_map/reduce_scatter | solution.py:59
  778.2 33.5 %collective-permute-start.43 = (bf16[2,176,2048]{2,1,0:T(8,128)(2,1)}, bf16[2,176,2048]{2,1,0:T(8,128)(2,1)}, u32[]{:S(2)}, u32[]{:S(2)}) collective-permute-start(bf16[2,176,2048]{2,1,0:T(8,128)(2,1)} %get-tuple-element.146), channel_id=1, source_target_pairs={{0,1},{1,0},{2,3},{3,2},{4,5},{5,4},{6,7},{7,6},{8,9},{9,8},{10,11... | collective-permute-start | bytes 4325384 | tf_op jit(solution)/shard_map/ppermute | solution.py:35
  817.1 91.8 %reduce-scatter.14.cloned.1.call-start = ((), (), s32[]{:S(2)}) async-start(), calls=%async_computation.12 | async-start | bytes 1310720 | tf_op jit(solution)/shard_map/reduce_scatter | solution.py:59
  819.6 24.2 %collective-permute-start.42 = (bf16[4,64,2048]{2,1,0:T(8,128)(2,1)}, bf16[4,64,2048]{2,1,0:T(8,128)(2,1)}, u32[]{:S(2)}, u32[]{:S(2)}) collective-permute-start(bf16[4,64,2048]{2,1,0:T(8,128)(2,1)} %dynamic-slice_bitcast_fusion.5), channel_id=1, source_target_pairs={{0,1},{1,0},{2,3},{3,2},{4,5},{5,4},{6,7},{7,6},{8,9},{9,8},{10,11... | collective-permute-start | bytes 3145736 | tf_op jit(solution)/shard_map/ppermute | solution.py:35
  820.8 36.1 %collective-permute-start.38 = (bf16[512,2048]{1,0:T(8,128)(2,1)}, bf16[512,2048]{1,0:T(8,128)(2,1)}, u32[]{:S(2)}, u32[]{:S(2)}) collective-permute-start(bf16[512,2048]{1,0:T(8,128)(2,1)} %get-tuple-element.132), channel_id=1, source_target_pairs={{0,8},{8,0},{16,24},{24,16},{1,9},{9,1},{17,25},{25,17},{2,10},{10... | collective-permute-start | bytes 6291464 | tf_op jit(solution)/shard_map/ppermute | solution.py:101
  822.0 47.5 %collective-permute-start.40 = (bf16[512,2048]{1,0:T(8,128)(2,1)}, bf16[512,2048]{1,0:T(8,128)(2,1)}, u32[]{:S(2)}, u32[]{:S(2)}) collective-permute-start(bf16[512,2048]{1,0:T(8,128)(2,1)} %add_convert_fusion.1), channel_id=1, source_target_pairs={{0,16},{8,24},{16,0},{24,8},{1,17},{9,25},{17,1},{25,9},{2,18},{10... | collective-permute-start | bytes 6291464 | tf_op jit(solution)/shard_map/ppermute | solution.py:106
  824.3 81.8 %collective-permute-start.41 = (bf16[4,256,640]{2,1,0:T(8,128)(2,1)}, bf16[4,256,640]{2,1,0:T(8,128)(2,1)}, u32[]{:S(2)}, u32[]{:S(2)}) collective-permute-start(bf16[4,256,640]{2,1,0:T(8,128)(2,1)} %dynamic-slice_bitcast_fusion.4), channel_id=1, source_target_pairs={{0,1},{1,0},{2,3},{3,2},{4,5},{5,4},{6,7},{7,6},{8,9},{9,8},{10,11... | collective-permute-start | bytes 3932168 | tf_op jit(solution)/shard_map/ppermute | solution.py:35
  846.7 54.5 %collective-permute-start.53 = (bf16[256,1408]{0,1:T(8,128)(2,1)}, bf16[256,1408]{0,1:T(8,128)(2,1)}, u32[]{:S(2)}, u32[]{:S(2)}) collective-permute-start(bf16[256,1408]{0,1:T(8,128)(2,1)} %reduce-scatter.6.cloned.1.call-done), channel_id=1, source_target_pairs={{0,8},{8,0},{16,24},{24,16},{1,9},{9,1},{17,25},{25,17},{2,10},{10... | collective-permute-start | bytes 2162696 | tf_op jit(solution)/shard_map/ppermute | solution.py:101
  849.8 35.1 %collective-permute-start.54 = (bf16[256,1408]{0,1:T(8,128)(2,1)}, bf16[256,1408]{0,1:T(8,128)(2,1)}, u32[]{:S(2)}, u32[]{:S(2)}) collective-permute-start(bf16[256,1408]{0,1:T(8,128)(2,1)} %reduce-scatter.6.cloned.1.call-done), channel_id=1, source_target_pairs={{0,16},{8,24},{16,0},{24,8},{1,17},{9,25},{17,1},{25,9},{2,18},{10... | collective-permute-start | bytes 2162696 | tf_op jit(solution)/shard_map/ppermute | solution.py:106
  850.1 144.8 %reduce-scatter.12.cloned.1.call-start = ((), (), s32[]{:S(2)}) async-start(), calls=%async_computation.11 | async-start | bytes 1638400 | tf_op jit(solution)/shard_map/reduce_scatter | solution.py:59
  856.9 48.4 %collective-permute-start.56 = (bf16[256,1408]{0,1:T(8,128)(2,1)S(1)}, bf16[256,1408]{0,1:T(8,128)(2,1)S(1)}, u32[]{:S(2)}, u32[]{:S(2)}) collective-permute-start(bf16[256,1408]{0,1:T(8,128)(2,1)S(1)} %copy-done.26), channel_id=1, source_target_pairs={{0,8},{8,0},{16,24},{24,16},{1,9},{9,1},{17,25},{25,17},{2,10},{10... | collective-permute-start | bytes 2162696 | tf_op jit(solution)/shard_map/ppermute | solution.py:101
  869.5 30.9 %collective-permute-start.57 = (bf16[256,1408]{0,1:T(8,128)(2,1)S(1)}, bf16[256,1408]{0,1:T(8,128)(2,1)}, u32[]{:S(2)}, u32[]{:S(2)}) collective-permute-start(bf16[256,1408]{0,1:T(8,128)(2,1)S(1)} %copy-done.26), channel_id=1, source_target_pairs={{0,16},{8,24},{16,0},{24,8},{1,17},{9,25},{17,1},{25,9},{2,18},{10... | collective-permute-start | bytes 2162696 | tf_op jit(solution)/shard_map/ppermute | solution.py:106
  884.9 30.4 %collective-permute-start.55 = (bf16[256,1408]{0,1:T(8,128)(2,1)}, bf16[256,1408]{0,1:T(8,128)(2,1)}, u32[]{:S(2)}, u32[]{:S(2)}) collective-permute-start(bf16[256,1408]{0,1:T(8,128)(2,1)} %collective-permute-done.54), channel_id=1, source_target_pairs={{0,8},{8,0},{16,24},{24,16},{1,9},{9,1},{17,25},{25,17},{2,10},{10... | collective-permute-start | bytes 2162696 | tf_op jit(solution)/shard_map/ppermute | solution.py:101
  900.4 17.0 %collective-permute-start.58 = (bf16[256,1408]{0,1:T(8,128)(2,1)}, bf16[256,1408]{0,1:T(8,128)(2,1)}, u32[]{:S(2)}, u32[]{:S(2)}) collective-permute-start(bf16[256,1408]{0,1:T(8,128)(2,1)} %collective-permute-done.57), channel_id=1, source_target_pairs={{0,8},{8,0},{16,24},{24,16},{1,9},{9,1},{17,25},{25,17},{2,10},{10... | collective-permute-start | bytes 2162696 | tf_op jit(solution)/shard_map/ppermute | solution.py:101
  908.9 4.9 collective-permute-start.47
  914.6 9.5 collective-permute-start.51
  919.4 51.0 %collective-permute-start.60 = (bf16[176,2048]{1,0:T(8,128)(2,1)}, bf16[176,2048]{1,0:T(8,128)(2,1)}, u32[]{:S(2)}, u32[]{:S(2)}) collective-permute-start(bf16[176,2048]{1,0:T(8,128)(2,1)} %reduce-scatter.10.cloned.1.call-done.refs_0_), channel_id=1, source_target_pairs={{0,16},{8,24},{16,0},{24,8},{1,17},{9,25},{17,1},{25,9},{2,18},{10... | collective-permute-start | bytes 2162696 | tf_op jit(solution)/shard_map/ppermute | solution.py:106
  925.5 69.5 %collective-permute-start.52 = (bf16[256,2048]{1,0:T(8,128)(2,1)}, bf16[256,2048]{1,0:T(8,128)(2,1)}, u32[]{:S(2)}, u32[]{:S(2)}) collective-permute-start(bf16[256,2048]{1,0:T(8,128)(2,1)} %add.244), channel_id=1, source_target_pairs={{0,8},{16,24},{1,9},{17,25},{10,2},{26,18},{11,3},{27,19},{4,12},{... | collective-permute-start | bytes 3145736 | tf_op jit(solution)/shard_map/ppermute | solution.py:198
  930.4 59.4 %collective-permute-start.59 = (bf16[176,2048]{1,0:T(8,128)(2,1)}, bf16[176,2048]{1,0:T(8,128)(2,1)}, u32[]{:S(2)}, u32[]{:S(2)}) collective-permute-start(bf16[176,2048]{1,0:T(8,128)(2,1)} %reduce-scatter.10.cloned.1.call-done.refs_0_), channel_id=1, source_target_pairs={{0,8},{8,0},{16,24},{24,16},{1,9},{9,1},{17,25},{25,17},{2,10},{10... | collective-permute-start | bytes 2162696 | tf_op jit(solution)/shard_map/ppermute | solution.py:101
  970.4 19.3 %collective-permute-start.61 = (bf16[176,2048]{1,0:T(8,128)(2,1)}, bf16[176,2048]{1,0:T(8,128)(2,1)}, u32[]{:S(2)}, u32[]{:S(2)}) collective-permute-start(bf16[176,2048]{1,0:T(8,128)(2,1)} %collective-permute-done.60.refs_2_), channel_id=1, source_target_pairs={{0,8},{8,0},{16,24},{24,16},{1,9},{9,1},{17,25},{25,17},{2,10},{10... | collective-permute-start | bytes 2162696 | tf_op jit(solution)/shard_map/ppermute | solution.py:101
  994.9 8.0 collective-permute-start.45
  998.2 8.6 collective-permute-start.44
  1002.9 5.3 collective-permute-start.46
  (56 other events, 1125.7 us)
Sparse Core Ops, SparseCore 0:
  12.2 32.0 all-gather.7
  81.9 51.3 all-gather.13
  167.9 57.6 all-gather.9
  232.8 57.1 all-gather.11
  314.8 57.6 all-gather.15
  653.0 55.1 reduce-scatter.5
  743.1 56.7 reduce-scatter.7
  817.2 55.8 reduce-scatter.9
  875.5 25.7 reduce-scatter.13
  913.7 34.6 reduce-scatter.11

commit v9 on v5

--- a/solution.py
+++ b/solution.py
@@ -61,29 +61,32 @@
     return lax.all_gather(block, F, axis=0, axis_index_groups=line_groups())
 
 
-def assemble_kernel(own, other, out, sems, *, m):
+def assemble_kernel(own, *refs, m, pieces):
     side = lax.rem(lax.axis_index(F), 2)
+    out, sems = refs[pieces], refs[pieces + 1]
+    size = m // pieces
     copies = []
     for k in range(m):
+        other = refs[k // size].at[k % size]
         copies.append(pltpu.make_async_copy(own.at[k], out.at[2 * k + side], sems.at[k]))
-        copies.append(pltpu.make_async_copy(other.at[k], out.at[2 * k + 1 - side], sems.at[m + k]))
+        copies.append(pltpu.make_async_copy(other, out.at[2 * k + 1 - side], sems.at[m + k]))
     for copy in copies:
         copy.start()
     for copy in copies:
         copy.wait()
 
 
-def assemble(own, other):
+def assemble(own, *other):
     m, rows, width = own.shape
     out = pl.pallas_call(
-        functools.partial(assemble_kernel, m=m),
+        functools.partial(assemble_kernel, m=m, pieces=len(other)),
         out_shape=jax.ShapeDtypeStruct((2 * m, rows, width), own.dtype),
-        in_specs=[pl.BlockSpec(memory_space=pl.ANY)] * 2,
+        in_specs=[pl.BlockSpec(memory_space=pl.ANY)] * (1 + len(other)),
         out_specs=pl.BlockSpec(memory_space=pltpu.VMEM),
         scratch_shapes=[pltpu.SemaphoreType.DMA((2 * m,))],
         cost_estimate=pl.CostEstimate(flops=0, transcendentals=0, bytes_accessed=1024),
         name="assemble",
-    )(own, other)
+    )(own, *other)
     return out.reshape(2 * m * rows, width)
 
 
@@ -560,9 +563,11 @@
     n_all = jnp.concatenate(spread(unit_two.astype(BF)), axis=0)
     g_all = jnp.concatenate(g_parts, axis=0)
     full_up = assemble(line_up, side_swap(after(line_up, unit_two)))
-    gate = mm(n_all, full_gate)
-    full_down = assemble(line_down, side_swap(after(line_down, n_all)))
-    up = mm(after(n_all, gate), full_up)
+    gate = mm(after(n_all, full_up), full_gate)
+    low, high = jnp.split(after(line_down, n_all), 2)
+    other_down = [side_swap(low), side_swap(high)]
+    up = mm(after(n_all, gate, other_down[0]), full_up)
+    full_down = assemble(line_down, *other_down)
     grad_hidden = mm_nt(after(g_all, up), full_down)
     sigmoid = jax.nn.sigmoid(gate)
     silu = gate * sigmoid
@@ -596,7 +601,7 @@
     both_up = add_sides(mine_up, after(sent_up, total_out))
     sum_up = scatter_lines(both_up)
     grad_qkv = attention_backward(
-        meta, qkv, seg_col, seg_row, after(grad_mixed, both_up, *out_sums), mixed, den, scale_one, heads, rows
+        meta, qkv, seg_col, seg_row, after(grad_mixed, both_up, sum_gate, *out_sums), mixed, den, scale_one, heads, rows
     )
     block_out = residual + after(add_chips([jnp.zeros_like(out_sums[0])] + out_sums[1:]), grad_qkv) + out_sums[0]
     back_one = mm_nt(after(grad_qkv, block_out), full_qkv).astype(BF)
@@ -606,12 +611,13 @@
     mine_qkv, sent_qkv = scatter_sides(total_qkv)
     grad_unit_one = add_chips(one_sums)
     sum_down = scatter_lines(both_down)
-    both_out = add_sides(mine_out, after(sent_out, both_down))
+    both_out = add_sides(mine_out, after(sent_out, both_down, sum_up))
     sum_out = scatter_lines(both_out)
-    both_qkv = add_sides(mine_qkv, after(sent_qkv, both_out, grad_unit_one))
+    both_qkv = add_sides(mine_qkv, after(sent_qkv, both_out, grad_unit_one, sum_down))
     sum_qkv = scatter_lines(both_qkv)
     sum_gate = after(sum_gate, both_qkv)
     sum_up = after(sum_up, both_qkv, grad_unit_one)
+    sum_out = after(sum_out, both_qkv)
 
     unit_one = own.astype(F32) * inverse_rms(own.astype(F32))
     input_grad = grad_residual + grad_unit_one - unit_one * jnp.mean(

time: 1020 us -> 1020 us (level)
  starting transfers between devices: 71.7 us -> 118 us
  waiting for transfers between devices: 406 us -> 364 us
    ppermute x24, starting transfers between devices: 26.3 us -> 78.6 us  [core_swap(): return lax.ppermute(value, C, [(i, i ^ 1) for i in range(n)])]
    ppermute x4, waiting for transfers between devices: 17 us -> 0.01 us  [ungroup_pieces(): lax.ppermute(piece, (C, F), pairs)]
    ppermute x10 -> x11, waiting for transfers between devices: 199 us -> 183 us  [side_swap(): return lax.ppermute(value, F, [(j, j ^ 1) for j in range(lax.axis_size(F))])]
    unnamed x85 -> x95, local copies, waits for them, and re-layouts: 26.4 us -> 26.2 us
  transfers between devices with their start and end apart: 69 -> 70, of which waited for: 26 -> 26; matrix products, arithmetic and copies ran while one was open for 34% -> 33% of each run, Pallas kernels for 8% -> 7%
where the time goes in v9:
time: 1020 us; the launch traced here: 1000 us
  waiting for transfers between devices  364 us (36%)
  matrix products  222 us (22%)
  starting transfers between devices  118 us (12%)
  other arithmetic  111 us (11%)
  Pallas kernels  87.5 us (9%)
  local copies, waits for them, and re-layouts  85 us (8%)
  between operations  15.6 us (2%)
    ppermute x11, waiting for transfers between devices, side_swap(): return lax.ppermute(value, F, [(j, j ^ 1) for j in range(lax.axis_size(F))])  183 us
    ppermute x12, waiting for transfers between devices, chip_shift(): return lax.ppermute(value, C, [(i, (i + 2 * k) % n) for i in range(n)])  107 us
    dot_general x5, matrix products, mm_nt(): lax.dot_general(a, b, (((1,), (1,)), ((), ())), preferred_element_type=F32)  80.7 us
    ppermute x24, starting transfers between devices, core_swap(): return lax.ppermute(value, C, [(i, i ^ 1) for i in range(n)])  78.6 us
    dot_general x5, matrix products, mm_tn(): lax.dot_general(a, b, (((0,), (0,)), ((), ())), preferred_element_type=F32)  73.3 us
    dot_general x5, matrix products, mm(): return jnp.dot(a, b, preferred_element_type=F32)  68.1 us
    all_gather x5, waiting for transfers between devices, gather_lines(): return lax.all_gather(block, F, axis=0, axis_index_groups=line_groups())  37.2 us
    pallas_call x1, Pallas kernels, attention_backward(): pl.pallas_call(functools.partial(backward_kernel, heads=heads, rows=rows,...  30.9 us
  transfers between devices with their start and end apart: 70, of which 26 were waited for; matrix products, arithmetic and copies ran while one was open for 33% of the time, Pallas kernels for 7%

profile of v9, /device:TPU:17, one launch (start us, length us, event | category | flops | bytes accessed | tf_op | source)
XLA Modules:
  0.0 1003.5 jit_solution(5173941586480280702)
XLA Ops:
  13.1 31.2 %all-gather.8.cloned.1.call-done.own = bf16[4,256,640]{2,1,0:T(8,128)(2,1)} async-done(((bf16[1,256,640]{2,1,0:T(8,128)(2,1)}), bf16[4,256,640]{2,1,0:T(8,128)(2,1)}) %all-gather.8.cloned.1.call-update) | async-done | bytes 1310736 | tf_op jit(solution)/shard_map/all_gather | solution.py:61
  44.3 9.9 collective-permute-done.4
  63.8 7.0 multiply_reduce_fusion
  72.0 6.9 collective-permute-done.10
  83.3 4.6 copy.50
  87.9 4.6 copy.52
  100.0 8.3 collective-permute-done.6.refs_0_
  119.8 11.1 %multiply_convert_fusion.3.qkv = bf16[2048,640]{1,0:T(8,128)(2,1)} fusion(bf16[2048,2048]{1,0:T(8,128)(2,1)} %get-tuple-element.120, bf16[2048,640]{1,0:T(8,128)(2,1)} %bitcast.189, f32[2048]{0:T(1024)S(1)} %add_rsqrt_fusion), kind=kOutput, calls=%fused_computation.34 | convolution fusion | flops 5371330560 | bytes 13639680 | tf_op jit(solution)/shard_map/dot_general | solution.py:466
  130.9 17.9 %attention_forward.1 = (bf16[2048,512]{1,0:T(8,128)(2,1)}, f32[2048,4]{1,0:T(8,128)}) custom-call(s32[12]{0:T(128)} %concatenate.53.meta, bf16[2048,640]{1,0:T(8,128)(2,1)} %multiply_convert_fusion.3.qkv, s32[2048,1]{1,0:T(8,128)} %copy.49.seg_col, s32[4,1,512]{2,1,0:T(1,128)} %copy-done.21), custom_call_target="tpu_custom_call" | custom-call | flops 4194304 | bytes 16384 | tf_op jit(solution)/shard_map/attention_forward/pallas_call | solution.py:341
  151.7 6.8 convolution_convert_fusion.2
  170.7 43.4 %collective-permute-done.17 = bf16[512,2048]{1,0:T(8,128)(2,1)} collective-permute-done((bf16[512,2048]{1,0:T(8,128)(2,1)}, bf16[512,2048]{1,0:T(8,128)(2,1)}, u32[]{:S(2)}, u32[]{:S(2)}) %collective-permute-start.17) | collective-permute-done | bytes 2097184 | tf_op jit(solution)/shard_map/ppermute | solution.py:104
  214.0 5.6 fusion.11
  219.7 7.7 fusion.17
  236.5 37.4 %collective-permute-done.19 = bf16[512,2048]{1,0:T(8,128)(2,1)} collective-permute-done((bf16[512,2048]{1,0:T(8,128)(2,1)}, bf16[512,2048]{1,0:T(8,128)(2,1)}, u32[]{:S(2)}, u32[]{:S(2)}) %collective-permute-start.19) | collective-permute-done | bytes 2097184 | tf_op jit(solution)/shard_map/ppermute | solution.py:104
  275.7 7.0 pad_maximum_fusion.2
  282.8 10.0 %collective-permute-done.22.refs_0_ = bf16[4,256,1408]{2,1,0:T(8,128)(2,1)S(1)} collective-permute-done((bf16[4,256,1408]{2,1,0:T(8,128)(2,1)}, bf16[4,256,1408]{2,1,0:T(8,128)(2,1)S(1)}, u32[]{:S(2)}, u32[]{:S(2)}) %collective-permute-start.22) | collective-permute-done | bytes 2883616 | tf_op jit(solution)/shard_map/ppermute | solution.py:35
  294.4 5.2 assemble.8
  299.6 55.0 %collective-permute-done.21.refs_0_ = bf16[4,256,1408]{2,1,0:T(8,128)(2,1)} collective-permute-done((bf16[4,256,1408]{2,1,0:T(8,128)(2,1)}, bf16[4,256,1408]{2,1,0:T(8,128)(2,1)}, u32[]{:S(2)}, u32[]{:S(2)}) %collective-permute-start.21) | collective-permute-done | bytes 2883616 | tf_op jit(solution)/shard_map/ppermute | solution.py:35
  354.6 5.2 assemble.7
  359.8 7.0 pad_maximum_fusion.1
  370.7 17.7 %fusion.28 = f32[2048,1408]{1,0:T(8,128)} fusion(bf16[2048,2048]{1,0:T(8,128)(2,1)} %pad_maximum_fusion.1, bf16[2048,1408]{1,0:T(8,128)(2,1)S(1)} %bitcast.178), kind=kOutput, calls=%fused_computation.115 | convolution fusion | flops 11811160064 | bytes 25690112 | tf_op jit(solution)/shard_map/dot_general | solution.py:466
  388.4 11.8 %collective-permute-done.23.refs_0_ = bf16[2,176,2048]{2,1,0:T(8,128)(2,1)S(1)} collective-permute-done((bf16[2,176,2048]{2,1,0:T(8,128)(2,1)S(1)}, bf16[2,176,2048]{2,1,0:T(8,128)(2,1)S(1)}, u32[]{:S(2)}, u32[]{:S(2)}) %collective-permute-start.23) | collective-permute-done | bytes 1441824 | tf_op jit(solution)/shard_map/ppermute | solution.py:35
  400.3 15.7 %fusion.29 = f32[2048,1408]{1,0:T(8,128)} fusion(bf16[2048,2048]{1,0:T(8,128)(2,1)S(1)} %bitcast.164, bf16[2048,1408]{1,0:T(8,128)(2,1)S(1)} %bitcast.182), kind=kOutput, calls=%fused_computation.116 | convolution fusion | flops 11811160064 | bytes 25690112 | tf_op jit(solution)/shard_map/dot_general | solution.py:466
  416.1 15.2 %collective-permute-done.24.refs_1_ = bf16[2,176,2048]{2,1,0:T(8,128)(2,1)} collective-permute-done((bf16[2,176,2048]{2,1,0:T(8,128)(2,1)S(1)}, bf16[2,176,2048]{2,1,0:T(8,128)(2,1)}, u32[]{:S(2)}, u32[]{:S(2)}) %collective-permute-start.24) | collective-permute-done | bytes 1441824 | tf_op jit(solution)/shard_map/ppermute | solution.py:35
  431.3 5.2 assemble.9
  436.5 26.0 %multiply_convert_fusion.1 = (bf16[2048,1408]{1,0:T(8,128)(2,1)}, bf16[2048,1408]{1,0:T(8,128)(2,1)}, bf16[2048,1408]{1,0:T(8,128)(2,1)}) fusion(f32[2048,1408]{1,0:T(8,128)} %fusion.28, f32[2048,1408]{1,0:T(8,128)} %fusion.29, bf16[2048,2048]{1,0:T(8,128)(2,1)} %pad_maximum_fusion.2, bf16[1408,2048]{1,0:T(8,128)(2,1)} %bitcast.169), kind=kOutput, calls=%fused_computation.3 | convolution fusion | flops 11854413824 | bytes 54525952 | tf_op jit(solution)/shard_map/dot_general | solution.py:474
  462.6 19.5 %fusion.30 = f32[2048,2048]{1,0:T(8,128)} fusion(bf16[2048,1408]{1,0:T(8,128)(2,1)} %get-tuple-element.61, bf16[2048,1408]{1,0:T(8,128)(2,1)} %bitcast.179), kind=kOutput, calls=%fused_computation.117 | convolution fusion | flops 11811160064 | bytes 28311552 | tf_op jit(solution)/shard_map/dot_general | solution.py:474
  482.0 21.4 %add_convert_fusion = bf16[2048,2048]{1,0:T(8,128)(2,1)} fusion(f32[2048,2048]{1,0:T(8,128)} %fusion.30, bf16[2048,1408]{1,0:T(8,128)(2,1)} %get-tuple-element.60, bf16[2048,1408]{1,0:T(8,128)(2,1)} %bitcast.177), kind=kOutput, calls=%fused_computation | convolution fusion | flops 11819548672 | bytes 36700160 | tf_op jit(solution)/shard_map/dot_general | solution.py:474
  503.5 4.8 fusion.20
  511.3 4.0 collective-permute-done.25
  518.4 6.2 add_convert_fusion.3
  524.8 17.7 %convolution_convert_fusion.5 = bf16[2048,1408]{1,0:T(8,128)(2,1)S(1)} fusion(bf16[2048,1408]{1,0:T(8,128)(2,1)} %get-tuple-element.60, bf16[512,2048]{1,0:T(8,128)(2,1)} %collective-permute-done.20, bf16[512,2048]{1,0:T(8,128)(2,1)} %collective-permute-done.19, bf16[512,2048]{1,0:T(8,128)(2,1)} %collective-permute-done.18, ...), kind=kOutput, calls=%fused_computation.16 | convolution fusion | flops 11847598080 | bytes 19922944 | tf_op jit(solution)/shard_map/dot_general | solution.py:470
  542.5 21.1 %convolution_convert_fusion.4 = bf16[2048,1408]{1,0:T(8,128)(2,1)} fusion(bf16[2048,1408]{1,0:T(8,128)(2,1)} %get-tuple-element.61, bf16[512,2048]{1,0:T(8,128)(2,1)} %collective-permute-done.20, bf16[512,2048]{1,0:T(8,128)(2,1)} %collective-permute-done.19, bf16[512,2048]{1,0:T(8,128)(2,1)} %collective-permute-done.18, ...), kind=kOutput, calls=%fused_computation.15 | convolution fusion | flops 11847598080 | bytes 19922944 | tf_op jit(solution)/shard_map/dot_general | solution.py:470
  566.8 4.8 collective-permute-done.27
  572.4 5.6 fusion.16
  579.8 18.6 %convolution_convert_fusion.3 = bf16[1408,2048]{1,0:T(8,128)(2,1)} fusion(bf16[2048,1408]{1,0:T(8,128)(2,1)} %get-tuple-element.64, bf16[512,2048]{1,0:T(8,128)(2,1)} %collective-permute-done.9, bf16[512,2048]{1,0:T(8,128)(2,1)} %collective-permute-done.8, bf16[512,2048]{1,0:T(8,128)(2,1)} %collective-permute-done.7, bf16[512,2048]{1,0:T(8,128)(2,1)} %bitcast.15), kind=kOutput, calls=%fused_computation.14 | convolution fusion | flops 11847598080 | bytes 19922944 | tf_op jit(solution)/shard_map/dot_general | solution.py:470
  598.4 16.8 %convolution_convert_fusion.1 = bf16[2048,2048]{1,0:T(8,128)(2,1)} fusion(bf16[2048,1408]{1,0:T(8,128)(2,1)} %get-tuple-element.64, bf16[1408,2048]{1,0:T(8,128)(2,1)S(1)} %bitcast.172), kind=kOutput, calls=%fused_computation.12 | convolution fusion | flops 11815354368 | bytes 19922944 | tf_op jit(solution)/shard_map/dot_general | solution.py:466
  615.2 13.9 %collective-permute-done.30 = bf16[4,256,1408]{2,1,0:T(8,128)(2,1)S(1)} collective-permute-done((bf16[4,256,1408]{2,1,0:T(8,128)(2,1)}, bf16[4,256,1408]{2,1,0:T(8,128)(2,1)S(1)}, u32[]{:S(2)}, u32[]{:S(2)}) %collective-permute-start.30) | collective-permute-done | bytes 2883616 | tf_op jit(solution)/shard_map/ppermute | solution.py:35
  635.9 3.9 collective-permute-done.31
  639.8 6.8 pad_maximum_fusion.3
  646.6 4.8 fusion.19
  656.7 4.3 dynamic-slice_bitcast_fusion
  661.6 6.3 fusion.31.gm
  668.6 4.6 add_convert_fusion.2
  674.5 5.7 convolution_convert_fusion.7
  680.2 39.2 %collective-permute-done.34 = bf16[4,256,1408]{2,1,0:T(8,128)(2,1)S(1)} collective-permute-done((bf16[4,256,1408]{2,1,0:T(8,128)(2,1)S(1)}, bf16[4,256,1408]{2,1,0:T(8,128)(2,1)S(1)}, u32[]{:S(2)}, u32[]{:S(2)}) %collective-permute-start.34) | collective-permute-done | bytes 2883616 | tf_op jit(solution)/shard_map/ppermute | solution.py:35
  723.1 30.9 %attention_backward.1 = bf16[2048,640]{1,0:T(8,128)(2,1)} custom-call(s32[12]{0:T(128)} %concatenate.53.meta, bf16[2048,640]{1,0:T(8,128)(2,1)} %multiply_convert_fusion.3.qkv, s32[2048,1]{1,0:T(8,128)} %copy.49.seg_col, s32[4,1,512]{2,1,0:T(1,128)} %copy-done.21, f32[2048,512]{1,0:T(8,128)} %fusion.31.gm, bf16[2048,512]{1,0:T(8,128)(2,1)} %get-tuple-element.52.mixed, ...), custom_call_target="tpu_custom_call" | custom-call | flops 10485760 | bytes 32768 | tf_op jit(solution)/shard_map/attention_backward/pallas_call | solution.py:369
  756.3 6.6 add_add_fusion
  762.9 7.5 convolution_convert_fusion
  781.3 4.6 fusion.1
  792.9 19.5 %collective-permute-done.41 = bf16[4,64,2048]{2,1,0:T(8,128)(2,1)} collective-permute-done((bf16[4,64,2048]{2,1,0:T(8,128)(2,1)}, bf16[4,64,2048]{2,1,0:T(8,128)(2,1)}, u32[]{:S(2)}, u32[]{:S(2)}) %collective-permute-start.41) | collective-permute-done | bytes 1048608 | tf_op jit(solution)/shard_map/ppermute | solution.py:35
  815.4 10.1 %convolution_convert_fusion.6 = bf16[2048,640]{1,0:T(8,128)(2,1)S(1)} fusion(bf16[2048,2048]{1,0:T(8,128)(2,1)} %get-tuple-element.120, bf16[2048,640]{1,0:T(8,128)(2,1)} %attention_backward.1), kind=kOutput, calls=%fused_computation.55 | convolution fusion | flops 5370019840 | bytes 13631488 | tf_op jit(solution)/shard_map/dot_general | solution.py:470
  827.0 12.1 %collective-permute-done.38 = bf16[512,2048]{1,0:T(8,128)(2,1)} collective-permute-done((bf16[512,2048]{1,0:T(8,128)(2,1)}, bf16[512,2048]{1,0:T(8,128)(2,1)}, u32[]{:S(2)}, u32[]{:S(2)}) %collective-permute-start.38) | collective-permute-done | bytes 2097184 | tf_op jit(solution)/shard_map/ppermute | solution.py:104
  839.1 4.2 fusion.8
  846.1 8.2 collective-permute-done.40
  861.4 10.3 %reduce-scatter.14.cloned.1.call-done = bf16[64,2048]{1,0:T(8,128)(2,1)} async-done(((bf16[256,2048]{1,0:T(8,128)(2,1)}), bf16[64,2048]{1,0:T(8,128)(2,1)}) %reduce-scatter.14.cloned.1.call-update) | async-done | bytes 262160 | tf_op jit(solution)/shard_map/reduce_scatter | solution.py:57
  883.8 28.9 %collective-permute-start.57 = (bf16[176,2048]{1,0:T(8,128)(2,1)}, bf16[176,2048]{1,0:T(8,128)(2,1)}, u32[]{:S(2)}, u32[]{:S(2)}) collective-permute-start(bf16[176,2048]{1,0:T(8,128)(2,1)} %reduce-scatter.10.cloned.1.call-done.refs_0_), channel_id=1, source_target_pairs={{0,8},{8,0},{16,24},{24,16},{1,9},{9,1},{17,25},{25,17},{2,10},{10... | collective-permute-start | bytes 2162696 | tf_op jit(solution)/shard_map/ppermute | solution.py:99
  916.1 11.2 %collective-permute-start.53 = (bf16[256,1408]{0,1:T(8,128)(2,1)}, bf16[256,1408]{0,1:T(8,128)(2,1)S(1)}, u32[]{:S(2)}, u32[]{:S(2)}) collective-permute-start(bf16[256,1408]{0,1:T(8,128)(2,1)} %collective-permute-done.52), channel_id=1, source_target_pairs={{0,8},{8,0},{16,24},{24,16},{1,9},{9,1},{17,25},{25,17},{2,10},{10... | collective-permute-start | bytes 2162696 | tf_op jit(solution)/shard_map/ppermute | solution.py:99
  935.4 6.0 bitcast_multiply_fusion
  941.4 6.2 copy.68
  947.6 6.2 copy.69
  954.4 5.2 finish_rows.1
  964.6 9.8 collective-permute-start.42
  990.1 4.3 finish_columns.5
  (297 shorter events, 182.6 us)
Async XLA Ops:
  7.2 37.1 %all-gather.8.cloned.1.call-start = ((), (), s32[]{:S(2)}) async-start(), calls=%async_computation.5 | async-start | bytes 1638400 | tf_op jit(solution)/shard_map/all_gather | solution.py:61
  7.2 46.9 %collective-permute-start.4 = (bf16[512,2048]{1,0:T(8,128)(2,1)}, bf16[512,2048]{1,0:T(8,128)(2,1)}, u32[]{:S(2)}, u32[]{:S(2)}) collective-permute-start(bf16[512,2048]{1,0:T(8,128)(2,1)} %bitcast.151), channel_id=1, source_target_pairs={{0,16},{8,24},{16,0},{24,8},{1,17},{9,25},{17,1},{25,9},{2,18},{10... | collective-permute-start | bytes 6291464 | tf_op jit(solution)/shard_map/ppermute | solution.py:104
  12.1 102.3 %all-gather.14.cloned.1.call-start = ((), (), s32[]{:S(2)}) async-start(), calls=%async_computation.13 | async-start | bytes 1310720 | tf_op jit(solution)/shard_map/all_gather | solution.py:61
  12.1 51.0 %collective-permute-start.3 = (bf16[512,2048]{1,0:T(8,128)(2,1)}, bf16[512,2048]{1,0:T(8,128)(2,1)}, u32[]{:S(2)}, u32[]{:S(2)}) collective-permute-start(bf16[512,2048]{1,0:T(8,128)(2,1)} %bitcast.152), channel_id=1, source_target_pairs={{0,8},{8,0},{16,24},{24,16},{1,9},{9,1},{17,25},{25,17},{2,10},{10... | collective-permute-start | bytes 6291464 | tf_op jit(solution)/shard_map/ppermute | solution.py:99
  54.1 9.6 collective-permute-start.5
  55.7 5.3 collective-permute-start.1
  59.7 19.2 %collective-permute-start.10 = (bf16[64,2048]{1,0:T(8,128)(2,1)S(1)}, bf16[64,2048]{1,0:T(8,128)(2,1)S(1)}, u32[]{:S(2)}, u32[]{:S(2)}) collective-permute-start(bf16[64,2048]{1,0:T(8,128)(2,1)S(1)} %get-tuple-element.141), channel_id=1, source_target_pairs={{0,0},{1,4},{10,8},{11,12},{20,16},{21,20},{30,24},{31,28}} | collective-permute-start | bytes 786440 | tf_op jit(solution)/shard_map/ppermute | solution.py:176
  61.0 17.9 %collective-permute-start.11 = (bf16[64,2048]{1,0:T(8,128)(2,1)S(1)}, bf16[64,2048]{1,0:T(8,128)(2,1)S(1)}, u32[]{:S(2)}, u32[]{:S(2)}) collective-permute-start(bf16[64,2048]{1,0:T(8,128)(2,1)S(1)} %get-tuple-element.140), channel_id=1, source_target_pairs={{0,1},{1,5},{10,9},{11,13},{20,17},{21,21},{30,25},{31,29}} | collective-permute-start | bytes 786440 | tf_op jit(solution)/shard_map/ppermute | solution.py:176
  61.7 17.2 %collective-permute-start.12 = (bf16[64,2048]{1,0:T(8,128)(2,1)S(1)}, bf16[64,2048]{1,0:T(8,128)(2,1)S(1)}, u32[]{:S(2)}, u32[]{:S(2)}) collective-permute-start(bf16[64,2048]{1,0:T(8,128)(2,1)S(1)} %get-tuple-element.143), channel_id=1, source_target_pairs={{0,2},{1,6},{10,10},{11,14},{20,18},{21,22},{30,26},{31,30}} | collective-permute-start | bytes 786440 | tf_op jit(solution)/shard_map/ppermute | solution.py:176
  63.1 15.9 %collective-permute-start.13 = (bf16[64,2048]{1,0:T(8,128)(2,1)S(1)}, bf16[64,2048]{1,0:T(8,128)(2,1)S(1)}, u32[]{:S(2)}, u32[]{:S(2)}) collective-permute-start(bf16[64,2048]{1,0:T(8,128)(2,1)S(1)} %get-tuple-element.142), channel_id=1, source_target_pairs={{0,3},{1,7},{10,11},{11,15},{20,19},{21,23},{30,27},{31,31}} | collective-permute-start | bytes 786440 | tf_op jit(solution)/shard_map/ppermute | solution.py:176
  70.8 45.9 %collective-permute-start.8 = (bf16[512,2048]{1,0:T(8,128)(2,1)}, bf16[512,2048]{1,0:T(8,128)(2,1)}, u32[]{:S(2)}, u32[]{:S(2)}) collective-permute-start(bf16[512,2048]{1,0:T(8,128)(2,1)} %bitcast.15), channel_id=1, source_target_pairs={{0,16},{8,24},{16,0},{24,8},{1,17},{9,25},{17,1},{25,9},{2,18},{10... | collective-permute-start | bytes 6291464 | tf_op jit(solution)/shard_map/ppermute | solution.py:104
  79.7 149.9 %all-gather.12.cloned.1.call-start = ((), (), s32[]{:S(2)}) async-start(), calls=%async_computation.7 | async-start | bytes 3604480 | tf_op jit(solution)/shard_map/all_gather | solution.py:61
  79.8 28.6 %collective-permute-start.6 = (bf16[4,256,640]{2,1,0:T(8,128)(2,1)}, bf16[4,256,640]{2,1,0:T(8,128)(2,1)}, u32[]{:S(2)}, u32[]{:S(2)}) collective-permute-start(bf16[4,256,640]{2,1,0:T(8,128)(2,1)} %all-gather.8.cloned.1.call-done.own), channel_id=1, source_target_pairs={{0,1},{1,0},{2,3},{3,2},{4,5},{5,4},{6,7},{7,6},{8,9},{9,8},{10,11... | collective-permute-start | bytes 3932168 | tf_op jit(solution)/shard_map/ppermute | solution.py:35
  97.6 136.6 %all-gather.10.cloned.1.call-start = ((), (), s32[]{:S(2)}) async-start(), calls=%async_computation.6 | async-start | bytes 3604480 | tf_op jit(solution)/shard_map/all_gather | solution.py:61
  114.4 34.3 %collective-permute-start.14 = (bf16[4,64,2048]{2,1,0:T(8,128)(2,1)}, bf16[4,64,2048]{2,1,0:T(8,128)(2,1)}, u32[]{:S(2)}, u32[]{:S(2)}) collective-permute-start(bf16[4,64,2048]{2,1,0:T(8,128)(2,1)} %bitcast.198), channel_id=1, source_target_pairs={{0,1},{1,0},{2,3},{3,2},{4,5},{5,4},{6,7},{7,6},{8,9},{9,8},{10,11... | collective-permute-start | bytes 3145736 | tf_op jit(solution)/shard_map/ppermute | solution.py:35
  115.6 36.1 %collective-permute-start.7 = (bf16[512,2048]{1,0:T(8,128)(2,1)}, bf16[512,2048]{1,0:T(8,128)(2,1)}, u32[]{:S(2)}, u32[]{:S(2)}) collective-permute-start(bf16[512,2048]{1,0:T(8,128)(2,1)} %bitcast.15), channel_id=1, source_target_pairs={{0,8},{8,0},{16,24},{24,16},{1,9},{9,1},{17,25},{25,17},{2,10},{10... | collective-permute-start | bytes 6291464 | tf_op jit(solution)/shard_map/ppermute | solution.py:99
  116.7 35.0 %collective-permute-start.9 = (bf16[512,2048]{1,0:T(8,128)(2,1)}, bf16[512,2048]{1,0:T(8,128)(2,1)}, u32[]{:S(2)}, u32[]{:S(2)}) collective-permute-start(bf16[512,2048]{1,0:T(8,128)(2,1)} %collective-permute-done.8), channel_id=1, source_target_pairs={{0,8},{8,0},{16,24},{24,16},{1,9},{9,1},{17,25},{25,17},{2,10},{10... | collective-permute-start | bytes 6291464 | tf_op jit(solution)/shard_map/ppermute | solution.py:99
  160.4 10.3 %collective-permute-start.15 = (bf16[512,2048]{1,0:T(8,128)(2,1)}, bf16[512,2048]{1,0:T(8,128)(2,1)}, u32[]{:S(2)}, u32[]{:S(2)}) collective-permute-start(bf16[512,2048]{1,0:T(8,128)(2,1)} %get-tuple-element.132), channel_id=1, source_target_pairs={{0,8},{8,0},{16,24},{24,16},{1,9},{9,1},{17,25},{25,17},{2,10},{10... | collective-permute-start | bytes 6291464 | tf_op jit(solution)/shard_map/ppermute | solution.py:99
  166.6 47.4 %collective-permute-start.17 = (bf16[512,2048]{1,0:T(8,128)(2,1)}, bf16[512,2048]{1,0:T(8,128)(2,1)}, u32[]{:S(2)}, u32[]{:S(2)}) collective-permute-start(bf16[512,2048]{1,0:T(8,128)(2,1)} %add_convert_fusion.4), channel_id=1, source_target_pairs={{0,16},{8,24},{16,0},{24,8},{1,17},{9,25},{17,1},{25,9},{2,18},{10... | collective-permute-start | bytes 6291464 | tf_op jit(solution)/shard_map/ppermute | solution.py:104
  170.1 196.7 %all-gather.16.cloned.1.call-start = ((), (), s32[]{:S(2)}) async-start(), calls=%async_computation.14 | async-start | bytes 3604480 | tf_op jit(solution)/shard_map/all_gather | solution.py:61
  227.4 46.5 %collective-permute-start.19 = (bf16[512,2048]{1,0:T(8,128)(2,1)}, bf16[512,2048]{1,0:T(8,128)(2,1)}, u32[]{:S(2)}, u32[]{:S(2)}) collective-permute-start(bf16[512,2048]{1,0:T(8,128)(2,1)} %get-tuple-element.117), channel_id=1, source_target_pairs={{0,16},{8,24},{16,0},{24,8},{1,17},{9,25},{17,1},{25,9},{2,18},{10... | collective-permute-start | bytes 6291464 | tf_op jit(solution)/shard_map/ppermute | solution.py:104
  229.6 493.5 %reduce-scatter.6.cloned.1.call-start = ((), (), s32[]{:S(2)}) async-start(), calls=%async_computation.8 | async-start | bytes 3604480 | tf_op jit(solution)/shard_map/reduce_scatter | solution.py:57
  229.6 63.2 %collective-permute-start.22 = (bf16[4,256,1408]{2,1,0:T(8,128)(2,1)}, bf16[4,256,1408]{2,1,0:T(8,128)(2,1)S(1)}, u32[]{:S(2)}, u32[]{:S(2)}) collective-permute-start(bf16[4,256,1408]{2,1,0:T(8,128)(2,1)} %all-gather.12.cloned.1.call-done.own), channel_id=1, source_target_pairs={{0,1},{1,0},{2,3},{3,2},{4,5},{5,4},{6,7},{7,6},{8,9},{9,8},{10,11... | collective-permute-start | bytes 8650760 | tf_op jit(solution)/shard_map/ppermute | solution.py:35
  234.2 120.4 %collective-permute-start.21 = (bf16[4,256,1408]{2,1,0:T(8,128)(2,1)}, bf16[4,256,1408]{2,1,0:T(8,128)(2,1)}, u32[]{:S(2)}, u32[]{:S(2)}) collective-permute-start(bf16[4,256,1408]{2,1,0:T(8,128)(2,1)} %all-gather.10.cloned.1.call-done.own), channel_id=1, source_target_pairs={{0,1},{1,0},{2,3},{3,2},{4,5},{5,4},{6,7},{7,6},{8,9},{9,8},{10,11... | collective-permute-start | bytes 8650760 | tf_op jit(solution)/shard_map/ppermute | solution.py:35
  235.4 124.4 %collective-permute-start.18 = (bf16[512,2048]{1,0:T(8,128)(2,1)}, bf16[512,2048]{1,0:T(8,128)(2,1)}, u32[]{:S(2)}, u32[]{:S(2)}) collective-permute-start(bf16[512,2048]{1,0:T(8,128)(2,1)} %get-tuple-element.117), channel_id=1, source_target_pairs={{0,8},{8,0},{16,24},{24,16},{1,9},{9,1},{17,25},{25,17},{2,10},{10... | collective-permute-start | bytes 6291464 | tf_op jit(solution)/shard_map/ppermute | solution.py:99
  273.9 86.0 %collective-permute-start.20 = (bf16[512,2048]{1,0:T(8,128)(2,1)}, bf16[512,2048]{1,0:T(8,128)(2,1)}, u32[]{:S(2)}, u32[]{:S(2)}) collective-permute-start(bf16[512,2048]{1,0:T(8,128)(2,1)} %collective-permute-done.19), channel_id=1, source_target_pairs={{0,8},{8,0},{16,24},{24,16},{1,9},{9,1},{17,25},{25,17},{2,10},{10... | collective-permute-start | bytes 6291464 | tf_op jit(solution)/shard_map/ppermute | solution.py:99
  369.2 31.1 %collective-permute-start.23 = (bf16[2,176,2048]{2,1,0:T(8,128)(2,1)S(1)}, bf16[2,176,2048]{2,1,0:T(8,128)(2,1)S(1)}, u32[]{:S(2)}, u32[]{:S(2)}) collective-permute-start(bf16[2,176,2048]{2,1,0:T(8,128)(2,1)S(1)} %get-tuple-element.139), channel_id=1, source_target_pairs={{0,1},{1,0},{2,3},{3,2},{4,5},{5,4},{6,7},{7,6},{8,9},{9,8},{10,11... | collective-permute-start | bytes 4325384 | tf_op jit(solution)/shard_map/ppermute | solution.py:35
  370.5 60.8 %collective-permute-start.24 = (bf16[2,176,2048]{2,1,0:T(8,128)(2,1)S(1)}, bf16[2,176,2048]{2,1,0:T(8,128)(2,1)}, u32[]{:S(2)}, u32[]{:S(2)}) collective-permute-start(bf16[2,176,2048]{2,1,0:T(8,128)(2,1)S(1)} %get-tuple-element.138), channel_id=1, source_target_pairs={{0,1},{1,0},{2,3},{3,2},{4,5},{5,4},{6,7},{7,6},{8,9},{9,8},{10,11... | collective-permute-start | bytes 4325384 | tf_op jit(solution)/shard_map/ppermute | solution.py:35
  508.3 7.0 collective-permute-start.25
  511.3 7.1 collective-permute-start.26
  524.6 47.0 %collective-permute-start.27 = (bf16[512,2048]{1,0:T(8,128)(2,1)}, bf16[512,2048]{1,0:T(8,128)(2,1)S(1)}, u32[]{:S(2)}, u32[]{:S(2)}) collective-permute-start(bf16[512,2048]{1,0:T(8,128)(2,1)} %get-tuple-element.128), channel_id=1, source_target_pairs={{0,16},{8,24},{16,0},{24,8},{1,17},{9,25},{17,1},{25,9},{2,18},{10... | collective-permute-start | bytes 6291464 | tf_op jit(solution)/shard_map/ppermute | solution.py:104
  565.5 63.6 %collective-permute-start.30 = (bf16[4,256,1408]{2,1,0:T(8,128)(2,1)}, bf16[4,256,1408]{2,1,0:T(8,128)(2,1)S(1)}, u32[]{:S(2)}, u32[]{:S(2)}) collective-permute-start(bf16[4,256,1408]{2,1,0:T(8,128)(2,1)} %dynamic-slice_bitcast_fusion.2), channel_id=1, source_target_pairs={{0,1},{1,0},{2,3},{3,2},{4,5},{5,4},{6,7},{7,6},{8,9},{9,8},{10,11... | collective-permute-start | bytes 8650760 | tf_op jit(solution)/shard_map/ppermute | solution.py:35
  578.0 56.3 %collective-permute-start.29 = (bf16[512,2048]{1,0:T(8,128)(2,1)}, bf16[512,2048]{1,0:T(8,128)(2,1)}, u32[]{:S(2)}, u32[]{:S(2)}) collective-permute-start(bf16[512,2048]{1,0:T(8,128)(2,1)} %get-tuple-element.115), channel_id=1, source_target_pairs={{0,16},{8,24},{16,0},{24,8},{1,17},{9,25},{17,1},{25,9},{2,18},{10... | collective-permute-start | bytes 6291464 | tf_op jit(solution)/shard_map/ppermute | solution.py:104
  578.3 57.7 %collective-permute-start.28 = (bf16[512,2048]{1,0:T(8,128)(2,1)}, bf16[512,2048]{1,0:T(8,128)(2,1)}, u32[]{:S(2)}, u32[]{:S(2)}) collective-permute-start(bf16[512,2048]{1,0:T(8,128)(2,1)} %get-tuple-element.115), channel_id=1, source_target_pairs={{0,8},{8,0},{16,24},{24,16},{1,9},{9,1},{17,25},{25,17},{2,10},{10... | collective-permute-start | bytes 6291464 | tf_op jit(solution)/shard_map/ppermute | solution.py:99
  634.3 5.5 collective-permute-start.31
  635.9 176.5 %reduce-scatter.8.cloned.1.call-start = ((), (), s32[]{:S(2)}) async-start(), calls=%async_computation.9 | async-start | bytes 3604480 | tf_op jit(solution)/shard_map/reduce_scatter | solution.py:57
  651.4 17.2 %collective-permute-start.32 = (bf16[512,2048]{1,0:T(8,128)(2,1)}, bf16[512,2048]{1,0:T(8,128)(2,1)}, u32[]{:S(2)}, u32[]{:S(2)}) collective-permute-start(bf16[512,2048]{1,0:T(8,128)(2,1)} %get-tuple-element.127), channel_id=1, source_target_pairs={{0,8},{8,0},{16,24},{24,16},{1,9},{9,1},{17,25},{25,17},{2,10},{10... | collective-permute-start | bytes 6291464 | tf_op jit(solution)/shard_map/ppermute | solution.py:99
  655.4 64.1 %collective-permute-start.34 = (bf16[4,256,1408]{2,1,0:T(8,128)(2,1)S(1)}, bf16[4,256,1408]{2,1,0:T(8,128)(2,1)S(1)}, u32[]{:S(2)}, u32[]{:S(2)}) collective-permute-start(bf16[4,256,1408]{2,1,0:T(8,128)(2,1)S(1)} %dynamic-slice_bitcast_fusion.1), channel_id=1, source_target_pairs={{0,1},{1,0},{2,3},{3,2},{4,5},{5,4},{6,7},{7,6},{8,9},{9,8},{10,11... | collective-permute-start | bytes 8650760 | tf_op jit(solution)/shard_map/ppermute | solution.py:35
  661.0 120.2 %collective-permute-start.39 = (bf16[4,176,2048]{2,1,0:T(8,128)(2,1)}, bf16[4,176,2048]{2,1,0:T(8,128)(2,1)}, u32[]{:S(2)}, u32[]{:S(2)}) collective-permute-start(bf16[4,176,2048]{2,1,0:T(8,128)(2,1)} %dynamic-slice_bitcast_fusion), channel_id=1, source_target_pairs={{0,1},{1,0},{2,3},{3,2},{4,5},{5,4},{6,7},{7,6},{8,9},{9,8},{10,11... | collective-permute-start | bytes 8650760 | tf_op jit(solution)/shard_map/ppermute | solution.py:35
  668.0 88.3 %collective-permute-start.35 = (bf16[512,2048]{1,0:T(8,128)(2,1)}, bf16[512,2048]{1,0:T(8,128)(2,1)}, u32[]{:S(2)}, u32[]{:S(2)}) collective-permute-start(bf16[512,2048]{1,0:T(8,128)(2,1)} %get-tuple-element.126), channel_id=1, source_target_pairs={{0,8},{8,0},{16,24},{24,16},{1,9},{9,1},{17,25},{25,17},{2,10},{10... | collective-permute-start | bytes 6291464 | tf_op jit(solution)/shard_map/ppermute | solution.py:99
  673.3 80.7 %collective-permute-start.33 = (bf16[512,2048]{1,0:T(8,128)(2,1)}, bf16[512,2048]{1,0:T(8,128)(2,1)}, u32[]{:S(2)}, u32[]{:S(2)}) collective-permute-start(bf16[512,2048]{1,0:T(8,128)(2,1)} %add_convert_fusion.2), channel_id=1, source_target_pairs={{0,16},{8,24},{16,0},{24,8},{1,17},{9,25},{17,1},{25,9},{2,18},{10... | collective-permute-start | bytes 6291464 | tf_op jit(solution)/shard_map/ppermute | solution.py:104
  723.0 131.3 %reduce-scatter.10.cloned.1.call-start = ((), (), s32[]{:S(2)}) async-start(), calls=%async_computation.10 | async-start | bytes 3604480 | tf_op jit(solution)/shard_map/reduce_scatter | solution.py:57
  772.5 5.3 collective-permute-start.37
  785.9 85.7 %reduce-scatter.14.cloned.1.call-start = ((), (), s32[]{:S(2)}) async-start(), calls=%async_computation.12 | async-start | bytes 1310720 | tf_op jit(solution)/shard_map/reduce_scatter | solution.py:57
  788.3 24.0 %collective-permute-start.41 = (bf16[4,64,2048]{2,1,0:T(8,128)(2,1)}, bf16[4,64,2048]{2,1,0:T(8,128)(2,1)}, u32[]{:S(2)}, u32[]{:S(2)}) collective-permute-start(bf16[4,64,2048]{2,1,0:T(8,128)(2,1)} %dynamic-slice_bitcast_fusion.4), channel_id=1, source_target_pairs={{0,1},{1,0},{2,3},{3,2},{4,5},{5,4},{6,7},{7,6},{8,9},{9,8},{10,11... | collective-permute-start | bytes 3145736 | tf_op jit(solution)/shard_map/ppermute | solution.py:35
  790.4 36.6 %collective-permute-start.36 = (bf16[512,2048]{1,0:T(8,128)(2,1)}, bf16[512,2048]{1,0:T(8,128)(2,1)}, u32[]{:S(2)}, u32[]{:S(2)}) collective-permute-start(bf16[512,2048]{1,0:T(8,128)(2,1)} %get-tuple-element.124), channel_id=1, source_target_pairs={{0,8},{8,0},{16,24},{24,16},{1,9},{9,1},{17,25},{25,17},{2,10},{10... | collective-permute-start | bytes 6291464 | tf_op jit(solution)/shard_map/ppermute | solution.py:99
  791.7 47.4 %collective-permute-start.38 = (bf16[512,2048]{1,0:T(8,128)(2,1)}, bf16[512,2048]{1,0:T(8,128)(2,1)}, u32[]{:S(2)}, u32[]{:S(2)}) collective-permute-start(bf16[512,2048]{1,0:T(8,128)(2,1)} %add_convert_fusion.1), channel_id=1, source_target_pairs={{0,16},{8,24},{16,0},{24,8},{1,17},{9,25},{17,1},{25,9},{2,18},{10... | collective-permute-start | bytes 6291464 | tf_op jit(solution)/shard_map/ppermute | solution.py:104
  815.4 144.2 %reduce-scatter.12.cloned.1.call-start = ((), (), s32[]{:S(2)}) async-start(), calls=%async_computation.11 | async-start | bytes 1638400 | tf_op jit(solution)/shard_map/reduce_scatter | solution.py:57
  825.7 28.6 %collective-permute-start.40 = (bf16[4,256,640]{2,1,0:T(8,128)(2,1)S(1)}, bf16[4,256,640]{2,1,0:T(8,128)(2,1)}, u32[]{:S(2)}, u32[]{:S(2)}) collective-permute-start(bf16[4,256,640]{2,1,0:T(8,128)(2,1)S(1)} %dynamic-slice_bitcast_fusion.3), channel_id=1, source_target_pairs={{0,1},{1,0},{2,3},{3,2},{4,5},{5,4},{6,7},{7,6},{8,9},{9,8},{10,11... | collective-permute-start | bytes 3932168 | tf_op jit(solution)/shard_map/ppermute | solution.py:35
  857.4 26.4 %collective-permute-start.51 = (bf16[256,1408]{0,1:T(8,128)(2,1)}, bf16[256,1408]{0,1:T(8,128)(2,1)}, u32[]{:S(2)}, u32[]{:S(2)}) collective-permute-start(bf16[256,1408]{0,1:T(8,128)(2,1)} %reduce-scatter.6.cloned.1.call-done), channel_id=1, source_target_pairs={{0,8},{8,0},{16,24},{24,16},{1,9},{9,1},{17,25},{25,17},{2,10},{10... | collective-permute-start | bytes 2162696 | tf_op jit(solution)/shard_map/ppermute | solution.py:99
  860.1 53.7 %collective-permute-start.52 = (bf16[256,1408]{0,1:T(8,128)(2,1)}, bf16[256,1408]{0,1:T(8,128)(2,1)}, u32[]{:S(2)}, u32[]{:S(2)}) collective-permute-start(bf16[256,1408]{0,1:T(8,128)(2,1)} %reduce-scatter.6.cloned.1.call-done), channel_id=1, source_target_pairs={{0,16},{8,24},{16,0},{24,8},{1,17},{9,25},{17,1},{25,9},{2,18},{10... | collective-permute-start | bytes 2162696 | tf_op jit(solution)/shard_map/ppermute | solution.py:104
  871.6 9.1 collective-permute-start.45
  873.8 7.6 collective-permute-start.46
  874.5 52.8 %collective-permute-start.54 = (bf16[256,1408]{0,1:T(8,128)(2,1)}, bf16[256,1408]{0,1:T(8,128)(2,1)S(1)}, u32[]{:S(2)}, u32[]{:S(2)}) collective-permute-start(bf16[256,1408]{0,1:T(8,128)(2,1)} %reduce-scatter.8.cloned.1.call-done), channel_id=1, source_target_pairs={{0,8},{8,0},{16,24},{24,16},{1,9},{9,1},{17,25},{25,17},{2,10},{10... | collective-permute-start | bytes 2162696 | tf_op jit(solution)/shard_map/ppermute | solution.py:99
  882.1 45.1 %collective-permute-start.55 = (bf16[256,1408]{0,1:T(8,128)(2,1)}, bf16[256,1408]{0,1:T(8,128)(2,1)S(1)}, u32[]{:S(2)}, u32[]{:S(2)}) collective-permute-start(bf16[256,1408]{0,1:T(8,128)(2,1)} %reduce-scatter.8.cloned.1.call-done), channel_id=1, source_target_pairs={{0,16},{8,24},{16,0},{24,8},{1,17},{9,25},{17,1},{25,9},{2,18},{10... | collective-permute-start | bytes 2162696 | tf_op jit(solution)/shard_map/ppermute | solution.py:104
  883.4 32.7 %collective-permute-start.58 = (bf16[176,2048]{1,0:T(8,128)(2,1)}, bf16[176,2048]{1,0:T(8,128)(2,1)}, u32[]{:S(2)}, u32[]{:S(2)}) collective-permute-start(bf16[176,2048]{1,0:T(8,128)(2,1)} %reduce-scatter.10.cloned.1.call-done.refs_0_), channel_id=1, source_target_pairs={{0,16},{8,24},{16,0},{24,8},{1,17},{9,25},{17,1},{25,9},{2,18},{10... | collective-permute-start | bytes 2162696 | tf_op jit(solution)/shard_map/ppermute | solution.py:104
  883.8 70.6 %collective-permute-start.57 = (bf16[176,2048]{1,0:T(8,128)(2,1)}, bf16[176,2048]{1,0:T(8,128)(2,1)}, u32[]{:S(2)}, u32[]{:S(2)}) collective-permute-start(bf16[176,2048]{1,0:T(8,128)(2,1)} %reduce-scatter.10.cloned.1.call-done.refs_0_), channel_id=1, source_target_pairs={{0,8},{8,0},{16,24},{24,16},{1,9},{9,1},{17,25},{25,17},{2,10},{10... | collective-permute-start | bytes 2162696 | tf_op jit(solution)/shard_map/ppermute | solution.py:99
  913.9 14.0 %collective-permute-start.49 = (bf16[256,2048]{1,0:T(8,128)(2,1)S(1)}, bf16[256,2048]{1,0:T(8,128)(2,1)S(1)}, u32[]{:S(2)}, u32[]{:S(2)}) collective-permute-start(bf16[256,2048]{1,0:T(8,128)(2,1)S(1)} %constant_dynamic-update-slice_fusion), channel_id=1, source_target_pairs={{0,16},{1,17},{10,26},{11,27},{20,4},{21,5},{30,14},{31,15}} | collective-permute-start | bytes 3145736 | tf_op jit(solution)/shard_map/ppermute | solution.py:189
  916.1 14.5 %collective-permute-start.53 = (bf16[256,1408]{0,1:T(8,128)(2,1)}, bf16[256,1408]{0,1:T(8,128)(2,1)S(1)}, u32[]{:S(2)}, u32[]{:S(2)}) collective-permute-start(bf16[256,1408]{0,1:T(8,128)(2,1)} %collective-permute-done.52), channel_id=1, source_target_pairs={{0,8},{8,0},{16,24},{24,16},{1,9},{9,1},{17,25},{25,17},{2,10},{10... | collective-permute-start | bytes 2162696 | tf_op jit(solution)/shard_map/ppermute | solution.py:99
  927.3 27.1 %collective-permute-start.59 = (bf16[176,2048]{1,0:T(8,128)(2,1)}, bf16[176,2048]{1,0:T(8,128)(2,1)}, u32[]{:S(2)}, u32[]{:S(2)}) collective-permute-start(bf16[176,2048]{1,0:T(8,128)(2,1)} %collective-permute-done.58.refs_2_), channel_id=1, source_target_pairs={{0,8},{8,0},{16,24},{24,16},{1,9},{9,1},{17,25},{25,17},{2,10},{10... | collective-permute-start | bytes 2162696 | tf_op jit(solution)/shard_map/ppermute | solution.py:99
  929.3 32.1 %collective-permute-start.50 = (bf16[256,2048]{1,0:T(8,128)(2,1)}, bf16[256,2048]{1,0:T(8,128)(2,1)}, u32[]{:S(2)}, u32[]{:S(2)}) collective-permute-start(bf16[256,2048]{1,0:T(8,128)(2,1)} %add.243), channel_id=1, source_target_pairs={{0,8},{16,24},{1,9},{17,25},{10,2},{26,18},{11,3},{27,19},{4,12},{... | collective-permute-start | bytes 3145736 | tf_op jit(solution)/shard_map/ppermute | solution.py:196
  959.6 16.2 %collective-permute-start.43 = (bf16[256,640]{1,0:T(8,128)(2,1)}, bf16[256,640]{1,0:T(8,128)(2,1)S(1)}, u32[]{:S(2)}, u32[]{:S(2)}) collective-permute-start(bf16[256,640]{1,0:T(8,128)(2,1)} %reduce-scatter.12.cloned.1.call-done), channel_id=1, source_target_pairs={{0,16},{8,24},{16,0},{24,8},{1,17},{9,25},{17,1},{25,9},{2,18},{10... | collective-permute-start | bytes 983048 | tf_op jit(solution)/shard_map/ppermute | solution.py:104
  964.6 15.3 %collective-permute-start.42 = (bf16[256,640]{1,0:T(8,128)(2,1)S(1)}, bf16[256,640]{1,0:T(8,128)(2,1)S(1)}, u32[]{:S(2)}, u32[]{:S(2)}) collective-permute-start(bf16[256,640]{1,0:T(8,128)(2,1)S(1)} %copy-done.20), channel_id=1, source_target_pairs={{0,8},{8,0},{16,24},{24,16},{1,9},{9,1},{17,25},{25,17},{2,10},{10... | collective-permute-start | bytes 983048 | tf_op jit(solution)/shard_map/ppermute | solution.py:99
  975.8 5.5 collective-permute-start.44
  (50 other events, 905.1 us)
Sparse Core Ops, SparseCore 0:
  12.2 32.0 all-gather.7
  79.8 34.5 all-gather.13
  116.5 57.7 all-gather.11
  176.4 57.7 all-gather.9
  235.6 57.7 all-gather.15
  636.0 56.6 reduce-scatter.5
  723.1 57.9 reduce-scatter.7
  786.0 57.4 reduce-scatter.9
  845.8 25.7 reduce-scatter.13
  874.6 37.3 reduce-scatter.11
